TPU v7x, 32 devices: a whole 2x2x4 slice. The times are simulated.
32 devices in a mesh: fsdp: 8 (over z, y), tp: 4 (over x, core).
Axes of the slice: x: 2, y: 2, z: 4, core: 2. Of those that a mesh axis runs over, the one named last changes fastest.
Arguments:
- tokens: bfloat16 [16384, 768], P(('fsdp', 'tp')), may hold values from -6 to 6
- pass_ids: int32 [16384], P(('fsdp', 'tp')), may hold values from 0 to 4
- prefix: int32 [8], P('fsdp'), may hold values from 0 to 2047
- cotangent: bfloat16 [16384, 768], P(('fsdp', 'tp')), may hold values from -6 to 6
- qkv_weight: bfloat16 [3, 768, 768], P(None, 'fsdp', 'tp'), may hold values from -0.21875 to 0.21875
- out_weight: bfloat16 [768, 768], P('tp', 'fsdp'), may hold values from -1.75 to 1.75
- fc1_weight: bfloat16 [768, 3072], P('fsdp', 'tp'), may hold values from -0.21875 to 0.21875
- fc2_weight: bfloat16 [3072, 768], P('tp', 'fsdp'), may hold values from -0.109375 to 0.109375
- ln1_gain: float32 [768], replicated, may hold values from 0.1 to 1.9
- ln1_bias: float32 [768], replicated, may hold values from -2 to 2
- qv_bias: float32 [2, 768], replicated, may hold values from -2 to 2
- out_bias: float32 [768], replicated, may hold values from -2 to 2
- ln2_gain: float32 [768], replicated, may hold values from 0.1 to 1.9
- ln2_bias: float32 [768], replicated, may hold values from -2 to 2
- fc1_bias: float32 [3072], replicated, may hold values from -3 to 3
- fc2_bias: float32 [768], replicated, may hold values from -2 to 2
- pass_table: float32 [5, 768], replicated, may hold values from -3 to 3
Outputs:
- activations: bfloat16 [16384, 768], P(('fsdp', 'tp'))
- input_grad: float32 [16384, 768], P(('fsdp', 'tp'))
- qkv_grad: float32 [3, 768, 768], P(None, 'fsdp', 'tp')
- out_grad: float32 [768, 768], P('tp', 'fsdp')
- fc1_grad: float32 [768, 3072], P('fsdp', 'tp')
- fc2_grad: float32 [3072, 768], P('tp', 'fsdp')
- ln1_gain_grad: float32 [768], replicated
- ln1_bias_grad: float32 [768], replicated
- qv_bias_grad: float32 [2, 768], replicated
- out_bias_grad: float32 [768], replicated
- ln2_gain_grad: float32 [768], replicated
- ln2_bias_grad: float32 [768], replicated
- fc1_bias_grad: float32 [3072], replicated
- fc2_bias_grad: float32 [768], replicated
- pass_table_grad: float32 [5, 768], replicated
All inputs are finite; a program needn't handle non-finite values.
Results may differ from a plain program's by a relative error of at most 0.009.
Values may be sent and summed in bfloat16 or wider, within the bound.
A program may use at most 128 MiB of HBM per device.

v0:
```python
from functools import partial

import jax
import jax.numpy as jnp
from jax import lax
from jax.sharding import PartitionSpec as P

HD = 64
NPASS = 5
QBLOCK = 512


HIGH = lax.Precision.HIGHEST
EPS = 1e-05
NEG_FILL = -1e30


def norm_forward(rows_in, gain, shift):
    center = rows_in - jnp.mean(rows_in, axis=-1, keepdims=True)
    scale_inv = lax.rsqrt(jnp.mean(center * center, axis=-1, keepdims=True) + EPS)
    unit_rows = center * scale_inv
    return (unit_rows * gain + shift, unit_rows, scale_inv)


def norm_backward(grad_out, unit_rows, scale_inv, gain):
    grad_unit = grad_out * gain
    first_mean = jnp.mean(grad_unit, axis=-1, keepdims=True)
    second_mean = jnp.mean(grad_unit * unit_rows, axis=-1, keepdims=True)
    grad_rows = scale_inv * (grad_unit - first_mean - unit_rows * second_mean)
    return (grad_rows, jnp.sum(grad_out * unit_rows, axis=0), jnp.sum(grad_out, axis=0))


def matmul_nt(left, right):
    return lax.dot_general(
        left, right, (((1,), (1,)), ((), ())), preferred_element_type=jnp.float32
    )


def matmul_tn(left, right):
    return lax.dot_general(
        left, right, (((0,), (0,)), ((), ())), preferred_element_type=jnp.float32
    )


def block_scores(query_block, keys_all, row_start, prefix_len, scale):
    raw = (
        jnp.einsum("qhe,khe->hqk", query_block, keys_all, preferred_element_type=jnp.float32)
        * scale
    )
    row_ids = row_start + jnp.arange(query_block.shape[0], dtype=jnp.int32)
    col_ids = jnp.arange(keys_all.shape[0], dtype=jnp.int32)
    allowed = (col_ids[None, :] <= row_ids[:, None]) | (col_ids[None, :] < prefix_len)
    return jnp.where(allowed[None], raw, NEG_FILL)


def attend_forward(queries, keys_all, values_all, prefix_len, scale):
    seq_len, heads_here, head_size = queries.shape
    block_count = seq_len // QBLOCK
    query_blocks = queries.reshape(block_count, QBLOCK, heads_here, head_size)
    block_starts = jnp.arange(block_count, dtype=jnp.int32) * QBLOCK

    def one_block(item):
        query_block, row_start = item
        masked = block_scores(query_block, keys_all, row_start, prefix_len, scale)
        peak = jnp.max(masked, axis=-1, keepdims=True)
        expo = jnp.exp(masked - peak)
        total_mass = jnp.sum(expo, axis=-1, keepdims=True)
        probs_low = (expo / total_mass).astype(jnp.bfloat16)
        out_block = jnp.einsum(
            "hqk,khe->qhe", probs_low, values_all, preferred_element_type=jnp.float32
        )
        return (out_block.astype(jnp.bfloat16), (peak + jnp.log(total_mass))[..., 0])

    outputs, log_mass = lax.map(one_block, (query_blocks, block_starts))
    return (outputs.reshape(seq_len, heads_here * head_size), log_mass)


def attend_backward(queries, keys_all, values_all, grad_mixed, log_mass, prefix_len, scale):
    seq_len, heads_here, head_size = queries.shape
    block_count = seq_len // QBLOCK
    query_blocks = queries.reshape(block_count, QBLOCK, heads_here, head_size)
    grad_blocks = grad_mixed.reshape(block_count, QBLOCK, heads_here, head_size)
    block_starts = jnp.arange(block_count, dtype=jnp.int32) * QBLOCK

    def one_block(carry, item):
        grad_keys, grad_values = carry
        query_block, grad_block, block_mass, row_start = item
        masked = block_scores(query_block, keys_all, row_start, prefix_len, scale)
        probs = jnp.exp(masked - block_mass[..., None])
        probs_low = probs.astype(jnp.bfloat16)
        grad_values = grad_values + jnp.einsum(
            "hqk,qhe->khe", probs_low, grad_block, preferred_element_type=jnp.float32
        )
        grad_probs = jnp.einsum(
            "qhe,khe->hqk", grad_block, values_all, preferred_element_type=jnp.float32
        )
        inner_sum = jnp.sum(probs * grad_probs, axis=-1, keepdims=True)
        grad_scores = (probs * (grad_probs - inner_sum)).astype(jnp.bfloat16)
        grad_query = (
            jnp.einsum("hqk,khe->qhe", grad_scores, keys_all, preferred_element_type=jnp.float32)
            * scale
        )
        grad_keys = (
            grad_keys
            + jnp.einsum(
                "hqk,qhe->khe", grad_scores, query_block, preferred_element_type=jnp.float32
            )
            * scale
        )
        return ((grad_keys, grad_values), grad_query)

    zero_state = jnp.zeros(keys_all.shape, jnp.float32)
    (grad_keys, grad_values), grad_queries = lax.scan(
        one_block, (zero_state, zero_state), (query_blocks, grad_blocks, log_mass, block_starts)
    )
    return (grad_queries.reshape(seq_len, heads_here, head_size), grad_keys, grad_values)


def on_device(
    tokens,
    pass_ids,
    prefix,
    cotangent,
    qkv_weight,
    out_weight,
    fc1_weight,
    fc2_weight,
    ln1_gain,
    ln1_bias,
    qv_bias,
    out_bias,
    ln2_gain,
    ln2_bias,
    fc1_bias,
    fc2_bias,
    pass_table,
):
    tp_count = lax.axis_size("tp")
    tp_rank = lax.axis_index("tp")
    local_rows = tokens.shape[0]
    seq_len = local_rows * tp_count
    cols_here = qkv_weight.shape[2]
    heads_here = cols_here // HD
    scale = HD ** (-0.5)
    prefix_len = prefix[0]
    gelu_tanh = partial(jax.nn.gelu, approximate=True)
    qkv_full, out_full, fc1_part, fc2_part = (
        lax.all_gather(qkv_weight, "fsdp", axis=1, tiled=True),
        lax.all_gather(out_weight, "fsdp", axis=1, tiled=True),
        lax.all_gather(fc1_weight, "fsdp", axis=0, tiled=True),
        lax.all_gather(fc2_weight, "fsdp", axis=1, tiled=True),
    )
    hidden_here = fc1_part.shape[1]
    qv_here = lax.dynamic_slice_in_dim(qv_bias, tp_rank * cols_here, cols_here, 1)
    one_hot = (pass_ids[:, None] == jnp.arange(NPASS, dtype=jnp.int32)[None, :]).astype(jnp.float32)
    block_in = tokens.astype(jnp.float32) + jnp.dot(
        one_hot, pass_table, precision=HIGH, preferred_element_type=jnp.float32
    )
    normed, unit_one, inv_one = norm_forward(block_in, ln1_gain, ln1_bias)
    normed_all = lax.all_gather(normed.astype(jnp.bfloat16), "tp", axis=0, tiled=True)
    projected = jnp.einsum("rd,kdc->krc", normed_all, qkv_full, preferred_element_type=jnp.float32)
    queries = (projected[0] + qv_here[0]).astype(jnp.bfloat16).reshape(seq_len, heads_here, HD)
    keys_all = projected[1].astype(jnp.bfloat16).reshape(seq_len, heads_here, HD)
    values_all = (projected[2] + qv_here[1]).astype(jnp.bfloat16).reshape(seq_len, heads_here, HD)
    mixed, log_mass = attend_forward(queries, keys_all, values_all, prefix_len, scale)
    middle = (
        block_in
        + lax.psum_scatter(
            jnp.dot(mixed, out_full, preferred_element_type=jnp.float32),
            "tp",
            scatter_dimension=0,
            tiled=True,
        )
        + out_bias
    )
    normed_two, unit_two, inv_two = norm_forward(middle, ln2_gain, ln2_bias)
    normed_two = normed_two.astype(jnp.bfloat16)
    grad_top = cotangent.astype(jnp.float32)
    fc1_bias_here = lax.dynamic_slice_in_dim(fc1_bias, tp_rank * hidden_here, hidden_here, 0)
    normed_rows = lax.all_gather(normed_two, "tp", axis=0, tiled=True)
    before = jnp.dot(normed_rows, fc1_part, preferred_element_type=jnp.float32) + fc1_bias_here
    hidden = gelu_tanh(before).astype(jnp.bfloat16)
    result = (
        middle
        + lax.psum_scatter(
            jnp.dot(
                lax.slice_in_dim(hidden, 0, local_rows * lax.axis_size("tp"), axis=0),
                fc2_part,
                preferred_element_type=jnp.float32,
            ).astype(jnp.bfloat16),
            "tp",
            scatter_dimension=0,
            tiled=True,
        ).astype(jnp.float32)
        + fc2_bias
    )
    grad_rows = lax.all_gather(cotangent, "tp", axis=0, tiled=True)
    grad_hidden = matmul_nt(grad_rows, fc2_part)
    grad_before = jax.vjp(gelu_tanh, before)[1](grad_hidden)[0].astype(jnp.bfloat16)
    grad_fc1_bias = lax.dynamic_update_slice_in_dim(
        jnp.zeros(fc1_bias.shape, jnp.float32),
        jnp.sum(grad_before.astype(jnp.float32), axis=0),
        tp_rank * hidden_here,
        0,
    )
    grad_fc1 = matmul_tn(normed_rows, grad_before)
    grad_fc2 = matmul_tn(hidden, grad_rows)
    grad_normed_two = lax.psum_scatter(
        matmul_nt(grad_before, fc1_part), "tp", scatter_dimension=0, tiled=True
    )
    grad_fc2_bias = jnp.sum(grad_top, axis=0)
    grad_from_norm, grad_ln2_gain, grad_ln2_bias = norm_backward(
        grad_normed_two, unit_two, inv_two, ln2_gain
    )
    grad_middle = grad_top + grad_from_norm
    grad_out_bias = jnp.sum(grad_middle, axis=0)
    grad_attn_rows = lax.all_gather(grad_middle.astype(jnp.bfloat16), "tp", axis=0, tiled=True)
    grad_out_w = matmul_tn(mixed, grad_attn_rows)
    grad_mixed = (
        matmul_nt(grad_attn_rows, out_full).astype(jnp.bfloat16).reshape(seq_len, heads_here, HD)
    )
    grad_queries, grad_keys, grad_values = attend_backward(
        queries, keys_all, values_all, grad_mixed, log_mass, prefix_len, scale
    )
    grad_q_low = grad_queries.astype(jnp.bfloat16).reshape(seq_len, cols_here)
    grad_k_low = grad_keys.astype(jnp.bfloat16).reshape(seq_len, cols_here)
    grad_v_low = grad_values.astype(jnp.bfloat16).reshape(seq_len, cols_here)
    grad_proj = jnp.stack([grad_q_low, grad_k_low, grad_v_low], axis=1)
    grad_qv_here = jnp.stack(
        [
            jnp.sum(grad_q_low.astype(jnp.float32), axis=0),
            jnp.sum(grad_v_low.astype(jnp.float32), axis=0),
        ],
        axis=0,
    )
    grad_qv_bias = lax.dynamic_update_slice_in_dim(
        jnp.zeros(qv_bias.shape, jnp.float32), grad_qv_here, tp_rank * cols_here, 1
    )
    grad_qkv_w = jnp.einsum(
        "rd,rkc->kdc", normed_all, grad_proj, preferred_element_type=jnp.float32
    )
    grad_normed = lax.psum_scatter(
        jnp.einsum("rkc,kdc->rd", grad_proj, qkv_full, preferred_element_type=jnp.float32),
        "tp",
        scatter_dimension=0,
        tiled=True,
    )
    grad_in_norm, grad_ln1_gain, grad_ln1_bias = norm_backward(
        grad_normed, unit_one, inv_one, ln1_gain
    )
    grad_input = grad_middle + grad_in_norm
    grad_table = lax.dot_general(
        one_hot,
        grad_input,
        (((0,), (0,)), ((), ())),
        precision=HIGH,
        preferred_element_type=jnp.float32,
    )
    qkv_shard, out_shard, fc1_shard, fc2_shard = (
        lax.psum_scatter(grad_qkv_w, "fsdp", scatter_dimension=1, tiled=True),
        lax.psum_scatter(grad_out_w, "fsdp", scatter_dimension=1, tiled=True),
        lax.psum_scatter(grad_fc1, "fsdp", scatter_dimension=0, tiled=True),
        lax.psum_scatter(grad_fc2, "fsdp", scatter_dimension=1, tiled=True),
    )
    summed = lax.psum(
        (
            grad_ln1_gain,
            grad_ln1_bias,
            grad_qv_bias,
            grad_out_bias,
            grad_ln2_gain,
            grad_ln2_bias,
            grad_fc1_bias,
            grad_fc2_bias,
            grad_table,
        ),
        ("fsdp", "tp"),
    )
    return (
        result.astype(jnp.bfloat16),
        grad_input,
        qkv_shard,
        out_shard,
        fc1_shard,
        fc2_shard,
        summed[0],
        summed[1],
        summed[2],
        summed[3],
        summed[4],
        summed[5],
        summed[6],
        summed[7],
        summed[8],
    )


def solution(mesh):
    placed = (
        P(("fsdp", "tp"), None),
        P(("fsdp", "tp")),
        P("fsdp"),
        P(("fsdp", "tp"), None),
        P(None, "fsdp", "tp"),
        P("tp", "fsdp"),
        P("fsdp", "tp"),
        P("tp", "fsdp"),
        P(),
        P(),
        P(),
        P(),
        P(),
        P(),
        P(),
        P(),
        P(),
    )
    return jax.shard_map(
        on_device,
        mesh=mesh,
        in_specs=placed,
        out_specs=(
            P(("fsdp", "tp"), None),
            P(("fsdp", "tp"), None),
            P(None, "fsdp", "tp"),
            P("tp", "fsdp"),
            P("fsdp", "tp"),
            P("tp", "fsdp"),
            P(),
            P(),
            P(),
            P(),
            P(),
            P(),
            P(),
            P(),
            P(),
        ),
        check_vma=False,
    )
```

profile of v0, /device:TPU:0, one launch (start us, length us, event | category | flops | bytes accessed | tf_op | source)
XLA Modules:
  0.0 949.1 jit_solution(15258059311466850779)
XLA Ops:
  14.6 38.7 %all_gather.25 = bf16[3,768,192]{2,0,1:T(4,128)(2,1)S(1)} all-gather(bf16[3,96,192]{2,0,1:T(4,128)(2,1)S(1)} %copy.45), channel_id=1, replica_groups=mesh['fsdp'=8,'tp'=4] {'fsdp'}, dimensions={1}, use_global_device_ids=true | all-gather | bytes 995328 | tf_op jit(solution)/shard_map/all_gather | solution.py:148
  54.2 33.2 %all_gather.26 = bf16[192,768]{0,1:T(8,128)(2,1)} all-gather(bf16[192,96]{0,1:T(8,128)(2,1)S(1)} %copy.49), channel_id=1, replica_groups=mesh['fsdp'=8,'tp'=4] {'fsdp'}, dimensions={1}, use_global_device_ids=true | all-gather | bytes 331776 | tf_op jit(solution)/shard_map/all_gather | solution.py:149
  97.6 88.6 %while.27 = (s32[]{:T(128)}, bf16[4,512,3,64]{1,3,2,0:T(8,128)(2,1)S(1)}, f32[4,3,512]{2,1,0:T(4,128)S(1)}, s32[4]{0:T(128)S(1)}, s32[]{:T(128)}, /*index=5*/bf1...) while((s32[]{:T(128)}, ...), condition=%wide.region_5.6_spmd, body=%wide.region_2.5_spmd.sunk | while | flops 845251584 | bytes 43976836 | solution.py:74
  112.9 6.8 fusion.128
  135.1 6.8 fusion.128
  157.2 6.8 fusion.128
  179.4 6.8 fusion.128
  191.9 57.4 %reduce-scatter.13.cloned.1.call-done = f32[512,768]{1,0:T(8,128)} async-done(((f32[2048,768]{1,0:T(8,128)}), f32[512,768]{1,0:T(8,128)}) %reduce-scatter.13.cloned.1.call-update) | async-done | bytes 1572880 | tf_op jit(solution)/shard_map/reduce_scatter | solution.py:168
  256.0 25.9 %all-gather.9.cloned.1.call-done = bf16[2048,768]{1,0:T(8,128)(2,1)} async-done(((bf16[512,768]{1,0:T(8,128)(2,1)}), bf16[2048,768]{1,0:T(8,128)(2,1)}) %all-gather.9.cloned.1.call-update) | async-done | bytes 3145744 | tf_op jit(solution)/shard_map/all_gather | solution.py:180
  281.9 7.5 fusion.69
  289.5 36.0 %all-gather.13.cloned.1.call-done = bf16[768,768]{0,1:T(8,128)(2,1)} async-done(((bf16[768,96]{0,1:T(8,128)(2,1)}), bf16[768,768]{0,1:T(8,128)(2,1)}) %all-gather.13.cloned.1.call-update) | async-done | bytes 1179664 | tf_op jit(solution)/shard_map/all_gather | solution.py:151
  325.4 28.3 %all-gather.15.cloned.1.call-done = bf16[2048,768]{1,0:T(8,128)(2,1)} async-done(((bf16[512,768]{1,0:T(8,128)(2,1)}), bf16[2048,768]{1,0:T(8,128)(2,1)}) %all-gather.15.cloned.1.call-update) | async-done | bytes 3145744 | tf_op jit(solution)/shard_map/all_gather | solution.py:197
  353.8 10.8 %convert_reduce_fusion = (f32[768]{0:T(1024)}, bf16[2048,768]{1,0:T(8,128)(2,1)S(1)}, bf16[2048,768]{1,0:T(8,128)(2,1)}) fusion(f32[2048,768]{1,0:T(8,128)} %fusion.69, f32[768]{0:T(1024)S(1)} %dynamic_slice.28, bf16[2048,768]{1,0:T(8,128)(2,1)} %all-gather.15.cloned.1.call-done, bf16[768,768]{0,1:T(8,128)(2,1)} %all-gather.13.cloned.1.call-done), kind=kOutput, calls=%fused_computation.64 | convolution fusion | flops 2455239936 | bytes 16914432 | tf_op jit(solution)/shard_map/dot_general | solution.py:34
  378.3 51.3 %reduce-scatter.17.cloned.1.call-done = f32[512,768]{1,0:T(8,128)} async-done(((f32[2048,768]{1,0:T(8,128)}), f32[512,768]{1,0:T(8,128)}) %reduce-scatter.17.cloned.1.call-update) | async-done | bytes 1572880 | tf_op jit(solution)/shard_map/reduce_scatter | solution.py:208
  432.4 37.5 %reduce-scatter.15.cloned.1.call-done = bf16[512,768]{1,0:T(8,128)(2,1)} async-done(((bf16[2048,768]{1,0:T(8,128)(2,1)}), bf16[512,768]{1,0:T(8,128)(2,1)}) %reduce-scatter.15.cloned.1.call-update) | async-done | bytes 786448 | tf_op jit(solution)/shard_map/reduce_scatter | solution.py:185
  476.3 28.6 %all-gather.17.cloned.1.call-done = bf16[2048,768]{1,0:T(8,128)(2,1)} async-done(((bf16[512,768]{1,0:T(8,128)(2,1)}), bf16[2048,768]{1,0:T(8,128)(2,1)}) %all-gather.17.cloned.1.call-update) | async-done | bytes 3145744 | tf_op jit(solution)/shard_map/all_gather | solution.py:217
  517.3 130.8 %while.28 = (s32[]{:T(128)}, f32[2048,3,64]{0,2,1:T(8,128)}, f32[2048,3,64]{0,2,1:T(8,128)}, bf16[4,512,3,64]{1,3,2,0:T(8,128)(2,1)}, bf16[4,512,3,64]{1,3,2,0:T...) while((s32[]{:T(128)}, f32[2048,3,64]{0,2,1:T(8,128)}, ...), condition=%wide.region_15.16_spmd.clone, body=%wide.region_13.15_spmd.clone.sunk | while | flops 2064614400 | bytes 156684688 | solution.py:113
  666.1 7.2 convolution_bitcast_fusion
  681.6 7.0 fusion.72
  692.5 41.2 %reduce-scatter.25.cloned.1.call-done = f32[96,576]{1,0:T(8,128)} async-done(((f32[768,576]{1,0:T(8,128)}), f32[96,576]{1,0:T(8,128)}) %reduce-scatter.25.cloned.1.call-update) | async-done | bytes 221200
  737.4 56.6 %reduce-scatter.19.cloned.1.call-done = f32[512,768]{1,0:T(8,128)} async-done(((f32[2048,768]{1,0:T(8,128)}), f32[512,768]{1,0:T(8,128)}) %reduce-scatter.19.cloned.1.call-update) | async-done | bytes 1572880 | tf_op jit(solution)/shard_map/reduce_scatter | solution.py:242
  798.8 41.9 %all-reduce = (f32[768]{0:T(1024)}, f32[768]{0:T(1024)}, f32[2,768]{1,0:T(2,128)}, f32[768]{0:T(1024)}, f32[768]{0:T(1024)}, /*index=5*/f32[768]{0:T(1024)}, f32[3072]{0:T(1024)}, f32[768]{0:T(1024)}, f32[5,768]{1,0:T(8,128)}) all-reduce(f32[768]{0:T(1024)S(1)} %get-tuple-element.238, ...), channel_id=1, replica_groups=mesh['fsdp'=8,'tp'=4] {'fsdp','tp'}, use_global_device_ids=true, to_apply=%region_24.25 | all-reduce | flops 13056 | bytes 104448 | tf_op jit(solution)/shard_map/psum | solution.py:265
  840.7 27.6 %reduce-scatter.21.cloned.1.call-done = f32[96,768]{1,0:T(8,128)} async-done(((f32[768,768]{1,0:T(8,128)}), f32[96,768]{1,0:T(8,128)}) %reduce-scatter.21.cloned.1.call-update) | async-done | bytes 294928 | tf_op jit(solution)/shard_map/reduce_scatter | solution.py:262
  868.3 73.2 %reduce-scatter.23.cloned.1.call-done = f32[768,96]{0,1:T(8,128)} async-done(((f32[768,768]{0,1:T(8,128)}), f32[768,96]{0,1:T(8,128)}) %reduce-scatter.23.cloned.1.call-update) | async-done | bytes 294928 | tf_op jit(solution)/shard_map/reduce_scatter | solution.py:263
  (323 shorter events, 294.5 us)
Async XLA Ops:
  8.1 79.4 %all-gather.7.cloned.1.call-start = ((), (), s32[]{:S(2)}) async-start(), calls=%async_computation.8 | async-start | bytes 3932160 | tf_op jit(solution)/shard_map/all_gather | solution.py:160
  13.2 236.1 %reduce-scatter.13.cloned.1.call-start = ((), (), s32[]{:S(2)}) async-start(), calls=%async_computation.9 | async-start | bytes 7864320 | tf_op jit(solution)/shard_map/reduce_scatter | solution.py:168
  191.2 64.8 %all-gather.11.cloned.1.call-start = ((), (), s32[]{:S(2)}) async-start(), calls=%async_computation.11 | async-start | bytes 1327104 | tf_op jit(solution)/shard_map/all_gather | solution.py:150
  191.8 60.5 %copy-start.34 = (f32[768]{0:T(1024)S(1)}, f32[768]{0:T(1024)}, u32[]{:S(2)}) copy-start(f32[768]{0:T(1024)} %param.33) | copy-start | bytes 9220
  191.8 60.4 %copy-start.46 = (f32[768]{0:T(1024)S(1)}, f32[768]{0:T(1024)}, u32[]{:S(2)}) copy-start(f32[768]{0:T(1024)} %param.34) | copy-start | bytes 9220
  191.8 90.1 %all-gather.9.cloned.1.call-start = ((), (), s32[]{:S(2)}) async-start(), calls=%async_computation.10 | async-start | bytes 3932160 | tf_op jit(solution)/shard_map/all_gather | solution.py:180
  253.5 72.0 %all-gather.13.cloned.1.call-start = ((), (), s32[]{:S(2)}) async-start(), calls=%async_computation.12 | async-start | bytes 1327104 | tf_op jit(solution)/shard_map/all_gather | solution.py:151
  254.0 99.7 %all-gather.15.cloned.1.call-start = ((), (), s32[]{:S(2)}) async-start(), calls=%async_computation.14 | async-start | bytes 3932160 | tf_op jit(solution)/shard_map/all_gather | solution.py:197
  254.8 174.8 %reduce-scatter.17.cloned.1.call-start = ((), (), s32[]{:S(2)}) async-start(), calls=%async_computation.15 | async-start | bytes 7864320 | tf_op jit(solution)/shard_map/reduce_scatter | solution.py:208
  289.5 76.7 %copy-start.50 = (bf16[768,768]{1,0:T(8,128)(2,1)S(1)}, bf16[768,768]{1,0:T(8,128)(2,1)}, u32[]{:S(2)}) copy-start(bf16[768,768]{1,0:T(8,128)(2,1)} %all-gather.11.cloned.1.call-done) | copy-start | bytes 3538948
  370.8 99.2 %reduce-scatter.15.cloned.1.call-start = ((), (), s32[]{:S(2)}) async-start(), calls=%async_computation.13 | async-start | bytes 3932160 | tf_op jit(solution)/shard_map/reduce_scatter | solution.py:185
  378.2 91.7 %copy-start.47 = (f32[768]{0:T(1024)S(1)}, f32[768]{0:T(1024)}, u32[]{:S(2)}) copy-start(f32[768]{0:T(1024)} %param.36) | copy-start | bytes 9220
  378.3 126.6 %all-gather.17.cloned.1.call-start = ((), (), s32[]{:S(2)}) async-start(), calls=%async_computation.16 | async-start | bytes 3932160 | tf_op jit(solution)/shard_map/all_gather | solution.py:217
  476.2 214.6 %reduce-scatter.27.cloned.1.call-start = ((), (), s32[]{:S(2)}) async-start(), calls=%async_computation.21 | async-start | bytes 884736
  517.3 216.5 %reduce-scatter.25.cloned.1.call-start = ((), (), s32[]{:S(2)}) async-start(), calls=%async_computation.20 | async-start | bytes 2211840
  666.0 127.9 %reduce-scatter.19.cloned.1.call-start = ((), (), s32[]{:S(2)}) async-start(), calls=%async_computation.17 | async-start | bytes 7864320 | tf_op jit(solution)/shard_map/reduce_scatter | solution.py:242
  673.3 195.0 %reduce-scatter.21.cloned.1.call-start = ((), (), s32[]{:S(2)}) async-start(), calls=%async_computation.18 | async-start | bytes 2654208 | tf_op jit(solution)/shard_map/reduce_scatter | solution.py:262
  681.3 260.2 %reduce-scatter.23.cloned.1.call-start = ((), (), s32[]{:S(2)}) async-start(), calls=%async_computation.19 | async-start | bytes 2654208 | tf_op jit(solution)/shard_map/reduce_scatter | solution.py:263
  688.5 105.4 %copy-start.8 = (f32[512,768]{1,0:T(8,128)S(1)}, f32[512,768]{1,0:T(8,128)}, u32[]{:S(2)}) copy-start(f32[512,768]{1,0:T(8,128)} %copy-done.6) | copy-start | bytes 4718596
  688.5 105.4 %copy-start.32 = (f32[512]{0:T(512)S(1)}, f32[512]{0:T(512)}, u32[]{:S(2)}) copy-start(f32[512]{0:T(512)} %copy-done.31) | copy-start | bytes 6148
  688.5 105.4 %copy-start.36 = (f32[768]{0:T(1024)S(1)}, f32[768]{0:T(1024)}, u32[]{:S(2)}) copy-start(f32[768]{0:T(1024)} %param.29) | copy-start | bytes 9220
  688.5 105.4 %copy-start.38 = (f32[512]{0:T(512)S(1)}, f32[512]{0:T(512)}, u32[]{:S(2)}) copy-start(f32[512]{0:T(512)} %copy-done.37) | copy-start | bytes 6148
  688.6 107.7 %copy-start.13 = (f32[512,768]{1,0:T(8,128)S(1)}, f32[512,768]{1,0:T(8,128)}, u32[]{:S(2)}) copy-start(f32[512,768]{1,0:T(8,128)} %copy-done.12) | copy-start | bytes 4718596
  796.3 145.3 %copy-start.1 = (f32[5,768]{1,0:T(8,128)S(1)}, f32[5,768]{1,0:T(8,128)}, u32[]{:S(2)}) copy-start(f32[5,768]{1,0:T(8,128)} %param.37) | copy-start | bytes 46084
  (67 other events, 570.6 us)
Sparse Core Ops, SparseCore 0:
  13.4 31.2 all-gather.6
  191.3 57.9 reduce-scatter.12
  476.3 28.5 all-gather.16
Sparse Core Ops, SparseCore 1:
  193.9 40.5 all-gather.10
  253.5 28.3 all-gather.8
  284.0 41.4 all-gather.12
  327.0 26.7 all-gather.14
  370.8 58.7 reduce-scatter.16
  432.2 37.7 reduce-scatter.14
  517.4 63.3 reduce-scatter.26
  666.1 67.5 reduce-scatter.24
  736.1 57.7 reduce-scatter.18
  798.0 70.2 reduce-scatter.20
  872.3 69.2 reduce-scatter.22
where the time goes:
time: 953 us; the launch traced here: 949 us
  waiting for transfers between devices  466 us (49%)
  matrix products  217 us (23%)
  blocking collectives  114 us (12%)
  other arithmetic  91.4 us (10%)
  local copies, waits for them, and re-layouts  42.1 us (4%)
  between operations  16.4 us (2%)
    reduce_scatter x1, waiting for transfers between devices, on_device(): lax.psum_scatter(grad_fc2, 'fsdp', scatter_dimension=1, tiled=True)  73.2 us
    reduce_scatter x1, waiting for transfers between devices, on_device(): lax.psum_scatter(jnp.dot(mixed, out_full, preferred_element_type=jnp.floa...  57.4 us
    reduce_scatter x1, waiting for transfers between devices, on_device(): lax.psum_scatter(jnp.einsum('rkc,kdc->rd', grad_proj, qkv_full, preferred...  56.6 us
    reduce_scatter x1, waiting for transfers between devices, on_device(): lax.psum_scatter(matmul_nt(grad_before, fc1_part), 'tp', scatter_dimensio...  51.3 us
    unnamed x16, waiting for transfers between devices  43.2 us
    psum x1, blocking collectives, on_device(): lax.psum((grad_ln1_gain, grad_ln1_bias, grad_qv_bias, grad_out_bias, grad...  41.9 us
    all_gather x1, blocking collectives, on_device(): lax.all_gather(qkv_weight, 'fsdp', axis=1, tiled=True)  38.7 us
    reduce_scatter x1, waiting for transfers between devices, on_device(): lax.psum_scatter(jnp.dot(lax.slice_in_dim(hidden, 0, local_rows * lax.axi...  37.5 us
  transfers between devices with their start and end apart: 14, of which 11 were waited for; matrix products, arithmetic and copies ran while one was open for 21% of the time, Pallas kernels for 0%

commit v1 on v0

--- a/solution.py
+++ b/solution.py
@@ -144,12 +144,23 @@
     scale = HD ** (-0.5)
     prefix_len = prefix[0]
     gelu_tanh = partial(jax.nn.gelu, approximate=True)
-    qkv_full, out_full, fc1_part, fc2_part = (
-        lax.all_gather(qkv_weight, "fsdp", axis=1, tiled=True),
-        lax.all_gather(out_weight, "fsdp", axis=1, tiled=True),
-        lax.all_gather(fc1_weight, "fsdp", axis=0, tiled=True),
-        lax.all_gather(fc2_weight, "fsdp", axis=1, tiled=True),
-    )
+    fsdp_count = lax.axis_size("fsdp")
+    shards = (qkv_weight, out_weight, fc1_weight, fc2_weight)
+    packed = jnp.concatenate([piece.reshape(-1) for piece in shards])
+    gathered = lax.all_gather(packed, "fsdp", axis=0, tiled=False)
+    pieces = []
+    offset = 0
+    for piece in shards:
+        size = piece.size
+        pieces.append(gathered[:, offset : offset + size].reshape((fsdp_count,) + piece.shape))
+        offset += size
+    qkv_cols = jnp.moveaxis(pieces[0], 0, 1).reshape(3, -1, cols_here)
+    out_heads = jnp.moveaxis(pieces[1], 0, 1).reshape(out_weight.shape[0], -1)
+    fc1_part = pieces[2].reshape(-1, fc1_weight.shape[1])
+    fc2_part = jnp.moveaxis(pieces[3], 0, 1).reshape(fc2_weight.shape[0], -1)
+    out_all = lax.all_gather(out_heads, "tp", axis=0, tiled=True)
+    qkv_all = lax.all_gather(qkv_cols, "tp", axis=2, tiled=True)
+    qkv_full, out_full = qkv_cols, out_heads
     hidden_here = fc1_part.shape[1]
     qv_here = lax.dynamic_slice_in_dim(qv_bias, tp_rank * cols_here, cols_here, 1)
     one_hot = (pass_ids[:, None] == jnp.arange(NPASS, dtype=jnp.int32)[None, :]).astype(jnp.float32)
@@ -163,16 +174,8 @@
     keys_all = projected[1].astype(jnp.bfloat16).reshape(seq_len, heads_here, HD)
     values_all = (projected[2] + qv_here[1]).astype(jnp.bfloat16).reshape(seq_len, heads_here, HD)
     mixed, log_mass = attend_forward(queries, keys_all, values_all, prefix_len, scale)
-    middle = (
-        block_in
-        + lax.psum_scatter(
-            jnp.dot(mixed, out_full, preferred_element_type=jnp.float32),
-            "tp",
-            scatter_dimension=0,
-            tiled=True,
-        )
-        + out_bias
-    )
+    mixed_rows = lax.all_to_all(mixed, "tp", 0, 1, tiled=True)
+    middle = block_in + jnp.dot(mixed_rows, out_all, preferred_element_type=jnp.float32) + out_bias
     normed_two, unit_two, inv_two = norm_forward(middle, ln2_gain, ln2_bias)
     normed_two = normed_two.astype(jnp.bfloat16)
     grad_top = cotangent.astype(jnp.float32)
@@ -239,11 +242,9 @@
     grad_qkv_w = jnp.einsum(
         "rd,rkc->kdc", normed_all, grad_proj, preferred_element_type=jnp.float32
     )
-    grad_normed = lax.psum_scatter(
-        jnp.einsum("rkc,kdc->rd", grad_proj, qkv_full, preferred_element_type=jnp.float32),
-        "tp",
-        scatter_dimension=0,
-        tiled=True,
+    grad_proj_rows = lax.all_to_all(grad_proj, "tp", 0, 2, tiled=True)
+    grad_normed = jnp.einsum(
+        "rkc,kdc->rd", grad_proj_rows, qkv_all, preferred_element_type=jnp.float32
     )
     grad_in_norm, grad_ln1_gain, grad_ln1_bias = norm_backward(
         grad_normed, unit_one, inv_one, ln1_gain

time: 953 us -> 843 us (0.88)
  waiting for transfers between devices: 466 us -> 363 us
  blocking collectives: 114 us -> 57.7 us
  local copies, waits for them, and re-layouts: 42.1 us -> 72.3 us
  matrix products: 217 us -> 228 us
    reduce_scatter x2 -> x0, waiting for transfers between devices: 114 us -> none  [the longest x1 57.4 us: on_device(): lax.psum_scatter(jnp.dot(mixed, out_full, preferred_element_type=jnp.floa...]
    all_gather x2 -> x0, blocking collectives: 72 us -> none  [the longest x1 38.7 us: on_device(): lax.all_gather(qkv_weight, 'fsdp', axis=1, tiled=True)]
    all_to_all x0 -> x1, waiting for transfers between devices: none -> 45.6 us  [on_device(): grad_proj_rows = lax.all_to_all(grad_proj, 'tp', 0, 2, tiled=True)]
    unnamed x16 -> x15, waiting for transfers between devices: 43.2 us -> 1.24 us
    all_gather x2 -> x3, waiting for transfers between devices: 36 us -> 62.3 us  [the longest x1 62.2 us: on_device(): gathered = lax.all_gather(packed, 'fsdp', axis=0, tiled=False)]
    all_gather x1, waiting for transfers between devices: 0.01 us -> 19.1 us  [on_device(): lax.all_gather(normed.astype(jnp.bfloat16), 'tp', axis=0, tiled=True)]
    reduce_scatter x1, waiting for transfers between devices: 27.6 us -> 8.75 us  [on_device(): lax.psum_scatter(grad_fc1, 'fsdp', scatter_dimension=0, tiled=True)]
    all_to_all x0 -> x1, blocking collectives: none -> 15.9 us  [on_device(): mixed_rows = lax.all_to_all(mixed, 'tp', 0, 1, tiled=True)]
  transfers between devices with their start and end apart: 14 -> 14, of which waited for: 11 -> 10; matrix products, arithmetic and copies ran while one was open for 21% -> 41% of each run, Pallas kernels for 0% -> 0%
where the time goes in v1:
time: 843 us; the launch traced here: 834 us
  waiting for transfers between devices  363 us (43%)
  matrix products  228 us (27%)
  other arithmetic  90 us (11%)
  local copies, waits for them, and re-layouts  72.3 us (9%)
  blocking collectives  57.7 us (7%)
  between operations  14.7 us (2%)
    reduce_scatter x1, waiting for transfers between devices, on_device(): lax.psum_scatter(grad_fc2, 'fsdp', scatter_dimension=1, tiled=True)  72.7 us
    all_gather x1, waiting for transfers between devices, on_device(): gathered = lax.all_gather(packed, 'fsdp', axis=0, tiled=False)  62.2 us
    reduce_scatter x1, waiting for transfers between devices, on_device(): lax.psum_scatter(matmul_nt(grad_before, fc1_part), 'tp', scatter_dimensio...  51.5 us
    all_to_all x1, waiting for transfers between devices, on_device(): grad_proj_rows = lax.all_to_all(grad_proj, 'tp', 0, 2, tiled=True)  45.6 us
    psum x1, blocking collectives, on_device(): lax.psum((grad_ln1_gain, grad_ln1_bias, grad_qv_bias, grad_out_bias, grad...  41.8 us
    dot_general x8, matrix products, block_scores(): jnp.einsum('qhe,khe->hqk', query_block, keys_all, preferred_element_type=...  39.3 us
    reduce_scatter x1, waiting for transfers between devices, on_device(): lax.psum_scatter(jnp.dot(lax.slice_in_dim(hidden, 0, local_rows * lax.axi...  37.7 us
    dot_general x4, matrix products, one_block(): jnp.einsum('hqk,khe->qhe', probs_low, values_all, preferred_element_type=...  29.5 us
  transfers between devices with their start and end apart: 14, of which 10 were waited for; matrix products, arithmetic and copies ran while one was open for 41% of the time, Pallas kernels for 0%

profile of v1, /device:TPU:0, one launch (start us, length us, event | category | flops | bytes accessed | tf_op | source)
XLA Modules:
  0.0 834.1 jit_solution(15173481824254641133)
XLA Ops:
  17.9 62.2 %all-gather.21.cloned.1.call-done = bf16[1769472]{0:T(1024)(128)(2,1)} async-done(((bf16[221184]{0:T(1024)(128)(2,1)}), bf16[1769472]{0:T(1024)(128)(2,1)}) %all-gather.21.cloned.1.call-update) | async-done | bytes 3538960 | tf_op jit(solution)/shard_map/all_gather | solution.py:150
  90.5 19.1 %all-gather.9.cloned.1.call-done = bf16[2048,768]{1,0:T(8,128)(2,1)} async-done(((bf16[512,768]{1,0:T(8,128)(2,1)}), bf16[2048,768]{1,0:T(8,128)(2,1)}) %all-gather.9.cloned.1.call-update) | async-done | bytes 3145744 | tf_op jit(solution)/shard_map/all_gather | solution.py:171
  122.6 94.6 %while.27 = (s32[]{:T(128)}, bf16[4,512,3,64]{1,3,2,0:T(8,128)(2,1)}, f32[4,3,512]{2,1,0:T(4,128)S(1)}, s32[4]{0:T(128)S(1)}, s32[]{:T(128)}, /*index=5*/bf16[4,...) while((s32[]{:T(128)}, ...), condition=%wide.region_5.6_spmd, body=%wide.region_2.5_spmd.sunk | while | flops 845251584 | bytes 43972740 | solution.py:74
  125.2 6.8 fusion.127
  138.9 7.4 fusion.129
  162.5 7.4 fusion.129
  186.1 7.4 fusion.129
  209.7 7.4 fusion.129
  217.2 15.9 %all_to_all.37 = bf16[4,512,192]{1,2,0:T(8,128)(2,1)} all-to-all(bf16[4,512,192]{1,2,0:T(8,128)(2,1)} %bitcast.195), channel_id=1, replica_groups=mesh['fsdp'=8,'tp'=4] {'tp'}, dimensions={0} | all-to-all | bytes 1572864 | tf_op jit(solution)/shard_map/all_to_all | solution.py:177
  250.4 16.2 %all-gather.13.cloned.1.call-done = bf16[2048,768]{1,0:T(8,128)(2,1)} async-done(((bf16[512,768]{1,0:T(8,128)(2,1)}), bf16[2048,768]{1,0:T(8,128)(2,1)}) %all-gather.13.cloned.1.call-update) | async-done | bytes 3145744 | tf_op jit(solution)/shard_map/all_gather | solution.py:183
  266.6 9.5 %multiply_convert_fusion.1 = (bf16[2048,768]{1,0:T(8,128)(2,1)}, f32[2048,768]{1,0:T(8,128)}) fusion(f32[768]{0:T(1024)S(1)} %dynamic_slice.28, bf16[2048,768]{1,0:T(8,128)(2,1)} %all-gather.13.cloned.1.call-done, bf16[768,768]{1,0:T(8,128)(2,1)S(1)} %reshape_reshape.8), kind=kOutput, calls=%fused_computation.70 | convolution fusion | flops 2431647744 | bytes 13765632 | tf_op jit(solution)/shard_map/dot_general | solution.py:184
  276.1 20.4 %all-gather.15.cloned.1.call-done = bf16[2048,768]{1,0:T(8,128)(2,1)} async-done(((bf16[512,768]{1,0:T(8,128)(2,1)}), bf16[2048,768]{1,0:T(8,128)(2,1)}) %all-gather.15.cloned.1.call-update) | async-done | bytes 3145744 | tf_op jit(solution)/shard_map/all_gather | solution.py:200
  296.5 9.7 %convert_reduce_fusion = (f32[768]{0:T(1024)}, bf16[2048,768]{1,0:T(8,128)(2,1)S(1)}) fusion(f32[2048,768]{1,0:T(8,128)} %get-tuple-element.338, f32[768]{0:T(1024)S(1)} %dynamic_slice.28, bf16[2048,768]{1,0:T(8,128)(2,1)} %all-gather.15.cloned.1.call-done, bf16[768,768]{0,1:T(8,128)(2,1)} %bitcast.204), kind=kOutput, calls=%fused_computation.69 | convolution fusion | flops 2452094208 | bytes 13768704 | tf_op jit(solution)/shard_map/dot_general | solution.py:34
  320.0 51.5 %reduce-scatter.13.cloned.1.call-done = f32[512,768]{1,0:T(8,128)} async-done(((f32[2048,768]{1,0:T(8,128)}), f32[512,768]{1,0:T(8,128)}) %reduce-scatter.13.cloned.1.call-update) | async-done | bytes 1572880 | tf_op jit(solution)/shard_map/reduce_scatter | solution.py:211
  374.2 37.7 %reduce-scatter.11.cloned.1.call-done = bf16[512,768]{1,0:T(8,128)(2,1)} async-done(((bf16[2048,768]{1,0:T(8,128)(2,1)}), bf16[512,768]{1,0:T(8,128)(2,1)}) %reduce-scatter.11.cloned.1.call-update) | async-done | bytes 786448 | tf_op jit(solution)/shard_map/reduce_scatter | solution.py:188
  419.1 27.8 %all-gather.17.cloned.1.call-done = bf16[2048,768]{1,0:T(8,128)(2,1)} async-done(((bf16[512,768]{1,0:T(8,128)(2,1)}), bf16[2048,768]{1,0:T(8,128)(2,1)}) %all-gather.17.cloned.1.call-update) | async-done | bytes 3145744 | tf_op jit(solution)/shard_map/all_gather | solution.py:220
  458.2 138.2 %while.28 = (s32[]{:T(128)}, f32[2048,3,64]{0,2,1:T(8,128)}, f32[2048,3,64]{0,2,1:T(8,128)}, bf16[4,512,3,64]{1,3,2,0:T(8,128)(2,1)}, bf16[4,512,3,64]{1,3,2,0:T...) while((s32[]{:T(128)}, f32[2048,3,64]{0,2,1:T(8,128)}, ...), condition=%wide.region_14.15_spmd.clone, body=%wide.region_12.14_spmd.clone.sunk | while | flops 2064614400 | bytes 156684720 | solution.py:113
  614.4 6.9 fusion.72
  621.4 7.0 fusion.73
  642.5 45.6 %all-to-all-done.1 = bf16[2048,3,192]{2,1,0:T(4,128)(2,1)} async-done(((bf16[2048,3,192]{2,1,0:T(4,128)(2,1)}), bf16[2048,3,192]{2,1,0:T(4,128)(2,1)}, u32[]{:S(2)}, u32[]{:S(2)}) %all-to-all-start.1) | async-done | bytes 2359328 | tf_op jit(solution)/shard_map/all_to_all | solution.py:245
  688.2 7.1 copy.72
  702.2 41.8 %all-reduce = (f32[768]{0:T(1024)}, f32[768]{0:T(1024)}, f32[2,768]{1,0:T(2,128)}, f32[768]{0:T(1024)}, f32[768]{0:T(1024)}, /*index=5*/f32[768]{0:T(1024)}, f32[3072]{0:T(1024)}, f32[768]{0:T(1024)}, f32[5,768]{1,0:T(8,128)}) all-reduce(f32[768]{0:T(1024)S(1)} %get-tuple-element.264, ...), channel_id=1, replica_groups=mesh['fsdp'=8,'tp'=4] {'fsdp','tp'}, use_global_device_ids=true, to_apply=%region_22.23 | all-reduce | flops 13056 | bytes 104448 | tf_op jit(solution)/shard_map/psum | solution.py:266
  745.9 8.8 %reduce-scatter.15.cloned.1.call-done = f32[96,768]{1,0:T(8,128)} async-done(((f32[768,768]{1,0:T(8,128)}), f32[96,768]{1,0:T(8,128)}) %reduce-scatter.15.cloned.1.call-update) | async-done | bytes 294928 | tf_op jit(solution)/shard_map/reduce_scatter | solution.py:263
  754.6 72.7 %reduce-scatter.17.cloned.1.call-done = f32[768,96]{0,1:T(8,128)} async-done(((f32[768,768]{0,1:T(8,128)}), f32[768,96]{0,1:T(8,128)}) %reduce-scatter.17.cloned.1.call-update) | async-done | bytes 294928 | tf_op jit(solution)/shard_map/reduce_scatter | solution.py:264
  (328 shorter events, 321.8 us)
Async XLA Ops:
  7.2 72.9 %all-gather.21.cloned.1.call-start = ((), (), s32[]{:S(2)}) async-start(), calls=%async_computation.18 | async-start | bytes 3981312 | tf_op jit(solution)/shard_map/all_gather | solution.py:150
  12.6 96.9 %all-gather.9.cloned.1.call-start = ((), (), s32[]{:S(2)}) async-start(), calls=%async_computation.8 | async-start | bytes 3932160 | tf_op jit(solution)/shard_map/all_gather | solution.py:171
  14.4 71.1 %copy-start.30 = (f32[512]{0:T(512)}, f32[512]{0:T(512)S(1)}, u32[]{:S(2)}) copy-start(f32[512]{0:T(512)S(1)} %broadcast_multiply_fusion.5) | copy-start | bytes 6148
  15.5 69.9 %copy-start.32 = (f32[512]{0:T(512)}, f32[512]{0:T(512)S(1)}, u32[]{:S(2)}) copy-start(f32[512]{0:T(512)S(1)} %add_rsqrt_fusion.1) | copy-start | bytes 6148
  16.8 216.3 %all-gather.11.cloned.1.call-start = ((), (), s32[]{:S(2)}) async-start(), calls=%async_computation.9 | async-start | bytes 1474560 | tf_op jit(solution)/shard_map/all_gather | solution.py:161
  90.4 19.1 %copy-start.19 = (bf16[3,768,192]{1,2,0:T(8,128)(2,1)}, bf16[3,768,192]{1,2,0:T(8,128)(2,1)S(1)}, u32[]{:S(2)}) copy-start(bf16[3,768,192]{1,2,0:T(8,128)(2,1)S(1)} %reshape.267) | copy-start | bytes 2654212
  116.7 149.9 %all-gather.13.cloned.1.call-start = ((), (), s32[]{:S(2)}) async-start(), calls=%async_computation.10 | async-start | bytes 3932160 | tf_op jit(solution)/shard_map/all_gather | solution.py:183
  122.6 110.5 %copy-start.9 = (f32[512,768]{1,0:T(8,128)S(1)}, f32[512,768]{1,0:T(8,128)}, u32[]{:S(2)}) copy-start(f32[512,768]{1,0:T(8,128)} %copy-done.8) | copy-start | bytes 4718596
  122.6 110.5 %copy-start.45 = (f32[768]{0:T(1024)S(1)}, f32[768]{0:T(1024)}, u32[]{:S(2)}) copy-start(f32[768]{0:T(1024)} %param.32) | copy-start | bytes 9220
  237.9 58.6 %all-gather.15.cloned.1.call-start = ((), (), s32[]{:S(2)}) async-start(), calls=%async_computation.12 | async-start | bytes 3932160 | tf_op jit(solution)/shard_map/all_gather | solution.py:200
  238.5 133.0 %reduce-scatter.13.cloned.1.call-start = ((), (), s32[]{:S(2)}) async-start(), calls=%async_computation.13 | async-start | bytes 7864320 | tf_op jit(solution)/shard_map/reduce_scatter | solution.py:211
  312.5 99.4 %reduce-scatter.11.cloned.1.call-start = ((), (), s32[]{:S(2)}) async-start(), calls=%async_computation.11 | async-start | bytes 3932160 | tf_op jit(solution)/shard_map/reduce_scatter | solution.py:188
  319.9 51.6 %copy-start.12 = (f32[512,768]{1,0:T(8,128)S(1)}, f32[512,768]{1,0:T(8,128)}, u32[]{:S(2)}) copy-start(f32[512,768]{1,0:T(8,128)} %copy-done.11) | copy-start | bytes 4718596
  319.9 92.0 %copy-start.43 = (f32[768]{0:T(1024)S(1)}, f32[768]{0:T(1024)}, u32[]{:S(2)}) copy-start(f32[768]{0:T(1024)} %param.36) | copy-start | bytes 9220
  319.9 127.0 %all-gather.17.cloned.1.call-start = ((), (), s32[]{:S(2)}) async-start(), calls=%async_computation.14 | async-start | bytes 3932160 | tf_op jit(solution)/shard_map/all_gather | solution.py:220
  418.3 222.6 %reduce-scatter.21.cloned.1.call-start = ((), (), s32[]{:S(2)}) async-start(), calls=%async_computation.20 | async-start | bytes 884736
  451.2 244.1 %all-gather.19.cloned.1.call-start = ((), (), s32[]{:S(2)}) async-start(), calls=%async_computation.15 | async-start | bytes 4423680 | tf_op jit(solution)/shard_map/all_gather | solution.py:162
  451.7 292.2 %reduce-scatter.19.cloned.1.call-start = ((), (), s32[]{:S(2)}) async-start(), calls=%async_computation.19 | async-start | bytes 2211840
  614.3 140.3 %reduce-scatter.15.cloned.1.call-start = ((), (), s32[]{:S(2)}) async-start(), calls=%async_computation.16 | async-start | bytes 2654208 | tf_op jit(solution)/shard_map/reduce_scatter | solution.py:263
  621.3 206.0 %reduce-scatter.17.cloned.1.call-start = ((), (), s32[]{:S(2)}) async-start(), calls=%async_computation.17 | async-start | bytes 2654208 | tf_op jit(solution)/shard_map/reduce_scatter | solution.py:264
  634.8 53.4 %all-to-all-start.1 = ((bf16[2048,3,192]{2,1,0:T(4,128)(2,1)}), bf16[2048,3,192]{2,1,0:T(4,128)(2,1)}, u32[]{:S(2)}, u32[]{:S(2)}) async-start(bf16[2048,3,192]{2,1,0:T(4,128)(2,1)} %copy.70), calls=%async_computation.3 | async-start | bytes 8388608 | tf_op jit(solution)/shard_map/all_to_all | solution.py:245
  688.2 7.1 copy-start.39
  700.7 126.6 %copy-start.1 = (f32[5,768]{1,0:T(8,128)S(1)}, f32[5,768]{1,0:T(8,128)}, u32[]{:S(2)}) copy-start(f32[5,768]{1,0:T(8,128)} %param.37) | copy-start | bytes 46084
  701.4 125.9 %copy-start.15 = (f32[512,768]{1,0:T(8,128)}, f32[512,768]{1,0:T(8,128)S(1)}, u32[]{:S(2)}) copy-start(f32[512,768]{1,0:T(8,128)S(1)} %multiply_add_fusion) | copy-start | bytes 4718596
  (62 other events, 259.2 us)
Sparse Core Ops, SparseCore 0:
  12.8 67.3 all-gather.20
  82.2 27.2 all-gather.8
  116.8 17.4 all-gather.10
  238.0 28.4 all-gather.12
  268.0 28.4 all-gather.14
  312.6 58.8 reduce-scatter.12
  374.0 37.8 reduce-scatter.10
  418.4 28.4 all-gather.16
  451.3 63.2 reduce-scatter.20
  516.0 29.8 all-gather.18
  614.5 67.4 reduce-scatter.18
  685.9 68.6 reduce-scatter.14
  758.7 68.6 reduce-scatter.16

commit v2 on v1

--- a/solution.py
+++ b/solution.py
@@ -174,6 +174,7 @@
     keys_all = projected[1].astype(jnp.bfloat16).reshape(seq_len, heads_here, HD)
     values_all = (projected[2] + qv_here[1]).astype(jnp.bfloat16).reshape(seq_len, heads_here, HD)
     mixed, log_mass = attend_forward(queries, keys_all, values_all, prefix_len, scale)
+    mixed, qkv_all = lax.optimization_barrier((mixed, qkv_all))
     mixed_rows = lax.all_to_all(mixed, "tp", 0, 1, tiled=True)
     middle = block_in + jnp.dot(mixed_rows, out_all, preferred_element_type=jnp.float32) + out_bias
     normed_two, unit_two, inv_two = norm_forward(middle, ln2_gain, ln2_bias)
@@ -183,20 +184,7 @@
     normed_rows = lax.all_gather(normed_two, "tp", axis=0, tiled=True)
     before = jnp.dot(normed_rows, fc1_part, preferred_element_type=jnp.float32) + fc1_bias_here
     hidden = gelu_tanh(before).astype(jnp.bfloat16)
-    result = (
-        middle
-        + lax.psum_scatter(
-            jnp.dot(
-                lax.slice_in_dim(hidden, 0, local_rows * lax.axis_size("tp"), axis=0),
-                fc2_part,
-                preferred_element_type=jnp.float32,
-            ).astype(jnp.bfloat16),
-            "tp",
-            scatter_dimension=0,
-            tiled=True,
-        ).astype(jnp.float32)
-        + fc2_bias
-    )
+    fc2_partial = jnp.dot(hidden, fc2_part, preferred_element_type=jnp.float32).astype(jnp.bfloat16)
     grad_rows = lax.all_gather(cotangent, "tp", axis=0, tiled=True)
     grad_hidden = matmul_nt(grad_rows, fc2_part)
     grad_before = jax.vjp(gelu_tanh, before)[1](grad_hidden)[0].astype(jnp.bfloat16)
@@ -218,7 +206,23 @@
     grad_middle = grad_top + grad_from_norm
     grad_out_bias = jnp.sum(grad_middle, axis=0)
     grad_attn_rows = lax.all_gather(grad_middle.astype(jnp.bfloat16), "tp", axis=0, tiled=True)
+    fc2_partial, grad_attn_rows = lax.optimization_barrier((fc2_partial, grad_attn_rows))
+    result = (
+        middle
+        + lax.psum_scatter(fc2_partial, "tp", scatter_dimension=0, tiled=True).astype(jnp.float32)
+        + fc2_bias
+    )
     grad_out_w = matmul_tn(mixed, grad_attn_rows)
+    fsdp_count = lax.axis_size("fsdp")
+    dense_grads = (
+        jnp.moveaxis(grad_out_w.reshape(grad_out_w.shape[0], fsdp_count, -1), 1, 0),
+        grad_fc1.reshape(fsdp_count, -1, grad_fc1.shape[1]),
+        jnp.moveaxis(grad_fc2.reshape(grad_fc2.shape[0], fsdp_count, -1), 1, 0),
+    )
+    dense_packed = jnp.concatenate([g.reshape(fsdp_count, -1) for g in dense_grads], axis=1)
+    dense_summed = lax.psum_scatter(
+        dense_packed.reshape(-1, grad_fc1.shape[1]), "fsdp", scatter_dimension=0, tiled=True
+    ).reshape(1, -1)
     grad_mixed = (
         matmul_nt(grad_attn_rows, out_full).astype(jnp.bfloat16).reshape(seq_len, heads_here, HD)
     )
@@ -229,6 +233,14 @@
     grad_k_low = grad_keys.astype(jnp.bfloat16).reshape(seq_len, cols_here)
     grad_v_low = grad_values.astype(jnp.bfloat16).reshape(seq_len, cols_here)
     grad_proj = jnp.stack([grad_q_low, grad_k_low, grad_v_low], axis=1)
+    grad_proj, result, dense_summed = lax.optimization_barrier((grad_proj, result, dense_summed))
+    dense_shards = []
+    offset = 0
+    for g in dense_grads:
+        size = g[0].size
+        dense_shards.append(dense_summed[0, offset : offset + size].reshape(g.shape[1:]))
+        offset += size
+    out_shard, fc1_shard, fc2_shard = dense_shards
     grad_qv_here = jnp.stack(
         [
             jnp.sum(grad_q_low.astype(jnp.float32), axis=0),
@@ -257,12 +269,7 @@
         precision=HIGH,
         preferred_element_type=jnp.float32,
     )
-    qkv_shard, out_shard, fc1_shard, fc2_shard = (
-        lax.psum_scatter(grad_qkv_w, "fsdp", scatter_dimension=1, tiled=True),
-        lax.psum_scatter(grad_out_w, "fsdp", scatter_dimension=1, tiled=True),
-        lax.psum_scatter(grad_fc1, "fsdp", scatter_dimension=0, tiled=True),
-        lax.psum_scatter(grad_fc2, "fsdp", scatter_dimension=1, tiled=True),
-    )
+    qkv_shard = lax.psum_scatter(grad_qkv_w, "fsdp", scatter_dimension=1, tiled=True)
     summed = lax.psum(
         (
             grad_ln1_gain,

time: 843 us -> 720 us (0.85)
  waiting for transfers between devices: 363 us -> 224 us
  local copies, waits for them, and re-layouts: 72.3 us -> 103 us
  blocking collectives: 57.7 us -> 41.5 us
    reduce_scatter x3 -> x2, waiting for transfers between devices: 119 us -> 0.01 us  [the longest x1 0.01 us: on_device(): lax.psum_scatter(dense_packed.reshape(-1, grad_fc1.shape[1]), 'fsdp', sca...]
    all_gather x1, waiting for transfers between devices: 27.8 us -> 0.01 us  [on_device(): lax.all_gather(grad_middle.astype(jnp.bfloat16), 'tp', axis=0, tiled=True)]
    all_to_all x1 -> x0, blocking collectives: 15.9 us -> none  [on_device(): mixed_rows = lax.all_to_all(mixed, 'tp', 0, 1, tiled=True)]
    reshape x0 -> x6, local copies, waits for them, and re-layouts: none -> 15.8 us  [the longest x1 6.38 us: on_device(): dense_packed.reshape(-1, grad_fc1.shape[1])]
    all_to_all x0 -> x1, waiting for transfers between devices: none -> 11.2 us  [on_device(): mixed_rows = lax.all_to_all(mixed, 'tp', 0, 1, tiled=True)]
    unnamed x87 -> x88, local copies, waits for them, and re-layouts: 19.1 us -> 19.6 us
  transfers between devices with their start and end apart: 14 -> 13, of which waited for: 10 -> 7; matrix products, arithmetic and copies ran while one was open for 41% -> 52% of each run, Pallas kernels for 0% -> 0%
where the time goes in v2:
time: 720 us; the launch traced here: 712 us
  waiting for transfers between devices  224 us (31%)
  matrix products  224 us (31%)
  local copies, waits for them, and re-layouts  103 us (14%)
  other arithmetic  93.4 us (13%)
  blocking collectives  41.5 us (6%)
  between operations  14.7 us (2%)
  starting transfers between devices  10.4 us (1%)
    all_gather x1, waiting for transfers between devices, on_device(): gathered = lax.all_gather(packed, 'fsdp', axis=0, tiled=False)  63.3 us
    reduce_scatter x1, waiting for transfers between devices, on_device(): lax.psum_scatter(matmul_nt(grad_before, fc1_part), 'tp', scatter_dimensio...  58.8 us
    all_to_all x1, waiting for transfers between devices, on_device(): grad_proj_rows = lax.all_to_all(grad_proj, 'tp', 0, 2, tiled=True)  43.1 us
    psum x1, blocking collectives, on_device(): lax.psum((grad_ln1_gain, grad_ln1_bias, grad_qv_bias, grad_out_bias, grad...  41.5 us
    dot_general x8, matrix products, block_scores(): jnp.einsum('qhe,khe->hqk', query_block, keys_all, preferred_element_type=...  36.6 us
    dot_general x4, matrix products, one_block(): jnp.einsum('hqk,khe->qhe', probs_low, values_all, preferred_element_type=...  27.1 us
    reduce_sum x4, other arithmetic, one_block(): total_mass = jnp.sum(expo, axis=-1, keepdims=True)  27.1 us
    convert_element_type x4, other arithmetic, one_block(): grad_scores = (probs * (grad_probs - inner_sum)).astype(jnp.bfloat16)  25.2 us
  transfers between devices with their start and end apart: 13, of which 7 were waited for; matrix products, arithmetic and copies ran while one was open for 52% of the time, Pallas kernels for 0%

profile of v2, /device:TPU:0, one launch (start us, length us, event | category | flops | bytes accessed | tf_op | source)
XLA Modules:
  0.0 712.1 jit_solution(5064491894830115045)
XLA Ops:
  16.8 63.3 %all-gather.21.cloned.1.call-done = bf16[1769472]{0:T(1024)(128)(2,1)} async-done(((bf16[221184]{0:T(1024)(128)(2,1)}), bf16[1769472]{0:T(1024)(128)(2,1)}) %all-gather.21.cloned.1.call-update) | async-done | bytes 3538960 | tf_op jit(solution)/shard_map/all_gather | solution.py:150
  94.3 15.2 %all-gather.9.cloned.1.call-done = bf16[2048,768]{1,0:T(8,128)(2,1)} async-done(((bf16[512,768]{1,0:T(8,128)(2,1)}), bf16[2048,768]{1,0:T(8,128)(2,1)}) %all-gather.9.cloned.1.call-update) | async-done | bytes 3145744 | tf_op jit(solution)/shard_map/all_gather | solution.py:171
  120.0 89.6 %while.27 = (s32[]{:T(128)}, bf16[4,512,3,64]{1,3,2,0:T(8,128)(2,1)S(1)}, f32[4,3,512]{2,1,0:T(4,128)S(1)}, s32[4]{0:T(128)S(1)}, s32[]{:T(128)}, /*index=5*/bf1...) while((s32[]{:T(128)}, ...), condition=%wide.region_5.6_spmd, body=%wide.region_2.5_spmd.sunk | while | flops 845251584 | bytes 43976836 | solution.py:74
  128.8 6.8 fusion.130
  135.6 6.8 fusion.131
  151.4 6.8 fusion.130
  158.1 6.8 fusion.131
  173.7 6.8 fusion.130
  180.5 6.8 fusion.131
  196.1 6.8 fusion.130
  202.8 6.8 fusion.131
  216.2 11.2 %all-to-all-done = bf16[4,512,192]{1,2,0:T(8,128)(2,1)} async-done(((bf16[4,512,192]{1,2,0:T(8,128)(2,1)}), bf16[4,512,192]{1,2,0:T(8,128)(2,1)}, u32[]{:S(2)}, u32[]{:S(2)}) %all-to-all-start) | async-done | bytes 786464 | tf_op jit(solution)/shard_map/all_to_all | solution.py:178
  248.6 12.1 %all-gather.15.cloned.1.call-done = bf16[2048,768]{1,0:T(8,128)(2,1)} async-done(((bf16[512,768]{1,0:T(8,128)(2,1)}), bf16[2048,768]{1,0:T(8,128)(2,1)}) %all-gather.15.cloned.1.call-update) | async-done | bytes 3145744 | tf_op jit(solution)/shard_map/all_gather | solution.py:184
  260.7 10.1 %multiply_convert_fusion.1 = (bf16[2048,768]{1,0:T(8,128)(2,1)}, f32[2048,768]{1,0:T(8,128)}) fusion(f32[768]{0:T(1024)S(1)} %dynamic_slice.28, bf16[2048,768]{1,0:T(8,128)(2,1)} %all-gather.15.cloned.1.call-done, bf16[768,768]{1,0:T(8,128)(2,1)} %reshape_reshape.11), kind=kOutput, calls=%fused_computation.70 | convolution fusion | flops 2431647744 | bytes 13765632 | tf_op jit(solution)/shard_map/dot_general | solution.py:185
  270.8 19.9 %all-gather.17.cloned.1.call-done = bf16[2048,768]{1,0:T(8,128)(2,1)} async-done(((bf16[512,768]{1,0:T(8,128)(2,1)}), bf16[2048,768]{1,0:T(8,128)(2,1)}) %all-gather.17.cloned.1.call-update) | async-done | bytes 3145744 | tf_op jit(solution)/shard_map/all_gather | solution.py:188
  290.6 9.8 %convert_reduce_fusion = (f32[768]{0:T(1024)}, bf16[2048,768]{1,0:T(8,128)(2,1)S(1)}) fusion(f32[2048,768]{1,0:T(8,128)} %get-tuple-element.353, f32[768]{0:T(1024)S(1)} %dynamic_slice.28, bf16[2048,768]{1,0:T(8,128)(2,1)} %all-gather.17.cloned.1.call-done, bf16[768,768]{0,1:T(8,128)(2,1)} %bitcast.218), kind=kOutput, calls=%fused_computation.69 | convolution fusion | flops 2452094208 | bytes 13768704 | tf_op jit(solution)/shard_map/dot_general | solution.py:34
  307.0 58.8 %reduce-scatter.7.cloned.1.call-done = f32[512,768]{1,0:T(8,128)} async-done(((f32[2048,768]{1,0:T(8,128)}), f32[512,768]{1,0:T(8,128)}) %reduce-scatter.7.cloned.1.call-update) | async-done | bytes 1572880 | tf_op jit(solution)/shard_map/reduce_scatter | solution.py:199
  372.2 6.9 fusion.73
  382.8 6.9 fusion.74
  426.5 137.5 %while.28 = (s32[]{:T(128)}, f32[2048,3,64]{0,2,1:T(8,128)}, f32[2048,3,64]{0,2,1:T(8,128)}, bf16[4,512,3,64]{1,3,2,0:T(8,128)(2,1)}, bf16[4,512,3,64]{1,3,2,0:T...) while((s32[]{:T(128)}, f32[2048,3,64]{0,2,1:T(8,128)}, ...), condition=%wide.region_13.14_spmd.clone, body=%wide.region_11.13_spmd.clone.sunk | while | flops 2064614400 | bytes 156684720 | solution.py:113
  587.8 7.0 copy.85
  604.9 43.1 %all-to-all-done.1 = bf16[2048,3,192]{2,1,0:T(4,128)(2,1)} async-done(((bf16[2048,3,192]{2,1,0:T(4,128)(2,1)}), bf16[2048,3,192]{2,1,0:T(4,128)(2,1)}, u32[]{:S(2)}, u32[]{:S(2)}) %all-to-all-start.1) | async-done | bytes 2359328 | tf_op jit(solution)/shard_map/all_to_all | solution.py:257
  648.0 7.1 copy.87
  662.0 41.5 %all-reduce = (f32[768]{0:T(1024)}, f32[768]{0:T(1024)}, f32[2,768]{1,0:T(2,128)}, f32[768]{0:T(1024)}, f32[768]{0:T(1024)}, /*index=5*/f32[768]{0:T(1024)}, f32[3072]{0:T(1024)}, f32[768]{0:T(1024)}, f32[5,768]{1,0:T(8,128)}) all-reduce(f32[768]{0:T(1024)S(1)} %get-tuple-element.278, ...), channel_id=1, replica_groups=mesh['fsdp'=8,'tp'=4] {'fsdp','tp'}, use_global_device_ids=true, to_apply=%region_20.21 | all-reduce | flops 13056 | bytes 104448 | tf_op jit(solution)/shard_map/psum | solution.py:273
  (339 shorter events, 329.0 us)
Async XLA Ops:
  7.2 72.9 %all-gather.21.cloned.1.call-start = ((), (), s32[]{:S(2)}) async-start(), calls=%async_computation.15 | async-start | bytes 3981312 | tf_op jit(solution)/shard_map/all_gather | solution.py:150
  12.7 96.9 %all-gather.9.cloned.1.call-start = ((), (), s32[]{:S(2)}) async-start(), calls=%async_computation.6 | async-start | bytes 3932160 | tf_op jit(solution)/shard_map/all_gather | solution.py:171
  14.4 71.0 %copy-start.30 = (f32[512]{0:T(512)}, f32[512]{0:T(512)S(1)}, u32[]{:S(2)}) copy-start(f32[512]{0:T(512)S(1)} %broadcast_multiply_fusion.5) | copy-start | bytes 6148
  15.6 69.8 %copy-start.32 = (f32[512]{0:T(512)}, f32[512]{0:T(512)S(1)}, u32[]{:S(2)}) copy-start(f32[512]{0:T(512)S(1)} %add_rsqrt_fusion.1) | copy-start | bytes 6148
  16.8 193.7 %all-gather.11.cloned.1.call-start = ((), (), s32[]{:S(2)}) async-start(), calls=%async_computation.7 | async-start | bytes 4423680 | tf_op jit(solution)/shard_map/all_gather | solution.py:162
  91.3 18.2 %copy-start.22 = (bf16[3,768,192]{1,2,0:T(8,128)(2,1)S(1)}, bf16[3,768,192]{1,2,0:T(8,128)(2,1)}, u32[]{:S(2)}) copy-start(bf16[3,768,192]{1,2,0:T(8,128)(2,1)} %reshape.284) | copy-start | bytes 2654212
  91.3 124.9 %all-gather.13.cloned.1.call-start = ((), (), s32[]{:S(2)}) async-start(), calls=%async_computation.8 | async-start | bytes 1474560 | tf_op jit(solution)/shard_map/all_gather | solution.py:161
  209.6 17.8 %copy-start.45 = (f32[768]{0:T(1024)S(1)}, f32[768]{0:T(1024)}, u32[]{:S(2)}) copy-start(f32[768]{0:T(1024)} %param.32) | copy-start | bytes 9220
  210.4 17.0 %copy-start.15 = (bf16[24,8,4,512]{3,1,2,0:T(8,128)(2,1)}, bf16[24,8,4,512]{3,1,2,0:T(8,128)(2,1)S(1)}, u32[]{:S(2)}) copy-start(bf16[24,8,4,512]{3,1,2,0:T(8,128)(2,1)S(1)} %copy.101) | copy-start | bytes 2359300
  211.6 15.9 %all-to-all-start = ((bf16[4,512,192]{1,2,0:T(8,128)(2,1)}), bf16[4,512,192]{1,2,0:T(8,128)(2,1)}, u32[]{:S(2)}, u32[]{:S(2)}) async-start(bf16[4,512,192]{1,2,0:T(8,128)(2,1)} %bitcast.207), calls=%async_computation | async-start | bytes 1572864 | tf_op jit(solution)/shard_map/all_to_all | solution.py:178
  215.8 44.9 %all-gather.15.cloned.1.call-start = ((), (), s32[]{:S(2)}) async-start(), calls=%async_computation.9 | async-start | bytes 3932160 | tf_op jit(solution)/shard_map/all_gather | solution.py:184
  230.4 138.3 %copy-start.8 = (f32[512,768]{1,0:T(8,128)}, f32[512,768]{1,0:T(8,128)S(1)}, u32[]{:S(2)}) copy-start(f32[512,768]{1,0:T(8,128)S(1)} %get-tuple-element.351) | copy-start | bytes 4718596
  232.0 58.7 %all-gather.17.cloned.1.call-start = ((), (), s32[]{:S(2)}) async-start(), calls=%async_computation.10 | async-start | bytes 3932160 | tf_op jit(solution)/shard_map/all_gather | solution.py:188
  232.5 133.2 %reduce-scatter.7.cloned.1.call-start = ((), (), s32[]{:S(2)}) async-start(), calls=%async_computation.11 | async-start | bytes 7864320 | tf_op jit(solution)/shard_map/reduce_scatter | solution.py:199
  290.6 11.5 %copy-start.26 = (bf16[768,768]{1,0:T(8,128)(2,1)S(1)}, bf16[768,768]{1,0:T(8,128)(2,1)}, u32[]{:S(2)}) copy-start(bf16[768,768]{1,0:T(8,128)(2,1)} %reshape_reshape.11) | copy-start | bytes 3538948
  306.8 98.0 %all-gather.19.cloned.1.call-start = ((), (), s32[]{:S(2)}) async-start(), calls=%async_computation.12 | async-start | bytes 3932160 | tf_op jit(solution)/shard_map/all_gather | solution.py:208
  372.2 199.2 %reduce-scatter.9.cloned.1.call-start = ((), (), s32[]{:S(2)}) async-start(), calls=%async_computation.13 | async-start | bytes 3932160 | tf_op jit(solution)/shard_map/reduce_scatter | solution.py:212
  407.5 166.1 %reduce-scatter.11.cloned.1.call-start = ((), (), s32[]{:S(2)}) async-start(), calls=%async_computation.14 | async-start | bytes 5971968 | tf_op jit(solution)/shard_map/reduce_scatter | solution.py:223
  426.4 277.1 %reduce-scatter.13.cloned.1.call-start = ((), (), s32[]{:S(2)}) async-start(), calls=%async_computation.16 | async-start | bytes 2211840
  594.8 53.2 %all-to-all-start.1 = ((bf16[2048,3,192]{2,1,0:T(4,128)(2,1)}), bf16[2048,3,192]{2,1,0:T(4,128)(2,1)}, u32[]{:S(2)}, u32[]{:S(2)}) async-start(bf16[2048,3,192]{2,1,0:T(4,128)(2,1)} %copy.85), calls=%async_computation.4 | async-start | bytes 8388608 | tf_op jit(solution)/shard_map/all_to_all | solution.py:257
  648.0 7.1 copy-start.33
  648.0 7.1 copy-start.39
  660.6 44.9 %copy-start.1 = (f32[5,768]{1,0:T(8,128)S(1)}, f32[5,768]{1,0:T(8,128)}, u32[]{:S(2)}) copy-start(f32[5,768]{1,0:T(8,128)} %param.37) | copy-start | bytes 46084
  661.3 44.1 %copy-start.17 = (f32[512,768]{1,0:T(8,128)}, f32[512,768]{1,0:T(8,128)S(1)}, u32[]{:S(2)}) copy-start(f32[512,768]{1,0:T(8,128)S(1)} %multiply_add_fusion) | copy-start | bytes 4718596
  (61 other events, 264.3 us)
Sparse Core Ops, SparseCore 0:
  12.8 67.3 all-gather.20
  82.3 27.2 all-gather.8
  111.1 30.7 all-gather.10
  143.9 17.4 all-gather.12
  232.1 28.5 all-gather.14
  262.1 28.4 all-gather.16
  306.9 58.8 reduce-scatter.6
  372.3 28.4 all-gather.18
  407.7 37.9 reduce-scatter.8
  449.1 104.4 reduce-scatter.10
  588.0 67.6 reduce-scatter.12

commit v3 on v2

--- a/solution.py
+++ b/solution.py
@@ -145,8 +145,19 @@
     prefix_len = prefix[0]
     gelu_tanh = partial(jax.nn.gelu, approximate=True)
     fsdp_count = lax.axis_size("fsdp")
-    shards = (qkv_weight, out_weight, fc1_weight, fc2_weight)
+    qkv_cols = lax.all_gather(qkv_weight, "fsdp", axis=1, tiled=True)
+    qkv_full = qkv_cols
+    hidden_here = fc1_weight.shape[1]
+    qv_here = lax.dynamic_slice_in_dim(qv_bias, tp_rank * cols_here, cols_here, 1)
+    one_hot = (pass_ids[:, None] == jnp.arange(NPASS, dtype=jnp.int32)[None, :]).astype(jnp.float32)
+    block_in = tokens.astype(jnp.float32) + jnp.dot(
+        one_hot, pass_table, precision=HIGH, preferred_element_type=jnp.float32
+    )
+    normed, unit_one, inv_one = norm_forward(block_in, ln1_gain, ln1_bias)
+    normed_all = lax.all_gather(normed.astype(jnp.bfloat16), "tp", axis=0, tiled=True)
+    shards = (out_weight, fc1_weight, fc2_weight)
     packed = jnp.concatenate([piece.reshape(-1) for piece in shards])
+    packed, normed_all = lax.optimization_barrier((packed, normed_all))
     gathered = lax.all_gather(packed, "fsdp", axis=0, tiled=False)
     pieces = []
     offset = 0
@@ -154,27 +165,19 @@
         size = piece.size
         pieces.append(gathered[:, offset : offset + size].reshape((fsdp_count,) + piece.shape))
         offset += size
-    qkv_cols = jnp.moveaxis(pieces[0], 0, 1).reshape(3, -1, cols_here)
-    out_heads = jnp.moveaxis(pieces[1], 0, 1).reshape(out_weight.shape[0], -1)
-    fc1_part = pieces[2].reshape(-1, fc1_weight.shape[1])
-    fc2_part = jnp.moveaxis(pieces[3], 0, 1).reshape(fc2_weight.shape[0], -1)
+    out_heads = jnp.moveaxis(pieces[0], 0, 1).reshape(out_weight.shape[0], -1)
+    fc1_part = pieces[1].reshape(-1, fc1_weight.shape[1])
+    fc2_part = jnp.moveaxis(pieces[2], 0, 1).reshape(fc2_weight.shape[0], -1)
     out_all = lax.all_gather(out_heads, "tp", axis=0, tiled=True)
     qkv_all = lax.all_gather(qkv_cols, "tp", axis=2, tiled=True)
-    qkv_full, out_full = qkv_cols, out_heads
-    hidden_here = fc1_part.shape[1]
-    qv_here = lax.dynamic_slice_in_dim(qv_bias, tp_rank * cols_here, cols_here, 1)
-    one_hot = (pass_ids[:, None] == jnp.arange(NPASS, dtype=jnp.int32)[None, :]).astype(jnp.float32)
-    block_in = tokens.astype(jnp.float32) + jnp.dot(
-        one_hot, pass_table, precision=HIGH, preferred_element_type=jnp.float32
-    )
-    normed, unit_one, inv_one = norm_forward(block_in, ln1_gain, ln1_bias)
-    normed_all = lax.all_gather(normed.astype(jnp.bfloat16), "tp", axis=0, tiled=True)
+    out_full = out_heads
+    grad_rows = lax.all_gather(cotangent, "tp", axis=0, tiled=True)
     projected = jnp.einsum("rd,kdc->krc", normed_all, qkv_full, preferred_element_type=jnp.float32)
     queries = (projected[0] + qv_here[0]).astype(jnp.bfloat16).reshape(seq_len, heads_here, HD)
     keys_all = projected[1].astype(jnp.bfloat16).reshape(seq_len, heads_here, HD)
     values_all = (projected[2] + qv_here[1]).astype(jnp.bfloat16).reshape(seq_len, heads_here, HD)
     mixed, log_mass = attend_forward(queries, keys_all, values_all, prefix_len, scale)
-    mixed, qkv_all = lax.optimization_barrier((mixed, qkv_all))
+    mixed, grad_rows = lax.optimization_barrier((mixed, grad_rows))
     mixed_rows = lax.all_to_all(mixed, "tp", 0, 1, tiled=True)
     middle = block_in + jnp.dot(mixed_rows, out_all, preferred_element_type=jnp.float32) + out_bias
     normed_two, unit_two, inv_two = norm_forward(middle, ln2_gain, ln2_bias)
@@ -185,7 +188,6 @@
     before = jnp.dot(normed_rows, fc1_part, preferred_element_type=jnp.float32) + fc1_bias_here
     hidden = gelu_tanh(before).astype(jnp.bfloat16)
     fc2_partial = jnp.dot(hidden, fc2_part, preferred_element_type=jnp.float32).astype(jnp.bfloat16)
-    grad_rows = lax.all_gather(cotangent, "tp", axis=0, tiled=True)
     grad_hidden = matmul_nt(grad_rows, fc2_part)
     grad_before = jax.vjp(gelu_tanh, before)[1](grad_hidden)[0].astype(jnp.bfloat16)
     grad_fc1_bias = lax.dynamic_update_slice_in_dim(
@@ -198,6 +200,9 @@
     grad_fc2 = matmul_tn(hidden, grad_rows)
     grad_normed_two = lax.psum_scatter(
         matmul_nt(grad_before, fc1_part), "tp", scatter_dimension=0, tiled=True
+    )
+    grad_normed_two, fc2_partial, grad_fc1, grad_fc2 = lax.optimization_barrier(
+        (grad_normed_two, fc2_partial, grad_fc1, grad_fc2)
     )
     grad_fc2_bias = jnp.sum(grad_top, axis=0)
     grad_from_norm, grad_ln2_gain, grad_ln2_bias = norm_backward(
@@ -255,6 +260,7 @@
         "rd,rkc->kdc", normed_all, grad_proj, preferred_element_type=jnp.float32
     )
     grad_proj_rows = lax.all_to_all(grad_proj, "tp", 0, 2, tiled=True)
+    grad_proj_rows, qkv_all = lax.optimization_barrier((grad_proj_rows, qkv_all))
     grad_normed = jnp.einsum(
         "rkc,kdc->rd", grad_proj_rows, qkv_all, preferred_element_type=jnp.float32
     )

time: 720 us -> 687 us (0.954)
  waiting for transfers between devices: 224 us -> 161 us
  blocking collectives: 41.5 us -> 82.7 us
    all_gather x1, waiting for transfers between devices: 63.3 us -> 11.5 us  [on_device(): gathered = lax.all_gather(packed, 'fsdp', axis=0, tiled=False)]
    all_gather x0 -> x1, blocking collectives: none -> 41.6 us  [on_device(): qkv_cols = lax.all_gather(qkv_weight, 'fsdp', axis=1, tiled=True)]
    all_gather x1, waiting for transfers between devices: 19.9 us -> 0.02 us  [on_device(): grad_rows = lax.all_gather(cotangent, 'tp', axis=0, tiled=True)]
    reduce_scatter x1, waiting for transfers between devices: 58.8 us -> 39.3 us  [on_device(): lax.psum_scatter(matmul_nt(grad_before, fc1_part), 'tp', scatter_dimensio...]
    all_gather x1, waiting for transfers between devices: 15.2 us -> 29.8 us  [on_device(): lax.all_gather(normed.astype(jnp.bfloat16), 'tp', axis=0, tiled=True)]
    all_gather x1, waiting for transfers between devices: 0.01 us -> 13.1 us  [on_device(): lax.all_gather(grad_middle.astype(jnp.bfloat16), 'tp', axis=0, tiled=True)]
    unnamed x88 -> x107, local copies, waits for them, and re-layouts: 19.6 us -> 20.7 us
  transfers between devices with their start and end apart: 13 -> 13, of which waited for: 7 -> 7; matrix products, arithmetic and copies ran while one was open for 52% -> 54% of each run, Pallas kernels for 0% -> 0%
where the time goes in v3:
time: 687 us; the launch traced here: 682 us
  matrix products  220 us (32%)
  waiting for transfers between devices  161 us (23%)
  local copies, waits for them, and re-layouts  99.6 us (14%)
  other arithmetic  92.7 us (13%)
  blocking collectives  82.7 us (12%)
  between operations  14.8 us (2%)
  starting transfers between devices  9.76 us (1%)
    all_to_all x1, waiting for transfers between devices, on_device(): grad_proj_rows = lax.all_to_all(grad_proj, 'tp', 0, 2, tiled=True)  43.1 us
    all_gather x1, blocking collectives, on_device(): qkv_cols = lax.all_gather(qkv_weight, 'fsdp', axis=1, tiled=True)  41.6 us
    psum x1, blocking collectives, on_device(): lax.psum((grad_ln1_gain, grad_ln1_bias, grad_qv_bias, grad_out_bias, grad...  41.1 us
    reduce_scatter x1, waiting for transfers between devices, on_device(): lax.psum_scatter(matmul_nt(grad_before, fc1_part), 'tp', scatter_dimensio...  39.3 us
    dot_general x8, matrix products, block_scores(): jnp.einsum('qhe,khe->hqk', query_block, keys_all, preferred_element_type=...  36.5 us
    all_gather x1, waiting for transfers between devices, on_device(): lax.all_gather(normed.astype(jnp.bfloat16), 'tp', axis=0, tiled=True)  29.8 us
    dot_general x4, matrix products, one_block(): jnp.einsum('hqk,khe->qhe', probs_low, values_all, preferred_element_type=...  29.6 us
    reduce_sum x4, other arithmetic, one_block(): total_mass = jnp.sum(expo, axis=-1, keepdims=True)  27.1 us
  transfers between devices with their start and end apart: 13, of which 7 were waited for; matrix products, arithmetic and copies ran while one was open for 54% of the time, Pallas kernels for 0%

profile of v3, /device:TPU:0, one launch (start us, length us, event | category | flops | bytes accessed | tf_op | source)
XLA Modules:
  0.0 681.6 jit_solution(4154857412298804447)
XLA Ops:
  14.0 29.8 %all-gather.9.cloned.1.call-done = bf16[2048,768]{1,0:T(8,128)(2,1)} async-done(((bf16[512,768]{1,0:T(8,128)(2,1)}), bf16[2048,768]{1,0:T(8,128)(2,1)}) %all-gather.9.cloned.1.call-update) | async-done | bytes 3145744 | tf_op jit(solution)/shard_map/all_gather | solution.py:157
  45.8 41.6 %all_gather.28 = bf16[3,768,192]{2,0,1:T(4,128)(2,1)S(1)} all-gather(bf16[3,96,192]{2,0,1:T(4,128)(2,1)S(1)} %copy.112), channel_id=1, replica_groups=mesh['fsdp'=8,'tp'=4] {'fsdp'}, dimensions={1}, use_global_device_ids=true | all-gather | bytes 995328 | tf_op jit(solution)/shard_map/all_gather | solution.py:148
  98.6 11.5 %all-gather.21.cloned.1.call-done = bf16[1327104]{0:T(1024)(128)(2,1)} async-done(((bf16[165888]{0:T(1024)(128)(2,1)}), bf16[1327104]{0:T(1024)(128)(2,1)}) %all-gather.21.cloned.1.call-update) | async-done | bytes 2654224 | tf_op jit(solution)/shard_map/all_gather | solution.py:161
  117.2 91.9 %while.27 = (s32[]{:T(128)}, bf16[4,512,3,64]{1,3,2,0:T(8,128)(2,1)}, f32[4,3,512]{2,1,0:T(4,128)S(1)}, s32[4]{0:T(128)S(1)}, s32[]{:T(128)}, /*index=5*/bf16[4,...) while((s32[]{:T(128)}, ...), condition=%wide.region_5.6_spmd, body=%wide.region_2.5_spmd.sunk | while | flops 845251584 | bytes 43972740 | solution.py:74
  126.0 6.8 fusion.130
  132.8 7.4 %fusion.131 = bf16[4,512,3,64]{1,3,2,0:T(8,128)(2,1)} fusion(bf16[4,512,3,64]{1,3,2,0:T(8,128)(2,1)} %get-tuple-element.560, s32[]{:T(128)S(6)} %copy.153, bf16[2048,3,64]{0,2,1:T(8,128)(2,1)S(1)} %get-tuple-element.575, f32[3,512,2048]{2,1,0:T(8,128)} %get-tuple-element.535, f32[3,512]{1,0:T(4,128)S(1)} %fusion.130, ...), kind=kOutput, calls=%fused_computation.10.clone.1 | convolution fusion | flops 418480128 | bytes 14626820 | tf_op jit(solution)/shard_map/while/body/eval_jaxpr/hqk,khe->qhe/dot_general | solution.py:69
  149.1 6.8 fusion.130
  155.9 7.4 %fusion.131 = bf16[4,512,3,64]{1,3,2,0:T(8,128)(2,1)} fusion(bf16[4,512,3,64]{1,3,2,0:T(8,128)(2,1)} %get-tuple-element.560, s32[]{:T(128)S(6)} %copy.153, bf16[2048,3,64]{0,2,1:T(8,128)(2,1)S(1)} %get-tuple-element.575, f32[3,512,2048]{2,1,0:T(8,128)} %get-tuple-element.535, f32[3,512]{1,0:T(4,128)S(1)} %fusion.130, ...), kind=kOutput, calls=%fused_computation.10.clone.1 | convolution fusion | flops 418480128 | bytes 14626820 | tf_op jit(solution)/shard_map/while/body/eval_jaxpr/hqk,khe->qhe/dot_general | solution.py:69
  172.1 6.8 fusion.130
  178.8 7.4 %fusion.131 = bf16[4,512,3,64]{1,3,2,0:T(8,128)(2,1)} fusion(bf16[4,512,3,64]{1,3,2,0:T(8,128)(2,1)} %get-tuple-element.560, s32[]{:T(128)S(6)} %copy.153, bf16[2048,3,64]{0,2,1:T(8,128)(2,1)S(1)} %get-tuple-element.575, f32[3,512,2048]{2,1,0:T(8,128)} %get-tuple-element.535, f32[3,512]{1,0:T(4,128)S(1)} %fusion.130, ...), kind=kOutput, calls=%fused_computation.10.clone.1 | convolution fusion | flops 418480128 | bytes 14626820 | tf_op jit(solution)/shard_map/while/body/eval_jaxpr/hqk,khe->qhe/dot_general | solution.py:69
  195.0 6.8 fusion.130
  201.7 7.4 %fusion.131 = bf16[4,512,3,64]{1,3,2,0:T(8,128)(2,1)} fusion(bf16[4,512,3,64]{1,3,2,0:T(8,128)(2,1)} %get-tuple-element.560, s32[]{:T(128)S(6)} %copy.153, bf16[2048,3,64]{0,2,1:T(8,128)(2,1)S(1)} %get-tuple-element.575, f32[3,512,2048]{2,1,0:T(8,128)} %get-tuple-element.535, f32[3,512]{1,0:T(4,128)S(1)} %fusion.130, ...), kind=kOutput, calls=%fused_computation.10.clone.1 | convolution fusion | flops 418480128 | bytes 14626820 | tf_op jit(solution)/shard_map/while/body/eval_jaxpr/hqk,khe->qhe/dot_general | solution.py:69
  217.0 10.8 %all-to-all-done = bf16[4,512,192]{1,2,0:T(8,128)(2,1)S(1)} async-done(((bf16[4,512,192]{1,2,0:T(8,128)(2,1)}), bf16[4,512,192]{1,2,0:T(8,128)(2,1)S(1)}, u32[]{:S(2)}, u32[]{:S(2)}) %all-to-all-start) | async-done | bytes 786464 | tf_op jit(solution)/shard_map/all_to_all | solution.py:181
  248.4 11.9 %all-gather.15.cloned.1.call-done = bf16[2048,768]{1,0:T(8,128)(2,1)} async-done(((bf16[512,768]{1,0:T(8,128)(2,1)}), bf16[2048,768]{1,0:T(8,128)(2,1)}) %all-gather.15.cloned.1.call-update) | async-done | bytes 3145744 | tf_op jit(solution)/shard_map/all_gather | solution.py:187
  265.4 8.3 %convert_reduce_fusion = (f32[768]{0:T(1024)}, bf16[2048,768]{1,0:T(8,128)(2,1)S(1)}, bf16[2048,768]{1,0:T(8,128)(2,1)}) fusion(f32[2048,768]{1,0:T(8,128)S(1)} %fusion.69, f32[768]{0:T(1024)S(1)} %dynamic_slice.28, bf16[2048,768]{1,0:T(8,128)(2,1)S(1)} %copy-done.51, bf16[768,768]{0,1:T(8,128)(2,1)S(1)} %bitcast.202), kind=kOutput, calls=%fused_computation.64 | convolution fusion | flops 2455239936 | bytes 16914432 | tf_op jit(solution)/shard_map/dot_general | solution.py:34
  280.4 6.6 convolution_convert_fusion
  287.1 8.6 %fusion.72 = f32[768,768]{1,0:T(8,128)} fusion(bf16[2048,768]{1,0:T(8,128)(2,1)} %get-tuple-element.413, bf16[2048,768]{1,0:T(8,128)(2,1)} %all-gather.11.cloned.1.call-done), kind=kOutput, calls=%fused_computation.130 | convolution fusion | flops 2415919104 | bytes 8650752 | tf_op jit(solution)/shard_map/dot_general | solution.py:40
  299.7 39.3 %reduce-scatter.7.cloned.1.call-done = f32[512,768]{1,0:T(8,128)} async-done(((f32[2048,768]{1,0:T(8,128)}), f32[512,768]{1,0:T(8,128)}) %reduce-scatter.7.cloned.1.call-update) | async-done | bytes 1572880 | tf_op jit(solution)/shard_map/reduce_scatter | solution.py:201
  360.9 13.1 %all-gather.17.cloned.1.call-done = bf16[2048,768]{1,0:T(8,128)(2,1)} async-done(((bf16[512,768]{1,0:T(8,128)(2,1)}), bf16[2048,768]{1,0:T(8,128)(2,1)}) %all-gather.17.cloned.1.call-update) | async-done | bytes 3145744 | tf_op jit(solution)/shard_map/all_gather | solution.py:213
  396.7 137.9 %while.28 = (s32[]{:T(128)}, f32[2048,3,64]{0,2,1:T(8,128)}, f32[2048,3,64]{0,2,1:T(8,128)}, bf16[4,512,3,64]{1,3,2,0:T(8,128)(2,1)}, bf16[4,512,3,64]{1,3,2,0:T...) while((s32[]{:T(128)}, f32[2048,3,64]{0,2,1:T(8,128)}, ...), condition=%wide.region_13.14_spmd.clone, body=%wide.region_11.13_spmd.clone.sunk | while | flops 2064614400 | bytes 156684720 | solution.py:113
  557.6 6.9 %copy.124 = bf16[2048,3,192]{2,1,0:T(4,128)(2,1)} copy(bf16[2048,3,192]{0,2,1:T(8,128)(2,1)} %pad_maximum_fusion.1) | data formatting | bytes 4718592 | tf_op jit(solution)/shard_map/optimization_barrier | solution.py:241
  574.7 43.1 %all-to-all-done.1 = bf16[2048,3,192]{2,1,0:T(4,128)(2,1)} async-done(((bf16[2048,3,192]{2,1,0:T(4,128)(2,1)}), bf16[2048,3,192]{2,1,0:T(4,128)(2,1)}, u32[]{:S(2)}, u32[]{:S(2)}) %all-to-all-start.1) | async-done | bytes 2359328 | tf_op jit(solution)/shard_map/all_to_all | solution.py:262
  617.8 7.1 %copy.126 = bf16[512,3,4,192]{0,3,2,1:T(8,128)(2,1)} copy(bf16[512,3,4,192]{3,1,0,2:T(4,128)(2,1)} %bitcast.25) | data formatting | bytes 4718592 | tf_op jit(solution)/shard_map/all_to_all | solution.py:262
  631.8 41.1 %all-reduce = (f32[768]{0:T(1024)}, f32[768]{0:T(1024)}, f32[2,768]{1,0:T(2,128)}, f32[768]{0:T(1024)}, f32[768]{0:T(1024)}, /*index=5*/f32[768]{0:T(1024)}, f32[3072]{0:T(1024)}, f32[768]{0:T(1024)}, f32[5,768]{1,0:T(8,128)}) all-reduce(f32[768]{0:T(1024)S(1)} %get-tuple-element.346, ...), channel_id=1, replica_groups=mesh['fsdp'=8,'tp'=4] {'fsdp','tp'}, use_global_device_ids=true, to_apply=%region_20.21 | all-reduce | flops 13056 | bytes 104448 | tf_op jit(solution)/shard_map/psum | solution.py:279
  (355 shorter events, 329.0 us)
Async XLA Ops:
  7.2 36.6 %all-gather.9.cloned.1.call-start = ((), (), s32[]{:S(2)}) async-start(), calls=%async_computation.6 | async-start | bytes 3932160 | tf_op jit(solution)/shard_map/all_gather | solution.py:157
  12.4 33.3 %copy-start.33 = (bf16[3,96,192]{2,1,0:T(8,128)(2,1)S(1)}, bf16[3,96,192]{2,1,0:T(8,128)(2,1)}, u32[]{:S(2)}) copy-start(bf16[3,96,192]{2,1,0:T(8,128)(2,1)} %param.25) | copy-start | bytes 331780
  12.4 97.7 %all-gather.21.cloned.1.call-start = ((), (), s32[]{:S(2)}) async-start(), calls=%async_computation.15 | async-start | bytes 2985984 | tf_op jit(solution)/shard_map/all_gather | solution.py:161
  43.8 167.6 %all-gather.11.cloned.1.call-start = ((), (), s32[]{:S(2)}) async-start(), calls=%async_computation.7 | async-start | bytes 3932160 | tf_op jit(solution)/shard_map/all_gather | solution.py:174
  44.5 183.2 %all-gather.13.cloned.1.call-start = ((), (), s32[]{:S(2)}) async-start(), calls=%async_computation.8 | async-start | bytes 1474560 | tf_op jit(solution)/shard_map/all_gather | solution.py:171
  211.2 17.5 %copy-start.53 = (f32[768]{0:T(1024)S(1)}, f32[768]{0:T(1024)}, u32[]{:S(2)}) copy-start(f32[768]{0:T(1024)} %param.32) | copy-start | bytes 9220
  211.4 16.4 %copy-start.15 = (bf16[24,8,4,512]{3,1,2,0:T(8,128)(2,1)}, bf16[24,8,4,512]{3,1,2,0:T(8,128)(2,1)S(1)}, u32[]{:S(2)}) copy-start(bf16[24,8,4,512]{3,1,2,0:T(8,128)(2,1)S(1)} %copy.140) | copy-start | bytes 2359300
  212.5 15.3 %all-to-all-start = ((bf16[4,512,192]{1,2,0:T(8,128)(2,1)}), bf16[4,512,192]{1,2,0:T(8,128)(2,1)S(1)}, u32[]{:S(2)}, u32[]{:S(2)}) async-start(bf16[4,512,192]{1,2,0:T(8,128)(2,1)} %bitcast.191), calls=%async_computation | async-start | bytes 1572864 | tf_op jit(solution)/shard_map/all_to_all | solution.py:181
  216.2 44.1 %all-gather.15.cloned.1.call-start = ((), (), s32[]{:S(2)}) async-start(), calls=%async_computation.9 | async-start | bytes 3932160 | tf_op jit(solution)/shard_map/all_gather | solution.py:187
  231.6 110.3 %copy-start.8 = (f32[512,768]{1,0:T(8,128)}, f32[512,768]{1,0:T(8,128)S(1)}, u32[]{:S(2)}) copy-start(f32[512,768]{1,0:T(8,128)S(1)} %get-tuple-element.422) | copy-start | bytes 4718596
  233.2 105.8 %reduce-scatter.7.cloned.1.call-start = ((), (), s32[]{:S(2)}) async-start(), calls=%async_computation.10 | async-start | bytes 7864320 | tf_op jit(solution)/shard_map/reduce_scatter | solution.py:201
  265.4 10.1 %copy-start.27 = (bf16[768,768]{1,0:T(8,128)(2,1)S(1)}, bf16[768,768]{1,0:T(8,128)(2,1)}, u32[]{:S(2)}) copy-start(bf16[768,768]{1,0:T(8,128)(2,1)} %reshape_reshape.11) | copy-start | bytes 3538948
  280.0 94.0 %all-gather.17.cloned.1.call-start = ((), (), s32[]{:S(2)}) async-start(), calls=%async_computation.11 | async-start | bytes 3932160 | tf_op jit(solution)/shard_map/all_gather | solution.py:213
  287.1 8.6 %copy-start.52 = (bf16[2048,768]{1,0:T(8,128)(2,1)S(1)}, bf16[2048,768]{1,0:T(8,128)(2,1)}, u32[]{:S(2)}) copy-start(bf16[2048,768]{1,0:T(8,128)(2,1)} %all-gather.15.cloned.1.call-done) | copy-start | bytes 9437188
  287.1 8.6 %copy-start.55 = (bf16[2048,768]{1,0:T(8,128)(2,1)S(1)}, bf16[2048,768]{1,0:T(8,128)(2,1)}, u32[]{:S(2)}) copy-start(bf16[2048,768]{1,0:T(8,128)(2,1)} %copy-done.54) | copy-start | bytes 9437188
  345.4 195.3 %reduce-scatter.9.cloned.1.call-start = ((), (), s32[]{:S(2)}) async-start(), calls=%async_computation.12 | async-start | bytes 3932160 | tf_op jit(solution)/shard_map/reduce_scatter | solution.py:217
  355.7 18.3 %copy-start.16 = (bf16[24,8,4,512]{3,1,2,0:T(8,128)(2,1)S(1)}, bf16[24,8,4,512]{3,1,2,0:T(8,128)(2,1)}, u32[]{:S(2)}) copy-start(bf16[24,8,4,512]{3,1,2,0:T(8,128)(2,1)} %copy-done.15) | copy-start | bytes 2359300
  376.8 166.4 %reduce-scatter.11.cloned.1.call-start = ((), (), s32[]{:S(2)}) async-start(), calls=%async_computation.13 | async-start | bytes 5971968 | tf_op jit(solution)/shard_map/reduce_scatter | solution.py:228
  389.3 235.6 %all-gather.19.cloned.1.call-start = ((), (), s32[]{:S(2)}) async-start(), calls=%async_computation.14 | async-start | bytes 4423680 | tf_op jit(solution)/shard_map/all_gather | solution.py:172
  389.8 283.1 %reduce-scatter.13.cloned.1.call-start = ((), (), s32[]{:S(2)}) async-start(), calls=%async_computation.16 | async-start | bytes 2211840
  564.5 53.2 %all-to-all-start.1 = ((bf16[2048,3,192]{2,1,0:T(4,128)(2,1)}), bf16[2048,3,192]{2,1,0:T(4,128)(2,1)}, u32[]{:S(2)}, u32[]{:S(2)}) async-start(bf16[2048,3,192]{2,1,0:T(4,128)(2,1)} %copy.124), calls=%async_computation.4 | async-start | bytes 8388608 | tf_op jit(solution)/shard_map/all_to_all | solution.py:262
  617.8 7.1 %copy-start.45 = (f32[768]{0:T(1024)S(1)}, f32[768]{0:T(1024)}, u32[]{:S(2)}) copy-start(f32[768]{0:T(1024)} %param.29) | copy-start | bytes 9220
  630.4 44.4 %copy-start.1 = (f32[5,768]{1,0:T(8,128)S(1)}, f32[5,768]{1,0:T(8,128)}, u32[]{:S(2)}) copy-start(f32[5,768]{1,0:T(8,128)} %param.37) | copy-start | bytes 46084
  631.1 43.8 %copy-start.17 = (f32[512,768]{1,0:T(8,128)}, f32[512,768]{1,0:T(8,128)S(1)}, u32[]{:S(2)}) copy-start(f32[512,768]{1,0:T(8,128)S(1)} %multiply_add_fusion) | copy-start | bytes 4718596
  (69 other events, 269.4 us)
Sparse Core Ops, SparseCore 0:
  12.5 31.2 all-gather.8
  46.0 64.1 all-gather.20
  111.7 27.5 all-gather.10
  141.2 17.4 all-gather.12
  233.3 26.9 all-gather.14
  280.1 58.8 reduce-scatter.6
  345.5 28.4 all-gather.16
  376.9 37.8 reduce-scatter.8
  418.4 104.4 reduce-scatter.10
  524.3 30.3 all-gather.18
  558.2 67.6 reduce-scatter.12

commit v4 on v3

--- a/solution.py
+++ b/solution.py
@@ -157,7 +157,8 @@
     normed_all = lax.all_gather(normed.astype(jnp.bfloat16), "tp", axis=0, tiled=True)
     shards = (out_weight, fc1_weight, fc2_weight)
     packed = jnp.concatenate([piece.reshape(-1) for piece in shards])
-    packed, normed_all = lax.optimization_barrier((packed, normed_all))
+    packed, qkv_cols, normed_all = lax.optimization_barrier((packed, qkv_cols, normed_all))
+    qkv_full = qkv_cols
     gathered = lax.all_gather(packed, "fsdp", axis=0, tiled=False)
     pieces = []
     offset = 0

time: 687 us -> 683 us (level)
    all_gather x1, waiting for transfers between devices: 29.8 us -> 0.01 us  [on_device(): lax.all_gather(normed.astype(jnp.bfloat16), 'tp', axis=0, tiled=True)]
    all_gather x1, waiting for transfers between devices: 11.5 us -> 40.9 us  [on_device(): gathered = lax.all_gather(packed, 'fsdp', axis=0, tiled=False)]
  transfers between devices with their start and end apart: 13 -> 13, of which waited for: 7 -> 6; matrix products, arithmetic and copies ran while one was open for 54% -> 55% of each run, Pallas kernels for 0% -> 0%
where the time goes in v4:
time: 683 us; the launch traced here: 678 us
  matrix products  220 us (32%)
  waiting for transfers between devices  160 us (23%)
  local copies, waits for them, and re-layouts  99.8 us (15%)
  other arithmetic  92.7 us (14%)
  blocking collectives  80 us (12%)
  between operations  14.8 us (2%)
  starting transfers between devices  9.77 us (1%)
    all_to_all x1, waiting for transfers between devices, on_device(): grad_proj_rows = lax.all_to_all(grad_proj, 'tp', 0, 2, tiled=True)  43.1 us
    psum x1, blocking collectives, on_device(): lax.psum((grad_ln1_gain, grad_ln1_bias, grad_qv_bias, grad_out_bias, grad...  41.1 us
    all_gather x1, waiting for transfers between devices, on_device(): gathered = lax.all_gather(packed, 'fsdp', axis=0, tiled=False)  40.9 us
    reduce_scatter x1, waiting for transfers between devices, on_device(): lax.psum_scatter(matmul_nt(grad_before, fc1_part), 'tp', scatter_dimensio...  39.3 us
    all_gather x1, blocking collectives, on_device(): qkv_cols = lax.all_gather(qkv_weight, 'fsdp', axis=1, tiled=True)  38.9 us
    dot_general x8, matrix products, block_scores(): jnp.einsum('qhe,khe->hqk', query_block, keys_all, preferred_element_type=...  36.5 us
    dot_general x4, matrix products, one_block(): jnp.einsum('hqk,khe->qhe', probs_low, values_all, preferred_element_type=...  29.6 us
    reduce_sum x4, other arithmetic, one_block(): total_mass = jnp.sum(expo, axis=-1, keepdims=True)  27.1 us
  transfers between devices with their start and end apart: 13, of which 6 were waited for; matrix products, arithmetic and copies ran while one was open for 55% of the time, Pallas kernels for 0%

profile of v4, /device:TPU:0, one launch (start us, length us, event | category | flops | bytes accessed | tf_op | source)
XLA Modules:
  0.0 677.8 jit_solution(10378885999588353219)
XLA Ops:
  13.4 38.9 %all_gather.27 = bf16[3,768,192]{2,0,1:T(4,128)(2,1)S(1)} all-gather(bf16[3,96,192]{2,0,1:T(4,128)(2,1)S(1)} %copy.107), channel_id=1, replica_groups=mesh['fsdp'=8,'tp'=4] {'fsdp'}, dimensions={1}, use_global_device_ids=true | all-gather | bytes 995328 | tf_op jit(solution)/shard_map/all_gather | solution.py:148
  66.2 40.9 %all-gather.21.cloned.1.call-done = bf16[1327104]{0:T(1024)(128)(2,1)} async-done(((bf16[165888]{0:T(1024)(128)(2,1)}), bf16[1327104]{0:T(1024)(128)(2,1)}) %all-gather.21.cloned.1.call-update) | async-done | bytes 2654224 | tf_op jit(solution)/shard_map/all_gather | solution.py:162
  114.2 91.9 %while.27 = (s32[]{:T(128)}, bf16[4,512,3,64]{1,3,2,0:T(8,128)(2,1)}, f32[4,3,512]{2,1,0:T(4,128)S(1)}, s32[4]{0:T(128)S(1)}, s32[]{:T(128)}, /*index=5*/bf16[4,...) while((s32[]{:T(128)}, ...), condition=%wide.region_5.6_spmd, body=%wide.region_2.5_spmd.sunk | while | flops 845251584 | bytes 43972740 | solution.py:74
  123.0 6.8 %fusion.129 = f32[3,512]{1,0:T(4,128)S(1)} fusion(f32[3,512,2048]{2,1,0:T(8,128)} %get-tuple-element.537, f32[3,512]{1,0:T(4,128)S(1)} %get-tuple-element.538, pred[512,2048]{1,0:T(8,128)(4,1)S(1)} %fusion.127), kind=kLoop, calls=%fused_computation.4.clone.1 | loop fusion | flops 12581376 | bytes 13643776 | tf_op jit(solution)/shard_map/while/body/eval_jaxpr/reduce_sum | solution.py:67
  129.8 7.4 %fusion.130 = bf16[4,512,3,64]{1,3,2,0:T(8,128)(2,1)} fusion(bf16[4,512,3,64]{1,3,2,0:T(8,128)(2,1)} %get-tuple-element.562, s32[]{:T(128)S(6)} %copy.148, bf16[2048,3,64]{0,2,1:T(8,128)(2,1)S(1)} %get-tuple-element.577, f32[3,512,2048]{2,1,0:T(8,128)} %get-tuple-element.537, f32[3,512]{1,0:T(4,128)S(1)} %fusion.129, ...), kind=kOutput, calls=%fused_computation.10.clone.1 | convolution fusion | flops 418480128 | bytes 14626820 | tf_op jit(solution)/shard_map/while/body/eval_jaxpr/hqk,khe->qhe/dot_general | solution.py:69
  146.1 6.8 %fusion.129 = f32[3,512]{1,0:T(4,128)S(1)} fusion(f32[3,512,2048]{2,1,0:T(8,128)} %get-tuple-element.537, f32[3,512]{1,0:T(4,128)S(1)} %get-tuple-element.538, pred[512,2048]{1,0:T(8,128)(4,1)S(1)} %fusion.127), kind=kLoop, calls=%fused_computation.4.clone.1 | loop fusion | flops 12581376 | bytes 13643776 | tf_op jit(solution)/shard_map/while/body/eval_jaxpr/reduce_sum | solution.py:67
  152.9 7.4 %fusion.130 = bf16[4,512,3,64]{1,3,2,0:T(8,128)(2,1)} fusion(bf16[4,512,3,64]{1,3,2,0:T(8,128)(2,1)} %get-tuple-element.562, s32[]{:T(128)S(6)} %copy.148, bf16[2048,3,64]{0,2,1:T(8,128)(2,1)S(1)} %get-tuple-element.577, f32[3,512,2048]{2,1,0:T(8,128)} %get-tuple-element.537, f32[3,512]{1,0:T(4,128)S(1)} %fusion.129, ...), kind=kOutput, calls=%fused_computation.10.clone.1 | convolution fusion | flops 418480128 | bytes 14626820 | tf_op jit(solution)/shard_map/while/body/eval_jaxpr/hqk,khe->qhe/dot_general | solution.py:69
  169.1 6.8 fusion.129
  175.8 7.4 %fusion.130 = bf16[4,512,3,64]{1,3,2,0:T(8,128)(2,1)} fusion(bf16[4,512,3,64]{1,3,2,0:T(8,128)(2,1)} %get-tuple-element.562, s32[]{:T(128)S(6)} %copy.148, bf16[2048,3,64]{0,2,1:T(8,128)(2,1)S(1)} %get-tuple-element.577, f32[3,512,2048]{2,1,0:T(8,128)} %get-tuple-element.537, f32[3,512]{1,0:T(4,128)S(1)} %fusion.129, ...), kind=kOutput, calls=%fused_computation.10.clone.1 | convolution fusion | flops 418480128 | bytes 14626820 | tf_op jit(solution)/shard_map/while/body/eval_jaxpr/hqk,khe->qhe/dot_general | solution.py:69
  192.0 6.8 fusion.129
  198.7 7.4 %fusion.130 = bf16[4,512,3,64]{1,3,2,0:T(8,128)(2,1)} fusion(bf16[4,512,3,64]{1,3,2,0:T(8,128)(2,1)} %get-tuple-element.562, s32[]{:T(128)S(6)} %copy.148, bf16[2048,3,64]{0,2,1:T(8,128)(2,1)S(1)} %get-tuple-element.577, f32[3,512,2048]{2,1,0:T(8,128)} %get-tuple-element.537, f32[3,512]{1,0:T(4,128)S(1)} %fusion.129, ...), kind=kOutput, calls=%fused_computation.10.clone.1 | convolution fusion | flops 418480128 | bytes 14626820 | tf_op jit(solution)/shard_map/while/body/eval_jaxpr/hqk,khe->qhe/dot_general | solution.py:69
  214.0 10.8 %all-to-all-done = bf16[4,512,192]{1,2,0:T(8,128)(2,1)S(1)} async-done(((bf16[4,512,192]{1,2,0:T(8,128)(2,1)}), bf16[4,512,192]{1,2,0:T(8,128)(2,1)S(1)}, u32[]{:S(2)}, u32[]{:S(2)}) %all-to-all-start) | async-done | bytes 786464 | tf_op jit(solution)/shard_map/all_to_all | solution.py:182
  245.4 11.1 %all-gather.15.cloned.1.call-done = bf16[2048,768]{1,0:T(8,128)(2,1)} async-done(((bf16[512,768]{1,0:T(8,128)(2,1)}), bf16[2048,768]{1,0:T(8,128)(2,1)}) %all-gather.15.cloned.1.call-update) | async-done | bytes 3145744 | tf_op jit(solution)/shard_map/all_gather | solution.py:188
  261.7 8.3 %convert_reduce_fusion = (f32[768]{0:T(1024)}, bf16[2048,768]{1,0:T(8,128)(2,1)S(1)}, bf16[2048,768]{1,0:T(8,128)(2,1)}) fusion(f32[2048,768]{1,0:T(8,128)S(1)} %fusion.69, f32[768]{0:T(1024)S(1)} %dynamic_slice.28, bf16[2048,768]{1,0:T(8,128)(2,1)S(1)} %copy-done.51, bf16[768,768]{0,1:T(8,128)(2,1)S(1)} %bitcast.196), kind=kOutput, calls=%fused_computation.64 | convolution fusion | flops 2455239936 | bytes 16914432 | tf_op jit(solution)/shard_map/dot_general | solution.py:34
  276.8 6.6 convolution_convert_fusion
  283.4 8.6 %fusion.72 = f32[768,768]{1,0:T(8,128)} fusion(bf16[2048,768]{1,0:T(8,128)(2,1)} %get-tuple-element.415, bf16[2048,768]{1,0:T(8,128)(2,1)} %all-gather.11.cloned.1.call-done), kind=kOutput, calls=%fused_computation.131 | convolution fusion | flops 2415919104 | bytes 8650752 | tf_op jit(solution)/shard_map/dot_general | solution.py:40
  296.0 39.3 %reduce-scatter.7.cloned.1.call-done = f32[512,768]{1,0:T(8,128)} async-done(((f32[2048,768]{1,0:T(8,128)}), f32[512,768]{1,0:T(8,128)}) %reduce-scatter.7.cloned.1.call-update) | async-done | bytes 1572880 | tf_op jit(solution)/shard_map/reduce_scatter | solution.py:202
  357.2 13.1 %all-gather.17.cloned.1.call-done = bf16[2048,768]{1,0:T(8,128)(2,1)} async-done(((bf16[512,768]{1,0:T(8,128)(2,1)}), bf16[2048,768]{1,0:T(8,128)(2,1)}) %all-gather.17.cloned.1.call-update) | async-done | bytes 3145744 | tf_op jit(solution)/shard_map/all_gather | solution.py:214
  393.0 137.9 %while.28 = (s32[]{:T(128)}, f32[2048,3,64]{0,2,1:T(8,128)}, f32[2048,3,64]{0,2,1:T(8,128)}, bf16[4,512,3,64]{1,3,2,0:T(8,128)(2,1)}, bf16[4,512,3,64]{1,3,2,0:T...) while((s32[]{:T(128)}, f32[2048,3,64]{0,2,1:T(8,128)}, ...), condition=%wide.region_13.14_spmd.clone, body=%wide.region_11.13_spmd.clone.sunk | while | flops 2064614400 | bytes 156684720 | solution.py:113
  466.9 6.4 fusion.143
  553.9 6.9 %copy.119 = bf16[2048,3,192]{2,1,0:T(4,128)(2,1)} copy(bf16[2048,3,192]{0,2,1:T(8,128)(2,1)} %pad_maximum_fusion.1) | data formatting | bytes 4718592 | tf_op jit(solution)/shard_map/optimization_barrier | solution.py:242
  570.9 43.1 %all-to-all-done.1 = bf16[2048,3,192]{2,1,0:T(4,128)(2,1)} async-done(((bf16[2048,3,192]{2,1,0:T(4,128)(2,1)}), bf16[2048,3,192]{2,1,0:T(4,128)(2,1)}, u32[]{:S(2)}, u32[]{:S(2)}) %all-to-all-start.1) | async-done | bytes 2359328 | tf_op jit(solution)/shard_map/all_to_all | solution.py:263
  614.1 7.1 %copy.121 = bf16[512,3,4,192]{0,3,2,1:T(8,128)(2,1)} copy(bf16[512,3,4,192]{3,1,0,2:T(4,128)(2,1)} %bitcast.22) | data formatting | bytes 4718592 | tf_op jit(solution)/shard_map/all_to_all | solution.py:263
  628.1 41.1 %all-reduce = (f32[768]{0:T(1024)}, f32[768]{0:T(1024)}, f32[2,768]{1,0:T(2,128)}, f32[768]{0:T(1024)}, f32[768]{0:T(1024)}, /*index=5*/f32[768]{0:T(1024)}, f32[3072]{0:T(1024)}, f32[768]{0:T(1024)}, f32[5,768]{1,0:T(8,128)}) all-reduce(f32[768]{0:T(1024)S(1)} %get-tuple-element.348, ...), channel_id=1, replica_groups=mesh['fsdp'=8,'tp'=4] {'fsdp','tp'}, use_global_device_ids=true, to_apply=%region_20.21 | all-reduce | flops 13056 | bytes 104448 | tf_op jit(solution)/shard_map/psum | solution.py:280
  (355 shorter events, 322.7 us)
Async XLA Ops:
  7.2 45.8 %all-gather.9.cloned.1.call-start = ((), (), s32[]{:S(2)}) async-start(), calls=%async_computation.6 | async-start | bytes 3932160 | tf_op jit(solution)/shard_map/all_gather | solution.py:157
  11.2 41.1 %copy-start.38 = (f32[512]{0:T(512)}, f32[512]{0:T(512)S(1)}, u32[]{:S(2)}) copy-start(f32[512]{0:T(512)S(1)} %add_rsqrt_fusion.1) | copy-start | bytes 6148
  12.4 94.7 %all-gather.21.cloned.1.call-start = ((), (), s32[]{:S(2)}) async-start(), calls=%async_computation.15 | async-start | bytes 2985984 | tf_op jit(solution)/shard_map/all_gather | solution.py:162
  53.1 155.3 %all-gather.11.cloned.1.call-start = ((), (), s32[]{:S(2)}) async-start(), calls=%async_computation.7 | async-start | bytes 3932160 | tf_op jit(solution)/shard_map/all_gather | solution.py:175
  53.8 171.0 %all-gather.13.cloned.1.call-start = ((), (), s32[]{:S(2)}) async-start(), calls=%async_computation.8 | async-start | bytes 1474560 | tf_op jit(solution)/shard_map/all_gather | solution.py:172
  208.2 17.5 %copy-start.53 = (f32[768]{0:T(1024)S(1)}, f32[768]{0:T(1024)}, u32[]{:S(2)}) copy-start(f32[768]{0:T(1024)} %param.32) | copy-start | bytes 9220
  208.4 16.4 %copy-start.15 = (bf16[24,8,4,512]{3,1,2,0:T(8,128)(2,1)}, bf16[24,8,4,512]{3,1,2,0:T(8,128)(2,1)S(1)}, u32[]{:S(2)}) copy-start(bf16[24,8,4,512]{3,1,2,0:T(8,128)(2,1)S(1)} %copy.135) | copy-start | bytes 2359300
  209.5 15.3 %all-to-all-start = ((bf16[4,512,192]{1,2,0:T(8,128)(2,1)}), bf16[4,512,192]{1,2,0:T(8,128)(2,1)S(1)}, u32[]{:S(2)}, u32[]{:S(2)}) async-start(bf16[4,512,192]{1,2,0:T(8,128)(2,1)} %bitcast.185), calls=%async_computation | async-start | bytes 1572864 | tf_op jit(solution)/shard_map/all_to_all | solution.py:182
  213.2 43.4 %all-gather.15.cloned.1.call-start = ((), (), s32[]{:S(2)}) async-start(), calls=%async_computation.9 | async-start | bytes 3932160 | tf_op jit(solution)/shard_map/all_gather | solution.py:188
  228.6 109.6 %copy-start.8 = (f32[512,768]{1,0:T(8,128)}, f32[512,768]{1,0:T(8,128)S(1)}, u32[]{:S(2)}) copy-start(f32[512,768]{1,0:T(8,128)S(1)} %get-tuple-element.424) | copy-start | bytes 4718596
  230.2 105.1 %reduce-scatter.7.cloned.1.call-start = ((), (), s32[]{:S(2)}) async-start(), calls=%async_computation.10 | async-start | bytes 7864320 | tf_op jit(solution)/shard_map/reduce_scatter | solution.py:202
  261.7 10.1 %copy-start.27 = (bf16[768,768]{1,0:T(8,128)(2,1)S(1)}, bf16[768,768]{1,0:T(8,128)(2,1)}, u32[]{:S(2)}) copy-start(bf16[768,768]{1,0:T(8,128)(2,1)} %reshape_reshape.11) | copy-start | bytes 3538948
  276.3 94.0 %all-gather.17.cloned.1.call-start = ((), (), s32[]{:S(2)}) async-start(), calls=%async_computation.11 | async-start | bytes 3932160 | tf_op jit(solution)/shard_map/all_gather | solution.py:214
  283.4 8.6 %copy-start.52 = (bf16[2048,768]{1,0:T(8,128)(2,1)S(1)}, bf16[2048,768]{1,0:T(8,128)(2,1)}, u32[]{:S(2)}) copy-start(bf16[2048,768]{1,0:T(8,128)(2,1)} %all-gather.15.cloned.1.call-done) | copy-start | bytes 9437188
  283.4 8.6 %copy-start.55 = (bf16[2048,768]{1,0:T(8,128)(2,1)S(1)}, bf16[2048,768]{1,0:T(8,128)(2,1)}, u32[]{:S(2)}) copy-start(bf16[2048,768]{1,0:T(8,128)(2,1)} %copy-done.54) | copy-start | bytes 9437188
  341.7 195.3 %reduce-scatter.9.cloned.1.call-start = ((), (), s32[]{:S(2)}) async-start(), calls=%async_computation.12 | async-start | bytes 3932160 | tf_op jit(solution)/shard_map/reduce_scatter | solution.py:218
  352.1 18.3 %copy-start.16 = (bf16[24,8,4,512]{3,1,2,0:T(8,128)(2,1)S(1)}, bf16[24,8,4,512]{3,1,2,0:T(8,128)(2,1)}, u32[]{:S(2)}) copy-start(bf16[24,8,4,512]{3,1,2,0:T(8,128)(2,1)} %copy-done.15) | copy-start | bytes 2359300
  373.1 166.4 %reduce-scatter.11.cloned.1.call-start = ((), (), s32[]{:S(2)}) async-start(), calls=%async_computation.13 | async-start | bytes 5971968 | tf_op jit(solution)/shard_map/reduce_scatter | solution.py:229
  385.6 235.6 %all-gather.19.cloned.1.call-start = ((), (), s32[]{:S(2)}) async-start(), calls=%async_computation.14 | async-start | bytes 4423680 | tf_op jit(solution)/shard_map/all_gather | solution.py:173
  386.2 283.1 %reduce-scatter.13.cloned.1.call-start = ((), (), s32[]{:S(2)}) async-start(), calls=%async_computation.16 | async-start | bytes 2211840
  560.8 53.2 %all-to-all-start.1 = ((bf16[2048,3,192]{2,1,0:T(4,128)(2,1)}), bf16[2048,3,192]{2,1,0:T(4,128)(2,1)}, u32[]{:S(2)}, u32[]{:S(2)}) async-start(bf16[2048,3,192]{2,1,0:T(4,128)(2,1)} %copy.119), calls=%async_computation.4 | async-start | bytes 8388608 | tf_op jit(solution)/shard_map/all_to_all | solution.py:263
  614.0 7.1 %copy-start.45 = (f32[768]{0:T(1024)S(1)}, f32[768]{0:T(1024)}, u32[]{:S(2)}) copy-start(f32[768]{0:T(1024)} %param.29) | copy-start | bytes 9220
  626.7 44.4 %copy-start.1 = (f32[5,768]{1,0:T(8,128)S(1)}, f32[5,768]{1,0:T(8,128)}, u32[]{:S(2)}) copy-start(f32[5,768]{1,0:T(8,128)} %param.37) | copy-start | bytes 46084
  627.3 43.8 %copy-start.17 = (f32[512,768]{1,0:T(8,128)}, f32[512,768]{1,0:T(8,128)S(1)}, u32[]{:S(2)}) copy-start(f32[512,768]{1,0:T(8,128)S(1)} %multiply_add_fusion) | copy-start | bytes 4718596
  (69 other events, 269.3 us)
Sparse Core Ops, SparseCore 0:
  12.5 31.2 all-gather.8
  53.2 53.8 all-gather.20
  108.7 27.0 all-gather.10
  137.8 17.4 all-gather.12
  230.3 26.2 all-gather.14
  276.4 58.8 reduce-scatter.6
  341.8 28.4 all-gather.16
  373.2 37.8 reduce-scatter.8
  414.7 104.4 reduce-scatter.10
  520.6 30.3 all-gather.18
  554.6 67.5 reduce-scatter.12

commit v5 on v4

--- a/solution.py
+++ b/solution.py
@@ -155,30 +155,33 @@
     )
     normed, unit_one, inv_one = norm_forward(block_in, ln1_gain, ln1_bias)
     normed_all = lax.all_gather(normed.astype(jnp.bfloat16), "tp", axis=0, tiled=True)
-    shards = (out_weight, fc1_weight, fc2_weight)
+    out_pieces = lax.all_gather(out_weight, ("fsdp", "tp"), axis=0, tiled=False)
+    out_pieces = out_pieces.reshape((fsdp_count, tp_count) + out_weight.shape)
+    out_all = jnp.transpose(out_pieces, (1, 2, 0, 3)).reshape(
+        tp_count * out_weight.shape[0], fsdp_count * out_weight.shape[1]
+    )
+    out_full = lax.dynamic_slice_in_dim(out_all, tp_rank * out_weight.shape[0], out_weight.shape[0], 0)
+    shards = (fc1_weight, fc2_weight)
     packed = jnp.concatenate([piece.reshape(-1) for piece in shards])
     packed, qkv_cols, normed_all = lax.optimization_barrier((packed, qkv_cols, normed_all))
     qkv_full = qkv_cols
     gathered = lax.all_gather(packed, "fsdp", axis=0, tiled=False)
+    qkv_all = lax.all_gather(qkv_cols, "tp", axis=2, tiled=True)
+    grad_rows = lax.all_gather(cotangent, "tp", axis=0, tiled=True)
+    projected = jnp.einsum("rd,kdc->krc", normed_all, qkv_full, preferred_element_type=jnp.float32)
+    queries = (projected[0] + qv_here[0]).astype(jnp.bfloat16).reshape(seq_len, heads_here, HD)
+    keys_all = projected[1].astype(jnp.bfloat16).reshape(seq_len, heads_here, HD)
+    values_all = (projected[2] + qv_here[1]).astype(jnp.bfloat16).reshape(seq_len, heads_here, HD)
+    mixed, log_mass = attend_forward(queries, keys_all, values_all, prefix_len, scale)
+    mixed, grad_rows, gathered = lax.optimization_barrier((mixed, grad_rows, gathered))
     pieces = []
     offset = 0
     for piece in shards:
         size = piece.size
         pieces.append(gathered[:, offset : offset + size].reshape((fsdp_count,) + piece.shape))
         offset += size
-    out_heads = jnp.moveaxis(pieces[0], 0, 1).reshape(out_weight.shape[0], -1)
-    fc1_part = pieces[1].reshape(-1, fc1_weight.shape[1])
-    fc2_part = jnp.moveaxis(pieces[2], 0, 1).reshape(fc2_weight.shape[0], -1)
-    out_all = lax.all_gather(out_heads, "tp", axis=0, tiled=True)
-    qkv_all = lax.all_gather(qkv_cols, "tp", axis=2, tiled=True)
-    out_full = out_heads
-    grad_rows = lax.all_gather(cotangent, "tp", axis=0, tiled=True)
-    projected = jnp.einsum("rd,kdc->krc", normed_all, qkv_full, preferred_element_type=jnp.float32)
-    queries = (projected[0] + qv_here[0]).astype(jnp.bfloat16).reshape(seq_len, heads_here, HD)
-    keys_all = projected[1].astype(jnp.bfloat16).reshape(seq_len, heads_here, HD)
-    values_all = (projected[2] + qv_here[1]).astype(jnp.bfloat16).reshape(seq_len, heads_here, HD)
-    mixed, log_mass = attend_forward(queries, keys_all, values_all, prefix_len, scale)
-    mixed, grad_rows = lax.optimization_barrier((mixed, grad_rows))
+    fc1_part = pieces[0].reshape(-1, fc1_weight.shape[1])
+    fc2_part = jnp.moveaxis(pieces[1], 0, 1).reshape(fc2_weight.shape[0], -1)
     mixed_rows = lax.all_to_all(mixed, "tp", 0, 1, tiled=True)
     middle = block_in + jnp.dot(mixed_rows, out_all, preferred_element_type=jnp.float32) + out_bias
     normed_two, unit_two, inv_two = norm_forward(middle, ln2_gain, ln2_bias)

time: 683 us -> 650 us (0.952)
  waiting for transfers between devices: 160 us -> 132 us
    all_gather x1, waiting for transfers between devices: 40.9 us -> 0.02 us  [on_device(): gathered = lax.all_gather(packed, 'fsdp', axis=0, tiled=False)]
    all_gather x1, waiting for transfers between devices: 0.01 us -> 22 us  [on_device(): out_pieces = lax.all_gather(out_weight, ('fsdp', 'tp'), axis=0, tiled=False)]
    all_to_all x1, waiting for transfers between devices: 10.8 us -> 0.01 us  [on_device(): mixed_rows = lax.all_to_all(mixed, 'tp', 0, 1, tiled=True)]
    unnamed x107 -> x101, local copies, waits for them, and re-layouts: 20.7 us -> 19.9 us
  transfers between devices with their start and end apart: 13 -> 13, of which waited for: 6 -> 5; matrix products, arithmetic and copies ran while one was open for 55% -> 57% of each run, Pallas kernels for 0% -> 0%
where the time goes in v5:
time: 650 us; the launch traced here: 645 us
  matrix products  216 us (33%)
  waiting for transfers between devices  132 us (20%)
  local copies, waits for them, and re-layouts  97.3 us (15%)
  other arithmetic  93.4 us (14%)
  blocking collectives  80.1 us (12%)
  between operations  14.8 us (2%)
  starting transfers between devices  10.4 us (2%)
    all_to_all x1, waiting for transfers between devices, on_device(): grad_proj_rows = lax.all_to_all(grad_proj, 'tp', 0, 2, tiled=True)  43.1 us
    psum x1, blocking collectives, on_device(): lax.psum((grad_ln1_gain, grad_ln1_bias, grad_qv_bias, grad_out_bias, grad...  41.2 us
    reduce_scatter x1, waiting for transfers between devices, on_device(): lax.psum_scatter(matmul_nt(grad_before, fc1_part), 'tp', scatter_dimensio...  39.7 us
    all_gather x1, blocking collectives, on_device(): qkv_cols = lax.all_gather(qkv_weight, 'fsdp', axis=1, tiled=True)  38.9 us
    dot_general x8, matrix products, block_scores(): jnp.einsum('qhe,khe->hqk', query_block, keys_all, preferred_element_type=...  36.4 us
    reduce_sum x4, other arithmetic, one_block(): total_mass = jnp.sum(expo, axis=-1, keepdims=True)  27.2 us
    dot_general x4, matrix products, one_block(): jnp.einsum('hqk,khe->qhe', probs_low, values_all, preferred_element_type=...  27.1 us
    convert_element_type x4, other arithmetic, one_block(): grad_scores = (probs * (grad_probs - inner_sum)).astype(jnp.bfloat16)  25.2 us
  transfers between devices with their start and end apart: 13, of which 5 were waited for; matrix products, arithmetic and copies ran while one was open for 57% of the time, Pallas kernels for 0%

profile of v5, /device:TPU:0, one launch (start us, length us, event | category | flops | bytes accessed | tf_op | source)
XLA Modules:
  0.0 645.1 jit_solution(12459462399136723489)
XLA Ops:
  13.2 38.9 %all_gather.30 = bf16[3,768,192]{2,0,1:T(4,128)(2,1)S(1)} all-gather(bf16[3,96,192]{2,0,1:T(4,128)(2,1)S(1)} %copy.92), channel_id=1, replica_groups=mesh['fsdp'=8,'tp'=4] {'fsdp'}, dimensions={1}, use_global_device_ids=true | all-gather | bytes 995328 | tf_op jit(solution)/shard_map/all_gather | solution.py:148
  66.7 89.5 %while.27 = (s32[]{:T(128)}, bf16[4,512,3,64]{1,3,2,0:T(8,128)(2,1)S(1)}, f32[4,3,512]{2,1,0:T(4,128)S(1)}, s32[4]{0:T(128)S(1)}, s32[]{:T(128)}, /*index=5*/bf1...) while((s32[]{:T(128)}, ...), condition=%wide.region_5.6_spmd, body=%wide.region_2.5_spmd.sunk | while | flops 845251584 | bytes 43976836 | solution.py:74
  75.4 6.9 %fusion.130 = f32[3,512]{1,0:T(4,128)S(1)} fusion(f32[3,512,2048]{2,1,0:T(8,128)} %get-tuple-element.513, f32[3,512]{1,0:T(4,128)S(1)} %get-tuple-element.514, pred[512,2048]{1,0:T(8,128)(4,1)S(1)} %fusion.128), kind=kLoop, calls=%fused_computation.4.clone.1 | loop fusion | flops 12581376 | bytes 13643776 | tf_op jit(solution)/shard_map/while/body/eval_jaxpr/reduce_sum | solution.py:67
  82.3 6.8 %fusion.131 = bf16[4,512,3,64]{1,3,2,0:T(8,128)(2,1)S(1)} fusion(bf16[4,512,3,64]{1,3,2,0:T(8,128)(2,1)S(1)} %get-tuple-element.538, s32[]{:T(128)S(6)} %copy.135, bf16[2048,3,64]{0,2,1:T(8,128)(2,1)S(1)} %get-tuple-element.553, f32[3,512,2048]{2,1,0:T(8,128)} %get-tuple-element.513, f32[3,512]{1,0:T(4,128)S(1)} %fusion.130, ...), kind=kOutput, calls=%fused_computation.10.clone.1 | convolution fusion | flops 418480128 | bytes 14630916 | tf_op jit(solution)/shard_map/while/body/eval_jaxpr/hqk,khe->qhe/dot_general | solution.py:69
  97.9 6.8 %fusion.130 = f32[3,512]{1,0:T(4,128)S(1)} fusion(f32[3,512,2048]{2,1,0:T(8,128)} %get-tuple-element.513, f32[3,512]{1,0:T(4,128)S(1)} %get-tuple-element.514, pred[512,2048]{1,0:T(8,128)(4,1)S(1)} %fusion.128), kind=kLoop, calls=%fused_computation.4.clone.1 | loop fusion | flops 12581376 | bytes 13643776 | tf_op jit(solution)/shard_map/while/body/eval_jaxpr/reduce_sum | solution.py:67
  104.6 6.8 %fusion.131 = bf16[4,512,3,64]{1,3,2,0:T(8,128)(2,1)S(1)} fusion(bf16[4,512,3,64]{1,3,2,0:T(8,128)(2,1)S(1)} %get-tuple-element.538, s32[]{:T(128)S(6)} %copy.135, bf16[2048,3,64]{0,2,1:T(8,128)(2,1)S(1)} %get-tuple-element.553, f32[3,512,2048]{2,1,0:T(8,128)} %get-tuple-element.513, f32[3,512]{1,0:T(4,128)S(1)} %fusion.130, ...), kind=kOutput, calls=%fused_computation.10.clone.1 | convolution fusion | flops 418480128 | bytes 14630916 | tf_op jit(solution)/shard_map/while/body/eval_jaxpr/hqk,khe->qhe/dot_general | solution.py:69
  120.2 6.8 %fusion.130 = f32[3,512]{1,0:T(4,128)S(1)} fusion(f32[3,512,2048]{2,1,0:T(8,128)} %get-tuple-element.513, f32[3,512]{1,0:T(4,128)S(1)} %get-tuple-element.514, pred[512,2048]{1,0:T(8,128)(4,1)S(1)} %fusion.128), kind=kLoop, calls=%fused_computation.4.clone.1 | loop fusion | flops 12581376 | bytes 13643776 | tf_op jit(solution)/shard_map/while/body/eval_jaxpr/reduce_sum | solution.py:67
  127.0 6.8 %fusion.131 = bf16[4,512,3,64]{1,3,2,0:T(8,128)(2,1)S(1)} fusion(bf16[4,512,3,64]{1,3,2,0:T(8,128)(2,1)S(1)} %get-tuple-element.538, s32[]{:T(128)S(6)} %copy.135, bf16[2048,3,64]{0,2,1:T(8,128)(2,1)S(1)} %get-tuple-element.553, f32[3,512,2048]{2,1,0:T(8,128)} %get-tuple-element.513, f32[3,512]{1,0:T(4,128)S(1)} %fusion.130, ...), kind=kOutput, calls=%fused_computation.10.clone.1 | convolution fusion | flops 418480128 | bytes 14630916 | tf_op jit(solution)/shard_map/while/body/eval_jaxpr/hqk,khe->qhe/dot_general | solution.py:69
  142.6 6.8 %fusion.130 = f32[3,512]{1,0:T(4,128)S(1)} fusion(f32[3,512,2048]{2,1,0:T(8,128)} %get-tuple-element.513, f32[3,512]{1,0:T(4,128)S(1)} %get-tuple-element.514, pred[512,2048]{1,0:T(8,128)(4,1)S(1)} %fusion.128), kind=kLoop, calls=%fused_computation.4.clone.1 | loop fusion | flops 12581376 | bytes 13643776 | tf_op jit(solution)/shard_map/while/body/eval_jaxpr/reduce_sum | solution.py:67
  149.4 6.8 %fusion.131 = bf16[4,512,3,64]{1,3,2,0:T(8,128)(2,1)S(1)} fusion(bf16[4,512,3,64]{1,3,2,0:T(8,128)(2,1)S(1)} %get-tuple-element.538, s32[]{:T(128)S(6)} %copy.135, bf16[2048,3,64]{0,2,1:T(8,128)(2,1)S(1)} %get-tuple-element.553, f32[3,512,2048]{2,1,0:T(8,128)} %get-tuple-element.513, f32[3,512]{1,0:T(4,128)S(1)} %fusion.130, ...), kind=kOutput, calls=%fused_computation.10.clone.1 | convolution fusion | flops 418480128 | bytes 14630916 | tf_op jit(solution)/shard_map/while/body/eval_jaxpr/hqk,khe->qhe/dot_general | solution.py:69
  167.8 22.0 %all-gather.22.cloned.1.call-done = bf16[6144,96]{1,0:T(8,128)(2,1)} async-done(((bf16[192,96]{1,0:T(8,128)(2,1)}), bf16[6144,96]{1,0:T(8,128)(2,1)}) %all-gather.22.cloned.1.call-update) | async-done | bytes 1179664 | tf_op jit(solution)/shard_map/all_gather | solution.py:158
  214.2 12.4 %all-gather.14.cloned.1.call-done = bf16[2048,768]{1,0:T(8,128)(2,1)} async-done(((bf16[512,768]{1,0:T(8,128)(2,1)}), bf16[2048,768]{1,0:T(8,128)(2,1)}) %all-gather.14.cloned.1.call-update) | async-done | bytes 3145744 | tf_op jit(solution)/shard_map/all_gather | solution.py:191
  231.7 8.3 %convert_reduce_fusion = (f32[768]{0:T(1024)}, bf16[2048,768]{1,0:T(8,128)(2,1)S(1)}, bf16[2048,768]{1,0:T(8,128)(2,1)}) fusion(f32[2048,768]{1,0:T(8,128)S(1)} %fusion.71, f32[768]{0:T(1024)S(1)} %dynamic_slice.31, bf16[2048,768]{1,0:T(8,128)(2,1)S(1)} %copy-done.48, bf16[768,768]{0,1:T(8,128)(2,1)S(1)} %bitcast.200), kind=kOutput, calls=%fused_computation.64 | convolution fusion | flops 2455239936 | bytes 16914432 | tf_op jit(solution)/shard_map/dot_general | solution.py:34
  246.6 6.6 %convolution_convert_fusion = bf16[2048,768]{1,0:T(8,128)(2,1)} fusion(bf16[2048,768]{1,0:T(8,128)(2,1)} %get-tuple-element.391, bf16[768,768]{0,1:T(8,128)(2,1)} %bitcast.199), kind=kOutput, calls=%fused_computation.67 | convolution fusion | flops 2417491968 | bytes 7471104 | tf_op jit(solution)/shard_map/dot_general | solution.py:194
  253.2 8.3 %fusion.74 = f32[768,768]{1,0:T(8,128)} fusion(bf16[2048,768]{1,0:T(8,128)(2,1)} %get-tuple-element.391, bf16[2048,768]{1,0:T(8,128)(2,1)} %all-gather.12.cloned.1.call-done), kind=kOutput, calls=%fused_computation.134 | convolution fusion | flops 2415919104 | bytes 8650752 | tf_op jit(solution)/shard_map/dot_general | solution.py:40
  265.7 39.7 %reduce-scatter.7.cloned.1.call-done = f32[512,768]{1,0:T(8,128)} async-done(((f32[2048,768]{1,0:T(8,128)}), f32[512,768]{1,0:T(8,128)}) %reduce-scatter.7.cloned.1.call-update) | async-done | bytes 1572880 | tf_op jit(solution)/shard_map/reduce_scatter | solution.py:205
  327.1 13.3 %all-gather.16.cloned.1.call-done = bf16[2048,768]{1,0:T(8,128)(2,1)} async-done(((bf16[512,768]{1,0:T(8,128)(2,1)}), bf16[2048,768]{1,0:T(8,128)(2,1)}) %all-gather.16.cloned.1.call-update) | async-done | bytes 3145744 | tf_op jit(solution)/shard_map/all_gather | solution.py:217
  349.2 6.4 reshape.278
  360.1 137.6 %while.28 = (s32[]{:T(128)}, f32[2048,3,64]{0,2,1:T(8,128)}, f32[2048,3,64]{0,2,1:T(8,128)}, bf16[4,512,3,64]{1,3,2,0:T(8,128)(2,1)}, bf16[4,512,3,64]{1,3,2,0:T...) while((s32[]{:T(128)}, f32[2048,3,64]{0,2,1:T(8,128)}, ...), condition=%wide.region_13.14_spmd.clone, body=%wide.region_11.13_spmd.clone.sunk | while | flops 2064614400 | bytes 156684720 | solution.py:113
  433.9 6.3 fusion.144
  521.0 7.0 %copy.104 = bf16[2048,3,192]{2,1,0:T(4,128)(2,1)} copy(bf16[2048,3,192]{0,2,1:T(8,128)(2,1)} %pad_maximum_fusion.1) | data formatting | bytes 4718592 | tf_op jit(solution)/shard_map/optimization_barrier | solution.py:245
  538.1 43.1 %all-to-all-done.1 = bf16[2048,3,192]{2,1,0:T(4,128)(2,1)} async-done(((bf16[2048,3,192]{2,1,0:T(4,128)(2,1)}), bf16[2048,3,192]{2,1,0:T(4,128)(2,1)}, u32[]{:S(2)}, u32[]{:S(2)}) %all-to-all-start.1) | async-done | bytes 2359328 | tf_op jit(solution)/shard_map/all_to_all | solution.py:266
  581.2 7.1 %copy.106 = bf16[512,3,4,192]{0,3,2,1:T(8,128)(2,1)} copy(bf16[512,3,4,192]{3,1,0,2:T(4,128)(2,1)} %bitcast.23) | data formatting | bytes 4718592 | tf_op jit(solution)/shard_map/all_to_all | solution.py:266
  595.3 41.2 %all-reduce = (f32[768]{0:T(1024)}, f32[768]{0:T(1024)}, f32[2,768]{1,0:T(2,128)}, f32[768]{0:T(1024)}, f32[768]{0:T(1024)}, /*index=5*/f32[768]{0:T(1024)}, f32[3072]{0:T(1024)}, f32[768]{0:T(1024)}, f32[5,768]{1,0:T(8,128)}) all-reduce(f32[768]{0:T(1024)S(1)} %get-tuple-element.324, ...), channel_id=1, replica_groups=mesh['fsdp'=8,'tp'=4] {'fsdp','tp'}, use_global_device_ids=true, to_apply=%region_20.21 | all-reduce | flops 13056 | bytes 104448 | tf_op jit(solution)/shard_map/psum | solution.py:283
  (346 shorter events, 313.9 us)
Async XLA Ops:
  7.2 45.7 %all-gather.10.cloned.1.call-start = ((), (), s32[]{:S(2)}) async-start(), calls=%async_computation.6 | async-start | bytes 3932160 | tf_op jit(solution)/shard_map/all_gather | solution.py:157
  11.2 41.0 %copy-start.35 = (f32[512]{0:T(512)}, f32[512]{0:T(512)S(1)}, u32[]{:S(2)}) copy-start(f32[512]{0:T(512)S(1)} %add_rsqrt_fusion.1) | copy-start | bytes 6148
  12.4 144.6 %all-gather.20.cloned.1.call-start = ((), (), s32[]{:S(2)}) async-start(), calls=%async_computation.14 | async-start | bytes 2654208 | tf_op jit(solution)/shard_map/all_gather | solution.py:168
  52.9 108.5 %all-gather.12.cloned.1.call-start = ((), (), s32[]{:S(2)}) async-start(), calls=%async_computation.7 | async-start | bytes 3932160 | tf_op jit(solution)/shard_map/all_gather | solution.py:170
  53.7 136.2 %all-gather.22.cloned.1.call-start = ((), (), s32[]{:S(2)}) async-start(), calls=%async_computation.15 | async-start | bytes 1622016 | tf_op jit(solution)/shard_map/all_gather | solution.py:158
  162.4 32.1 %all-to-all-start = ((bf16[4,512,192]{1,2,0:T(8,128)(2,1)}), bf16[4,512,192]{1,2,0:T(8,128)(2,1)}, u32[]{:S(2)}, u32[]{:S(2)}) async-start(bf16[4,512,192]{1,2,0:T(8,128)(2,1)} %bitcast.141), calls=%async_computation | async-start | bytes 1572864 | tf_op jit(solution)/shard_map/all_to_all | solution.py:185
  166.6 60.1 %all-gather.14.cloned.1.call-start = ((), (), s32[]{:S(2)}) async-start(), calls=%async_computation.8 | async-start | bytes 3932160 | tf_op jit(solution)/shard_map/all_gather | solution.py:191
  197.4 110.9 %copy-start.8 = (f32[512,768]{1,0:T(8,128)}, f32[512,768]{1,0:T(8,128)S(1)}, u32[]{:S(2)}) copy-start(f32[512,768]{1,0:T(8,128)S(1)} %get-tuple-element.400) | copy-start | bytes 4718596
  199.0 106.4 %reduce-scatter.7.cloned.1.call-start = ((), (), s32[]{:S(2)}) async-start(), calls=%async_computation.9 | async-start | bytes 7864320 | tf_op jit(solution)/shard_map/reduce_scatter | solution.py:205
  231.7 10.1 %copy-start.27 = (bf16[768,768]{1,0:T(8,128)(2,1)S(1)}, bf16[768,768]{1,0:T(8,128)(2,1)}, u32[]{:S(2)}) copy-start(bf16[768,768]{1,0:T(8,128)(2,1)} %reshape_reshape.11) | copy-start | bytes 3538948
  246.4 94.0 %all-gather.16.cloned.1.call-start = ((), (), s32[]{:S(2)}) async-start(), calls=%async_computation.10 | async-start | bytes 3932160 | tf_op jit(solution)/shard_map/all_gather | solution.py:217
  253.2 8.4 %copy-start.49 = (bf16[2048,768]{1,0:T(8,128)(2,1)S(1)}, bf16[2048,768]{1,0:T(8,128)(2,1)}, u32[]{:S(2)}) copy-start(bf16[2048,768]{1,0:T(8,128)(2,1)} %all-gather.14.cloned.1.call-done) | copy-start | bytes 9437188
  253.2 8.4 %copy-start.52 = (bf16[2048,768]{1,0:T(8,128)(2,1)S(1)}, bf16[2048,768]{1,0:T(8,128)(2,1)}, u32[]{:S(2)}) copy-start(bf16[2048,768]{1,0:T(8,128)(2,1)} %copy-done.51) | copy-start | bytes 9437188
  311.7 192.4 %reduce-scatter.9.cloned.1.call-start = ((), (), s32[]{:S(2)}) async-start(), calls=%async_computation.11 | async-start | bytes 3932160 | tf_op jit(solution)/shard_map/reduce_scatter | solution.py:221
  321.9 18.5 %copy-start.16 = (bf16[24,8,4,512]{3,1,2,0:T(8,128)(2,1)S(1)}, bf16[24,8,4,512]{3,1,2,0:T(8,128)(2,1)}, u32[]{:S(2)}) copy-start(bf16[24,8,4,512]{3,1,2,0:T(8,128)(2,1)} %copy-done.15) | copy-start | bytes 2359300
  343.1 163.4 %reduce-scatter.11.cloned.1.call-start = ((), (), s32[]{:S(2)}) async-start(), calls=%async_computation.12 | async-start | bytes 5971968 | tf_op jit(solution)/shard_map/reduce_scatter | solution.py:232
  355.6 232.7 %all-gather.18.cloned.1.call-start = ((), (), s32[]{:S(2)}) async-start(), calls=%async_computation.13 | async-start | bytes 4423680 | tf_op jit(solution)/shard_map/all_gather | solution.py:169
  356.2 280.2 %reduce-scatter.13.cloned.1.call-start = ((), (), s32[]{:S(2)}) async-start(), calls=%async_computation.16 | async-start | bytes 2211840
  527.9 53.2 %all-to-all-start.1 = ((bf16[2048,3,192]{2,1,0:T(4,128)(2,1)}), bf16[2048,3,192]{2,1,0:T(4,128)(2,1)}, u32[]{:S(2)}, u32[]{:S(2)}) async-start(bf16[2048,3,192]{2,1,0:T(4,128)(2,1)} %copy.104), calls=%async_computation.4 | async-start | bytes 8388608 | tf_op jit(solution)/shard_map/all_to_all | solution.py:266
  581.2 7.2 %copy-start.34 = (f32[512]{0:T(512)S(1)}, f32[512]{0:T(512)}, u32[]{:S(2)}) copy-start(f32[512]{0:T(512)} %copy-done.33) | copy-start | bytes 6148
  581.2 7.2 %copy-start.36 = (f32[512]{0:T(512)S(1)}, f32[512]{0:T(512)}, u32[]{:S(2)}) copy-start(f32[512]{0:T(512)} %copy-done.35) | copy-start | bytes 6148
  581.2 7.2 %copy-start.42 = (f32[768]{0:T(1024)S(1)}, f32[768]{0:T(1024)}, u32[]{:S(2)}) copy-start(f32[768]{0:T(1024)} %param.29) | copy-start | bytes 9220
  593.9 44.4 %copy-start.1 = (f32[5,768]{1,0:T(8,128)S(1)}, f32[5,768]{1,0:T(8,128)}, u32[]{:S(2)}) copy-start(f32[5,768]{1,0:T(8,128)} %param.37) | copy-start | bytes 46084
  594.5 43.8 %copy-start.17 = (f32[512,768]{1,0:T(8,128)}, f32[512,768]{1,0:T(8,128)S(1)}, u32[]{:S(2)}) copy-start(f32[512,768]{1,0:T(8,128)S(1)} %multiply_add_fusion) | copy-start | bytes 4718596
  (66 other events, 260.9 us)
Sparse Core Ops, SparseCore 0:
  12.5 31.2 all-gather.9
  53.0 50.5 all-gather.19
  105.2 27.0 all-gather.11
  135.0 54.8 all-gather.21
  199.1 27.4 all-gather.13
  246.5 58.8 reduce-scatter.6
  311.9 28.4 all-gather.15
  343.3 37.8 reduce-scatter.8
  384.8 104.4 reduce-scatter.10
  490.7 30.3 all-gather.17
  524.6 67.4 reduce-scatter.12

commit v6 on v5

--- a/solution.py
+++ b/solution.py
@@ -1,8 +1,11 @@
+import functools
 from functools import partial
 
 import jax
 import jax.numpy as jnp
 from jax import lax
+from jax.experimental import pallas as pl
+from jax.experimental.pallas import tpu as pltpu
 from jax.sharding import PartitionSpec as P
 
 HD = 64
@@ -53,67 +56,115 @@
     return jnp.where(allowed[None], raw, NEG_FILL)
 
 
-def attend_forward(queries, keys_all, values_all, prefix_len, scale):
-    seq_len, heads_here, head_size = queries.shape
-    block_count = seq_len // QBLOCK
-    query_blocks = queries.reshape(block_count, QBLOCK, heads_here, head_size)
-    block_starts = jnp.arange(block_count, dtype=jnp.int32) * QBLOCK
-
-    def one_block(item):
-        query_block, row_start = item
-        masked = block_scores(query_block, keys_all, row_start, prefix_len, scale)
-        peak = jnp.max(masked, axis=-1, keepdims=True)
-        expo = jnp.exp(masked - peak)
-        total_mass = jnp.sum(expo, axis=-1, keepdims=True)
-        probs_low = (expo / total_mass).astype(jnp.bfloat16)
-        out_block = jnp.einsum(
-            "hqk,khe->qhe", probs_low, values_all, preferred_element_type=jnp.float32
-        )
-        return (out_block.astype(jnp.bfloat16), (peak + jnp.log(total_mass))[..., 0])
-
-    outputs, log_mass = lax.map(one_block, (query_blocks, block_starts))
-    return (outputs.reshape(seq_len, heads_here * head_size), log_mass)
-
-
-def attend_backward(queries, keys_all, values_all, grad_mixed, log_mass, prefix_len, scale):
-    seq_len, heads_here, head_size = queries.shape
-    block_count = seq_len // QBLOCK
-    query_blocks = queries.reshape(block_count, QBLOCK, heads_here, head_size)
-    grad_blocks = grad_mixed.reshape(block_count, QBLOCK, heads_here, head_size)
-    block_starts = jnp.arange(block_count, dtype=jnp.int32) * QBLOCK
-
-    def one_block(carry, item):
-        grad_keys, grad_values = carry
-        query_block, grad_block, block_mass, row_start = item
-        masked = block_scores(query_block, keys_all, row_start, prefix_len, scale)
-        probs = jnp.exp(masked - block_mass[..., None])
-        probs_low = probs.astype(jnp.bfloat16)
-        grad_values = grad_values + jnp.einsum(
-            "hqk,qhe->khe", probs_low, grad_block, preferred_element_type=jnp.float32
-        )
-        grad_probs = jnp.einsum(
-            "qhe,khe->hqk", grad_block, values_all, preferred_element_type=jnp.float32
-        )
-        inner_sum = jnp.sum(probs * grad_probs, axis=-1, keepdims=True)
-        grad_scores = (probs * (grad_probs - inner_sum)).astype(jnp.bfloat16)
-        grad_query = (
-            jnp.einsum("hqk,khe->qhe", grad_scores, keys_all, preferred_element_type=jnp.float32)
-            * scale
-        )
-        grad_keys = (
-            grad_keys
-            + jnp.einsum(
-                "hqk,qhe->khe", grad_scores, query_block, preferred_element_type=jnp.float32
-            )
-            * scale
-        )
-        return ((grad_keys, grad_values), grad_query)
-
-    zero_state = jnp.zeros(keys_all.shape, jnp.float32)
-    (grad_keys, grad_values), grad_queries = lax.scan(
-        one_block, (zero_state, zero_state), (query_blocks, grad_blocks, log_mass, block_starts)
-    )
-    return (grad_queries.reshape(seq_len, heads_here, head_size), grad_keys, grad_values)
+ATT_QB = 256
+
+
+def _mask(prefix_len, qb, rows, cols):
+    row = qb * rows + lax.broadcasted_iota(jnp.int32, (rows, cols), 0)
+    col = lax.broadcasted_iota(jnp.int32, (rows, cols), 1)
+    return (col <= row) | (col < prefix_len)
+
+
+def _nt(a, b):
+    return lax.dot_general(a, b, (((1,), (1,)), ((), ())), preferred_element_type=jnp.float32)
+
+
+def _tn(a, b):
+    return lax.dot_general(a, b, (((0,), (0,)), ((), ())), preferred_element_type=jnp.float32)
+
+
+def _fwd_kernel(scale, prefix_ref, q_ref, k_ref, v_ref, o_ref, lse_ref):
+    qb = pl.program_id(1)
+    q = q_ref[0]
+    rows, cols = q.shape[0], k_ref.shape[1]
+    scores = _nt(q, k_ref[0]) * scale
+    scores = jnp.where(_mask(prefix_ref[0], qb, rows, cols), scores, NEG_FILL)
+    peak = jnp.max(scores, axis=-1, keepdims=True)
+    expo = jnp.exp(scores - peak)
+    total = jnp.sum(expo, axis=-1, keepdims=True)
+    probs_low = (expo / total).astype(jnp.bfloat16)
+    out = jnp.dot(probs_low, v_ref[0], preferred_element_type=jnp.float32)
+    o_ref[0] = out.astype(o_ref.dtype)
+    lse_ref[0] = peak + jnp.log(total)
+
+
+def _bwd_kernel(scale, prefix_ref, q_ref, k_ref, v_ref, do_ref, lse_ref,
+                dq_ref, dk_ref, dv_ref, dk_acc, dv_acc):
+    qb = pl.program_id(1)
+
+    @pl.when(qb == 0)
+    def _():
+        dk_acc[...] = jnp.zeros_like(dk_acc)
+        dv_acc[...] = jnp.zeros_like(dv_acc)
+
+    q = q_ref[0]
+    k = k_ref[0]
+    grad_out = do_ref[0]
+    rows, cols = q.shape[0], k.shape[0]
+    scores = _nt(q, k) * scale
+    scores = jnp.where(_mask(prefix_ref[0], qb, rows, cols), scores, NEG_FILL)
+    probs = jnp.exp(scores - lse_ref[0])
+    dv_acc[...] += _tn(probs.astype(jnp.bfloat16), grad_out)
+    grad_probs = _nt(grad_out, v_ref[0])
+    inner = jnp.sum(probs * grad_probs, axis=-1, keepdims=True)
+    grad_scores = (probs * (grad_probs - inner)).astype(jnp.bfloat16)
+    dq_ref[0] = (jnp.dot(grad_scores, k, preferred_element_type=jnp.float32) * scale).astype(dq_ref.dtype)
+    dk_acc[...] += _tn(grad_scores, q)
+
+    @pl.when(qb == pl.num_programs(1) - 1)
+    def _():
+        dk_ref[0] = (dk_acc[...] * scale).astype(dk_ref.dtype)
+        dv_ref[0] = dv_acc[...].astype(dv_ref.dtype)
+
+
+def attn_forward(prefix, q, k, v, scale):
+    heads, seq, hd = q.shape
+    qb = min(ATT_QB, seq)
+    grid = (heads, seq // qb)
+    q_spec = pl.BlockSpec((1, qb, hd), lambda h, i, p: (h, i, 0))
+    kv_spec = pl.BlockSpec((1, seq, hd), lambda h, i, p: (h, 0, 0))
+    lse_spec = pl.BlockSpec((1, qb, 1), lambda h, i, p: (h, i, 0))
+    return pl.pallas_call(
+        functools.partial(_fwd_kernel, scale),
+        out_shape=(jax.ShapeDtypeStruct((heads, seq, hd), jnp.bfloat16),
+                   jax.ShapeDtypeStruct((heads, seq, 1), jnp.float32)),
+        grid_spec=pltpu.PrefetchScalarGridSpec(
+            num_scalar_prefetch=1, grid=grid,
+            in_specs=[q_spec, kv_spec, kv_spec],
+            out_specs=[q_spec, lse_spec]),
+        compiler_params=pltpu.CompilerParams(
+            dimension_semantics=("arbitrary", "arbitrary"),
+            vmem_limit_bytes=48 * 1024 * 1024),
+        cost_estimate=pl.CostEstimate(
+            flops=4 * heads * seq * seq * hd, transcendentals=heads * seq * seq,
+            bytes_accessed=4 * heads * seq * hd * 2),
+    )(prefix, q, k, v)
+
+
+def attn_backward(prefix, q, k, v, grad_out, lse, scale):
+    heads, seq, hd = q.shape
+    qb = min(ATT_QB, seq)
+    grid = (heads, seq // qb)
+    q_spec = pl.BlockSpec((1, qb, hd), lambda h, i, p: (h, i, 0))
+    kv_spec = pl.BlockSpec((1, seq, hd), lambda h, i, p: (h, 0, 0))
+    lse_spec = pl.BlockSpec((1, qb, 1), lambda h, i, p: (h, i, 0))
+    shape = jax.ShapeDtypeStruct((heads, seq, hd), jnp.bfloat16)
+    return pl.pallas_call(
+        functools.partial(_bwd_kernel, scale),
+        out_shape=(shape, shape, shape),
+        grid_spec=pltpu.PrefetchScalarGridSpec(
+            num_scalar_prefetch=1, grid=grid,
+            in_specs=[q_spec, kv_spec, kv_spec, q_spec, lse_spec],
+            out_specs=[q_spec, kv_spec, kv_spec],
+            scratch_shapes=[pltpu.VMEM((seq, hd), jnp.float32),
+                            pltpu.VMEM((seq, hd), jnp.float32)]),
+        compiler_params=pltpu.CompilerParams(
+            dimension_semantics=("arbitrary", "arbitrary"),
+            vmem_limit_bytes=48 * 1024 * 1024),
+        cost_estimate=pl.CostEstimate(
+            flops=10 * heads * seq * seq * hd, transcendentals=heads * seq * seq,
+            bytes_accessed=8 * heads * seq * hd * 2),
+    )(prefix, q, k, v, grad_out, lse)
 
 
 def on_device(
@@ -172,7 +223,11 @@
     queries = (projected[0] + qv_here[0]).astype(jnp.bfloat16).reshape(seq_len, heads_here, HD)
     keys_all = projected[1].astype(jnp.bfloat16).reshape(seq_len, heads_here, HD)
     values_all = (projected[2] + qv_here[1]).astype(jnp.bfloat16).reshape(seq_len, heads_here, HD)
-    mixed, log_mass = attend_forward(queries, keys_all, values_all, prefix_len, scale)
+    q_heads = jnp.transpose(queries, (1, 0, 2))
+    k_heads = jnp.transpose(keys_all, (1, 0, 2))
+    v_heads = jnp.transpose(values_all, (1, 0, 2))
+    out_heads, log_mass = attn_forward(prefix, q_heads, k_heads, v_heads, scale)
+    mixed = jnp.transpose(out_heads, (1, 0, 2)).reshape(seq_len, cols_here)
     mixed, grad_rows, gathered = lax.optimization_barrier((mixed, grad_rows, gathered))
     pieces = []
     offset = 0
@@ -235,12 +290,12 @@
     grad_mixed = (
         matmul_nt(grad_attn_rows, out_full).astype(jnp.bfloat16).reshape(seq_len, heads_here, HD)
     )
-    grad_queries, grad_keys, grad_values = attend_backward(
-        queries, keys_all, values_all, grad_mixed, log_mass, prefix_len, scale
-    )
-    grad_q_low = grad_queries.astype(jnp.bfloat16).reshape(seq_len, cols_here)
-    grad_k_low = grad_keys.astype(jnp.bfloat16).reshape(seq_len, cols_here)
-    grad_v_low = grad_values.astype(jnp.bfloat16).reshape(seq_len, cols_here)
+    grad_q_heads, grad_k_heads, grad_v_heads = attn_backward(
+        prefix, q_heads, k_heads, v_heads, jnp.transpose(grad_mixed, (1, 0, 2)), log_mass, scale
+    )
+    grad_q_low = jnp.transpose(grad_q_heads, (1, 0, 2)).reshape(seq_len, cols_here)
+    grad_k_low = jnp.transpose(grad_k_heads, (1, 0, 2)).reshape(seq_len, cols_here)
+    grad_v_low = jnp.transpose(grad_v_heads, (1, 0, 2)).reshape(seq_len, cols_here)
     grad_proj = jnp.stack([grad_q_low, grad_k_low, grad_v_low], axis=1)
     grad_proj, result, dense_summed = lax.optimization_barrier((grad_proj, result, dense_summed))
     dense_shards = []

time: 650 us -> 643 us (0.989)
  matrix products: 216 us -> 63 us
  waiting for transfers between devices: 132 us -> 237 us
  Pallas kernels: 0 us -> 103 us
  other arithmetic: 93.4 us -> 24.8 us
    dot_general x28 -> x0, matrix products: 152 us -> none  [the longest x8 36.4 us: block_scores(): jnp.einsum('qhe,khe->hqk', query_block, keys_all, preferred_element_type=...]
    pallas_call x0 -> x2, Pallas kernels: none -> 103 us  [the longest x1 63.9 us: attn_backward(): pl.pallas_call(functools.partial(_bwd_kernel, scale), out_shape=(shape, s...]
    reduce_scatter x1, waiting for transfers between devices: 0.01 us -> 51.6 us  [on_device(): lax.psum_scatter(dense_packed.reshape(-1, grad_fc1.shape[1]), 'fsdp', sca...]
    all_gather x1, waiting for transfers between devices: 22 us -> 51.5 us  [on_device(): out_pieces = lax.all_gather(out_weight, ('fsdp', 'tp'), axis=0, tiled=False)]
    convert_element_type x7 -> x0, other arithmetic: 29.2 us -> none  [the longest x4 25.2 us: one_block(): grad_scores = (probs * (grad_probs - inner_sum)).astype(jnp.bfloat16)]
    reduce_sum x4 -> x0, other arithmetic: 27.2 us -> none  [one_block(): total_mass = jnp.sum(expo, axis=-1, keepdims=True)]
    all_gather x1, waiting for transfers between devices: 0.01 us -> 15.8 us  [on_device(): grad_rows = lax.all_gather(cotangent, 'tp', axis=0, tiled=True)]
    unnamed x101 -> x83, local copies, waits for them, and re-layouts: 19.9 us -> 24.4 us
  transfers between devices with their start and end apart: 13 -> 13, of which waited for: 5 -> 7; matrix products, arithmetic and copies ran while one was open for 57% -> 22% of each run, Pallas kernels for 0% -> 16%
where the time goes in v6:
time: 643 us; the launch traced here: 634 us
  waiting for transfers between devices  237 us (37%)
  Pallas kernels  103 us (16%)
  local copies, waits for them, and re-layouts  100 us (16%)
  blocking collectives  80.3 us (12%)
  matrix products  63 us (10%)
  other arithmetic  24.8 us (4%)
  between operations  15.3 us (2%)
  starting transfers between devices  10.7 us (2%)
    pallas_call x1, Pallas kernels, attn_backward(): pl.pallas_call(functools.partial(_bwd_kernel, scale), out_shape=(shape, s...  63.9 us
    reduce_scatter x1, waiting for transfers between devices, on_device(): lax.psum_scatter(dense_packed.reshape(-1, grad_fc1.shape[1]), 'fsdp', sca...  51.6 us
    all_gather x1, waiting for transfers between devices, on_device(): out_pieces = lax.all_gather(out_weight, ('fsdp', 'tp'), axis=0, tiled=False)  51.5 us
    all_to_all x1, waiting for transfers between devices, on_device(): grad_proj_rows = lax.all_to_all(grad_proj, 'tp', 0, 2, tiled=True)  42.2 us
    psum x1, blocking collectives, on_device(): lax.psum((grad_ln1_gain, grad_ln1_bias, grad_qv_bias, grad_out_bias, grad...  41.4 us
    reduce_scatter x1, waiting for transfers between devices, on_device(): lax.psum_scatter(matmul_nt(grad_before, fc1_part), 'tp', scatter_dimensio...  40.2 us
    all_gather x1, blocking collectives, on_device(): qkv_cols = lax.all_gather(qkv_weight, 'fsdp', axis=1, tiled=True)  38.9 us
    pallas_call x1, Pallas kernels, attn_forward(): pl.pallas_call(functools.partial(_fwd_kernel, scale), out_shape=(jax.Shap...  38.9 us
  transfers between devices with their start and end apart: 13, of which 7 were waited for; matrix products, arithmetic and copies ran while one was open for 22% of the time, Pallas kernels for 16%

profile of v6, /device:TPU:0, one launch (start us, length us, event | category | flops | bytes accessed | tf_op | source)
XLA Modules:
  0.0 634.4 jit_solution(7509239813657032145)
XLA Ops:
  13.3 38.9 %all_gather.30 = bf16[3,768,192]{2,0,1:T(4,128)(2,1)S(1)} all-gather(bf16[3,96,192]{2,0,1:T(4,128)(2,1)S(1)} %copy.102), channel_id=1, replica_groups=mesh['fsdp'=8,'tp'=4] {'fsdp'}, dimensions={1}, use_global_device_ids=true | all-gather | bytes 995328 | tf_op jit(solution)/shard_map/all_gather | solution.py:199
  67.7 5.1 fusion.10
  72.8 38.9 %shard_map.280 = (bf16[3,2048,64]{2,1,0:T(8,128)(2,1)S(1)}, f32[3,2048,1]{2,1,0:T(8,128)}) custom-call(s32[1]{0:T(128)S(6)} %copy.141.prefix_ref, bf16[3,2048,64]{2,1,0:T(8,128)(2,1)S(1)} %get-tuple-element.170.q_ref, bf16[3,2048,64]{2,1,0:T(8,128)(2,1)S(1)} %bitcast.98, bf16[3,2048,64]{2,1,0:T(8,128)(2,1)} %get-tuple-element.171.v_ref), custom_call_target="tpu_custom_call" | custom-call | flops 3221225472 | bytes 3145728 | tf_op jit(solution)/shard_map/pallas_call | solution.py:127
  116.7 15.8 %all-gather.12.cloned.1.call-done = bf16[2048,768]{1,0:T(8,128)(2,1)} async-done(((bf16[512,768]{1,0:T(8,128)(2,1)}), bf16[2048,768]{1,0:T(8,128)(2,1)}) %all-gather.12.cloned.1.call-update) | async-done | bytes 3145744 | tf_op jit(solution)/shard_map/all_gather | solution.py:221
  138.7 51.5 %all-gather.22.cloned.1.call-done = bf16[6144,96]{1,0:T(8,128)(2,1)} async-done(((bf16[192,96]{1,0:T(8,128)(2,1)}), bf16[6144,96]{1,0:T(8,128)(2,1)}) %all-gather.22.cloned.1.call-update) | async-done | bytes 1179664 | tf_op jit(solution)/shard_map/all_gather | solution.py:209
  210.8 16.1 %all-gather.14.cloned.1.call-done = bf16[2048,768]{1,0:T(8,128)(2,1)} async-done(((bf16[512,768]{1,0:T(8,128)(2,1)}), bf16[2048,768]{1,0:T(8,128)(2,1)}) %all-gather.14.cloned.1.call-update) | async-done | bytes 3145744 | tf_op jit(solution)/shard_map/all_gather | solution.py:246
  226.9 5.1 fusion.28
  231.9 7.8 %convert_reduce_fusion = (f32[768]{0:T(1024)S(1)}, bf16[2048,768]{1,0:T(8,128)(2,1)S(1)}, bf16[2048,768]{1,0:T(8,128)(2,1)}) fusion(f32[2048,768]{1,0:T(8,128)S(1)} %fusion.28, f32[768]{0:T(1024)S(1)} %dynamic_slice.10, bf16[2048,768]{1,0:T(8,128)(2,1)S(1)} %copy-done.32, bf16[768,768]{0,1:T(8,128)(2,1)S(1)} %bitcast.121), kind=kOutput, calls=%fused_computation.9 | convolution fusion | flops 2455239936 | bytes 16914432 | tf_op jit(solution)/shard_map/dot_general | solution.py:37
  246.2 6.4 %convolution_convert_fusion = bf16[2048,768]{1,0:T(8,128)(2,1)} fusion(bf16[2048,768]{1,0:T(8,128)(2,1)} %get-tuple-element.159, bf16[768,768]{0,1:T(8,128)(2,1)S(1)} %bitcast.122), kind=kOutput, calls=%fused_computation.12 | convolution fusion | flops 2417491968 | bytes 7471104 | tf_op jit(solution)/shard_map/dot_general | solution.py:249
  252.6 8.0 %fusion.31 = f32[768,768]{1,0:T(8,128)} fusion(bf16[2048,768]{1,0:T(8,128)(2,1)} %get-tuple-element.159, bf16[2048,768]{1,0:T(8,128)(2,1)} %all-gather.12.cloned.1.call-done), kind=kOutput, calls=%fused_computation.79 | convolution fusion | flops 2415919104 | bytes 8650752 | tf_op jit(solution)/shard_map/dot_general | solution.py:43
  264.7 40.2 %reduce-scatter.7.cloned.1.call-done = f32[512,768]{1,0:T(8,128)} async-done(((f32[2048,768]{1,0:T(8,128)}), f32[512,768]{1,0:T(8,128)}) %reduce-scatter.7.cloned.1.call-update) | async-done | bytes 1572880 | tf_op jit(solution)/shard_map/reduce_scatter | solution.py:260
  320.8 18.0 %all-gather.16.cloned.1.call-done = bf16[2048,768]{1,0:T(8,128)(2,1)} async-done(((bf16[512,768]{1,0:T(8,128)(2,1)}), bf16[2048,768]{1,0:T(8,128)(2,1)}) %all-gather.16.cloned.1.call-update) | async-done | bytes 3145744 | tf_op jit(solution)/shard_map/all_gather | solution.py:272
  346.4 4.8 pad_maximum_fusion
  351.2 6.0 reshape.158
  364.6 63.9 %shard_map.281 = (bf16[3,2048,64]{2,1,0:T(8,128)(2,1)S(1)}, bf16[3,2048,64]{2,1,0:T(8,128)(2,1)S(1)}, bf16[3,2048,64]{2,1,0:T(8,128)(2,1)S(1)}) custom-call(s32[1]{0:T(128)S(6)} %copy.141.prefix_ref, bf16[3,2048,64]{2,1,0:T(8,128)(2,1)} %copy-done.4, bf16[3,2048,64]{2,1,0:T(8,128)(2,1)} %bitcast.99, bf16[3,2048,64]{2,1,0:T(8,128)(2,1)} %get-tuple-element.171.v_ref, ...), custom_call_target="tpu_custom_call" | custom-call | flops 8053063680 | bytes 6291456 | tf_op jit(solution)/shard_map/pallas_call | solution.py:152
  441.0 51.6 %reduce-scatter.11.cloned.1.call-done = f32[216,768]{1,0:T(8,128)} async-done(((f32[1728,768]{1,0:T(8,128)}), f32[216,768]{1,0:T(8,128)}) %reduce-scatter.11.cloned.1.call-update) | async-done | bytes 663568 | tf_op jit(solution)/shard_map/reduce_scatter | solution.py:287
  495.2 5.8 fusion.13
  505.3 4.7 reshape.165
  510.0 7.0 %copy.118 = bf16[2048,3,192]{2,1,0:T(4,128)(2,1)} copy(bf16[2048,3,192]{0,2,1:T(8,128)(2,1)} %pad_maximum_fusion.1) | data formatting | bytes 4718592 | tf_op jit(solution)/shard_map/optimization_barrier | solution.py:300
  517.0 5.1 all-to-all-start.1
  528.1 42.2 %all-to-all-done.1 = bf16[2048,3,192]{2,1,0:T(4,128)(2,1)} async-done(((bf16[2048,3,192]{2,1,0:T(4,128)(2,1)}), bf16[2048,3,192]{2,1,0:T(4,128)(2,1)}, u32[]{:S(2)}, u32[]{:S(2)}) %all-to-all-start.1) | async-done | bytes 2359328 | tf_op jit(solution)/shard_map/all_to_all | solution.py:321
  570.3 7.1 %copy.120 = bf16[512,3,4,192]{0,3,2,1:T(8,128)(2,1)} copy(bf16[512,3,4,192]{3,1,0,2:T(4,128)(2,1)} %bitcast.29) | data formatting | bytes 4718592 | tf_op jit(solution)/shard_map/all_to_all | solution.py:321
  577.5 5.4 fusion.12
  584.3 41.4 %all-reduce = (f32[768]{0:T(1024)}, f32[768]{0:T(1024)}, f32[2,768]{1,0:T(2,128)}, f32[768]{0:T(1024)}, f32[768]{0:T(1024)}, /*index=5*/f32[768]{0:T(1024)}, f32[3072]{0:T(1024)}, f32[768]{0:T(1024)}, f32[5,768]{1,0:T(8,128)}) all-reduce(f32[768]{0:T(1024)S(1)} %get-tuple-element.136, ...), channel_id=1, replica_groups=mesh['fsdp'=8,'tp'=4] {'fsdp','tp'}, use_global_device_ids=true, to_apply=%region_13.0 | all-reduce | flops 13056 | bytes 104448 | tf_op jit(solution)/shard_map/psum | solution.py:338
  (184 shorter events, 122.3 us)
Async XLA Ops:
  7.2 45.7 %all-gather.10.cloned.1.call-start = ((), (), s32[]{:S(2)}) async-start(), calls=%async_computation.6 | async-start | bytes 3932160 | tf_op jit(solution)/shard_map/all_gather | solution.py:208
  12.4 100.0 %all-gather.20.cloned.1.call-start = ((), (), s32[]{:S(2)}) async-start(), calls=%async_computation.14 | async-start | bytes 2654208 | tf_op jit(solution)/shard_map/all_gather | solution.py:219
  52.9 79.6 %all-gather.12.cloned.1.call-start = ((), (), s32[]{:S(2)}) async-start(), calls=%async_computation.7 | async-start | bytes 3932160 | tf_op jit(solution)/shard_map/all_gather | solution.py:221
  53.7 136.5 %all-gather.22.cloned.1.call-start = ((), (), s32[]{:S(2)}) async-start(), calls=%async_computation.15 | async-start | bytes 1622016 | tf_op jit(solution)/shard_map/all_gather | solution.py:209
  72.8 38.9 %copy-start.4 = (bf16[3,2048,64]{2,1,0:T(8,128)(2,1)}, bf16[3,2048,64]{2,1,0:T(8,128)(2,1)S(1)}, u32[]{:S(2)}) copy-start(bf16[3,2048,64]{2,1,0:T(8,128)(2,1)S(1)} %get-tuple-element.170.q_ref) | copy-start | bytes 2359300
  112.4 20.2 %copy-start.11 = (bf16[2048,3,64]{0,2,1:T(8,128)(2,1)}, bf16[2048,3,64]{0,2,1:T(8,128)(2,1)S(1)}, u32[]{:S(2)}) copy-start(bf16[2048,3,64]{0,2,1:T(8,128)(2,1)S(1)} %copy.107) | copy-start | bytes 2359300
  133.5 61.3 %all-to-all-start = ((bf16[4,512,192]{1,2,0:T(8,128)(2,1)}), bf16[4,512,192]{1,2,0:T(8,128)(2,1)}, u32[]{:S(2)}, u32[]{:S(2)}) async-start(bf16[4,512,192]{1,2,0:T(8,128)(2,1)} %bitcast.95), calls=%async_computation | async-start | bytes 1572864 | tf_op jit(solution)/shard_map/all_to_all | solution.py:240
  137.7 89.2 %all-gather.14.cloned.1.call-start = ((), (), s32[]{:S(2)}) async-start(), calls=%async_computation.8 | async-start | bytes 3932160 | tf_op jit(solution)/shard_map/all_gather | solution.py:246
  197.2 110.0 %copy-start.5 = (f32[512,768]{1,0:T(8,128)}, f32[512,768]{1,0:T(8,128)S(1)}, u32[]{:S(2)}) copy-start(f32[512,768]{1,0:T(8,128)S(1)} %get-tuple-element.168) | copy-start | bytes 4718596
  199.2 105.7 %reduce-scatter.7.cloned.1.call-start = ((), (), s32[]{:S(2)}) async-start(), calls=%async_computation.9 | async-start | bytes 7864320 | tf_op jit(solution)/shard_map/reduce_scatter | solution.py:260
  210.8 21.2 %copy-start.22 = (bf16[768,8,96]{0,2,1:T(8,128)(2,1)S(1)}, bf16[768,8,96]{0,2,1:T(8,128)(2,1)}, u32[]{:S(2)}) copy-start(bf16[768,8,96]{0,2,1:T(8,128)(2,1)} %copy.108) | copy-start | bytes 3538948
  231.9 9.4 %copy-start.21 = (bf16[768,768]{1,0:T(8,128)(2,1)S(1)}, bf16[768,768]{1,0:T(8,128)(2,1)}, u32[]{:S(2)}) copy-start(bf16[768,768]{1,0:T(8,128)(2,1)} %reshape_reshape.6) | copy-start | bytes 3538948
  245.9 93.0 %all-gather.16.cloned.1.call-start = ((), (), s32[]{:S(2)}) async-start(), calls=%async_computation.10 | async-start | bytes 3932160 | tf_op jit(solution)/shard_map/all_gather | solution.py:272
  252.6 8.0 %copy-start.33 = (bf16[2048,768]{1,0:T(8,128)(2,1)S(1)}, bf16[2048,768]{1,0:T(8,128)(2,1)}, u32[]{:S(2)}) copy-start(bf16[2048,768]{1,0:T(8,128)(2,1)} %all-gather.14.cloned.1.call-done) | copy-start | bytes 9437188
  252.6 8.0 %copy-start.36 = (bf16[2048,768]{1,0:T(8,128)(2,1)S(1)}, bf16[2048,768]{1,0:T(8,128)(2,1)}, u32[]{:S(2)}) copy-start(bf16[2048,768]{1,0:T(8,128)(2,1)} %copy-done.35) | copy-start | bytes 9437188
  264.7 42.5 %copy-start.16 = (bf16[512,768]{1,0:T(8,128)(2,1)S(1)}, bf16[512,768]{1,0:T(8,128)(2,1)}, u32[]{:S(2)}) copy-start(bf16[512,768]{1,0:T(8,128)(2,1)} %param.20) | copy-start | bytes 2359300
  310.2 128.0 %reduce-scatter.9.cloned.1.call-start = ((), (), s32[]{:S(2)}) async-start(), calls=%async_computation.11 | async-start | bytes 3932160 | tf_op jit(solution)/shard_map/reduce_scatter | solution.py:276
  318.5 20.3 %copy-start.12 = (bf16[2048,3,64]{0,2,1:T(8,128)(2,1)S(1)}, bf16[2048,3,64]{0,2,1:T(8,128)(2,1)}, u32[]{:S(2)}) copy-start(bf16[2048,3,64]{0,2,1:T(8,128)(2,1)} %copy-done.11) | copy-start | bytes 2359300
  346.4 146.2 %reduce-scatter.11.cloned.1.call-start = ((), (), s32[]{:S(2)}) async-start(), calls=%async_computation.12 | async-start | bytes 5971968 | tf_op jit(solution)/shard_map/reduce_scatter | solution.py:287
  357.2 220.3 %all-gather.18.cloned.1.call-start = ((), (), s32[]{:S(2)}) async-start(), calls=%async_computation.13 | async-start | bytes 4423680 | tf_op jit(solution)/shard_map/all_gather | solution.py:220
  357.8 267.9 %reduce-scatter.13.cloned.1.call-start = ((), (), s32[]{:S(2)}) async-start(), calls=%async_computation.16 | async-start | bytes 2211840
  517.0 53.3 %all-to-all-start.1 = ((bf16[2048,3,192]{2,1,0:T(4,128)(2,1)}), bf16[2048,3,192]{2,1,0:T(4,128)(2,1)}, u32[]{:S(2)}, u32[]{:S(2)}) async-start(bf16[2048,3,192]{2,1,0:T(4,128)(2,1)} %copy.118), calls=%async_computation.4 | async-start | bytes 8388608 | tf_op jit(solution)/shard_map/all_to_all | solution.py:321
  582.9 44.7 %copy-start.1 = (f32[5,768]{1,0:T(8,128)S(1)}, f32[5,768]{1,0:T(8,128)}, u32[]{:S(2)}) copy-start(f32[5,768]{1,0:T(8,128)} %param.33) | copy-start | bytes 46084
  583.6 44.0 %copy-start.13 = (f32[512,768]{1,0:T(8,128)}, f32[512,768]{1,0:T(8,128)S(1)}, u32[]{:S(2)}) copy-start(f32[512,768]{1,0:T(8,128)S(1)} %multiply_add_fusion) | copy-start | bytes 4718596
  (26 other events, 64.8 us)
Sparse Core Ops, SparseCore 0:
  12.5 31.2 all-gather.9
  53.0 50.7 all-gather.19
  105.4 27.1 all-gather.11
  135.3 54.8 all-gather.21
  199.3 27.4 all-gather.13
  246.0 58.8 reduce-scatter.6
  310.3 28.5 all-gather.15
  346.5 37.8 reduce-scatter.8
  388.0 104.5 reduce-scatter.10
  494.0 30.4 all-gather.17
  528.0 67.4 reduce-scatter.12

commit v7 on v6

--- a/solution.py
+++ b/solution.py
@@ -206,13 +206,7 @@
     )
     normed, unit_one, inv_one = norm_forward(block_in, ln1_gain, ln1_bias)
     normed_all = lax.all_gather(normed.astype(jnp.bfloat16), "tp", axis=0, tiled=True)
-    out_pieces = lax.all_gather(out_weight, ("fsdp", "tp"), axis=0, tiled=False)
-    out_pieces = out_pieces.reshape((fsdp_count, tp_count) + out_weight.shape)
-    out_all = jnp.transpose(out_pieces, (1, 2, 0, 3)).reshape(
-        tp_count * out_weight.shape[0], fsdp_count * out_weight.shape[1]
-    )
-    out_full = lax.dynamic_slice_in_dim(out_all, tp_rank * out_weight.shape[0], out_weight.shape[0], 0)
-    shards = (fc1_weight, fc2_weight)
+    shards = (out_weight, fc1_weight, fc2_weight)
     packed = jnp.concatenate([piece.reshape(-1) for piece in shards])
     packed, qkv_cols, normed_all = lax.optimization_barrier((packed, qkv_cols, normed_all))
     qkv_full = qkv_cols
@@ -228,15 +222,19 @@
     v_heads = jnp.transpose(values_all, (1, 0, 2))
     out_heads, log_mass = attn_forward(prefix, q_heads, k_heads, v_heads, scale)
     mixed = jnp.transpose(out_heads, (1, 0, 2)).reshape(seq_len, cols_here)
-    mixed, grad_rows, gathered = lax.optimization_barrier((mixed, grad_rows, gathered))
     pieces = []
     offset = 0
     for piece in shards:
         size = piece.size
         pieces.append(gathered[:, offset : offset + size].reshape((fsdp_count,) + piece.shape))
         offset += size
-    fc1_part = pieces[0].reshape(-1, fc1_weight.shape[1])
-    fc2_part = jnp.moveaxis(pieces[1], 0, 1).reshape(fc2_weight.shape[0], -1)
+    out_full = jnp.moveaxis(pieces[0], 0, 1).reshape(out_weight.shape[0], -1)
+    fc1_part = pieces[1].reshape(-1, fc1_weight.shape[1])
+    fc2_part = jnp.moveaxis(pieces[2], 0, 1).reshape(fc2_weight.shape[0], -1)
+    out_all = lax.all_gather(out_full, "tp", axis=0, tiled=True)
+    mixed, grad_rows, out_all, fc1_part, fc2_part = lax.optimization_barrier(
+        (mixed, grad_rows, out_all, fc1_part, fc2_part)
+    )
     mixed_rows = lax.all_to_all(mixed, "tp", 0, 1, tiled=True)
     middle = block_in + jnp.dot(mixed_rows, out_all, preferred_element_type=jnp.float32) + out_bias
     normed_two, unit_two, inv_two = norm_forward(middle, ln2_gain, ln2_bias)
@@ -271,11 +269,10 @@
     grad_out_bias = jnp.sum(grad_middle, axis=0)
     grad_attn_rows = lax.all_gather(grad_middle.astype(jnp.bfloat16), "tp", axis=0, tiled=True)
     fc2_partial, grad_attn_rows = lax.optimization_barrier((fc2_partial, grad_attn_rows))
-    result = (
-        middle
-        + lax.psum_scatter(fc2_partial, "tp", scatter_dimension=0, tiled=True).astype(jnp.float32)
-        + fc2_bias
-    )
+    fc2_parts = lax.all_to_all(
+        fc2_partial.reshape(tp_count, local_rows, -1), "tp", 0, 0, tiled=True
+    )
+    result = middle + jnp.sum(fc2_parts.astype(jnp.float32), axis=0) + fc2_bias
     grad_out_w = matmul_tn(mixed, grad_attn_rows)
     fsdp_count = lax.axis_size("fsdp")
     dense_grads = (
@@ -293,10 +290,7 @@
     grad_q_heads, grad_k_heads, grad_v_heads = attn_backward(
         prefix, q_heads, k_heads, v_heads, jnp.transpose(grad_mixed, (1, 0, 2)), log_mass, scale
     )
-    grad_q_low = jnp.transpose(grad_q_heads, (1, 0, 2)).reshape(seq_len, cols_here)
-    grad_k_low = jnp.transpose(grad_k_heads, (1, 0, 2)).reshape(seq_len, cols_here)
-    grad_v_low = jnp.transpose(grad_v_heads, (1, 0, 2)).reshape(seq_len, cols_here)
-    grad_proj = jnp.stack([grad_q_low, grad_k_low, grad_v_low], axis=1)
+    grad_proj = jnp.stack([grad_q_heads, grad_k_heads, grad_v_heads], axis=0)
     grad_proj, result, dense_summed = lax.optimization_barrier((grad_proj, result, dense_summed))
     dense_shards = []
     offset = 0
@@ -307,8 +301,8 @@
     out_shard, fc1_shard, fc2_shard = dense_shards
     grad_qv_here = jnp.stack(
         [
-            jnp.sum(grad_q_low.astype(jnp.float32), axis=0),
-            jnp.sum(grad_v_low.astype(jnp.float32), axis=0),
+            jnp.sum(grad_q_heads.astype(jnp.float32), axis=1).reshape(-1),
+            jnp.sum(grad_v_heads.astype(jnp.float32), axis=1).reshape(-1),
         ],
         axis=0,
     )
@@ -316,12 +310,15 @@
         jnp.zeros(qv_bias.shape, jnp.float32), grad_qv_here, tp_rank * cols_here, 1
     )
     grad_qkv_w = jnp.einsum(
-        "rd,rkc->kdc", normed_all, grad_proj, preferred_element_type=jnp.float32
-    )
-    grad_proj_rows = lax.all_to_all(grad_proj, "tp", 0, 2, tiled=True)
+        "rd,khre->kdhe", normed_all, grad_proj, preferred_element_type=jnp.float32
+    ).reshape(3, normed_all.shape[1], cols_here)
+    grad_proj_rows = lax.all_to_all(grad_proj, "tp", 2, 1, tiled=True)
     grad_proj_rows, qkv_all = lax.optimization_barrier((grad_proj_rows, qkv_all))
     grad_normed = jnp.einsum(
-        "rkc,kdc->rd", grad_proj_rows, qkv_all, preferred_element_type=jnp.float32
+        "khre,kdhe->rd",
+        grad_proj_rows,
+        qkv_all.reshape(3, qkv_all.shape[1], -1, HD),
+        preferred_element_type=jnp.float32,
     )
     grad_in_norm, grad_ln1_gain, grad_ln1_bias = norm_backward(
         grad_normed, unit_one, inv_one, ln1_gain

time: 643 us -> 573 us (0.89)
  waiting for transfers between devices: 237 us -> 159 us
  blocking collectives: 80.3 us -> 95.2 us
    all_gather x1, waiting for transfers between devices: 51.5 us -> 19.5 us  [on_device(): out_all = lax.all_gather(out_full, 'tp', axis=0, tiled=True)]
    reduce_scatter x1, waiting for transfers between devices: 51.6 us -> 23.6 us  [on_device(): lax.psum_scatter(dense_packed.reshape(-1, grad_fc1.shape[1]), 'fsdp', sca...]
    all_to_all x2, waiting for transfers between devices: 42.2 us -> 15.8 us  [the longest x1 15.8 us: on_device(): grad_proj_rows = lax.all_to_all(grad_proj, 'tp', 2, 1, tiled=True)]
    all_to_all x0 -> x1, blocking collectives: none -> 14.2 us  [on_device(): mixed_rows = lax.all_to_all(mixed, 'tp', 0, 1, tiled=True)]
    all_gather x1, waiting for transfers between devices: 16.1 us -> 27.8 us  [on_device(): normed_rows = lax.all_gather(normed_two, 'tp', axis=0, tiled=True)]
    unnamed x83 -> x95, local copies, waits for them, and re-layouts: 24.4 us -> 27.7 us
  transfers between devices with their start and end apart: 13 -> 12, of which waited for: 7 -> 7; matrix products, arithmetic and copies ran while one was open for 22% -> 23% of each run, Pallas kernels for 16% -> 18%
where the time goes in v7:
time: 573 us; the launch traced here: 564 us
  waiting for transfers between devices  159 us (28%)
  Pallas kernels  103 us (18%)
  local copies, waits for them, and re-layouts  97.2 us (17%)
  blocking collectives  95.2 us (17%)
  matrix products  57.7 us (10%)
  other arithmetic  25.3 us (4%)
  between operations  15.9 us (3%)
  starting transfers between devices  11.3 us (2%)
    pallas_call x1, Pallas kernels, attn_backward(): pl.pallas_call(functools.partial(_bwd_kernel, scale), out_shape=(shape, s...  63.9 us
    psum x1, blocking collectives, on_device(): lax.psum((grad_ln1_gain, grad_ln1_bias, grad_qv_bias, grad_out_bias, grad...  42.2 us
    reduce_scatter x1, waiting for transfers between devices, on_device(): lax.psum_scatter(matmul_nt(grad_before, fc1_part), 'tp', scatter_dimensio...  42.2 us
    all_gather x1, blocking collectives, on_device(): qkv_cols = lax.all_gather(qkv_weight, 'fsdp', axis=1, tiled=True)  38.9 us
    pallas_call x1, Pallas kernels, attn_forward(): pl.pallas_call(functools.partial(_fwd_kernel, scale), out_shape=(jax.Shap...  38.9 us
    all_gather x1, waiting for transfers between devices, on_device(): normed_rows = lax.all_gather(normed_two, 'tp', axis=0, tiled=True)  27.8 us
    unnamed x95, local copies, waits for them, and re-layouts  27.7 us
    reduce_scatter x1, waiting for transfers between devices, on_device(): lax.psum_scatter(dense_packed.reshape(-1, grad_fc1.shape[1]), 'fsdp', sca...  23.6 us
  transfers between devices with their start and end apart: 12, of which 7 were waited for; matrix products, arithmetic and copies ran while one was open for 23% of the time, Pallas kernels for 18%

profile of v7, /device:TPU:0, one launch (start us, length us, event | category | flops | bytes accessed | tf_op | source)
XLA Modules:
  0.0 564.2 jit_solution(6939663938585396673)
XLA Ops:
  13.4 38.9 %all_gather.27 = bf16[3,768,192]{2,0,1:T(4,128)(2,1)S(1)} all-gather(bf16[3,96,192]{2,0,1:T(4,128)(2,1)S(1)} %copy.58), channel_id=1, replica_groups=mesh['fsdp'=8,'tp'=4] {'fsdp'}, dimensions={1}, use_global_device_ids=true | all-gather | bytes 995328 | tf_op jit(solution)/shard_map/all_gather | solution.py:199
  67.3 5.1 fusion.12
  72.4 38.9 %shard_map.280 = (bf16[3,2048,64]{2,1,0:T(8,128)(2,1)S(1)}, f32[3,2048,1]{2,1,0:T(8,128)}) custom-call(s32[1]{0:T(128)S(6)} %copy.95.prefix_ref, bf16[3,2048,64]{2,1,0:T(8,128)(2,1)S(1)} %get-tuple-element.129.q_ref, bf16[3,2048,64]{2,1,0:T(8,128)(2,1)S(1)} %bitcast.97, bf16[3,2048,64]{2,1,0:T(8,128)(2,1)} %get-tuple-element.130.v_ref), custom_call_target="tpu_custom_call" | custom-call | flops 3221225472 | bytes 3145728 | tf_op jit(solution)/shard_map/pallas_call | solution.py:127
  125.5 10.3 %all-gather.11.cloned.1.call-done = bf16[2048,768]{1,0:T(8,128)(2,1)} async-done(((bf16[512,768]{1,0:T(8,128)(2,1)}), bf16[2048,768]{1,0:T(8,128)(2,1)}) %all-gather.11.cloned.1.call-update) | async-done | bytes 3145744 | tf_op jit(solution)/shard_map/all_gather | solution.py:215
  135.8 19.5 %all-gather.13.cloned.1.call-done = bf16[768,768]{1,0:T(8,128)(2,1)} async-done(((bf16[192,768]{1,0:T(8,128)(2,1)}), bf16[768,768]{1,0:T(8,128)(2,1)}) %all-gather.13.cloned.1.call-update) | async-done | bytes 1179664 | tf_op jit(solution)/shard_map/all_gather | solution.py:234
  155.4 14.2 %all_to_all.42 = bf16[4,512,192]{1,2,0:T(8,128)(2,1)S(1)} all-to-all(bf16[4,512,192]{1,2,0:T(8,128)(2,1)S(1)} %bitcast.108), channel_id=1, replica_groups=mesh['fsdp'=8,'tp'=4] {'tp'}, dimensions={0} | all-to-all | bytes 1572864 | tf_op jit(solution)/shard_map/all_to_all | solution.py:238
  173.3 27.8 %all-gather.15.cloned.1.call-done = bf16[2048,768]{1,0:T(8,128)(2,1)} async-done(((bf16[512,768]{1,0:T(8,128)(2,1)}), bf16[2048,768]{1,0:T(8,128)(2,1)}) %all-gather.15.cloned.1.call-update) | async-done | bytes 3145744 | tf_op jit(solution)/shard_map/all_gather | solution.py:244
  201.1 4.7 fusion.25
  205.9 7.8 %convert_reduce_fusion = (f32[768]{0:T(1024)S(1)}, bf16[2048,768]{1,0:T(8,128)(2,1)S(1)}, bf16[2048,768]{1,0:T(8,128)(2,1)}) fusion(f32[2048,768]{1,0:T(8,128)S(1)} %fusion.25, f32[768]{0:T(1024)S(1)} %dynamic_slice.7, bf16[2048,768]{1,0:T(8,128)(2,1)S(1)} %copy-done.36, bf16[768,768]{0,1:T(8,128)(2,1)S(1)} %bitcast.117), kind=kOutput, calls=%fused_computation.9 | convolution fusion | flops 2455239936 | bytes 16914432 | tf_op jit(solution)/shard_map/dot_general | solution.py:37
  221.2 6.3 %convolution_convert_fusion = bf16[2048,768]{1,0:T(8,128)(2,1)} fusion(bf16[2048,768]{1,0:T(8,128)(2,1)} %get-tuple-element.118, bf16[768,768]{0,1:T(8,128)(2,1)S(1)} %bitcast.118), kind=kOutput, calls=%fused_computation.16 | convolution fusion | flops 2417491968 | bytes 7471104 | tf_op jit(solution)/shard_map/dot_general | solution.py:247
  236.8 42.2 %reduce-scatter.4.cloned.1.call-done = f32[512,768]{1,0:T(8,128)} async-done(((f32[2048,768]{1,0:T(8,128)}), f32[512,768]{1,0:T(8,128)}) %reduce-scatter.4.cloned.1.call-update) | async-done | bytes 1572880 | tf_op jit(solution)/shard_map/reduce_scatter | solution.py:258
  294.9 18.1 %all-gather.17.cloned.1.call-done = bf16[2048,768]{1,0:T(8,128)(2,1)} async-done(((bf16[512,768]{1,0:T(8,128)(2,1)}), bf16[2048,768]{1,0:T(8,128)(2,1)}) %all-gather.17.cloned.1.call-update) | async-done | bytes 3145744 | tf_op jit(solution)/shard_map/all_gather | solution.py:270
  325.2 5.6 reshape.166
  331.6 5.2 all-to-all-start.1
  341.3 63.9 %shard_map.281 = (bf16[3,2048,64]{2,1,0:T(8,128)(2,1)S(1)}, bf16[3,2048,64]{2,1,0:T(8,128)(2,1)S(1)}, bf16[3,2048,64]{2,1,0:T(8,128)(2,1)S(1)}) custom-call(s32[1]{0:T(128)S(6)} %copy.95.prefix_ref, bf16[3,2048,64]{2,1,0:T(8,128)(2,1)} %copy-done.3, bf16[3,2048,64]{2,1,0:T(8,128)(2,1)} %bitcast.98, bf16[3,2048,64]{2,1,0:T(8,128)(2,1)} %get-tuple-element.130.v_ref, ...), custom_call_target="tpu_custom_call" | custom-call | flops 8053063680 | bytes 6291456 | tf_op jit(solution)/shard_map/pallas_call | solution.py:152
  411.8 23.6 %reduce-scatter.6.cloned.1.call-done = f32[216,768]{1,0:T(8,128)} async-done(((f32[1728,768]{1,0:T(8,128)}), f32[216,768]{1,0:T(8,128)}) %reduce-scatter.6.cloned.1.call-update) | async-done | bytes 663568 | tf_op jit(solution)/shard_map/reduce_scatter | solution.py:284
  438.1 9.5 %copy.92 = bf16[3,3,2048,64]{3,1,0,2:T(4,128)(2,1)} copy(bf16[3,3,2048,64]{3,2,1,0:T(8,128)(2,1)} %pad_maximum_fusion.1) | data formatting | bytes 4718592 | tf_op jit(solution)/shard_map/optimization_barrier | solution.py:294
  447.6 7.1 %reshape.203 = bf16[4,2,147456]{2,1,0:T(2,128)(2,1)} reshape(bf16[2048,3,3,64]{3,2,1,0:T(4,128)(2,1)} %bitcast.101) | data formatting | bytes 4718592
  459.6 6.9 %fusion.9 = f32[3,3,64,768]{3,2,1,0:T(8,128)} fusion(bf16[3,3,2048,64]{3,2,1,0:T(8,128)(2,1)} %pad_maximum_fusion.1, bf16[2048,768]{1,0:T(8,128)(2,1)} %all-gather.9.cloned.1.call-done), kind=kOutput, calls=%fused_computation.18 | convolution fusion | flops 1811939328 | bytes 7274496 | tf_op jit(solution)/shard_map/rd,khre->kdhe/dot_general | solution.py:312
  475.4 15.8 %all-to-all-done.2 = bf16[4,2,147456]{2,1,0:T(2,128)(2,1)} async-done(((bf16[4,2,147456]{2,1,0:T(2,128)(2,1)}), bf16[4,2,147456]{2,1,0:T(2,128)(2,1)}, u32[]{:S(2)}, u32[]{:S(2)}) %all-to-all-start.2) | async-done | bytes 2359328 | tf_op jit(solution)/shard_map/all_to_all | solution.py:315
  491.2 6.9 %reshape.204 = bf16[2048,3,3,64]{3,2,1,0:T(4,128)(2,1)} reshape(bf16[4,2,147456]{2,1,0:T(2,128)(2,1)} %all-to-all-done.2) | data formatting | bytes 4718592
  498.1 9.6 %copy.72 = bf16[3,4,3,512,64]{3,4,0,2,1:T(8,128)(2,1)} copy(bf16[3,4,3,512,64]{4,2,0,3,1:T(4,128)(2,1)} %bitcast.100) | data formatting | bytes 4718592 | tf_op jit(solution)/shard_map/all_to_all | solution.py:315
  507.8 5.5 fusion.14
  514.7 42.2 %all-reduce = (f32[768]{0:T(1024)}, f32[768]{0:T(1024)}, f32[2,768]{1,0:T(2,128)}, f32[768]{0:T(1024)}, f32[768]{0:T(1024)}, /*index=5*/f32[768]{0:T(1024)}, f32[3072]{0:T(1024)}, f32[768]{0:T(1024)}, f32[5,768]{1,0:T(8,128)}) all-reduce(f32[768]{0:T(1024)S(1)} %get-tuple-element.95, ...), channel_id=1, replica_groups=mesh['fsdp'=8,'tp'=4] {'fsdp','tp'}, use_global_device_ids=true, to_apply=%region_13.0 | all-reduce | flops 13056 | bytes 104448 | tf_op jit(solution)/shard_map/psum | solution.py:335
  (196 shorter events, 112.7 us)
Async XLA Ops:
  7.2 45.9 %all-gather.9.cloned.1.call-start = ((), (), s32[]{:S(2)}) async-start(), calls=%async_computation.6 | async-start | bytes 3932160 | tf_op jit(solution)/shard_map/all_gather | solution.py:208
  12.4 100.3 %all-gather.21.cloned.1.call-start = ((), (), s32[]{:S(2)}) async-start(), calls=%async_computation.15 | async-start | bytes 2985984 | tf_op jit(solution)/shard_map/all_gather | solution.py:213
  53.1 82.7 %all-gather.11.cloned.1.call-start = ((), (), s32[]{:S(2)}) async-start(), calls=%async_computation.7 | async-start | bytes 3932160 | tf_op jit(solution)/shard_map/all_gather | solution.py:215
  53.9 101.4 %all-gather.13.cloned.1.call-start = ((), (), s32[]{:S(2)}) async-start(), calls=%async_computation.8 | async-start | bytes 1474560 | tf_op jit(solution)/shard_map/all_gather | solution.py:234
  72.4 38.9 %copy-start.3 = (bf16[3,2048,64]{2,1,0:T(8,128)(2,1)}, bf16[3,2048,64]{2,1,0:T(8,128)(2,1)S(1)}, u32[]{:S(2)}) copy-start(bf16[3,2048,64]{2,1,0:T(8,128)(2,1)S(1)} %get-tuple-element.129.q_ref) | copy-start | bytes 2359300
  117.5 83.6 %all-gather.15.cloned.1.call-start = ((), (), s32[]{:S(2)}) async-start(), calls=%async_computation.9 | async-start | bytes 3932160 | tf_op jit(solution)/shard_map/all_gather | solution.py:244
  124.0 31.3 %copy-start.11 = (bf16[2048,3,64]{0,2,1:T(8,128)(2,1)S(1)}, bf16[2048,3,64]{0,2,1:T(8,128)(2,1)}, u32[]{:S(2)}) copy-start(bf16[2048,3,64]{0,2,1:T(8,128)(2,1)} %copy.63) | copy-start | bytes 2359300
  155.3 14.3 %copy-start.7 = (f32[512,768]{1,0:T(8,128)S(1)}, f32[512,768]{1,0:T(8,128)}, u32[]{:S(2)}) copy-start(f32[512,768]{1,0:T(8,128)} %copy-done.6) | copy-start | bytes 4718596
  155.3 14.3 %copy-start.39 = (bf16[768,768]{1,0:T(8,128)(2,1)S(1)}, bf16[768,768]{1,0:T(8,128)(2,1)}, u32[]{:S(2)}) copy-start(bf16[768,768]{1,0:T(8,128)(2,1)} %all-gather.13.cloned.1.call-done) | copy-start | bytes 3538948
  155.3 14.3 %copy-start.40 = (f32[768]{0:T(1024)S(1)}, f32[768]{0:T(1024)}, u32[]{:S(2)}) copy-start(f32[768]{0:T(1024)} %param.28) | copy-start | bytes 9220
  170.5 110.8 %copy-start.4 = (f32[512,768]{1,0:T(8,128)}, f32[512,768]{1,0:T(8,128)S(1)}, u32[]{:S(2)}) copy-start(f32[512,768]{1,0:T(8,128)S(1)} %get-tuple-element.127) | copy-start | bytes 4718596
  171.2 29.9 %copy-start.22 = (bf16[768,768]{1,0:T(8,128)(2,1)S(1)}, bf16[768,768]{1,0:T(8,128)(2,1)}, u32[]{:S(2)}) copy-start(bf16[768,768]{1,0:T(8,128)(2,1)} %reshape_reshape.6) | copy-start | bytes 3538948
  172.4 106.5 %reduce-scatter.4.cloned.1.call-start = ((), (), s32[]{:S(2)}) async-start(), calls=%async_computation.10 | async-start | bytes 7864320 | tf_op jit(solution)/shard_map/reduce_scatter | solution.py:258
  220.0 93.0 %all-gather.17.cloned.1.call-start = ((), (), s32[]{:S(2)}) async-start(), calls=%async_computation.11 | async-start | bytes 3932160 | tf_op jit(solution)/shard_map/all_gather | solution.py:270
  236.8 44.5 %copy-start.17 = (bf16[512,768]{1,0:T(8,128)(2,1)S(1)}, bf16[512,768]{1,0:T(8,128)(2,1)}, u32[]{:S(2)}) copy-start(bf16[512,768]{1,0:T(8,128)(2,1)} %param.20) | copy-start | bytes 2359300
  284.3 151.2 %reduce-scatter.6.cloned.1.call-start = ((), (), s32[]{:S(2)}) async-start(), calls=%async_computation.12 | async-start | bytes 5971968 | tf_op jit(solution)/shard_map/reduce_scatter | solution.py:284
  292.6 20.3 %copy-start.12 = (bf16[2048,3,64]{0,2,1:T(8,128)(2,1)S(1)}, bf16[2048,3,64]{0,2,1:T(8,128)(2,1)}, u32[]{:S(2)}) copy-start(bf16[2048,3,64]{0,2,1:T(8,128)(2,1)} %copy.63) | copy-start | bytes 2359300
  330.8 176.9 %all-gather.19.cloned.1.call-start = ((), (), s32[]{:S(2)}) async-start(), calls=%async_computation.13 | async-start | bytes 4423680 | tf_op jit(solution)/shard_map/all_gather | solution.py:214
  331.6 76.5 %all-to-all-start.1 = ((bf16[4,512,768]{2,1,0:T(8,128)(2,1)}), bf16[4,512,768]{2,1,0:T(8,128)(2,1)}, u32[]{:S(2)}, u32[]{:S(2)}) async-start(bf16[4,512,768]{2,1,0:T(8,128)(2,1)} %bitcast.20), calls=%async_computation.2 | async-start | bytes 6291456 | tf_op jit(solution)/shard_map/all_to_all | solution.py:272
  454.7 36.5 %all-to-all-start.2 = ((bf16[4,2,147456]{2,1,0:T(2,128)(2,1)}), bf16[4,2,147456]{2,1,0:T(2,128)(2,1)}, u32[]{:S(2)}, u32[]{:S(2)}) async-start(bf16[4,2,147456]{2,1,0:T(2,128)(2,1)} %reshape.203), calls=%async_computation.4 | async-start | bytes 4718592 | tf_op jit(solution)/shard_map/all_to_all | solution.py:315
  459.2 97.6 %reduce-scatter.8.cloned.1.call-start = ((), (), s32[]{:S(2)}) async-start(), calls=%async_computation.14 | async-start | bytes 2654208 | tf_op jit(solution)/shard_map/reduce_scatter | solution.py:334
  498.1 9.6 %copy-start.8 = (f32[512,768]{1,0:T(8,128)S(1)}, f32[512,768]{1,0:T(8,128)}, u32[]{:S(2)}) copy-start(f32[512,768]{1,0:T(8,128)} %copy-done.6) | copy-start | bytes 4718596
  513.3 43.6 %copy-start.1 = (f32[5,768]{1,0:T(8,128)S(1)}, f32[5,768]{1,0:T(8,128)}, u32[]{:S(2)}) copy-start(f32[5,768]{1,0:T(8,128)} %param.33) | copy-start | bytes 46084
  514.0 42.9 %copy-start.13 = (f32[512,768]{1,0:T(8,128)}, f32[512,768]{1,0:T(8,128)S(1)}, u32[]{:S(2)}) copy-start(f32[512,768]{1,0:T(8,128)S(1)} %multiply_add_fusion) | copy-start | bytes 4718596
  (32 other events, 93.0 us)
Sparse Core Ops, SparseCore 0:
  12.5 31.2 all-gather.8
  53.2 53.8 all-gather.20
  108.7 27.0 all-gather.10
  137.8 17.4 all-gather.12
  172.6 28.4 all-gather.14
  220.1 58.8 reduce-scatter.3
  284.4 28.4 all-gather.16
  330.9 104.4 reduce-scatter.5
  437.0 33.9 all-gather.18
  474.9 71.5 reduce-scatter.7

commit v8 on v7

--- a/solution.py
+++ b/solution.py
@@ -211,7 +211,8 @@
     packed, qkv_cols, normed_all = lax.optimization_barrier((packed, qkv_cols, normed_all))
     qkv_full = qkv_cols
     gathered = lax.all_gather(packed, "fsdp", axis=0, tiled=False)
-    qkv_all = lax.all_gather(qkv_cols, "tp", axis=2, tiled=True)
+    qkv_copies = jnp.broadcast_to(qkv_cols[None], (tp_count,) + qkv_cols.shape)
+    qkv_all = lax.all_to_all(qkv_copies, "tp", 0, 0, tiled=True)
     grad_rows = lax.all_gather(cotangent, "tp", axis=0, tiled=True)
     projected = jnp.einsum("rd,kdc->krc", normed_all, qkv_full, preferred_element_type=jnp.float32)
     queries = (projected[0] + qv_here[0]).astype(jnp.bfloat16).reshape(seq_len, heads_here, HD)
@@ -221,6 +222,7 @@
     k_heads = jnp.transpose(keys_all, (1, 0, 2))
     v_heads = jnp.transpose(values_all, (1, 0, 2))
     out_heads, log_mass = attn_forward(prefix, q_heads, k_heads, v_heads, scale)
+    out_heads, qkv_all = lax.optimization_barrier((out_heads, qkv_all))
     mixed = jnp.transpose(out_heads, (1, 0, 2)).reshape(seq_len, cols_here)
     pieces = []
     offset = 0
@@ -291,7 +293,28 @@
         prefix, q_heads, k_heads, v_heads, jnp.transpose(grad_mixed, (1, 0, 2)), log_mass, scale
     )
     grad_proj = jnp.stack([grad_q_heads, grad_k_heads, grad_v_heads], axis=0)
-    grad_proj, result, dense_summed = lax.optimization_barrier((grad_proj, result, dense_summed))
+    grad_proj, result = lax.optimization_barrier((grad_proj, result))
+    grad_qv_here = jnp.stack(
+        [
+            jnp.sum(grad_q_heads.astype(jnp.float32), axis=1).reshape(-1),
+            jnp.sum(grad_v_heads.astype(jnp.float32), axis=1).reshape(-1),
+        ],
+        axis=0,
+    )
+    grad_qv_bias = lax.dynamic_update_slice_in_dim(
+        jnp.zeros(qv_bias.shape, jnp.float32), grad_qv_here, tp_rank * cols_here, 1
+    )
+    grad_qkv_w = jnp.einsum(
+        "rd,khre->kdhe", normed_all, grad_proj, preferred_element_type=jnp.float32
+    ).reshape(3, normed_all.shape[1], cols_here)
+    grad_proj_rows = lax.all_to_all(grad_proj, "tp", 2, 1, tiled=True)
+    grad_proj_rows, dense_summed = lax.optimization_barrier((grad_proj_rows, dense_summed))
+    grad_normed = jnp.einsum(
+        "kshre,skdhe->rd",
+        grad_proj_rows.reshape(3, tp_count, heads_here, local_rows, HD),
+        qkv_all.reshape(tp_count, 3, qkv_all.shape[2], heads_here, HD),
+        preferred_element_type=jnp.float32,
+    )
     dense_shards = []
     offset = 0
     for g in dense_grads:
@@ -299,27 +322,6 @@
         dense_shards.append(dense_summed[0, offset : offset + size].reshape(g.shape[1:]))
         offset += size
     out_shard, fc1_shard, fc2_shard = dense_shards
-    grad_qv_here = jnp.stack(
-        [
-            jnp.sum(grad_q_heads.astype(jnp.float32), axis=1).reshape(-1),
-            jnp.sum(grad_v_heads.astype(jnp.float32), axis=1).reshape(-1),
-        ],
-        axis=0,
-    )
-    grad_qv_bias = lax.dynamic_update_slice_in_dim(
-        jnp.zeros(qv_bias.shape, jnp.float32), grad_qv_here, tp_rank * cols_here, 1
-    )
-    grad_qkv_w = jnp.einsum(
-        "rd,khre->kdhe", normed_all, grad_proj, preferred_element_type=jnp.float32
-    ).reshape(3, normed_all.shape[1], cols_here)
-    grad_proj_rows = lax.all_to_all(grad_proj, "tp", 2, 1, tiled=True)
-    grad_proj_rows, qkv_all = lax.optimization_barrier((grad_proj_rows, qkv_all))
-    grad_normed = jnp.einsum(
-        "khre,kdhe->rd",
-        grad_proj_rows,
-        qkv_all.reshape(3, qkv_all.shape[1], -1, HD),
-        preferred_element_type=jnp.float32,
-    )
     grad_in_norm, grad_ln1_gain, grad_ln1_bias = norm_backward(
         grad_normed, unit_one, inv_one, ln1_gain
     )

time: 573 us -> 570 us (level)
  waiting for transfers between devices: 159 us -> 130 us
  local copies, waits for them, and re-layouts: 97.2 us -> 122 us
    reduce_scatter x1, waiting for transfers between devices: 23.6 us -> 0.01 us  [on_device(): lax.psum_scatter(dense_packed.reshape(-1, grad_fc1.shape[1]), 'fsdp', sca...]
    optimization_barrier x1, local copies, waits for them, and re-layouts: 9.49 us -> 31.8 us  [on_device(): grad_proj, result = lax.optimization_barrier((grad_proj, result))]
    unnamed x95 -> x92, local copies, waits for them, and re-layouts: 27.7 us -> 27.9 us
  transfers between devices with their start and end apart: 12 -> 12, of which waited for: 7 -> 6; matrix products, arithmetic and copies ran while one was open for 23% -> 27% of each run, Pallas kernels for 18% -> 18%
where the time goes in v8:
time: 570 us; the launch traced here: 560 us
  waiting for transfers between devices  130 us (23%)
  local copies, waits for them, and re-layouts  122 us (21%)
  Pallas kernels  102 us (18%)
  blocking collectives  91.8 us (16%)
  matrix products  58 us (10%)
  other arithmetic  25.3 us (4%)
  starting transfers between devices  15.8 us (3%)
  between operations  15.5 us (3%)
    pallas_call x1, Pallas kernels, attn_backward(): pl.pallas_call(functools.partial(_bwd_kernel, scale), out_shape=(shape, s...  63.9 us
    psum x1, blocking collectives, on_device(): lax.psum((grad_ln1_gain, grad_ln1_bias, grad_qv_bias, grad_out_bias, grad...  42.4 us
    reduce_scatter x1, waiting for transfers between devices, on_device(): lax.psum_scatter(matmul_nt(grad_before, fc1_part), 'tp', scatter_dimensio...  42 us
    pallas_call x1, Pallas kernels, attn_forward(): pl.pallas_call(functools.partial(_fwd_kernel, scale), out_shape=(jax.Shap...  38.5 us
    all_gather x1, blocking collectives, on_device(): qkv_cols = lax.all_gather(qkv_weight, 'fsdp', axis=1, tiled=True)  35.2 us
    optimization_barrier x1, local copies, waits for them, and re-layouts, on_device(): grad_proj, result = lax.optimization_barrier((grad_proj, result))  31.8 us
    unnamed x92, local copies, waits for them, and re-layouts  27.9 us
    all_gather x1, waiting for transfers between devices, on_device(): normed_rows = lax.all_gather(normed_two, 'tp', axis=0, tiled=True)  27.8 us
  transfers between devices with their start and end apart: 12, of which 6 were waited for; matrix products, arithmetic and copies ran while one was open for 27% of the time, Pallas kernels for 18%

profile of v8, /device:TPU:0, one launch (start us, length us, event | category | flops | bytes accessed | tf_op | source)
XLA Modules:
  0.0 560.2 jit_solution(9582585619135735637)
XLA Ops:
  13.3 35.2 %all_gather.24 = bf16[3,768,192]{2,1,0:T(8,128)(2,1)S(1)} all-gather(bf16[3,96,192]{2,1,0:T(8,128)(2,1)S(1)} %copy-done.27), channel_id=1, replica_groups=mesh['fsdp'=8,'tp'=4] {'fsdp'}, dimensions={1}, use_global_device_ids=true | all-gather | bytes 995328 | tf_op jit(solution)/shard_map/all_gather | solution.py:199
  52.8 4.7 all-to-all-start
  70.6 5.0 fusion.13
  75.6 38.5 %shard_map.280 = (bf16[3,2048,64]{2,1,0:T(8,128)(2,1)S(1)}, f32[3,2048,1]{2,1,0:T(8,128)}) custom-call(s32[1]{0:T(128)S(6)} %copy.123.prefix_ref, bf16[3,2048,64]{2,1,0:T(8,128)(2,1)S(1)} %get-tuple-element.146.q_ref, bf16[3,2048,64]{2,1,0:T(8,128)(2,1)S(1)} %bitcast.98, bf16[3,2048,64]{2,1,0:T(8,128)(2,1)} %get-tuple-element.147.v_ref), custom_call_target="tpu_custom_call" | custom-call | flops 3221225472 | bytes 3145728 | tf_op jit(solution)/shard_map/pallas_call | solution.py:127
  133.7 19.5 %all-gather.12.cloned.1.call-done = bf16[768,768]{1,0:T(8,128)(2,1)} async-done(((bf16[192,768]{1,0:T(8,128)(2,1)}), bf16[768,768]{1,0:T(8,128)(2,1)}) %all-gather.12.cloned.1.call-update) | async-done | bytes 1179664 | tf_op jit(solution)/shard_map/all_gather | solution.py:236
  153.2 14.2 %all_to_all.47 = bf16[4,512,192]{1,2,0:T(8,128)(2,1)S(1)} all-to-all(bf16[4,512,192]{1,2,0:T(8,128)(2,1)S(1)} %bitcast.109), channel_id=1, replica_groups=mesh['fsdp'=8,'tp'=4] {'tp'}, dimensions={0} | all-to-all | bytes 1572864 | tf_op jit(solution)/shard_map/all_to_all | solution.py:240
  171.1 27.8 %all-gather.14.cloned.1.call-done = bf16[2048,768]{1,0:T(8,128)(2,1)} async-done(((bf16[512,768]{1,0:T(8,128)(2,1)}), bf16[2048,768]{1,0:T(8,128)(2,1)}) %all-gather.14.cloned.1.call-update) | async-done | bytes 3145744 | tf_op jit(solution)/shard_map/all_gather | solution.py:246
  199.0 4.7 fusion.26
  203.7 7.9 %convert_reduce_fusion = (f32[768]{0:T(1024)S(1)}, bf16[2048,768]{1,0:T(8,128)(2,1)S(1)}, bf16[2048,768]{1,0:T(8,128)(2,1)}) fusion(f32[2048,768]{1,0:T(8,128)S(1)} %fusion.26, f32[768]{0:T(1024)S(1)} %dynamic_slice.7, bf16[2048,768]{1,0:T(8,128)(2,1)S(1)} %copy-done.35, bf16[768,768]{0,1:T(8,128)(2,1)S(1)} %bitcast.117), kind=kOutput, calls=%fused_computation.9 | convolution fusion | flops 2455239936 | bytes 16914432 | tf_op jit(solution)/shard_map/dot_general | solution.py:37
  219.0 6.4 %convolution_convert_fusion = bf16[2048,768]{1,0:T(8,128)(2,1)} fusion(bf16[2048,768]{1,0:T(8,128)(2,1)} %get-tuple-element.135, bf16[768,768]{0,1:T(8,128)(2,1)S(1)} %bitcast.118), kind=kOutput, calls=%fused_computation.16 | convolution fusion | flops 2417491968 | bytes 7471104 | tf_op jit(solution)/shard_map/dot_general | solution.py:249
  234.8 42.0 %reduce-scatter.4.cloned.1.call-done = f32[512,768]{1,0:T(8,128)} async-done(((f32[2048,768]{1,0:T(8,128)}), f32[512,768]{1,0:T(8,128)}) %reduce-scatter.4.cloned.1.call-update) | async-done | bytes 1572880 | tf_op jit(solution)/shard_map/reduce_scatter | solution.py:260
  292.7 18.0 %all-gather.16.cloned.1.call-done = bf16[2048,768]{1,0:T(8,128)(2,1)} async-done(((bf16[512,768]{1,0:T(8,128)(2,1)}), bf16[2048,768]{1,0:T(8,128)(2,1)}) %all-gather.16.cloned.1.call-update) | async-done | bytes 3145744 | tf_op jit(solution)/shard_map/all_gather | solution.py:272
  318.2 4.7 pad_maximum_fusion
  322.9 5.7 %reshape.170 = f32[1728,768]{1,0:T(8,128)} reshape(f32[8,165888]{1,0:T(8,128)} %pad_maximum_fusion) | data formatting | bytes 10616832 | tf_op jit(solution)/shard_map/reshape | solution.py:287
  328.6 5.2 all-to-all-start.2
  338.3 63.9 %shard_map.281 = (bf16[3,2048,64]{2,1,0:T(8,128)(2,1)S(1)}, bf16[3,2048,64]{2,1,0:T(8,128)(2,1)S(1)}, bf16[3,2048,64]{2,1,0:T(8,128)(2,1)S(1)}) custom-call(s32[1]{0:T(128)S(6)} %copy.123.prefix_ref, bf16[3,2048,64]{2,1,0:T(8,128)(2,1)} %copy-done.3, bf16[3,2048,64]{2,1,0:T(8,128)(2,1)} %bitcast.99, bf16[3,2048,64]{2,1,0:T(8,128)(2,1)} %get-tuple-element.147.v_ref, ...), custom_call_target="tpu_custom_call" | custom-call | flops 8053063680 | bytes 6291456 | tf_op jit(solution)/shard_map/pallas_call | solution.py:152
  409.6 31.8 %copy.120 = bf16[3,3,2048,64]{3,1,0,2:T(4,128)(2,1)} copy(bf16[3,3,2048,64]{3,2,1,0:T(8,128)(2,1)S(1)} %copy-done.9) | data formatting | bytes 4718592 | tf_op jit(solution)/shard_map/optimization_barrier | solution.py:296
  441.4 7.1 %reshape.208 = bf16[4,2,147456]{2,1,0:T(2,128)(2,1)} reshape(bf16[2048,3,3,64]{3,2,1,0:T(4,128)(2,1)} %bitcast.102) | data formatting | bytes 4718592
  453.3 6.8 %fusion.9 = f32[3,3,64,768]{3,2,1,0:T(8,128)} fusion(bf16[3,3,2048,64]{3,2,1,0:T(8,128)(2,1)} %pad_maximum_fusion.1, bf16[2048,768]{1,0:T(8,128)(2,1)} %all-gather.8.cloned.1.call-done), kind=kOutput, calls=%fused_computation.18 | convolution fusion | flops 1811939328 | bytes 7274496 | tf_op jit(solution)/shard_map/rd,khre->kdhe/dot_general | solution.py:307
  464.4 17.1 %all-to-all-done.3 = bf16[4,2,147456]{2,1,0:T(2,128)(2,1)} async-done(((bf16[4,2,147456]{2,1,0:T(2,128)(2,1)}), bf16[4,2,147456]{2,1,0:T(2,128)(2,1)}, u32[]{:S(2)}, u32[]{:S(2)}) %all-to-all-start.3) | async-done | bytes 2359328 | tf_op jit(solution)/shard_map/all_to_all | solution.py:310
  481.5 6.9 %reshape.209 = bf16[2048,3,3,64]{3,2,1,0:T(4,128)(2,1)} reshape(bf16[4,2,147456]{2,1,0:T(2,128)(2,1)} %all-to-all-done.3) | data formatting | bytes 4718592
  488.4 9.5 %copy.90 = bf16[3,4,3,512,64]{3,4,2,1,0:T(8,128)(2,1)} copy(bf16[3,4,3,512,64]{4,2,0,3,1:T(4,128)(2,1)} %bitcast.101) | data formatting | bytes 4718592 | tf_op jit(solution)/shard_map/all_to_all | solution.py:310
  504.0 5.4 fusion.15
  510.8 42.4 %all-reduce = (f32[768]{0:T(1024)}, f32[768]{0:T(1024)}, f32[2,768]{1,0:T(2,128)}, f32[768]{0:T(1024)}, f32[768]{0:T(1024)}, /*index=5*/f32[768]{0:T(1024)}, f32[3072]{0:T(1024)}, f32[768]{0:T(1024)}, f32[5,768]{1,0:T(8,128)}) all-reduce(f32[768]{0:T(1024)S(1)} %get-tuple-element.112, ...), channel_id=1, replica_groups=mesh['fsdp'=8,'tp'=4] {'fsdp','tp'}, use_global_device_ids=true, to_apply=%region_13.0 | all-reduce | flops 13056 | bytes 104448 | tf_op jit(solution)/shard_map/psum | solution.py:337
  (193 shorter events, 114.2 us)
Async XLA Ops:
  7.2 42.0 %all-gather.8.cloned.1.call-start = ((), (), s32[]{:S(2)}) async-start(), calls=%async_computation.7 | async-start | bytes 3932160 | tf_op jit(solution)/shard_map/all_gather | solution.py:208
  12.4 104.2 %all-gather.18.cloned.1.call-start = ((), (), s32[]{:S(2)}) async-start(), calls=%async_computation.15 | async-start | bytes 2985984 | tf_op jit(solution)/shard_map/all_gather | solution.py:213
  49.3 84.4 %all-gather.10.cloned.1.call-start = ((), (), s32[]{:S(2)}) async-start(), calls=%async_computation.8 | async-start | bytes 3932160 | tf_op jit(solution)/shard_map/all_gather | solution.py:216
  52.8 62.4 %all-to-all-start = ((bf16[4,3,768,192]{2,3,1,0:T(8,128)(2,1)}), bf16[4,3,768,192]{2,3,1,0:T(8,128)(2,1)}, u32[]{:S(2)}, u32[]{:S(2)}) async-start(bf16[4,3,768,192]{2,3,1,0:T(8,128)(2,1)} %broadcast_in_dim.6), calls=%async_computation | async-start | bytes 7077888 | tf_op jit(solution)/shard_map/all_to_all | solution.py:215
  57.6 95.6 %all-gather.12.cloned.1.call-start = ((), (), s32[]{:S(2)}) async-start(), calls=%async_computation.9 | async-start | bytes 1474560 | tf_op jit(solution)/shard_map/all_gather | solution.py:236
  121.3 77.7 %all-gather.14.cloned.1.call-start = ((), (), s32[]{:S(2)}) async-start(), calls=%async_computation.10 | async-start | bytes 3932160 | tf_op jit(solution)/shard_map/all_gather | solution.py:246
  127.5 25.7 %copy-start.12 = (bf16[2048,3,64]{0,2,1:T(8,128)(2,1)S(1)}, bf16[2048,3,64]{0,2,1:T(8,128)(2,1)}, u32[]{:S(2)}) copy-start(bf16[2048,3,64]{0,2,1:T(8,128)(2,1)} %copy.83) | copy-start | bytes 2359300
  153.1 14.3 %copy-start.7 = (f32[512,768]{1,0:T(8,128)S(1)}, f32[512,768]{1,0:T(8,128)}, u32[]{:S(2)}) copy-start(f32[512,768]{1,0:T(8,128)} %copy-done.6) | copy-start | bytes 4718596
  153.1 14.3 %copy-start.38 = (bf16[768,768]{1,0:T(8,128)(2,1)S(1)}, bf16[768,768]{1,0:T(8,128)(2,1)}, u32[]{:S(2)}) copy-start(bf16[768,768]{1,0:T(8,128)(2,1)} %all-gather.12.cloned.1.call-done) | copy-start | bytes 3538948
  153.1 14.3 %copy-start.39 = (f32[768]{0:T(1024)S(1)}, f32[768]{0:T(1024)}, u32[]{:S(2)}) copy-start(f32[768]{0:T(1024)} %param.28) | copy-start | bytes 9220
  168.3 110.8 %copy-start.4 = (f32[512,768]{1,0:T(8,128)}, f32[512,768]{1,0:T(8,128)S(1)}, u32[]{:S(2)}) copy-start(f32[512,768]{1,0:T(8,128)S(1)} %get-tuple-element.144) | copy-start | bytes 4718596
  169.1 29.9 %copy-start.21 = (bf16[768,768]{1,0:T(8,128)(2,1)S(1)}, bf16[768,768]{1,0:T(8,128)(2,1)}, u32[]{:S(2)}) copy-start(bf16[768,768]{1,0:T(8,128)(2,1)} %reshape_reshape.6) | copy-start | bytes 3538948
  170.3 106.5 %reduce-scatter.4.cloned.1.call-start = ((), (), s32[]{:S(2)}) async-start(), calls=%async_computation.11 | async-start | bytes 7864320 | tf_op jit(solution)/shard_map/reduce_scatter | solution.py:260
  217.8 92.9 %all-gather.16.cloned.1.call-start = ((), (), s32[]{:S(2)}) async-start(), calls=%async_computation.12 | async-start | bytes 3932160 | tf_op jit(solution)/shard_map/all_gather | solution.py:272
  219.0 6.4 %copy-start.36 = (bf16[2048,768]{1,0:T(8,128)(2,1)S(1)}, bf16[2048,768]{1,0:T(8,128)(2,1)}, u32[]{:S(2)}) copy-start(bf16[2048,768]{1,0:T(8,128)(2,1)} %all-gather.10.cloned.1.call-done) | copy-start | bytes 9437188
  219.0 6.4 %copy-start.42 = (bf16[2048,768]{1,0:T(8,128)(2,1)S(1)}, bf16[2048,768]{1,0:T(8,128)(2,1)}, u32[]{:S(2)}) copy-start(bf16[2048,768]{1,0:T(8,128)(2,1)} %get-tuple-element.135) | copy-start | bytes 9437188
  234.8 44.3 %copy-start.17 = (bf16[512,768]{1,0:T(8,128)(2,1)S(1)}, bf16[512,768]{1,0:T(8,128)(2,1)}, u32[]{:S(2)}) copy-start(bf16[512,768]{1,0:T(8,128)(2,1)} %param.20) | copy-start | bytes 2359300
  282.0 215.9 %reduce-scatter.6.cloned.1.call-start = ((), (), s32[]{:S(2)}) async-start(), calls=%async_computation.13 | async-start | bytes 5971968 | tf_op jit(solution)/shard_map/reduce_scatter | solution.py:286
  290.4 20.2 %copy-start.13 = (bf16[2048,3,64]{0,2,1:T(8,128)(2,1)S(1)}, bf16[2048,3,64]{0,2,1:T(8,128)(2,1)}, u32[]{:S(2)}) copy-start(bf16[2048,3,64]{0,2,1:T(8,128)(2,1)} %copy.83) | copy-start | bytes 2359300
  328.6 76.5 %all-to-all-start.2 = ((bf16[4,512,768]{2,1,0:T(8,128)(2,1)}), bf16[4,512,768]{2,1,0:T(8,128)(2,1)}, u32[]{:S(2)}, u32[]{:S(2)}) async-start(bf16[4,512,768]{2,1,0:T(8,128)(2,1)} %bitcast.20), calls=%async_computation.3 | async-start | bytes 6291456 | tf_op jit(solution)/shard_map/all_to_all | solution.py:274
  448.5 33.1 %all-to-all-start.3 = ((bf16[4,2,147456]{2,1,0:T(2,128)(2,1)}), bf16[4,2,147456]{2,1,0:T(2,128)(2,1)}, u32[]{:S(2)}, u32[]{:S(2)}) async-start(bf16[4,2,147456]{2,1,0:T(2,128)(2,1)} %reshape.208), calls=%async_computation.4 | async-start | bytes 4718592 | tf_op jit(solution)/shard_map/all_to_all | solution.py:310
  453.0 100.3 %reduce-scatter.8.cloned.1.call-start = ((), (), s32[]{:S(2)}) async-start(), calls=%async_computation.14 | async-start | bytes 2654208 | tf_op jit(solution)/shard_map/reduce_scatter | solution.py:336
  509.5 43.8 %copy-start.1 = (f32[5,768]{1,0:T(8,128)S(1)}, f32[5,768]{1,0:T(8,128)}, u32[]{:S(2)}) copy-start(f32[5,768]{1,0:T(8,128)} %param.33) | copy-start | bytes 46084
  510.1 43.1 %copy-start.14 = (f32[512,768]{1,0:T(8,128)}, f32[512,768]{1,0:T(8,128)S(1)}, u32[]{:S(2)}) copy-start(f32[512,768]{1,0:T(8,128)S(1)} %multiply_add_fusion) | copy-start | bytes 4718596
  (31 other events, 86.2 us)
Sparse Core Ops, SparseCore 0:
  12.6 31.2 all-gather.7
  49.4 55.5 all-gather.17
  106.5 27.1 all-gather.9
  135.7 17.4 all-gather.11
  170.4 28.4 all-gather.13
  217.9 58.8 reduce-scatter.3
  282.1 28.4 all-gather.15
  328.7 104.4 reduce-scatter.5
  463.2 71.4 reduce-scatter.7

commit v9 on v8

--- a/solution.py
+++ b/solution.py
@@ -84,7 +84,7 @@
     total = jnp.sum(expo, axis=-1, keepdims=True)
     probs_low = (expo / total).astype(jnp.bfloat16)
     out = jnp.dot(probs_low, v_ref[0], preferred_element_type=jnp.float32)
-    o_ref[0] = out.astype(o_ref.dtype)
+    o_ref[0, 0] = out.astype(o_ref.dtype)
     lse_ref[0] = peak + jnp.log(total)
 
 
@@ -108,30 +108,33 @@
     grad_probs = _nt(grad_out, v_ref[0])
     inner = jnp.sum(probs * grad_probs, axis=-1, keepdims=True)
     grad_scores = (probs * (grad_probs - inner)).astype(jnp.bfloat16)
-    dq_ref[0] = (jnp.dot(grad_scores, k, preferred_element_type=jnp.float32) * scale).astype(dq_ref.dtype)
+    dq_ref[0, 0] = (jnp.dot(grad_scores, k, preferred_element_type=jnp.float32) * scale).astype(dq_ref.dtype)
     dk_acc[...] += _tn(grad_scores, q)
 
     @pl.when(qb == pl.num_programs(1) - 1)
     def _():
-        dk_ref[0] = (dk_acc[...] * scale).astype(dk_ref.dtype)
-        dv_ref[0] = dv_acc[...].astype(dv_ref.dtype)
-
-
-def attn_forward(prefix, q, k, v, scale):
+        groups, rows, hd = dk_ref.shape[0], dk_ref.shape[2], dk_ref.shape[3]
+        dk_ref[:, 0] = (dk_acc[...] * scale).astype(dk_ref.dtype).reshape(groups, rows, hd)
+        dv_ref[:, 0] = dv_acc[...].astype(dv_ref.dtype).reshape(groups, rows, hd)
+
+
+def attn_forward(prefix, q, k, v, scale, groups):
     heads, seq, hd = q.shape
-    qb = min(ATT_QB, seq)
+    qb = min(ATT_QB, seq // groups)
+    per = seq // groups // qb
     grid = (heads, seq // qb)
     q_spec = pl.BlockSpec((1, qb, hd), lambda h, i, p: (h, i, 0))
     kv_spec = pl.BlockSpec((1, seq, hd), lambda h, i, p: (h, 0, 0))
     lse_spec = pl.BlockSpec((1, qb, 1), lambda h, i, p: (h, i, 0))
+    o_spec = pl.BlockSpec((1, 1, qb, hd), lambda h, i, p: (i // per, h, i % per, 0))
     return pl.pallas_call(
         functools.partial(_fwd_kernel, scale),
-        out_shape=(jax.ShapeDtypeStruct((heads, seq, hd), jnp.bfloat16),
+        out_shape=(jax.ShapeDtypeStruct((groups, heads, seq // groups, hd), jnp.bfloat16),
                    jax.ShapeDtypeStruct((heads, seq, 1), jnp.float32)),
         grid_spec=pltpu.PrefetchScalarGridSpec(
             num_scalar_prefetch=1, grid=grid,
             in_specs=[q_spec, kv_spec, kv_spec],
-            out_specs=[q_spec, lse_spec]),
+            out_specs=[o_spec, lse_spec]),
         compiler_params=pltpu.CompilerParams(
             dimension_semantics=("arbitrary", "arbitrary"),
             vmem_limit_bytes=48 * 1024 * 1024),
@@ -141,21 +144,24 @@
     )(prefix, q, k, v)
 
 
-def attn_backward(prefix, q, k, v, grad_out, lse, scale):
+def attn_backward(prefix, q, k, v, grad_out, lse, scale, groups):
     heads, seq, hd = q.shape
-    qb = min(ATT_QB, seq)
+    qb = min(ATT_QB, seq // groups)
+    per = seq // groups // qb
     grid = (heads, seq // qb)
     q_spec = pl.BlockSpec((1, qb, hd), lambda h, i, p: (h, i, 0))
     kv_spec = pl.BlockSpec((1, seq, hd), lambda h, i, p: (h, 0, 0))
     lse_spec = pl.BlockSpec((1, qb, 1), lambda h, i, p: (h, i, 0))
-    shape = jax.ShapeDtypeStruct((heads, seq, hd), jnp.bfloat16)
+    dq_spec = pl.BlockSpec((1, 1, qb, hd), lambda h, i, p: (i // per, h, i % per, 0))
+    dkv_spec = pl.BlockSpec((groups, 1, seq // groups, hd), lambda h, i, p: (0, h, 0, 0))
+    shape = jax.ShapeDtypeStruct((groups, heads, seq // groups, hd), jnp.bfloat16)
     return pl.pallas_call(
         functools.partial(_bwd_kernel, scale),
         out_shape=(shape, shape, shape),
         grid_spec=pltpu.PrefetchScalarGridSpec(
             num_scalar_prefetch=1, grid=grid,
             in_specs=[q_spec, kv_spec, kv_spec, q_spec, lse_spec],
-            out_specs=[q_spec, kv_spec, kv_spec],
+            out_specs=[dq_spec, dkv_spec, dkv_spec],
             scratch_shapes=[pltpu.VMEM((seq, hd), jnp.float32),
                             pltpu.VMEM((seq, hd), jnp.float32)]),
         compiler_params=pltpu.CompilerParams(
@@ -221,9 +227,8 @@
     q_heads = jnp.transpose(queries, (1, 0, 2))
     k_heads = jnp.transpose(keys_all, (1, 0, 2))
     v_heads = jnp.transpose(values_all, (1, 0, 2))
-    out_heads, log_mass = attn_forward(prefix, q_heads, k_heads, v_heads, scale)
-    out_heads, qkv_all = lax.optimization_barrier((out_heads, qkv_all))
-    mixed = jnp.transpose(out_heads, (1, 0, 2)).reshape(seq_len, cols_here)
+    mixed, log_mass = attn_forward(prefix, q_heads, k_heads, v_heads, scale, tp_count)
+    mixed, qkv_all = lax.optimization_barrier((mixed, qkv_all))
     pieces = []
     offset = 0
     for piece in shards:
@@ -237,8 +242,17 @@
     mixed, grad_rows, out_all, fc1_part, fc2_part = lax.optimization_barrier(
         (mixed, grad_rows, out_all, fc1_part, fc2_part)
     )
-    mixed_rows = lax.all_to_all(mixed, "tp", 0, 1, tiled=True)
-    middle = block_in + jnp.dot(mixed_rows, out_all, preferred_element_type=jnp.float32) + out_bias
+    mixed_rows = lax.all_to_all(mixed, "tp", 0, 0, tiled=True)
+    middle = (
+        block_in
+        + jnp.einsum(
+            "shre,shem->rm",
+            mixed_rows,
+            out_all.reshape(tp_count, heads_here, HD, -1),
+            preferred_element_type=jnp.float32,
+        )
+        + out_bias
+    )
     normed_two, unit_two, inv_two = norm_forward(middle, ln2_gain, ln2_bias)
     normed_two = normed_two.astype(jnp.bfloat16)
     grad_top = cotangent.astype(jnp.float32)
@@ -275,7 +289,12 @@
         fc2_partial.reshape(tp_count, local_rows, -1), "tp", 0, 0, tiled=True
     )
     result = middle + jnp.sum(fc2_parts.astype(jnp.float32), axis=0) + fc2_bias
-    grad_out_w = matmul_tn(mixed, grad_attn_rows)
+    grad_out_w = jnp.einsum(
+        "thre,trm->hem",
+        mixed,
+        grad_attn_rows.reshape(tp_count, local_rows, -1),
+        preferred_element_type=jnp.float32,
+    ).reshape(cols_here, -1)
     fsdp_count = lax.axis_size("fsdp")
     dense_grads = (
         jnp.moveaxis(grad_out_w.reshape(grad_out_w.shape[0], fsdp_count, -1), 1, 0),
@@ -290,30 +309,36 @@
         matmul_nt(grad_attn_rows, out_full).astype(jnp.bfloat16).reshape(seq_len, heads_here, HD)
     )
     grad_q_heads, grad_k_heads, grad_v_heads = attn_backward(
-        prefix, q_heads, k_heads, v_heads, jnp.transpose(grad_mixed, (1, 0, 2)), log_mass, scale
-    )
-    grad_proj = jnp.stack([grad_q_heads, grad_k_heads, grad_v_heads], axis=0)
-    grad_proj, result = lax.optimization_barrier((grad_proj, result))
+        prefix, q_heads, k_heads, v_heads, jnp.transpose(grad_mixed, (1, 0, 2)), log_mass, scale,
+        tp_count,
+    )
+    grad_q_heads, grad_k_heads, grad_v_heads, result = lax.optimization_barrier(
+        (grad_q_heads, grad_k_heads, grad_v_heads, result)
+    )
+    grad_kinds = (grad_q_heads, grad_k_heads, grad_v_heads)
     grad_qv_here = jnp.stack(
         [
-            jnp.sum(grad_q_heads.astype(jnp.float32), axis=1).reshape(-1),
-            jnp.sum(grad_v_heads.astype(jnp.float32), axis=1).reshape(-1),
+            jnp.sum(grad_q_heads.astype(jnp.float32), axis=(0, 2)).reshape(-1),
+            jnp.sum(grad_v_heads.astype(jnp.float32), axis=(0, 2)).reshape(-1),
         ],
         axis=0,
     )
     grad_qv_bias = lax.dynamic_update_slice_in_dim(
         jnp.zeros(qv_bias.shape, jnp.float32), grad_qv_here, tp_rank * cols_here, 1
     )
-    grad_qkv_w = jnp.einsum(
-        "rd,khre->kdhe", normed_all, grad_proj, preferred_element_type=jnp.float32
+    normed_groups = normed_all.reshape(tp_count, local_rows, -1)
+    grad_qkv_w = jnp.stack(
+        [
+            jnp.einsum("trd,thre->dhe", normed_groups, g, preferred_element_type=jnp.float32)
+            for g in grad_kinds
+        ]
     ).reshape(3, normed_all.shape[1], cols_here)
-    grad_proj_rows = lax.all_to_all(grad_proj, "tp", 2, 1, tiled=True)
-    grad_proj_rows, dense_summed = lax.optimization_barrier((grad_proj_rows, dense_summed))
-    grad_normed = jnp.einsum(
-        "kshre,skdhe->rd",
-        grad_proj_rows.reshape(3, tp_count, heads_here, local_rows, HD),
-        qkv_all.reshape(tp_count, 3, qkv_all.shape[2], heads_here, HD),
-        preferred_element_type=jnp.float32,
+    grad_rows_kinds = [lax.all_to_all(g, "tp", 0, 0, tiled=True) for g in grad_kinds]
+    grad_rows_kinds, dense_summed = lax.optimization_barrier((grad_rows_kinds, dense_summed))
+    qkv_split = qkv_all.reshape(tp_count, 3, qkv_all.shape[2], heads_here, HD)
+    grad_normed = sum(
+        jnp.einsum("shre,sdhe->rd", g, qkv_split[:, kind], preferred_element_type=jnp.float32)
+        for kind, g in enumerate(grad_rows_kinds)
     )
     dense_shards = []
     offset = 0

time: 570 us -> 693 us (1.22)
  waiting for transfers between devices: 130 us -> 254 us
  local copies, waits for them, and re-layouts: 122 us -> 106 us
  matrix products: 58 us -> 65.9 us
  starting transfers between devices: 15.8 us -> 23.1 us
    reduce_scatter x1, waiting for transfers between devices: 0.01 us -> 105 us  [on_device(): lax.psum_scatter(dense_packed.reshape(-1, grad_fc1.shape[1]), 'fsdp', sca...]
    optimization_barrier x1 -> x4, local copies, waits for them, and re-layouts: 31.8 us -> 5.89 us  [the longest x3 5.23 us: on_device(): lax.optimization_barrier((grad_q_heads, grad_k_heads, grad_v_heads, result))]
    unnamed x9 -> x10, waiting for transfers between devices: 0.81 us -> 15.5 us
    all_gather x1, waiting for transfers between devices: 18 us -> 28.7 us  [on_device(): lax.all_gather(grad_middle.astype(jnp.bfloat16), 'tp', axis=0, tiled=True)]
    all_to_all x2 -> x0, local copies, waits for them, and re-layouts: 9.57 us -> none  [the longest x1 9.5 us: on_device(): grad_proj_rows = lax.all_to_all(grad_proj, 'tp', 2, 1, tiled=True)]
    dot_general x3 -> x8, matrix products: 13.2 us -> 21.9 us  [the longest x3 9.57 us: on_device(): jnp.einsum('trd,thre->dhe', normed_groups, g, preferred_element_type=jnp....]
    all_to_all x1 -> x3, starting transfers between devices: 4.48 us -> 12.6 us  [on_device(): lax.all_to_all(g, 'tp', 0, 0, tiled=True)]
    all_to_all x1 -> x3, waiting for transfers between devices: 17.1 us -> 20.6 us  [on_device(): lax.all_to_all(g, 'tp', 0, 0, tiled=True)]
  transfers between devices with their start and end apart: 12 -> 14, of which waited for: 6 -> 8; matrix products, arithmetic and copies ran while one was open for 27% -> 17% of each run, Pallas kernels for 18% -> 15%
where the time goes in v9:
time: 693 us; the launch traced here: 683 us
  waiting for transfers between devices  254 us (37%)
  local copies, waits for them, and re-layouts  106 us (15%)
  Pallas kernels  103 us (15%)
  blocking collectives  91.7 us (13%)
  matrix products  65.9 us (10%)
  other arithmetic  24 us (3%)
  starting transfers between devices  23.1 us (3%)
  between operations  15.6 us (2%)
    reduce_scatter x1, waiting for transfers between devices, on_device(): lax.psum_scatter(dense_packed.reshape(-1, grad_fc1.shape[1]), 'fsdp', sca...  105 us
    pallas_call x1, Pallas kernels, attn_backward(): pl.pallas_call(functools.partial(_bwd_kernel, scale), out_shape=(shape, s...  64.6 us
    reduce_scatter x1, waiting for transfers between devices, on_device(): lax.psum_scatter(matmul_nt(grad_before, fc1_part), 'tp', scatter_dimensio...  42.9 us
    psum x1, blocking collectives, on_device(): lax.psum((grad_ln1_gain, grad_ln1_bias, grad_qv_bias, grad_out_bias, grad...  42.3 us
    pallas_call x1, Pallas kernels, attn_forward(): pl.pallas_call(functools.partial(_fwd_kernel, scale), out_shape=(jax.Shap...  38.6 us
    all_gather x1, blocking collectives, on_device(): qkv_cols = lax.all_gather(qkv_weight, 'fsdp', axis=1, tiled=True)  35.2 us
    all_gather x1, waiting for transfers between devices, on_device(): lax.all_gather(grad_middle.astype(jnp.bfloat16), 'tp', axis=0, tiled=True)  28.7 us
    all_gather x1, waiting for transfers between devices, on_device(): normed_rows = lax.all_gather(normed_two, 'tp', axis=0, tiled=True)  27.8 us
  transfers between devices with their start and end apart: 14, of which 8 were waited for; matrix products, arithmetic and copies ran while one was open for 17% of the time, Pallas kernels for 15%

profile of v9, /device:TPU:0, one launch (start us, length us, event | category | flops | bytes accessed | tf_op | source)
XLA Modules:
  0.0 683.4 jit_solution(14387724639919658607)
XLA Ops:
  13.3 35.2 %all_gather.24 = bf16[3,768,192]{2,1,0:T(8,128)(2,1)S(1)} all-gather(bf16[3,96,192]{2,1,0:T(8,128)(2,1)S(1)} %copy-done.30), channel_id=1, replica_groups=mesh['fsdp'=8,'tp'=4] {'fsdp'}, dimensions={1}, use_global_device_ids=true | all-gather | bytes 995328 | tf_op jit(solution)/shard_map/all_gather | solution.py:205
  52.8 4.7 all-to-all-start
  59.2 4.7 convolution_bitcast_fusion
  76.3 4.8 fusion.14
  81.2 38.6 %shard_map.280 = (bf16[4,3,512,64]{3,2,1,0:T(8,128)(2,1)S(1)}, f32[3,2048,1]{2,1,0:T(8,128)}) custom-call(s32[1]{0:T(128)S(6)} %copy.141.prefix_ref, bf16[3,2048,64]{2,1,0:T(8,128)(2,1)S(1)} %get-tuple-element.157.q_ref, bf16[3,2048,64]{2,1,0:T(8,128)(2,1)S(1)} %bitcast.135, bf16[3,2048,64]{2,1,0:T(8,128)(2,1)} %get-tuple-element.158.v_ref), custom_call_target="tpu_custom_call" | custom-call | flops 3221225472 | bytes 3145728 | tf_op jit(solution)/shard_map/pallas_call | solution.py:130
  139.8 13.3 %all-gather.12.cloned.1.call-done = bf16[768,768]{1,0:T(8,128)(2,1)} async-done(((bf16[192,768]{1,0:T(8,128)(2,1)}), bf16[768,768]{1,0:T(8,128)(2,1)}) %all-gather.12.cloned.1.call-update) | async-done | bytes 1179664 | tf_op jit(solution)/shard_map/all_gather | solution.py:241
  153.8 14.2 %all_to_all.30 = bf16[4,3,512,64]{2,3,1,0:T(8,128)(2,1)S(1)} all-to-all(bf16[4,3,512,64]{2,3,1,0:T(8,128)(2,1)S(1)} %copy.76), channel_id=1, replica_groups=mesh['fsdp'=8,'tp'=4] {'tp'}, dimensions={0} | all-to-all | bytes 1572864 | tf_op jit(solution)/shard_map/all_to_all | solution.py:245
  173.0 27.8 %all-gather.14.cloned.1.call-done = bf16[2048,768]{1,0:T(8,128)(2,1)} async-done(((bf16[512,768]{1,0:T(8,128)(2,1)}), bf16[2048,768]{1,0:T(8,128)(2,1)}) %all-gather.14.cloned.1.call-update) | async-done | bytes 3145744 | tf_op jit(solution)/shard_map/all_gather | solution.py:260
  200.8 5.1 fusion.43
  205.9 7.8 %convert_reduce_fusion = (f32[768]{0:T(1024)S(1)}, bf16[2048,768]{1,0:T(8,128)(2,1)S(1)}, bf16[2048,768]{1,0:T(8,128)(2,1)}) fusion(f32[2048,768]{1,0:T(8,128)S(1)} %fusion.43, f32[768]{0:T(1024)S(1)} %dynamic_slice.7, bf16[2048,768]{1,0:T(8,128)(2,1)S(1)} %copy-done.38, bf16[768,768]{0,1:T(8,128)(2,1)S(1)} %bitcast.153), kind=kOutput, calls=%fused_computation.9 | convolution fusion | flops 2455239936 | bytes 16914432 | tf_op jit(solution)/shard_map/dot_general | solution.py:37
  220.5 6.7 convolution_convert_fusion
  236.1 42.9 %reduce-scatter.6.cloned.1.call-done = f32[512,768]{1,0:T(8,128)} async-done(((f32[2048,768]{1,0:T(8,128)}), f32[512,768]{1,0:T(8,128)}) %reduce-scatter.6.cloned.1.call-update) | async-done | bytes 1572880 | tf_op jit(solution)/shard_map/reduce_scatter | solution.py:274
  284.3 28.7 %all-gather.16.cloned.1.call-done = bf16[2048,768]{1,0:T(8,128)(2,1)} async-done(((bf16[512,768]{1,0:T(8,128)(2,1)}), bf16[2048,768]{1,0:T(8,128)(2,1)}) %all-gather.16.cloned.1.call-update) | async-done | bytes 3145744 | tf_op jit(solution)/shard_map/all_gather | solution.py:286
  313.0 4.7 all-to-all-start.2
  317.9 4.7 copy.94
  349.0 64.6 %shard_map.281 = (bf16[4,3,512,64]{3,2,1,0:T(8,128)(2,1)S(1)}, bf16[4,3,512,64]{3,2,1,0:T(8,128)(2,1)S(1)}, bf16[4,3,512,64]{3,2,1,0:T(8,128)(2,1)S(1)}) custom-call(s32[1]{0:T(128)S(6)} %copy.141.prefix_ref, bf16[3,2048,64]{2,1,0:T(8,128)(2,1)} %copy-done.4, bf16[3,2048,64]{2,1,0:T(8,128)(2,1)} %bitcast.136, bf16[3,2048,64]{2,1,0:T(8,128)(2,1)} %get-tuple-element.158.v_ref, ...), custom_call_target="tpu_custom_call" | custom-call | flops 8053063680 | bytes 6291456 | tf_op jit(solution)/shard_map/pallas_call | solution.py:158
  439.1 4.6 reshape.203
  443.9 5.1 pad_maximum_fusion
  449.0 5.6 reshape.188
  462.7 10.3 %all-to-all-done.4 = bf16[4,3,512,64]{2,3,1,0:T(8,128)(2,1)} async-done(((bf16[4,3,512,64]{2,3,1,0:T(8,128)(2,1)}), bf16[4,3,512,64]{2,3,1,0:T(8,128)(2,1)}, u32[]{:S(2)}, u32[]{:S(2)}) %all-to-all-start.4) | async-done | bytes 786464 | tf_op jit(solution)/shard_map/all_to_all | solution.py:336
  478.5 10.3 %all-to-all-done.3 = bf16[4,3,512,64]{2,3,1,0:T(8,128)(2,1)} async-done(((bf16[4,3,512,64]{2,3,1,0:T(8,128)(2,1)}), bf16[4,3,512,64]{2,3,1,0:T(8,128)(2,1)}, u32[]{:S(2)}, u32[]{:S(2)}) %all-to-all-start.3) | async-done | bytes 786464 | tf_op jit(solution)/shard_map/all_to_all | solution.py:336
  498.2 14.7 %reduce-scatter.10.cloned.1.call-done = f32[96,576]{1,0:T(8,128)} async-done(((f32[768,576]{1,0:T(8,128)}), f32[96,576]{1,0:T(8,128)}) %reduce-scatter.10.cloned.1.call-update) | async-done | bytes 221200
  514.8 105.0 %reduce-scatter.8.cloned.1.call-done = f32[216,768]{1,0:T(8,128)} async-done(((f32[1728,768]{1,0:T(8,128)}), f32[216,768]{1,0:T(8,128)}) %reduce-scatter.8.cloned.1.call-update) | async-done | bytes 663568 | tf_op jit(solution)/shard_map/reduce_scatter | solution.py:305
  634.1 42.3 %all-reduce = (f32[768]{0:T(1024)}, f32[768]{0:T(1024)}, f32[2,768]{1,0:T(2,128)}, f32[768]{0:T(1024)}, f32[768]{0:T(1024)}, /*index=5*/f32[768]{0:T(1024)}, f32[3072]{0:T(1024)}, f32[768]{0:T(1024)}, f32[5,768]{1,0:T(8,128)}) all-reduce(f32[768]{0:T(1024)S(1)} %get-tuple-element.120, ...), channel_id=1, replica_groups=mesh['fsdp'=8,'tp'=4] {'fsdp','tp'}, use_global_device_ids=true, to_apply=%region_13.0 | all-reduce | flops 13056 | bytes 104448 | tf_op jit(solution)/shard_map/psum | solution.py:362
  (211 shorter events, 161.4 us)
Async XLA Ops:
  7.2 42.0 %all-gather.8.cloned.1.call-start = ((), (), s32[]{:S(2)}) async-start(), calls=%async_computation.9 | async-start | bytes 3932160 | tf_op jit(solution)/shard_map/all_gather | solution.py:214
  12.4 108.5 %all-gather.18.cloned.1.call-start = ((), (), s32[]{:S(2)}) async-start(), calls=%async_computation.16 | async-start | bytes 2985984 | tf_op jit(solution)/shard_map/all_gather | solution.py:219
  49.2 90.6 %all-gather.10.cloned.1.call-start = ((), (), s32[]{:S(2)}) async-start(), calls=%async_computation.10 | async-start | bytes 3932160 | tf_op jit(solution)/shard_map/all_gather | solution.py:222
  52.8 68.2 %all-to-all-start = ((bf16[4,3,768,192]{2,3,1,0:T(8,128)(2,1)}), bf16[4,3,768,192]{2,3,1,0:T(8,128)(2,1)}, u32[]{:S(2)}, u32[]{:S(2)}) async-start(bf16[4,3,768,192]{2,3,1,0:T(8,128)(2,1)} %broadcast_in_dim.6), calls=%async_computation | async-start | bytes 7077888 | tf_op jit(solution)/shard_map/all_to_all | solution.py:221
  57.5 95.6 %all-gather.12.cloned.1.call-start = ((), (), s32[]{:S(2)}) async-start(), calls=%async_computation.11 | async-start | bytes 1474560 | tf_op jit(solution)/shard_map/all_gather | solution.py:241
  66.9 14.3 %copy-start.3 = (bf16[2048,3,64]{2,0,1:T(8,128)(2,1)}, bf16[2048,3,64]{2,0,1:T(8,128)(2,1)S(1)}, u32[]{:S(2)}) copy-start(bf16[2048,3,64]{2,0,1:T(8,128)(2,1)S(1)} %copy.71) | copy-start | bytes 2359300
  128.0 72.7 %all-gather.14.cloned.1.call-start = ((), (), s32[]{:S(2)}) async-start(), calls=%async_computation.12 | async-start | bytes 3932160 | tf_op jit(solution)/shard_map/all_gather | solution.py:260
  153.1 14.9 %copy-start.41 = (f32[768]{0:T(1024)S(1)}, f32[768]{0:T(1024)}, u32[]{:S(2)}) copy-start(f32[768]{0:T(1024)} %param.28) | copy-start | bytes 9220
  153.8 14.2 %copy-start.8 = (f32[512,768]{1,0:T(8,128)S(1)}, f32[512,768]{1,0:T(8,128)}, u32[]{:S(2)}) copy-start(f32[512,768]{1,0:T(8,128)} %copy-done.7) | copy-start | bytes 4718596
  170.1 111.2 %copy-start.5 = (f32[512,768]{1,0:T(8,128)}, f32[512,768]{1,0:T(8,128)S(1)}, u32[]{:S(2)}) copy-start(f32[512,768]{1,0:T(8,128)S(1)} %get-tuple-element.155) | copy-start | bytes 4718596
  172.1 106.9 %reduce-scatter.6.cloned.1.call-start = ((), (), s32[]{:S(2)}) async-start(), calls=%async_computation.13 | async-start | bytes 7864320 | tf_op jit(solution)/shard_map/reduce_scatter | solution.py:274
  205.9 9.6 %copy-start.22 = (bf16[768,768]{1,0:T(8,128)(2,1)S(1)}, bf16[768,768]{1,0:T(8,128)(2,1)}, u32[]{:S(2)}) copy-start(bf16[768,768]{1,0:T(8,128)(2,1)} %reshape_reshape.7) | copy-start | bytes 3538948
  220.0 93.0 %all-gather.16.cloned.1.call-start = ((), (), s32[]{:S(2)}) async-start(), calls=%async_computation.14 | async-start | bytes 3932160 | tf_op jit(solution)/shard_map/all_gather | solution.py:286
  220.5 6.7 copy-start.39
  220.5 6.7 copy-start.44
  313.0 101.7 %all-to-all-start.2 = ((bf16[4,512,768]{2,1,0:T(8,128)(2,1)}), bf16[4,512,768]{2,1,0:T(8,128)(2,1)}, u32[]{:S(2)}, u32[]{:S(2)}) async-start(bf16[4,512,768]{2,1,0:T(8,128)(2,1)} %bitcast.143), calls=%async_computation.3 | async-start | bytes 6291456 | tf_op jit(solution)/shard_map/all_to_all | solution.py:288
  317.7 195.2 %reduce-scatter.10.cloned.1.call-start = ((), (), s32[]{:S(2)}) async-start(), calls=%async_computation.17 | async-start | bytes 2211840
  335.0 6.6 copy-start.17
  443.8 175.9 %reduce-scatter.8.cloned.1.call-start = ((), (), s32[]{:S(2)}) async-start(), calls=%async_computation.15 | async-start | bytes 5971968 | tf_op jit(solution)/shard_map/reduce_scatter | solution.py:305
  457.1 15.9 %all-to-all-start.4 = ((bf16[4,3,512,64]{2,3,1,0:T(8,128)(2,1)}), bf16[4,3,512,64]{2,3,1,0:T(8,128)(2,1)}, u32[]{:S(2)}, u32[]{:S(2)}) async-start(bf16[4,3,512,64]{2,3,1,0:T(8,128)(2,1)} %copy.81), calls=%async_computation.5 | async-start | bytes 1572864 | tf_op jit(solution)/shard_map/all_to_all | solution.py:336
  472.9 15.9 %all-to-all-start.3 = ((bf16[4,3,512,64]{2,3,1,0:T(8,128)(2,1)}), bf16[4,3,512,64]{2,3,1,0:T(8,128)(2,1)}, u32[]{:S(2)}, u32[]{:S(2)}) async-start(bf16[4,3,512,64]{2,3,1,0:T(8,128)(2,1)} %copy.80), calls=%async_computation.4 | async-start | bytes 1572864 | tf_op jit(solution)/shard_map/all_to_all | solution.py:336
  488.8 132.7 %all-to-all-start.5 = ((bf16[4,3,512,64]{2,3,1,0:T(8,128)(2,1)}), bf16[4,3,512,64]{2,3,1,0:T(8,128)(2,1)}, u32[]{:S(2)}, u32[]{:S(2)}) async-start(bf16[4,3,512,64]{2,3,1,0:T(8,128)(2,1)} %copy.82), calls=%async_computation.6 | async-start | bytes 1572864 | tf_op jit(solution)/shard_map/all_to_all | solution.py:336
  632.7 43.7 %copy-start.1 = (f32[5,768]{1,0:T(8,128)S(1)}, f32[5,768]{1,0:T(8,128)}, u32[]{:S(2)}) copy-start(f32[5,768]{1,0:T(8,128)} %param.33) | copy-start | bytes 46084
  633.4 43.1 %copy-start.12 = (f32[512,768]{1,0:T(8,128)}, f32[512,768]{1,0:T(8,128)S(1)}, u32[]{:S(2)}) copy-start(f32[512,768]{1,0:T(8,128)S(1)} %multiply_add_fusion) | copy-start | bytes 4718596
  (35 other events, 90.1 us)
Sparse Core Ops, SparseCore 0:
  12.6 31.2 all-gather.7
  49.4 55.5 all-gather.17
  106.5 27.0 all-gather.9
  135.6 17.4 all-gather.11
  172.2 28.4 all-gather.13
  220.1 58.8 reduce-scatter.5
  284.5 28.4 all-gather.15
  443.9 68.9 reduce-scatter.9
  516.5 103.2 reduce-scatter.7

commit v10 on v9

--- a/solution.py
+++ b/solution.py
@@ -312,8 +312,8 @@
         prefix, q_heads, k_heads, v_heads, jnp.transpose(grad_mixed, (1, 0, 2)), log_mass, scale,
         tp_count,
     )
-    grad_q_heads, grad_k_heads, grad_v_heads, result = lax.optimization_barrier(
-        (grad_q_heads, grad_k_heads, grad_v_heads, result)
+    grad_q_heads, grad_k_heads, grad_v_heads, result, dense_summed = lax.optimization_barrier(
+        (grad_q_heads, grad_k_heads, grad_v_heads, result, dense_summed)
     )
     grad_kinds = (grad_q_heads, grad_k_heads, grad_v_heads)
     grad_qv_here = jnp.stack(
@@ -334,7 +334,6 @@
         ]
     ).reshape(3, normed_all.shape[1], cols_here)
     grad_rows_kinds = [lax.all_to_all(g, "tp", 0, 0, tiled=True) for g in grad_kinds]
-    grad_rows_kinds, dense_summed = lax.optimization_barrier((grad_rows_kinds, dense_summed))
     qkv_split = qkv_all.reshape(tp_count, 3, qkv_all.shape[2], heads_here, HD)
     grad_normed = sum(
         jnp.einsum("shre,sdhe->rd", g, qkv_split[:, kind], preferred_element_type=jnp.float32)

time: 693 us -> 579 us (0.84)
  waiting for transfers between devices: 254 us -> 134 us
    reduce_scatter x1, waiting for transfers between devices: 105 us -> 22.1 us  [on_device(): lax.psum_scatter(dense_packed.reshape(-1, grad_fc1.shape[1]), 'fsdp', sca...]
    unnamed x10, waiting for transfers between devices: 15.5 us -> 0.81 us
    all_gather x1, waiting for transfers between devices: 28.7 us -> 15.8 us  [on_device(): lax.all_gather(grad_middle.astype(jnp.bfloat16), 'tp', axis=0, tiled=True)]
    all_to_all x3, waiting for transfers between devices: 20.6 us -> 11.9 us  [on_device(): lax.all_to_all(g, 'tp', 0, 0, tiled=True)]
    unnamed x98 -> x102, local copies, waits for them, and re-layouts: 25.3 us -> 25.9 us
  transfers between devices with their start and end apart: 14 -> 14, of which waited for: 8 -> 7; matrix products, arithmetic and copies ran while one was open for 17% -> 21% of each run, Pallas kernels for 15% -> 18%
where the time goes in v10:
time: 579 us; the launch traced here: 569 us
  waiting for transfers between devices  134 us (23%)
  local copies, waits for them, and re-layouts  107 us (18%)
  Pallas kernels  103 us (18%)
  blocking collectives  91.1 us (16%)
  matrix products  69.6 us (12%)
  other arithmetic  25.5 us (4%)
  starting transfers between devices  23.3 us (4%)
  between operations  15.6 us (3%)
    pallas_call x1, Pallas kernels, attn_backward(): pl.pallas_call(functools.partial(_bwd_kernel, scale), out_shape=(shape, s...  64.6 us
    reduce_scatter x1, waiting for transfers between devices, on_device(): lax.psum_scatter(matmul_nt(grad_before, fc1_part), 'tp', scatter_dimensio...  43.1 us
    psum x1, blocking collectives, on_device(): lax.psum((grad_ln1_gain, grad_ln1_bias, grad_qv_bias, grad_out_bias, grad...  41.8 us
    pallas_call x1, Pallas kernels, attn_forward(): pl.pallas_call(functools.partial(_fwd_kernel, scale), out_shape=(jax.Shap...  38.6 us
    all_gather x1, blocking collectives, on_device(): qkv_cols = lax.all_gather(qkv_weight, 'fsdp', axis=1, tiled=True)  35.2 us
    all_gather x1, waiting for transfers between devices, on_device(): normed_rows = lax.all_gather(normed_two, 'tp', axis=0, tiled=True)  27.8 us
    unnamed x102, local copies, waits for them, and re-layouts  25.9 us
    reduce_scatter x1, waiting for transfers between devices, on_device(): lax.psum_scatter(dense_packed.reshape(-1, grad_fc1.shape[1]), 'fsdp', sca...  22.1 us
  transfers between devices with their start and end apart: 14, of which 7 were waited for; matrix products, arithmetic and copies ran while one was open for 21% of the time, Pallas kernels for 18%

profile of v10, /device:TPU:0, one launch (start us, length us, event | category | flops | bytes accessed | tf_op | source)
XLA Modules:
  0.0 569.3 jit_solution(2955361480396625294)
XLA Ops:
  13.3 35.2 %all_gather.24 = bf16[3,768,192]{2,1,0:T(8,128)(2,1)S(1)} all-gather(bf16[3,96,192]{2,1,0:T(8,128)(2,1)S(1)} %copy-done.32), channel_id=1, replica_groups=mesh['fsdp'=8,'tp'=4] {'fsdp'}, dimensions={1}, use_global_device_ids=true | all-gather | bytes 995328 | tf_op jit(solution)/shard_map/all_gather | solution.py:205
  52.9 4.7 all-to-all-start
  59.3 4.7 convolution_bitcast_fusion
  76.7 4.8 fusion.14
  81.5 38.6 %shard_map.280 = (bf16[4,3,512,64]{3,2,1,0:T(8,128)(2,1)S(1)}, f32[3,2048,1]{2,1,0:T(8,128)}) custom-call(s32[1]{0:T(128)S(6)} %copy.141.prefix_ref, bf16[3,2048,64]{2,1,0:T(8,128)(2,1)S(1)} %get-tuple-element.151.q_ref, bf16[3,2048,64]{2,1,0:T(8,128)(2,1)S(1)} %bitcast.135, bf16[3,2048,64]{2,1,0:T(8,128)(2,1)} %get-tuple-element.152.v_ref), custom_call_target="tpu_custom_call" | custom-call | flops 3221225472 | bytes 3145728 | tf_op jit(solution)/shard_map/pallas_call | solution.py:130
  140.2 12.9 %all-gather.12.cloned.1.call-done = bf16[768,768]{1,0:T(8,128)(2,1)} async-done(((bf16[192,768]{1,0:T(8,128)(2,1)}), bf16[768,768]{1,0:T(8,128)(2,1)}) %all-gather.12.cloned.1.call-update) | async-done | bytes 1179664 | tf_op jit(solution)/shard_map/all_gather | solution.py:241
  153.8 14.2 %all_to_all.30 = bf16[4,3,512,64]{2,3,1,0:T(8,128)(2,1)S(1)} all-to-all(bf16[4,3,512,64]{2,3,1,0:T(8,128)(2,1)S(1)} %copy.76), channel_id=1, replica_groups=mesh['fsdp'=8,'tp'=4] {'tp'}, dimensions={0} | all-to-all | bytes 1572864 | tf_op jit(solution)/shard_map/all_to_all | solution.py:245
  173.0 27.8 %all-gather.14.cloned.1.call-done = bf16[2048,768]{1,0:T(8,128)(2,1)} async-done(((bf16[512,768]{1,0:T(8,128)(2,1)}), bf16[2048,768]{1,0:T(8,128)(2,1)}) %all-gather.14.cloned.1.call-update) | async-done | bytes 3145744 | tf_op jit(solution)/shard_map/all_gather | solution.py:260
  200.8 5.1 fusion.43
  205.9 7.8 %convert_reduce_fusion = (f32[768]{0:T(1024)S(1)}, bf16[2048,768]{1,0:T(8,128)(2,1)S(1)}, bf16[2048,768]{1,0:T(8,128)(2,1)}) fusion(f32[2048,768]{1,0:T(8,128)S(1)} %fusion.43, f32[768]{0:T(1024)S(1)} %dynamic_slice.7, bf16[2048,768]{1,0:T(8,128)(2,1)S(1)} %copy-done.40, bf16[768,768]{0,1:T(8,128)(2,1)S(1)} %bitcast.153), kind=kOutput, calls=%fused_computation.9 | convolution fusion | flops 2455239936 | bytes 16914432 | tf_op jit(solution)/shard_map/dot_general | solution.py:37
  215.3 4.5 fusion.44
  220.3 6.7 %convolution_convert_fusion = bf16[2048,768]{1,0:T(8,128)(2,1)} fusion(bf16[2048,768]{1,0:T(8,128)(2,1)} %get-tuple-element.137, bf16[768,768]{0,1:T(8,128)(2,1)} %bitcast.152), kind=kOutput, calls=%fused_computation.13 | convolution fusion | flops 2417491968 | bytes 7471104 | tf_op jit(solution)/shard_map/dot_general | solution.py:263
  235.7 43.1 %reduce-scatter.6.cloned.1.call-done = f32[512,768]{1,0:T(8,128)} async-done(((f32[2048,768]{1,0:T(8,128)}), f32[512,768]{1,0:T(8,128)}) %reduce-scatter.6.cloned.1.call-update) | async-done | bytes 1572880 | tf_op jit(solution)/shard_map/reduce_scatter | solution.py:274
  296.9 15.8 %all-gather.16.cloned.1.call-done = bf16[2048,768]{1,0:T(8,128)(2,1)} async-done(((bf16[512,768]{1,0:T(8,128)(2,1)}), bf16[2048,768]{1,0:T(8,128)(2,1)}) %all-gather.16.cloned.1.call-update) | async-done | bytes 3145744 | tf_op jit(solution)/shard_map/all_gather | solution.py:286
  312.7 4.8 copy.81
  323.2 4.8 pad_maximum_fusion
  328.0 5.7 reshape.188
  333.7 5.2 all-to-all-start.2
  346.3 64.6 %shard_map.281 = (bf16[4,3,512,64]{3,2,1,0:T(8,128)(2,1)S(1)}, bf16[4,3,512,64]{3,2,1,0:T(8,128)(2,1)S(1)}, bf16[4,3,512,64]{3,2,1,0:T(8,128)(2,1)S(1)}) custom-call(s32[1]{0:T(128)S(6)} %copy.141.prefix_ref, bf16[3,2048,64]{2,1,0:T(8,128)(2,1)} %copy-done.4, bf16[3,2048,64]{2,1,0:T(8,128)(2,1)} %bitcast.136, bf16[3,2048,64]{2,1,0:T(8,128)(2,1)} %get-tuple-element.152.v_ref, ...), custom_call_target="tpu_custom_call" | custom-call | flops 8053063680 | bytes 6291456 | tf_op jit(solution)/shard_map/pallas_call | solution.py:158
  416.3 22.1 %reduce-scatter.8.cloned.1.call-done = f32[216,768]{1,0:T(8,128)} async-done(((f32[1728,768]{1,0:T(8,128)}), f32[216,768]{1,0:T(8,128)}) %reduce-scatter.8.cloned.1.call-update) | async-done | bytes 663568 | tf_op jit(solution)/shard_map/reduce_scatter | solution.py:305
  470.2 4.7 reshape.203
  490.8 6.7 %all-to-all-done.3 = bf16[4,3,512,64]{2,3,1,0:T(8,128)(2,1)S(1)} async-done(((bf16[4,3,512,64]{2,3,1,0:T(8,128)(2,1)}), bf16[4,3,512,64]{2,3,1,0:T(8,128)(2,1)S(1)}, u32[]{:S(2)}, u32[]{:S(2)}) %all-to-all-start.3) | async-done | bytes 786464 | tf_op jit(solution)/shard_map/all_to_all | solution.py:336
  508.3 5.2 all-to-all-done.5
  518.6 41.8 %all-reduce = (f32[768]{0:T(1024)}, f32[768]{0:T(1024)}, f32[2,768]{1,0:T(2,128)}, f32[768]{0:T(1024)}, f32[768]{0:T(1024)}, /*index=5*/f32[768]{0:T(1024)}, f32[3072]{0:T(1024)}, f32[768]{0:T(1024)}, f32[5,768]{1,0:T(8,128)}) all-reduce(f32[768]{0:T(1024)S(1)} %get-tuple-element.114, ...), channel_id=1, replica_groups=mesh['fsdp'=8,'tp'=4] {'fsdp','tp'}, use_global_device_ids=true, to_apply=%region_13.0 | all-reduce | flops 13056 | bytes 104448 | tf_op jit(solution)/shard_map/psum | solution.py:361
  (215 shorter events, 162.5 us)
Async XLA Ops:
  7.2 42.0 %all-gather.8.cloned.1.call-start = ((), (), s32[]{:S(2)}) async-start(), calls=%async_computation.9 | async-start | bytes 3932160 | tf_op jit(solution)/shard_map/all_gather | solution.py:214
  12.4 108.8 %all-gather.18.cloned.1.call-start = ((), (), s32[]{:S(2)}) async-start(), calls=%async_computation.16 | async-start | bytes 2985984 | tf_op jit(solution)/shard_map/all_gather | solution.py:219
  49.3 91.0 %all-gather.10.cloned.1.call-start = ((), (), s32[]{:S(2)}) async-start(), calls=%async_computation.10 | async-start | bytes 3932160 | tf_op jit(solution)/shard_map/all_gather | solution.py:222
  52.9 68.4 %all-to-all-start = ((bf16[4,3,768,192]{2,3,1,0:T(8,128)(2,1)}), bf16[4,3,768,192]{2,3,1,0:T(8,128)(2,1)}, u32[]{:S(2)}, u32[]{:S(2)}) async-start(bf16[4,3,768,192]{2,3,1,0:T(8,128)(2,1)} %broadcast_in_dim.6), calls=%async_computation | async-start | bytes 7077888 | tf_op jit(solution)/shard_map/all_to_all | solution.py:221
  57.6 95.5 %all-gather.12.cloned.1.call-start = ((), (), s32[]{:S(2)}) async-start(), calls=%async_computation.11 | async-start | bytes 1474560 | tf_op jit(solution)/shard_map/all_gather | solution.py:241
  67.1 14.4 %copy-start.3 = (bf16[2048,3,64]{2,0,1:T(8,128)(2,1)}, bf16[2048,3,64]{2,0,1:T(8,128)(2,1)S(1)}, u32[]{:S(2)}) copy-start(bf16[2048,3,64]{2,0,1:T(8,128)(2,1)S(1)} %copy.71) | copy-start | bytes 2359300
  128.4 72.4 %all-gather.14.cloned.1.call-start = ((), (), s32[]{:S(2)}) async-start(), calls=%async_computation.12 | async-start | bytes 3932160 | tf_op jit(solution)/shard_map/all_gather | solution.py:260
  153.1 14.9 %copy-start.43 = (f32[768]{0:T(1024)S(1)}, f32[768]{0:T(1024)}, u32[]{:S(2)}) copy-start(f32[768]{0:T(1024)} %param.28) | copy-start | bytes 9220
  153.8 14.2 %copy-start.8 = (f32[512,768]{1,0:T(8,128)S(1)}, f32[512,768]{1,0:T(8,128)}, u32[]{:S(2)}) copy-start(f32[512,768]{1,0:T(8,128)} %copy-done.7) | copy-start | bytes 4718596
  170.1 111.0 %copy-start.5 = (f32[512,768]{1,0:T(8,128)}, f32[512,768]{1,0:T(8,128)S(1)}, u32[]{:S(2)}) copy-start(f32[512,768]{1,0:T(8,128)S(1)} %get-tuple-element.149) | copy-start | bytes 4718596
  172.1 106.7 %reduce-scatter.6.cloned.1.call-start = ((), (), s32[]{:S(2)}) async-start(), calls=%async_computation.13 | async-start | bytes 7864320 | tf_op jit(solution)/shard_map/reduce_scatter | solution.py:274
  205.9 9.5 %copy-start.24 = (bf16[768,768]{1,0:T(8,128)(2,1)S(1)}, bf16[768,768]{1,0:T(8,128)(2,1)}, u32[]{:S(2)}) copy-start(bf16[768,768]{1,0:T(8,128)(2,1)} %reshape_reshape.7) | copy-start | bytes 3538948
  219.8 92.9 %all-gather.16.cloned.1.call-start = ((), (), s32[]{:S(2)}) async-start(), calls=%async_computation.14 | async-start | bytes 3932160 | tf_op jit(solution)/shard_map/all_gather | solution.py:286
  284.0 154.3 %reduce-scatter.8.cloned.1.call-start = ((), (), s32[]{:S(2)}) async-start(), calls=%async_computation.15 | async-start | bytes 5971968 | tf_op jit(solution)/shard_map/reduce_scatter | solution.py:305
  333.7 78.4 %all-to-all-start.2 = ((bf16[4,512,768]{2,1,0:T(8,128)(2,1)}), bf16[4,512,768]{2,1,0:T(8,128)(2,1)}, u32[]{:S(2)}, u32[]{:S(2)}) async-start(bf16[4,512,768]{2,1,0:T(8,128)(2,1)} %bitcast.143), calls=%async_computation.3 | async-start | bytes 6291456 | tf_op jit(solution)/shard_map/all_to_all | solution.py:288
  458.9 23.2 %all-to-all-start.4 = ((bf16[4,3,512,64]{2,3,1,0:T(8,128)(2,1)}), bf16[4,3,512,64]{2,3,1,0:T(8,128)(2,1)}, u32[]{:S(2)}, u32[]{:S(2)}) async-start(bf16[4,3,512,64]{2,3,1,0:T(8,128)(2,1)} %copy.88), calls=%async_computation.6 | async-start | bytes 1572864 | tf_op jit(solution)/shard_map/all_to_all | solution.py:336
  463.2 97.2 %reduce-scatter.10.cloned.1.call-start = ((), (), s32[]{:S(2)}) async-start(), calls=%async_computation.17 | async-start | bytes 2211840
  482.1 15.5 %all-to-all-start.3 = ((bf16[4,3,512,64]{2,3,1,0:T(8,128)(2,1)}), bf16[4,3,512,64]{2,3,1,0:T(8,128)(2,1)S(1)}, u32[]{:S(2)}, u32[]{:S(2)}) async-start(bf16[4,3,512,64]{2,3,1,0:T(8,128)(2,1)} %copy.85), calls=%async_computation.5 | async-start | bytes 1572864 | tf_op jit(solution)/shard_map/all_to_all | solution.py:336
  489.0 12.8 %copy-start.23 = (bf16[4,1,768,3,64]{2,4,3,1,0:T(8,128)(2,1)S(1)}, bf16[4,1,768,3,64]{2,4,3,1,0:T(8,128)(2,1)}, u32[]{:S(2)}) copy-start(bf16[4,1,768,3,64]{2,4,3,1,0:T(8,128)(2,1)} %get-tuple-element.141) | copy-start | bytes 3538948
  497.6 15.9 %all-to-all-start.5 = ((bf16[4,3,512,64]{2,3,1,0:T(8,128)(2,1)}), bf16[4,3,512,64]{2,3,1,0:T(8,128)(2,1)}, u32[]{:S(2)}, u32[]{:S(2)}) async-start(bf16[4,3,512,64]{2,3,1,0:T(8,128)(2,1)} %copy.91), calls=%async_computation.7 | async-start | bytes 1572864 | tf_op jit(solution)/shard_map/all_to_all | solution.py:336
  505.1 8.4 %copy-start.9 = (f32[512,768]{1,0:T(8,128)S(1)}, f32[512,768]{1,0:T(8,128)}, u32[]{:S(2)}) copy-start(f32[512,768]{1,0:T(8,128)} %copy-done.7) | copy-start | bytes 4718596
  505.1 8.4 %copy-start.21 = (bf16[4,1,768,3,64]{2,4,3,1,0:T(8,128)(2,1)S(1)}, bf16[4,1,768,3,64]{2,4,3,1,0:T(8,128)(2,1)}, u32[]{:S(2)}) copy-start(bf16[4,1,768,3,64]{2,4,3,1,0:T(8,128)(2,1)} %get-tuple-element.140) | copy-start | bytes 3538948
  517.2 45.1 %copy-start.1 = (f32[5,768]{1,0:T(8,128)S(1)}, f32[5,768]{1,0:T(8,128)}, u32[]{:S(2)}) copy-start(f32[5,768]{1,0:T(8,128)} %param.33) | copy-start | bytes 46084
  517.9 44.4 %copy-start.13 = (f32[512,768]{1,0:T(8,128)}, f32[512,768]{1,0:T(8,128)S(1)}, u32[]{:S(2)}) copy-start(f32[512,768]{1,0:T(8,128)S(1)} %multiply_add_fusion) | copy-start | bytes 4718596
  (37 other events, 118.3 us)
Sparse Core Ops, SparseCore 0:
  12.6 31.2 all-gather.7
  49.4 55.5 all-gather.17
  106.5 27.0 all-gather.9
  135.6 17.4 all-gather.11
  172.2 28.4 all-gather.13
  219.9 58.8 reduce-scatter.5
  284.1 28.4 all-gather.15
  333.8 104.5 reduce-scatter.7
  475.0 67.7 reduce-scatter.9

commit v11 on v10

--- a/solution.py
+++ b/solution.py
@@ -272,8 +272,8 @@
     grad_fc1 = matmul_tn(normed_rows, grad_before)
     grad_fc2 = matmul_tn(hidden, grad_rows)
     grad_normed_two = lax.psum_scatter(
-        matmul_nt(grad_before, fc1_part), "tp", scatter_dimension=0, tiled=True
-    )
+        matmul_nt(grad_before, fc1_part).astype(jnp.bfloat16), "tp", scatter_dimension=0, tiled=True
+    ).astype(jnp.float32)
     grad_normed_two, fc2_partial, grad_fc1, grad_fc2 = lax.optimization_barrier(
         (grad_normed_two, fc2_partial, grad_fc1, grad_fc2)
     )
@@ -303,8 +303,11 @@
     )
     dense_packed = jnp.concatenate([g.reshape(fsdp_count, -1) for g in dense_grads], axis=1)
     dense_summed = lax.psum_scatter(
-        dense_packed.reshape(-1, grad_fc1.shape[1]), "fsdp", scatter_dimension=0, tiled=True
-    ).reshape(1, -1)
+        dense_packed.reshape(-1, grad_fc1.shape[1]).astype(jnp.bfloat16),
+        "fsdp",
+        scatter_dimension=0,
+        tiled=True,
+    ).reshape(1, -1).astype(jnp.float32)
     grad_mixed = (
         matmul_nt(grad_attn_rows, out_full).astype(jnp.bfloat16).reshape(seq_len, heads_here, HD)
     )

time: 579 us -> 529 us (0.914)
  waiting for transfers between devices: 134 us -> 97.2 us
  local copies, waits for them, and re-layouts: 107 us -> 96 us
    reduce_scatter x2, waiting for transfers between devices: 65.2 us -> 23.3 us  [the longest x1 23.3 us: on_device(): lax.psum_scatter(matmul_nt(grad_before, fc1_part).astype(jnp.bfloat16), '...]
    unnamed x102 -> x99, local copies, waits for them, and re-layouts: 25.9 us -> 26.8 us
  transfers between devices with their start and end apart: 14 -> 14, of which waited for: 7 -> 6; matrix products, arithmetic and copies ran while one was open for 21% -> 22% of each run, Pallas kernels for 18% -> 20%
where the time goes in v11:
time: 529 us; the launch traced here: 519 us
  Pallas kernels  103 us (19%)
  waiting for transfers between devices  97.2 us (18%)
  local copies, waits for them, and re-layouts  96 us (18%)
  blocking collectives  91.4 us (17%)
  matrix products  67.5 us (13%)
  other arithmetic  24.9 us (5%)
  starting transfers between devices  23.3 us (4%)
  between operations  15.6 us (3%)
    pallas_call x1, Pallas kernels, attn_backward(): pl.pallas_call(functools.partial(_bwd_kernel, scale), out_shape=(shape, s...  64.6 us
    psum x1, blocking collectives, on_device(): lax.psum((grad_ln1_gain, grad_ln1_bias, grad_qv_bias, grad_out_bias, grad...  42 us
    pallas_call x1, Pallas kernels, attn_forward(): pl.pallas_call(functools.partial(_fwd_kernel, scale), out_shape=(jax.Shap...  38.6 us
    all_gather x1, blocking collectives, on_device(): qkv_cols = lax.all_gather(qkv_weight, 'fsdp', axis=1, tiled=True)  35.2 us
    all_gather x1, waiting for transfers between devices, on_device(): normed_rows = lax.all_gather(normed_two, 'tp', axis=0, tiled=True)  27.8 us
    unnamed x99, local copies, waits for them, and re-layouts  26.8 us
    reduce_scatter x1, waiting for transfers between devices, on_device(): lax.psum_scatter(matmul_nt(grad_before, fc1_part).astype(jnp.bfloat16), '...  23.3 us
    all_gather x1, waiting for transfers between devices, on_device(): lax.all_gather(grad_middle.astype(jnp.bfloat16), 'tp', axis=0, tiled=True)  20.2 us
  transfers between devices with their start and end apart: 14, of which 6 were waited for; matrix products, arithmetic and copies ran while one was open for 22% of the time, Pallas kernels for 20%

profile of v11, /device:TPU:0, one launch (start us, length us, event | category | flops | bytes accessed | tf_op | source)
XLA Modules:
  0.0 519.2 jit_solution(14191867984865654094)
XLA Ops:
  13.3 35.2 %all_gather.24 = bf16[3,768,192]{2,1,0:T(8,128)(2,1)S(1)} all-gather(bf16[3,96,192]{2,1,0:T(8,128)(2,1)S(1)} %copy-done.30), channel_id=1, replica_groups=mesh['fsdp'=8,'tp'=4] {'fsdp'}, dimensions={1}, use_global_device_ids=true | all-gather | bytes 995328 | tf_op jit(solution)/shard_map/all_gather | solution.py:205
  52.8 4.7 all-to-all-start
  59.3 4.6 convolution_bitcast_fusion
  76.5 4.8 fusion.14
  81.3 38.6 %shard_map.280 = (bf16[4,3,512,64]{3,2,1,0:T(8,128)(2,1)S(1)}, f32[3,2048,1]{2,1,0:T(8,128)}) custom-call(s32[1]{0:T(128)S(6)} %copy.141.prefix_ref, bf16[3,2048,64]{2,1,0:T(8,128)(2,1)S(1)} %get-tuple-element.151.q_ref, bf16[3,2048,64]{2,1,0:T(8,128)(2,1)S(1)} %bitcast.140, bf16[3,2048,64]{2,1,0:T(8,128)(2,1)} %get-tuple-element.152.v_ref), custom_call_target="tpu_custom_call" | custom-call | flops 3221225472 | bytes 3145728 | tf_op jit(solution)/shard_map/pallas_call | solution.py:130
  121.1 4.4 reshape.205
  140.0 13.1 %all-gather.12.cloned.1.call-done = bf16[768,768]{1,0:T(8,128)(2,1)} async-done(((bf16[192,768]{1,0:T(8,128)(2,1)}), bf16[768,768]{1,0:T(8,128)(2,1)}) %all-gather.12.cloned.1.call-update) | async-done | bytes 1179664 | tf_op jit(solution)/shard_map/all_gather | solution.py:241
  153.8 14.2 %all_to_all.30 = bf16[4,3,512,64]{2,3,1,0:T(8,128)(2,1)S(1)} all-to-all(bf16[4,3,512,64]{2,3,1,0:T(8,128)(2,1)S(1)} %copy.76), channel_id=1, replica_groups=mesh['fsdp'=8,'tp'=4] {'tp'}, dimensions={0} | all-to-all | bytes 1572864 | tf_op jit(solution)/shard_map/all_to_all | solution.py:245
  173.0 27.8 %all-gather.14.cloned.1.call-done = bf16[2048,768]{1,0:T(8,128)(2,1)} async-done(((bf16[512,768]{1,0:T(8,128)(2,1)}), bf16[2048,768]{1,0:T(8,128)(2,1)}) %all-gather.14.cloned.1.call-update) | async-done | bytes 3145744 | tf_op jit(solution)/shard_map/all_gather | solution.py:260
  200.8 5.1 fusion.45
  205.9 7.8 %convert_reduce_fusion = (f32[768]{0:T(1024)S(1)}, bf16[2048,768]{1,0:T(8,128)(2,1)S(1)}, bf16[2048,768]{1,0:T(8,128)(2,1)}) fusion(f32[2048,768]{1,0:T(8,128)S(1)} %fusion.45, f32[768]{0:T(1024)S(1)} %dynamic_slice.7, bf16[2048,768]{1,0:T(8,128)(2,1)S(1)} %copy-done.38, bf16[768,768]{0,1:T(8,128)(2,1)S(1)} %bitcast.158), kind=kOutput, calls=%fused_computation.9 | convolution fusion | flops 2455239936 | bytes 16914432 | tf_op jit(solution)/shard_map/dot_general | solution.py:37
  219.9 6.7 %convolution_convert_fusion = bf16[2048,768]{1,0:T(8,128)(2,1)} fusion(bf16[2048,768]{1,0:T(8,128)(2,1)} %get-tuple-element.137, bf16[768,768]{0,1:T(8,128)(2,1)} %bitcast.157), kind=kOutput, calls=%fused_computation.12 | convolution fusion | flops 2417491968 | bytes 7471104 | tf_op jit(solution)/shard_map/dot_general | solution.py:263
  234.2 23.3 %reduce-scatter.6.cloned.1.call-done = bf16[512,768]{1,0:T(8,128)(2,1)} async-done(((bf16[2048,768]{1,0:T(8,128)(2,1)}), bf16[512,768]{1,0:T(8,128)(2,1)}) %reduce-scatter.6.cloned.1.call-update) | async-done | bytes 786448 | tf_op jit(solution)/shard_map/reduce_scatter | solution.py:274
  271.1 20.2 %all-gather.16.cloned.1.call-done = bf16[2048,768]{1,0:T(8,128)(2,1)} async-done(((bf16[512,768]{1,0:T(8,128)(2,1)}), bf16[2048,768]{1,0:T(8,128)(2,1)}) %all-gather.16.cloned.1.call-update) | async-done | bytes 3145744 | tf_op jit(solution)/shard_map/all_gather | solution.py:286
  305.9 5.1 all-to-all-start.2
  318.5 64.6 %shard_map.281 = (bf16[4,3,512,64]{3,2,1,0:T(8,128)(2,1)S(1)}, bf16[4,3,512,64]{3,2,1,0:T(8,128)(2,1)S(1)}, bf16[4,3,512,64]{3,2,1,0:T(8,128)(2,1)S(1)}) custom-call(s32[1]{0:T(128)S(6)} %copy.141.prefix_ref, bf16[3,2048,64]{2,1,0:T(8,128)(2,1)} %copy-done.4, bf16[3,2048,64]{2,1,0:T(8,128)(2,1)} %bitcast.141, bf16[3,2048,64]{2,1,0:T(8,128)(2,1)} %get-tuple-element.152.v_ref, ...), custom_call_target="tpu_custom_call" | custom-call | flops 8053063680 | bytes 6291456 | tf_op jit(solution)/shard_map/pallas_call | solution.py:158
  393.4 4.2 fusion.23
  408.5 4.2 all-to-all-start.4
  415.6 4.2 copy.106
  419.8 4.7 reshape.216
  440.5 6.7 %all-to-all-done.3 = bf16[4,3,512,64]{2,3,1,0:T(8,128)(2,1)S(1)} async-done(((bf16[4,3,512,64]{2,3,1,0:T(8,128)(2,1)}), bf16[4,3,512,64]{2,3,1,0:T(8,128)(2,1)S(1)}, u32[]{:S(2)}, u32[]{:S(2)}) %all-to-all-start.3) | async-done | bytes 786464 | tf_op jit(solution)/shard_map/all_to_all | solution.py:339
  447.2 4.2 all-to-all-start.5
  458.0 5.1 all-to-all-done.5
  468.3 42.0 %all-reduce = (f32[768]{0:T(1024)}, f32[768]{0:T(1024)}, f32[2,768]{1,0:T(2,128)}, f32[768]{0:T(1024)}, f32[768]{0:T(1024)}, /*index=5*/f32[768]{0:T(1024)}, f32[3072]{0:T(1024)}, f32[768]{0:T(1024)}, f32[5,768]{1,0:T(8,128)}) all-reduce(f32[768]{0:T(1024)S(1)} %get-tuple-element.114, ...), channel_id=1, replica_groups=mesh['fsdp'=8,'tp'=4] {'fsdp','tp'}, use_global_device_ids=true, to_apply=%region_13.0 | all-reduce | flops 13056 | bytes 104448 | tf_op jit(solution)/shard_map/psum | solution.py:364
  (214 shorter events, 147.8 us)
Async XLA Ops:
  7.2 42.0 %all-gather.8.cloned.1.call-start = ((), (), s32[]{:S(2)}) async-start(), calls=%async_computation.9 | async-start | bytes 3932160 | tf_op jit(solution)/shard_map/all_gather | solution.py:214
  12.4 108.7 %all-gather.18.cloned.1.call-start = ((), (), s32[]{:S(2)}) async-start(), calls=%async_computation.16 | async-start | bytes 2985984 | tf_op jit(solution)/shard_map/all_gather | solution.py:219
  49.3 90.7 %all-gather.10.cloned.1.call-start = ((), (), s32[]{:S(2)}) async-start(), calls=%async_computation.10 | async-start | bytes 3932160 | tf_op jit(solution)/shard_map/all_gather | solution.py:222
  52.8 68.3 %all-to-all-start = ((bf16[4,3,768,192]{2,3,1,0:T(8,128)(2,1)}), bf16[4,3,768,192]{2,3,1,0:T(8,128)(2,1)}, u32[]{:S(2)}, u32[]{:S(2)}) async-start(bf16[4,3,768,192]{2,3,1,0:T(8,128)(2,1)} %broadcast_in_dim.6), calls=%async_computation | async-start | bytes 7077888 | tf_op jit(solution)/shard_map/all_to_all | solution.py:221
  57.6 95.5 %all-gather.12.cloned.1.call-start = ((), (), s32[]{:S(2)}) async-start(), calls=%async_computation.11 | async-start | bytes 1474560 | tf_op jit(solution)/shard_map/all_gather | solution.py:241
  67.0 14.3 %copy-start.3 = (bf16[2048,3,64]{2,0,1:T(8,128)(2,1)}, bf16[2048,3,64]{2,0,1:T(8,128)(2,1)S(1)}, u32[]{:S(2)}) copy-start(bf16[2048,3,64]{2,0,1:T(8,128)(2,1)S(1)} %copy.71) | copy-start | bytes 2359300
  128.2 72.6 %all-gather.14.cloned.1.call-start = ((), (), s32[]{:S(2)}) async-start(), calls=%async_computation.12 | async-start | bytes 3932160 | tf_op jit(solution)/shard_map/all_gather | solution.py:260
  153.1 14.9 %copy-start.41 = (f32[768]{0:T(1024)S(1)}, f32[768]{0:T(1024)}, u32[]{:S(2)}) copy-start(f32[768]{0:T(1024)} %param.28) | copy-start | bytes 9220
  153.8 14.2 %copy-start.8 = (f32[512,768]{1,0:T(8,128)S(1)}, f32[512,768]{1,0:T(8,128)}, u32[]{:S(2)}) copy-start(f32[512,768]{1,0:T(8,128)} %copy-done.7) | copy-start | bytes 4718596
  170.2 89.3 %copy-start.5 = (f32[512,768]{1,0:T(8,128)}, f32[512,768]{1,0:T(8,128)S(1)}, u32[]{:S(2)}) copy-start(f32[512,768]{1,0:T(8,128)S(1)} %get-tuple-element.149) | copy-start | bytes 4718596
  172.1 85.3 %reduce-scatter.6.cloned.1.call-start = ((), (), s32[]{:S(2)}) async-start(), calls=%async_computation.13 | async-start | bytes 3932160 | tf_op jit(solution)/shard_map/reduce_scatter | solution.py:274
  205.9 9.4 %copy-start.21 = (bf16[768,768]{1,0:T(8,128)(2,1)S(1)}, bf16[768,768]{1,0:T(8,128)(2,1)}, u32[]{:S(2)}) copy-start(bf16[768,768]{1,0:T(8,128)(2,1)} %reshape_reshape.8) | copy-start | bytes 3538948
  219.4 71.9 %all-gather.16.cloned.1.call-start = ((), (), s32[]{:S(2)}) async-start(), calls=%async_computation.14 | async-start | bytes 3932160 | tf_op jit(solution)/shard_map/all_gather | solution.py:286
  262.7 125.3 %reduce-scatter.8.cloned.1.call-start = ((), (), s32[]{:S(2)}) async-start(), calls=%async_computation.15 | async-start | bytes 2985984 | tf_op jit(solution)/shard_map/reduce_scatter | solution.py:305
  305.9 78.4 %all-to-all-start.2 = ((bf16[4,512,768]{2,1,0:T(8,128)(2,1)}), bf16[4,512,768]{2,1,0:T(8,128)(2,1)}, u32[]{:S(2)}, u32[]{:S(2)}) async-start(bf16[4,512,768]{2,1,0:T(8,128)(2,1)} %bitcast.148), calls=%async_computation.3 | async-start | bytes 6291456 | tf_op jit(solution)/shard_map/all_to_all | solution.py:288
  408.5 23.3 %all-to-all-start.4 = ((bf16[4,3,512,64]{2,3,1,0:T(8,128)(2,1)}), bf16[4,3,512,64]{2,3,1,0:T(8,128)(2,1)}, u32[]{:S(2)}, u32[]{:S(2)}) async-start(bf16[4,3,512,64]{2,3,1,0:T(8,128)(2,1)} %copy.88), calls=%async_computation.6 | async-start | bytes 1572864 | tf_op jit(solution)/shard_map/all_to_all | solution.py:339
  412.8 97.6 %reduce-scatter.10.cloned.1.call-start = ((), (), s32[]{:S(2)}) async-start(), calls=%async_computation.17 | async-start | bytes 2211840
  431.8 15.5 %all-to-all-start.3 = ((bf16[4,3,512,64]{2,3,1,0:T(8,128)(2,1)}), bf16[4,3,512,64]{2,3,1,0:T(8,128)(2,1)S(1)}, u32[]{:S(2)}, u32[]{:S(2)}) async-start(bf16[4,3,512,64]{2,3,1,0:T(8,128)(2,1)} %copy.85), calls=%async_computation.5 | async-start | bytes 1572864 | tf_op jit(solution)/shard_map/all_to_all | solution.py:339
  438.6 12.8 %copy-start.20 = (bf16[4,1,768,3,64]{2,4,3,1,0:T(8,128)(2,1)S(1)}, bf16[4,1,768,3,64]{2,4,3,1,0:T(8,128)(2,1)}, u32[]{:S(2)}) copy-start(bf16[4,1,768,3,64]{2,4,3,1,0:T(8,128)(2,1)} %get-tuple-element.141) | copy-start | bytes 3538948
  447.2 15.9 %all-to-all-start.5 = ((bf16[4,3,512,64]{2,3,1,0:T(8,128)(2,1)}), bf16[4,3,512,64]{2,3,1,0:T(8,128)(2,1)}, u32[]{:S(2)}, u32[]{:S(2)}) async-start(bf16[4,3,512,64]{2,3,1,0:T(8,128)(2,1)} %copy.91), calls=%async_computation.7 | async-start | bytes 1572864 | tf_op jit(solution)/shard_map/all_to_all | solution.py:339
  454.7 8.4 %copy-start.9 = (f32[512,768]{1,0:T(8,128)S(1)}, f32[512,768]{1,0:T(8,128)}, u32[]{:S(2)}) copy-start(f32[512,768]{1,0:T(8,128)} %copy-done.7) | copy-start | bytes 4718596
  454.7 8.4 %copy-start.18 = (bf16[4,1,768,3,64]{2,4,3,1,0:T(8,128)(2,1)S(1)}, bf16[4,1,768,3,64]{2,4,3,1,0:T(8,128)(2,1)}, u32[]{:S(2)}) copy-start(bf16[4,1,768,3,64]{2,4,3,1,0:T(8,128)(2,1)} %get-tuple-element.140) | copy-start | bytes 3538948
  466.9 45.3 %copy-start.1 = (f32[5,768]{1,0:T(8,128)S(1)}, f32[5,768]{1,0:T(8,128)}, u32[]{:S(2)}) copy-start(f32[5,768]{1,0:T(8,128)} %param.33) | copy-start | bytes 46084
  467.6 44.7 %copy-start.12 = (f32[512,768]{1,0:T(8,128)}, f32[512,768]{1,0:T(8,128)S(1)}, u32[]{:S(2)}) copy-start(f32[512,768]{1,0:T(8,128)S(1)} %multiply_add_fusion) | copy-start | bytes 4718596
  (35 other events, 101.8 us)
Sparse Core Ops, SparseCore 0:
  12.6 31.2 all-gather.7
  49.4 55.5 all-gather.17
  106.5 27.0 all-gather.9
  135.6 17.4 all-gather.11
  172.2 28.4 all-gather.13
  219.5 37.8 reduce-scatter.5
  262.8 28.4 all-gather.15
  306.0 71.7 reduce-scatter.7
  424.6 68.9 reduce-scatter.9

commit v12 on v11

--- a/solution.py
+++ b/solution.py
@@ -89,7 +89,7 @@
 
 
 def _bwd_kernel(scale, prefix_ref, q_ref, k_ref, v_ref, do_ref, lse_ref,
-                dq_ref, dk_ref, dv_ref, dk_acc, dv_acc):
+                g_ref, dk_acc, dv_acc):
     qb = pl.program_id(1)
 
     @pl.when(qb == 0)
@@ -108,14 +108,19 @@
     grad_probs = _nt(grad_out, v_ref[0])
     inner = jnp.sum(probs * grad_probs, axis=-1, keepdims=True)
     grad_scores = (probs * (grad_probs - inner)).astype(jnp.bfloat16)
-    dq_ref[0, 0] = (jnp.dot(grad_scores, k, preferred_element_type=jnp.float32) * scale).astype(dq_ref.dtype)
+    groups, rows_per = g_ref.shape[0], g_ref.shape[3]
+    per = rows_per // rows
+    start = pl.multiple_of((qb % per) * rows, rows)
+    g_ref[qb // per, 0, 0, pl.ds(start, rows), :] = (
+        jnp.dot(grad_scores, k, preferred_element_type=jnp.float32) * scale
+    ).astype(g_ref.dtype)
     dk_acc[...] += _tn(grad_scores, q)
 
     @pl.when(qb == pl.num_programs(1) - 1)
     def _():
-        groups, rows, hd = dk_ref.shape[0], dk_ref.shape[2], dk_ref.shape[3]
-        dk_ref[:, 0] = (dk_acc[...] * scale).astype(dk_ref.dtype).reshape(groups, rows, hd)
-        dv_ref[:, 0] = dv_acc[...].astype(dv_ref.dtype).reshape(groups, rows, hd)
+        hd = g_ref.shape[4]
+        g_ref[:, 1, 0] = (dk_acc[...] * scale).astype(g_ref.dtype).reshape(groups, rows_per, hd)
+        g_ref[:, 2, 0] = dv_acc[...].astype(g_ref.dtype).reshape(groups, rows_per, hd)
 
 
 def attn_forward(prefix, q, k, v, scale, groups):
@@ -152,16 +157,15 @@
     q_spec = pl.BlockSpec((1, qb, hd), lambda h, i, p: (h, i, 0))
     kv_spec = pl.BlockSpec((1, seq, hd), lambda h, i, p: (h, 0, 0))
     lse_spec = pl.BlockSpec((1, qb, 1), lambda h, i, p: (h, i, 0))
-    dq_spec = pl.BlockSpec((1, 1, qb, hd), lambda h, i, p: (i // per, h, i % per, 0))
-    dkv_spec = pl.BlockSpec((groups, 1, seq // groups, hd), lambda h, i, p: (0, h, 0, 0))
-    shape = jax.ShapeDtypeStruct((groups, heads, seq // groups, hd), jnp.bfloat16)
+    g_spec = pl.BlockSpec((groups, 3, 1, seq // groups, hd), lambda h, i, p: (0, 0, h, 0, 0))
+    shape = jax.ShapeDtypeStruct((groups, 3, heads, seq // groups, hd), jnp.bfloat16)
     return pl.pallas_call(
         functools.partial(_bwd_kernel, scale),
-        out_shape=(shape, shape, shape),
+        out_shape=shape,
         grid_spec=pltpu.PrefetchScalarGridSpec(
             num_scalar_prefetch=1, grid=grid,
             in_specs=[q_spec, kv_spec, kv_spec, q_spec, lse_spec],
-            out_specs=[dq_spec, dkv_spec, dkv_spec],
+            out_specs=g_spec,
             scratch_shapes=[pltpu.VMEM((seq, hd), jnp.float32),
                             pltpu.VMEM((seq, hd), jnp.float32)]),
         compiler_params=pltpu.CompilerParams(
@@ -311,14 +315,12 @@
     grad_mixed = (
         matmul_nt(grad_attn_rows, out_full).astype(jnp.bfloat16).reshape(seq_len, heads_here, HD)
     )
-    grad_q_heads, grad_k_heads, grad_v_heads = attn_backward(
+    grad_all = attn_backward(
         prefix, q_heads, k_heads, v_heads, jnp.transpose(grad_mixed, (1, 0, 2)), log_mass, scale,
         tp_count,
     )
-    grad_q_heads, grad_k_heads, grad_v_heads, result, dense_summed = lax.optimization_barrier(
-        (grad_q_heads, grad_k_heads, grad_v_heads, result, dense_summed)
-    )
-    grad_kinds = (grad_q_heads, grad_k_heads, grad_v_heads)
+    grad_all, result, dense_summed = lax.optimization_barrier((grad_all, result, dense_summed))
+    grad_q_heads, grad_v_heads = grad_all[:, 0], grad_all[:, 2]
     grad_qv_here = jnp.stack(
         [
             jnp.sum(grad_q_heads.astype(jnp.float32), axis=(0, 2)).reshape(-1),
@@ -330,17 +332,13 @@
         jnp.zeros(qv_bias.shape, jnp.float32), grad_qv_here, tp_rank * cols_here, 1
     )
     normed_groups = normed_all.reshape(tp_count, local_rows, -1)
-    grad_qkv_w = jnp.stack(
-        [
-            jnp.einsum("trd,thre->dhe", normed_groups, g, preferred_element_type=jnp.float32)
-            for g in grad_kinds
-        ]
+    grad_qkv_w = jnp.einsum(
+        "trd,tkhre->kdhe", normed_groups, grad_all, preferred_element_type=jnp.float32
     ).reshape(3, normed_all.shape[1], cols_here)
-    grad_rows_kinds = [lax.all_to_all(g, "tp", 0, 0, tiled=True) for g in grad_kinds]
+    grad_rows_all = lax.all_to_all(grad_all, "tp", 0, 0, tiled=True)
     qkv_split = qkv_all.reshape(tp_count, 3, qkv_all.shape[2], heads_here, HD)
-    grad_normed = sum(
-        jnp.einsum("shre,sdhe->rd", g, qkv_split[:, kind], preferred_element_type=jnp.float32)
-        for kind, g in enumerate(grad_rows_kinds)
+    grad_normed = jnp.einsum(
+        "skhre,skdhe->rd", grad_rows_all, qkv_split, preferred_element_type=jnp.float32
     )
     dense_shards = []
     offset = 0

time: 529 us -> 511 us (0.966)
  waiting for transfers between devices: 97.2 us -> 86.7 us
  matrix products: 67.5 us -> 59.4 us
  starting transfers between devices: 23.3 us -> 15.7 us
    dot_general x6 -> x2, matrix products: 20.5 us -> 11.3 us  [the longest x1 5.84 us: on_device(): jnp.einsum('trd,tkhre->kdhe', normed_groups, grad_all, preferred_element_...]
    all_to_all x3 -> x1, starting transfers between devices: 12.3 us -> 4.78 us  [on_device(): grad_rows_all = lax.all_to_all(grad_all, 'tp', 0, 0, tiled=True)]
    all_gather x1, waiting for transfers between devices: 13.1 us -> 6.71 us  [on_device(): out_all = lax.all_gather(out_full, 'tp', axis=0, tiled=True)]
    all_gather x1, waiting for transfers between devices: 20.2 us -> 14.8 us  [on_device(): lax.all_gather(grad_middle.astype(jnp.bfloat16), 'tp', axis=0, tiled=True)]
    all_to_all x3 -> x1, waiting for transfers between devices: 11.9 us -> 9.42 us  [on_device(): grad_rows_all = lax.all_to_all(grad_all, 'tp', 0, 0, tiled=True)]
    unnamed x99 -> x89, local copies, waits for them, and re-layouts: 26.8 us -> 27 us
  transfers between devices with their start and end apart: 14 -> 12, of which waited for: 6 -> 6; matrix products, arithmetic and copies ran while one was open for 22% -> 23% of each run, Pallas kernels for 20% -> 21%
where the time goes in v12:
time: 511 us; the launch traced here: 501 us
  Pallas kernels  105 us (21%)
  local copies, waits for them, and re-layouts  99 us (19%)
  blocking collectives  92.2 us (18%)
  waiting for transfers between devices  86.7 us (17%)
  matrix products  59.4 us (12%)
  other arithmetic  28.1 us (5%)
  starting transfers between devices  15.7 us (3%)
  between operations  15.4 us (3%)
    pallas_call x1, Pallas kernels, attn_backward(): pl.pallas_call(functools.partial(_bwd_kernel, scale), out_shape=shape, gr...  65.9 us
    psum x1, blocking collectives, on_device(): lax.psum((grad_ln1_gain, grad_ln1_bias, grad_qv_bias, grad_out_bias, grad...  41.8 us
    pallas_call x1, Pallas kernels, attn_forward(): pl.pallas_call(functools.partial(_fwd_kernel, scale), out_shape=(jax.Shap...  38.6 us
    all_gather x1, blocking collectives, on_device(): qkv_cols = lax.all_gather(qkv_weight, 'fsdp', axis=1, tiled=True)  35.2 us
    all_gather x1, waiting for transfers between devices, on_device(): normed_rows = lax.all_gather(normed_two, 'tp', axis=0, tiled=True)  27.8 us
    unnamed x89, local copies, waits for them, and re-layouts  27 us
    reduce_scatter x1, waiting for transfers between devices, on_device(): lax.psum_scatter(matmul_nt(grad_before, fc1_part).astype(jnp.bfloat16), '...  23.3 us
    dot_general x3, matrix products, matmul_nt(): lax.dot_general(left, right, (((1,), (1,)), ((), ())), preferred_element_...  15.7 us
  transfers between devices with their start and end apart: 12, of which 6 were waited for; matrix products, arithmetic and copies ran while one was open for 23% of the time, Pallas kernels for 21%

profile of v12, /device:TPU:0, one launch (start us, length us, event | category | flops | bytes accessed | tf_op | source)
XLA Modules:
  0.0 501.0 jit_solution(5495192712042109527)
XLA Ops:
  13.3 35.2 %all_gather.24 = bf16[3,768,192]{2,1,0:T(8,128)(2,1)S(1)} all-gather(bf16[3,96,192]{2,1,0:T(8,128)(2,1)S(1)} %copy-done.25), channel_id=1, replica_groups=mesh['fsdp'=8,'tp'=4] {'fsdp'}, dimensions={1}, use_global_device_ids=true | all-gather | bytes 995328 | tf_op jit(solution)/shard_map/all_gather | solution.py:209
  52.8 4.7 all-to-all-start
  59.3 4.6 convolution_bitcast_fusion
  75.9 4.7 fusion.11
  80.6 38.6 %shard_map.280 = (bf16[4,3,512,64]{3,2,1,0:T(8,128)(2,1)S(1)}, f32[3,2048,1]{2,1,0:T(8,128)}) custom-call(s32[1]{0:T(128)S(6)} %copy.160.prefix_ref, bf16[3,2048,64]{2,1,0:T(8,128)(2,1)S(1)} %get-tuple-element.155.q_ref, bf16[3,2048,64]{2,1,0:T(8,128)(2,1)S(1)} %bitcast.106, bf16[3,2048,64]{2,1,0:T(8,128)(2,1)} %get-tuple-element.156.v_ref), custom_call_target="tpu_custom_call" | custom-call | flops 3221225472 | bytes 3145728 | tf_op jit(solution)/shard_map/pallas_call | solution.py:135
  146.4 6.7 %all-gather.12.cloned.1.call-done = bf16[768,768]{1,0:T(8,128)(2,1)} async-done(((bf16[192,768]{1,0:T(8,128)(2,1)}), bf16[768,768]{1,0:T(8,128)(2,1)}) %all-gather.12.cloned.1.call-update) | async-done | bytes 1179664 | tf_op jit(solution)/shard_map/all_gather | solution.py:245
  154.5 15.2 %all_to_all.20 = bf16[4,3,512,64]{2,3,1,0:T(8,128)(2,1)S(1)} all-to-all(bf16[4,3,512,64]{2,3,1,0:T(8,128)(2,1)} %copy.112), channel_id=1, replica_groups=mesh['fsdp'=8,'tp'=4] {'tp'}, dimensions={0} | all-to-all | bytes 1572864 | tf_op jit(solution)/shard_map/all_to_all | solution.py:249
  175.1 27.8 %all-gather.14.cloned.1.call-done = bf16[2048,768]{1,0:T(8,128)(2,1)} async-done(((bf16[512,768]{1,0:T(8,128)(2,1)}), bf16[2048,768]{1,0:T(8,128)(2,1)}) %all-gather.14.cloned.1.call-update) | async-done | bytes 3145744 | tf_op jit(solution)/shard_map/all_gather | solution.py:264
  203.0 5.1 %fusion.29 = f32[2048,768]{1,0:T(8,128)S(1)} fusion(bf16[2048,768]{1,0:T(8,128)(2,1)} %all-gather.14.cloned.1.call-done, bf16[768,768]{1,0:T(8,128)(2,1)} %reshape_reshape.8), kind=kOutput, calls=%fused_computation.81 | convolution fusion | flops 2415919104 | bytes 10616832 | tf_op jit(solution)/shard_map/dot_general | solution.py:265
  208.0 7.8 %convert_reduce_fusion = (f32[768]{0:T(1024)S(1)}, bf16[2048,768]{1,0:T(8,128)(2,1)S(1)}, bf16[2048,768]{1,0:T(8,128)(2,1)}) fusion(f32[2048,768]{1,0:T(8,128)S(1)} %fusion.29, f32[768]{0:T(1024)S(1)} %dynamic_slice.7, bf16[2048,768]{1,0:T(8,128)(2,1)S(1)} %copy-done.33, bf16[768,768]{0,1:T(8,128)(2,1)S(1)} %bitcast.125), kind=kOutput, calls=%fused_computation.9 | convolution fusion | flops 2455239936 | bytes 16914432 | tf_op jit(solution)/shard_map/dot_general | solution.py:37
  222.1 6.6 %convolution_convert_fusion = bf16[2048,768]{1,0:T(8,128)(2,1)} fusion(bf16[2048,768]{1,0:T(8,128)(2,1)} %get-tuple-element.144, bf16[768,768]{0,1:T(8,128)(2,1)} %bitcast.124), kind=kOutput, calls=%fused_computation.14 | convolution fusion | flops 2417491968 | bytes 7471104 | tf_op jit(solution)/shard_map/dot_general | solution.py:267
  236.3 23.3 %reduce-scatter.6.cloned.1.call-done = bf16[512,768]{1,0:T(8,128)(2,1)} async-done(((bf16[2048,768]{1,0:T(8,128)(2,1)}), bf16[512,768]{1,0:T(8,128)(2,1)}) %reduce-scatter.6.cloned.1.call-update) | async-done | bytes 786448 | tf_op jit(solution)/shard_map/reduce_scatter | solution.py:278
  279.2 14.8 %all-gather.16.cloned.1.call-done = bf16[2048,768]{1,0:T(8,128)(2,1)} async-done(((bf16[512,768]{1,0:T(8,128)(2,1)}), bf16[2048,768]{1,0:T(8,128)(2,1)}) %all-gather.16.cloned.1.call-update) | async-done | bytes 3145744 | tf_op jit(solution)/shard_map/all_gather | solution.py:290
  294.0 4.6 copy.117
  302.6 8.0 %pad_maximum_fusion = bf16[8,165888]{1,0:T(8,128)(2,1)} fusion(bf16[8,73728]{1,0:T(8,128)(2,1)} %reshape.184, bf16[8,73728]{1,0:T(8,128)(2,1)S(1)} %copy-done.14, bf16[8,18432]{1,0:T(8,128)(2,1)S(1)} %reshape.182), kind=kLoop, calls=%fused_computation.22 | loop fusion | flops 7962624 | bytes 5308416 | tf_op jit(solution)/shard_map/concatenate | solution.py:308
  310.6 4.5 convert_element_type.97
  315.2 5.0 all-to-all-start.2
  328.1 65.9 %shard_map.281 = bf16[4,3,3,512,64]{4,3,2,1,0:T(8,128)(2,1)} custom-call(s32[1]{0:T(128)S(6)} %copy.160.prefix_ref, bf16[3,2048,64]{2,1,0:T(8,128)(2,1)S(1)} %copy-done.3, bf16[3,2048,64]{2,1,0:T(8,128)(2,1)S(1)} %bitcast.107, bf16[3,2048,64]{2,1,0:T(8,128)(2,1)S(1)} %copy-done.4, bf16[3,2048,64]{2,1,0:T(8,128)(2,1)} %bitcast.121, ...), custom_call_target="tpu_custom_call" | custom-call | flops 8053063680 | bytes 6291456 | tf_op jit(solution)/shard_map/pallas_call | solution.py:162
  400.3 6.0 %copy.121 = bf16[4,3,3,512,64]{3,4,2,1,0:T(8,128)(2,1)} copy(bf16[4,3,3,512,64]{4,3,2,1,0:T(8,128)(2,1)} %shard_map.281) | data formatting | bytes 4718592 | tf_op jit(solution)/shard_map/optimization_barrier | solution.py:322
  406.4 4.8 all-to-all-start.3
  411.2 5.8 %fusion.32 = f32[3,3,64,768,1]{3,2,1,0,4:T(8,128)} fusion(bf16[4,3,3,512,64]{4,3,2,1,0:T(8,128)(2,1)} %shard_map.281, bf16[4,512,768,1,1]{2,1,4,3,0:T(8,128)(2,1)S(1)} %bitcast.118), kind=kOutput, calls=%fused_computation.84 | convolution fusion | flops 1811939328 | bytes 7274496 | tf_op jit(solution)/shard_map/trd,tkhre->kdhe/dot_general | solution.py:335
  430.3 9.4 %all-to-all-done.3 = bf16[4,3,3,512,64]{3,4,2,1,0:T(8,128)(2,1)} async-done(((bf16[4,3,3,512,64]{3,4,2,1,0:T(8,128)(2,1)}), bf16[4,3,3,512,64]{3,4,2,1,0:T(8,128)(2,1)}, u32[]{:S(2)}, u32[]{:S(2)}) %all-to-all-start.3) | async-done | bytes 2359328 | tf_op jit(solution)/shard_map/all_to_all | solution.py:338
  439.7 5.4 %fusion.14 = (f32[768]{0:T(1024)S(1)}, f32[512]{0:T(512)S(1)}, f32[512]{0:T(512)S(1)}, f32[768]{0:T(1024)S(1)}, f32[512,768,1,1,1]{1,0,4,3,2:T(8,128)S(1)}) fusion(f32[512,768]{1,0:T(8,128)S(1)} %copy-done.10, f32[512]{0:T(512)S(1)} %add_rsqrt_fusion.1, f32[512]{0:T(512)S(1)} %broadcast_multiply_fusion.5, f32[768]{0:T(1024)S(1)} %copy-done.28, ...), kind=kOutput, calls=%fused_computation.35 | convolution fusion | flops 1815475712 | bytes 9061376 | tf_op jit(solution)/shard_map/skhre,skdhe->rd/dot_general | solution.py:340
  446.6 41.8 %all-reduce = (f32[768]{0:T(1024)}, f32[768]{0:T(1024)}, f32[2,768]{1,0:T(2,128)}, f32[768]{0:T(1024)}, f32[768]{0:T(1024)}, /*index=5*/f32[768]{0:T(1024)}, f32[3072]{0:T(1024)}, f32[768]{0:T(1024)}, f32[5,768]{1,0:T(8,128)}) all-reduce(f32[768]{0:T(1024)S(1)} %get-tuple-element.121, ...), channel_id=1, replica_groups=mesh['fsdp'=8,'tp'=4] {'fsdp','tp'}, use_global_device_ids=true, to_apply=%region_13.0 | all-reduce | flops 13056 | bytes 104448 | tf_op jit(solution)/shard_map/psum | solution.py:362
  (187 shorter events, 128.9 us)
Async XLA Ops:
  7.2 42.0 %all-gather.8.cloned.1.call-start = ((), (), s32[]{:S(2)}) async-start(), calls=%async_computation.7 | async-start | bytes 3932160 | tf_op jit(solution)/shard_map/all_gather | solution.py:218
  12.4 108.0 %all-gather.18.cloned.1.call-start = ((), (), s32[]{:S(2)}) async-start(), calls=%async_computation.14 | async-start | bytes 2985984 | tf_op jit(solution)/shard_map/all_gather | solution.py:223
  49.3 97.1 %all-gather.10.cloned.1.call-start = ((), (), s32[]{:S(2)}) async-start(), calls=%async_computation.8 | async-start | bytes 3932160 | tf_op jit(solution)/shard_map/all_gather | solution.py:226
  52.8 67.6 %all-to-all-start = ((bf16[4,3,768,192]{2,3,1,0:T(8,128)(2,1)}), bf16[4,3,768,192]{2,3,1,0:T(8,128)(2,1)}, u32[]{:S(2)}, u32[]{:S(2)}) async-start(bf16[4,3,768,192]{2,3,1,0:T(8,128)(2,1)} %broadcast_in_dim.6), calls=%async_computation | async-start | bytes 7077888 | tf_op jit(solution)/shard_map/all_to_all | solution.py:225
  57.5 95.6 %all-gather.12.cloned.1.call-start = ((), (), s32[]{:S(2)}) async-start(), calls=%async_computation.9 | async-start | bytes 1474560 | tf_op jit(solution)/shard_map/all_gather | solution.py:245
  131.1 71.9 %all-gather.14.cloned.1.call-start = ((), (), s32[]{:S(2)}) async-start(), calls=%async_computation.10 | async-start | bytes 3932160 | tf_op jit(solution)/shard_map/all_gather | solution.py:264
  153.1 16.6 %copy-start.36 = (f32[768]{0:T(1024)S(1)}, f32[768]{0:T(1024)}, u32[]{:S(2)}) copy-start(f32[768]{0:T(1024)} %param.28) | copy-start | bytes 9220
  154.5 15.2 %copy-start.9 = (f32[512,768]{1,0:T(8,128)S(1)}, f32[512,768]{1,0:T(8,128)}, u32[]{:S(2)}) copy-start(f32[512,768]{1,0:T(8,128)} %copy-done.8) | copy-start | bytes 4718596
  174.3 85.4 %reduce-scatter.6.cloned.1.call-start = ((), (), s32[]{:S(2)}) async-start(), calls=%async_computation.11 | async-start | bytes 3932160 | tf_op jit(solution)/shard_map/reduce_scatter | solution.py:278
  202.9 5.1 %copy-start.22 = (bf16[768,8,96]{0,2,1:T(8,128)(2,1)S(1)}, bf16[768,8,96]{0,2,1:T(8,128)(2,1)}, u32[]{:S(2)}) copy-start(bf16[768,8,96]{0,2,1:T(8,128)(2,1)} %copy.111) | copy-start | bytes 3538948
  202.9 5.1 %copy-start.33 = (bf16[2048,768]{1,0:T(8,128)(2,1)S(1)}, bf16[2048,768]{1,0:T(8,128)(2,1)}, u32[]{:S(2)}) copy-start(bf16[2048,768]{1,0:T(8,128)(2,1)} %all-gather.10.cloned.1.call-done) | copy-start | bytes 9437188
  208.0 9.6 %copy-start.19 = (bf16[768,768]{1,0:T(8,128)(2,1)S(1)}, bf16[768,768]{1,0:T(8,128)(2,1)}, u32[]{:S(2)}) copy-start(bf16[768,768]{1,0:T(8,128)(2,1)} %reshape_reshape.8) | copy-start | bytes 3538948
  221.6 72.4 %all-gather.16.cloned.1.call-start = ((), (), s32[]{:S(2)}) async-start(), calls=%async_computation.12 | async-start | bytes 3932160 | tf_op jit(solution)/shard_map/all_gather | solution.py:290
  222.1 6.7 %copy-start.34 = (bf16[2048,768]{1,0:T(8,128)(2,1)S(1)}, bf16[2048,768]{1,0:T(8,128)(2,1)}, u32[]{:S(2)}) copy-start(bf16[2048,768]{1,0:T(8,128)(2,1)} %all-gather.10.cloned.1.call-done) | copy-start | bytes 9437188
  222.1 6.6 %copy-start.39 = (bf16[2048,768]{1,0:T(8,128)(2,1)S(1)}, bf16[2048,768]{1,0:T(8,128)(2,1)}, u32[]{:S(2)}) copy-start(bf16[2048,768]{1,0:T(8,128)(2,1)} %get-tuple-element.144) | copy-start | bytes 9437188
  265.3 132.5 %reduce-scatter.8.cloned.1.call-start = ((), (), s32[]{:S(2)}) async-start(), calls=%async_computation.13 | async-start | bytes 2985984 | tf_op jit(solution)/shard_map/reduce_scatter | solution.py:309
  315.2 5.0 %copy-start.21 = (bf16[192,768]{1,0:T(8,128)(2,1)S(1)}, bf16[192,768]{1,0:T(8,128)(2,1)}, u32[]{:S(2)}) copy-start(bf16[192,768]{1,0:T(8,128)(2,1)} %reshape.175) | copy-start | bytes 884740
  315.2 78.9 %all-to-all-start.2 = ((bf16[4,512,768]{2,1,0:T(8,128)(2,1)}), bf16[4,512,768]{2,1,0:T(8,128)(2,1)}, u32[]{:S(2)}, u32[]{:S(2)}) async-start(bf16[4,512,768]{2,1,0:T(8,128)(2,1)} %bitcast.114), calls=%async_computation.3 | async-start | bytes 6291456 | tf_op jit(solution)/shard_map/all_to_all | solution.py:292
  406.4 33.4 %all-to-all-start.3 = ((bf16[4,3,3,512,64]{3,4,2,1,0:T(8,128)(2,1)}), bf16[4,3,3,512,64]{3,4,2,1,0:T(8,128)(2,1)}, u32[]{:S(2)}, u32[]{:S(2)}) async-start(bf16[4,3,3,512,64]{3,4,2,1,0:T(8,128)(2,1)} %copy.121), calls=%async_computation.5 | async-start | bytes 4718592 | tf_op jit(solution)/shard_map/all_to_all | solution.py:338
  411.1 81.0 %reduce-scatter.10.cloned.1.call-start = ((), (), s32[]{:S(2)}) async-start(), calls=%async_computation.15 | async-start | bytes 2211840
  426.8 12.9 %copy-start.10 = (f32[512,768]{1,0:T(8,128)S(1)}, f32[512,768]{1,0:T(8,128)}, u32[]{:S(2)}) copy-start(f32[512,768]{1,0:T(8,128)} %copy-done.8) | copy-start | bytes 4718596
  439.7 5.5 %copy-start.12 = (f32[512,768]{1,0:T(8,128)S(1)}, f32[512,768]{1,0:T(8,128)}, u32[]{:S(2)}) copy-start(f32[512,768]{1,0:T(8,128)} %copy-done.11) | copy-start | bytes 4718596
  445.2 48.9 %copy-start.1 = (f32[5,768]{1,0:T(8,128)S(1)}, f32[5,768]{1,0:T(8,128)}, u32[]{:S(2)}) copy-start(f32[5,768]{1,0:T(8,128)} %param.33) | copy-start | bytes 46084
  445.9 48.2 %copy-start.13 = (f32[512,768]{1,0:T(8,128)}, f32[512,768]{1,0:T(8,128)S(1)}, u32[]{:S(2)}) copy-start(f32[512,768]{1,0:T(8,128)S(1)} %multiply_add_fusion) | copy-start | bytes 4718596
  (28 other events, 60.9 us)
Sparse Core Ops, SparseCore 0:
  12.6 31.2 all-gather.7
  49.4 55.5 all-gather.17
  106.5 27.0 all-gather.9
  135.6 17.4 all-gather.11
  174.4 28.4 all-gather.13
  221.7 37.8 reduce-scatter.5
  265.4 28.5 all-gather.15
  315.3 71.6 reduce-scatter.7
  423.0 69.1 reduce-scatter.9

commit v13 on v12

--- a/solution.py
+++ b/solution.py
@@ -371,8 +371,9 @@
             grad_fc2_bias,
             grad_table,
         ),
-        ("fsdp", "tp"),
-    )
+        "fsdp",
+    )
+    summed = lax.psum(summed, "tp")
     return (
         result.astype(jnp.bfloat16),
         grad_input,

time: 511 us -> 516 us (level)
  blocking collectives: 92.2 us -> 101 us
    psum x0 -> x1, blocking collectives: none -> 11.9 us  [on_device(): summed = lax.psum(summed, 'tp')]
  transfers between devices with their start and end apart: 12 -> 12, of which waited for: 6 -> 5; matrix products, arithmetic and copies ran while one was open for 23% -> 23% of each run, Pallas kernels for 21% -> 21%
where the time goes in v13:
time: 516 us; the launch traced here: 506 us
  Pallas kernels  104 us (20%)
  blocking collectives  101 us (20%)
  local copies, waits for them, and re-layouts  99 us (19%)
  waiting for transfers between devices  83.1 us (16%)
  matrix products  59.4 us (12%)
  other arithmetic  28.1 us (5%)
  starting transfers between devices  15.6 us (3%)
  between operations  15.4 us (3%)
    pallas_call x1, Pallas kernels, attn_backward(): pl.pallas_call(functools.partial(_bwd_kernel, scale), out_shape=shape, gr...  65.9 us
    psum x1, blocking collectives, on_device(): lax.psum((grad_ln1_gain, grad_ln1_bias, grad_qv_bias, grad_out_bias, grad...  38.8 us
    pallas_call x1, Pallas kernels, attn_forward(): pl.pallas_call(functools.partial(_fwd_kernel, scale), out_shape=(jax.Shap...  38.4 us
    all_gather x1, blocking collectives, on_device(): qkv_cols = lax.all_gather(qkv_weight, 'fsdp', axis=1, tiled=True)  35.2 us
    all_gather x1, waiting for transfers between devices, on_device(): normed_rows = lax.all_gather(normed_two, 'tp', axis=0, tiled=True)  27.8 us
    unnamed x89, local copies, waits for them, and re-layouts  27 us
    reduce_scatter x1, waiting for transfers between devices, on_device(): lax.psum_scatter(matmul_nt(grad_before, fc1_part).astype(jnp.bfloat16), '...  23.3 us
    dot_general x3, matrix products, matmul_nt(): lax.dot_general(left, right, (((1,), (1,)), ((), ())), preferred_element_...  15.7 us
  transfers between devices with their start and end apart: 12, of which 5 were waited for; matrix products, arithmetic and copies ran while one was open for 23% of the time, Pallas kernels for 21%

profile of v13, /device:TPU:0, one launch (start us, length us, event | category | flops | bytes accessed | tf_op | source)
XLA Modules:
  0.0 506.1 jit_solution(5073199767784080200)
XLA Ops:
  13.3 35.2 %all_gather.24 = bf16[3,768,192]{2,1,0:T(8,128)(2,1)S(1)} all-gather(bf16[3,96,192]{2,1,0:T(8,128)(2,1)S(1)} %copy-done.25), channel_id=1, replica_groups=mesh['fsdp'=8,'tp'=4] {'fsdp'}, dimensions={1}, use_global_device_ids=true | all-gather | bytes 995328 | tf_op jit(solution)/shard_map/all_gather | solution.py:209
  52.8 4.7 all-to-all-start
  59.3 4.7 convolution_bitcast_fusion
  75.9 4.7 fusion.11
  80.6 38.4 %shard_map.280 = (bf16[4,3,512,64]{3,2,1,0:T(8,128)(2,1)S(1)}, f32[3,2048,1]{2,1,0:T(8,128)}) custom-call(s32[1]{0:T(128)S(6)} %copy.160.prefix_ref, bf16[3,2048,64]{2,1,0:T(8,128)(2,1)S(1)} %get-tuple-element.164.q_ref, bf16[3,2048,64]{2,1,0:T(8,128)(2,1)S(1)} %bitcast.106, bf16[3,2048,64]{2,1,0:T(8,128)(2,1)} %get-tuple-element.165.v_ref), custom_call_target="tpu_custom_call" | custom-call | flops 3221225472 | bytes 3145728 | tf_op jit(solution)/shard_map/pallas_call | solution.py:135
  146.2 6.9 %all-gather.12.cloned.1.call-done = bf16[768,768]{1,0:T(8,128)(2,1)} async-done(((bf16[192,768]{1,0:T(8,128)(2,1)}), bf16[768,768]{1,0:T(8,128)(2,1)}) %all-gather.12.cloned.1.call-update) | async-done | bytes 1179664 | tf_op jit(solution)/shard_map/all_gather | solution.py:245
  154.5 15.2 %all_to_all.20 = bf16[4,3,512,64]{2,3,1,0:T(8,128)(2,1)S(1)} all-to-all(bf16[4,3,512,64]{2,3,1,0:T(8,128)(2,1)} %copy.112), channel_id=1, replica_groups=mesh['fsdp'=8,'tp'=4] {'tp'}, dimensions={0} | all-to-all | bytes 1572864 | tf_op jit(solution)/shard_map/all_to_all | solution.py:249
  175.1 27.8 %all-gather.14.cloned.1.call-done = bf16[2048,768]{1,0:T(8,128)(2,1)} async-done(((bf16[512,768]{1,0:T(8,128)(2,1)}), bf16[2048,768]{1,0:T(8,128)(2,1)}) %all-gather.14.cloned.1.call-update) | async-done | bytes 3145744 | tf_op jit(solution)/shard_map/all_gather | solution.py:264
  203.0 5.1 fusion.29
  208.1 7.8 %convert_reduce_fusion = (f32[768]{0:T(1024)S(1)}, bf16[2048,768]{1,0:T(8,128)(2,1)S(1)}, bf16[2048,768]{1,0:T(8,128)(2,1)}) fusion(f32[2048,768]{1,0:T(8,128)S(1)} %fusion.29, f32[768]{0:T(1024)S(1)} %dynamic_slice.7, bf16[2048,768]{1,0:T(8,128)(2,1)S(1)} %copy-done.33, bf16[768,768]{0,1:T(8,128)(2,1)S(1)} %bitcast.125), kind=kOutput, calls=%fused_computation.9 | convolution fusion | flops 2455239936 | bytes 16914432 | tf_op jit(solution)/shard_map/dot_general | solution.py:37
  222.1 6.6 %convolution_convert_fusion = bf16[2048,768]{1,0:T(8,128)(2,1)} fusion(bf16[2048,768]{1,0:T(8,128)(2,1)} %get-tuple-element.153, bf16[768,768]{0,1:T(8,128)(2,1)} %bitcast.124), kind=kOutput, calls=%fused_computation.14 | convolution fusion | flops 2417491968 | bytes 7471104 | tf_op jit(solution)/shard_map/dot_general | solution.py:267
  236.3 23.3 %reduce-scatter.6.cloned.1.call-done = bf16[512,768]{1,0:T(8,128)(2,1)} async-done(((bf16[2048,768]{1,0:T(8,128)(2,1)}), bf16[512,768]{1,0:T(8,128)(2,1)}) %reduce-scatter.6.cloned.1.call-update) | async-done | bytes 786448 | tf_op jit(solution)/shard_map/reduce_scatter | solution.py:278
  279.2 14.8 %all-gather.16.cloned.1.call-done = bf16[2048,768]{1,0:T(8,128)(2,1)} async-done(((bf16[512,768]{1,0:T(8,128)(2,1)}), bf16[2048,768]{1,0:T(8,128)(2,1)}) %all-gather.16.cloned.1.call-update) | async-done | bytes 3145744 | tf_op jit(solution)/shard_map/all_gather | solution.py:290
  294.0 4.6 copy.117
  302.6 8.0 %pad_maximum_fusion = bf16[8,165888]{1,0:T(8,128)(2,1)} fusion(bf16[8,73728]{1,0:T(8,128)(2,1)} %reshape.184, bf16[8,73728]{1,0:T(8,128)(2,1)S(1)} %copy-done.14, bf16[8,18432]{1,0:T(8,128)(2,1)S(1)} %reshape.182), kind=kLoop, calls=%fused_computation.22 | loop fusion | flops 7962624 | bytes 5308416 | tf_op jit(solution)/shard_map/concatenate | solution.py:308
  315.2 5.0 all-to-all-start.2
  328.1 65.9 %shard_map.281 = bf16[4,3,3,512,64]{4,3,2,1,0:T(8,128)(2,1)} custom-call(s32[1]{0:T(128)S(6)} %copy.160.prefix_ref, bf16[3,2048,64]{2,1,0:T(8,128)(2,1)S(1)} %copy-done.3, bf16[3,2048,64]{2,1,0:T(8,128)(2,1)S(1)} %bitcast.107, bf16[3,2048,64]{2,1,0:T(8,128)(2,1)S(1)} %copy-done.4, bf16[3,2048,64]{2,1,0:T(8,128)(2,1)} %bitcast.121, ...), custom_call_target="tpu_custom_call" | custom-call | flops 8053063680 | bytes 6291456 | tf_op jit(solution)/shard_map/pallas_call | solution.py:162
  400.4 6.0 %copy.121 = bf16[4,3,3,512,64]{3,4,2,1,0:T(8,128)(2,1)} copy(bf16[4,3,3,512,64]{4,3,2,1,0:T(8,128)(2,1)} %shard_map.281) | data formatting | bytes 4718592 | tf_op jit(solution)/shard_map/optimization_barrier | solution.py:322
  406.4 4.8 all-to-all-start.3
  411.2 5.8 %fusion.32 = f32[3,3,64,768,1]{3,2,1,0,4:T(8,128)} fusion(bf16[4,3,3,512,64]{4,3,2,1,0:T(8,128)(2,1)} %shard_map.281, bf16[4,512,768,1,1]{2,1,4,3,0:T(8,128)(2,1)S(1)} %bitcast.118), kind=kOutput, calls=%fused_computation.84 | convolution fusion | flops 1811939328 | bytes 7274496 | tf_op jit(solution)/shard_map/trd,tkhre->kdhe/dot_general | solution.py:335
  430.3 9.4 %all-to-all-done.3 = bf16[4,3,3,512,64]{3,4,2,1,0:T(8,128)(2,1)} async-done(((bf16[4,3,3,512,64]{3,4,2,1,0:T(8,128)(2,1)}), bf16[4,3,3,512,64]{3,4,2,1,0:T(8,128)(2,1)}, u32[]{:S(2)}, u32[]{:S(2)}) %all-to-all-start.3) | async-done | bytes 2359328 | tf_op jit(solution)/shard_map/all_to_all | solution.py:338
  439.7 5.4 %fusion.14 = (f32[768]{0:T(1024)S(1)}, f32[512]{0:T(512)S(1)}, f32[512]{0:T(512)S(1)}, f32[768]{0:T(1024)S(1)}, f32[512,768,1,1,1]{1,0,4,3,2:T(8,128)S(1)}) fusion(f32[512,768]{1,0:T(8,128)S(1)} %copy-done.10, f32[512]{0:T(512)S(1)} %add_rsqrt_fusion.1, f32[512]{0:T(512)S(1)} %broadcast_multiply_fusion.5, f32[768]{0:T(1024)S(1)} %copy-done.28, ...), kind=kOutput, calls=%fused_computation.35 | convolution fusion | flops 1815475712 | bytes 9061376 | tf_op jit(solution)/shard_map/skhre,skdhe->rd/dot_general | solution.py:340
  446.6 38.8 %all-reduce = (f32[768]{0:T(1024)S(1)}, f32[768]{0:T(1024)S(1)}, f32[2,768]{1,0:T(2,128)S(1)}, f32[768]{0:T(1024)S(1)}, f32[768]{0:T(1024)S(1)}, /*index=5*/f32[...) all-reduce(f32[768]{0:T(1024)S(1)} %get-tuple-element.121, ...), channel_id=1, replica_groups=mesh['fsdp'=8,'tp'=4] {'fsdp'}, use_global_device_ids=true, to_apply=%region_13.0 | all-reduce | flops 13056 | bytes 104448 | tf_op jit(solution)/shard_map/psum | solution.py:362
  485.4 11.9 %all-reduce.1 = (f32[768]{0:T(1024)}, f32[768]{0:T(1024)}, f32[2,768]{1,0:T(2,128)}, f32[768]{0:T(1024)}, f32[768]{0:T(1024)}, /*index=5*/f32[768]{0:T(1024)}, f32[3072]{0:T(1024)}, f32[768]{0:T(1024)}, f32[5,768]{1,0:T(8,128)}) all-reduce(f32[768]{0:T(1024)S(1)} %get-tuple-element.131, ...), channel_id=1, replica_groups=mesh['fsdp'=8,'tp'=4] {'tp'}, use_global_device_ids=true, to_apply=%region_14.0 | all-reduce | flops 13056 | bytes 104448 | tf_op jit(solution)/shard_map/psum | solution.py:376
  (188 shorter events, 129.7 us)
Async XLA Ops:
  7.2 42.0 %all-gather.8.cloned.1.call-start = ((), (), s32[]{:S(2)}) async-start(), calls=%async_computation.7 | async-start | bytes 3932160 | tf_op jit(solution)/shard_map/all_gather | solution.py:218
  12.4 107.8 %all-gather.18.cloned.1.call-start = ((), (), s32[]{:S(2)}) async-start(), calls=%async_computation.14 | async-start | bytes 2985984 | tf_op jit(solution)/shard_map/all_gather | solution.py:223
  49.3 96.9 %all-gather.10.cloned.1.call-start = ((), (), s32[]{:S(2)}) async-start(), calls=%async_computation.8 | async-start | bytes 3932160 | tf_op jit(solution)/shard_map/all_gather | solution.py:226
  52.8 67.4 %all-to-all-start = ((bf16[4,3,768,192]{2,3,1,0:T(8,128)(2,1)}), bf16[4,3,768,192]{2,3,1,0:T(8,128)(2,1)}, u32[]{:S(2)}, u32[]{:S(2)}) async-start(bf16[4,3,768,192]{2,3,1,0:T(8,128)(2,1)} %broadcast_in_dim.6), calls=%async_computation | async-start | bytes 7077888 | tf_op jit(solution)/shard_map/all_to_all | solution.py:225
  57.5 95.6 %all-gather.12.cloned.1.call-start = ((), (), s32[]{:S(2)}) async-start(), calls=%async_computation.9 | async-start | bytes 1474560 | tf_op jit(solution)/shard_map/all_gather | solution.py:245
  130.8 72.1 %all-gather.14.cloned.1.call-start = ((), (), s32[]{:S(2)}) async-start(), calls=%async_computation.10 | async-start | bytes 3932160 | tf_op jit(solution)/shard_map/all_gather | solution.py:264
  153.1 16.6 %copy-start.36 = (f32[768]{0:T(1024)S(1)}, f32[768]{0:T(1024)}, u32[]{:S(2)}) copy-start(f32[768]{0:T(1024)} %param.28) | copy-start | bytes 9220
  154.5 15.2 %copy-start.9 = (f32[512,768]{1,0:T(8,128)S(1)}, f32[512,768]{1,0:T(8,128)}, u32[]{:S(2)}) copy-start(f32[512,768]{1,0:T(8,128)} %copy-done.8) | copy-start | bytes 4718596
  174.3 85.4 %reduce-scatter.6.cloned.1.call-start = ((), (), s32[]{:S(2)}) async-start(), calls=%async_computation.11 | async-start | bytes 3932160 | tf_op jit(solution)/shard_map/reduce_scatter | solution.py:278
  203.0 5.1 %copy-start.22 = (bf16[768,8,96]{0,2,1:T(8,128)(2,1)S(1)}, bf16[768,8,96]{0,2,1:T(8,128)(2,1)}, u32[]{:S(2)}) copy-start(bf16[768,8,96]{0,2,1:T(8,128)(2,1)} %copy.111) | copy-start | bytes 3538948
  203.0 5.1 %copy-start.33 = (bf16[2048,768]{1,0:T(8,128)(2,1)S(1)}, bf16[2048,768]{1,0:T(8,128)(2,1)}, u32[]{:S(2)}) copy-start(bf16[2048,768]{1,0:T(8,128)(2,1)} %all-gather.10.cloned.1.call-done) | copy-start | bytes 9437188
  208.1 9.6 %copy-start.19 = (bf16[768,768]{1,0:T(8,128)(2,1)S(1)}, bf16[768,768]{1,0:T(8,128)(2,1)}, u32[]{:S(2)}) copy-start(bf16[768,768]{1,0:T(8,128)(2,1)} %reshape_reshape.8) | copy-start | bytes 3538948
  221.6 72.3 %all-gather.16.cloned.1.call-start = ((), (), s32[]{:S(2)}) async-start(), calls=%async_computation.12 | async-start | bytes 3932160 | tf_op jit(solution)/shard_map/all_gather | solution.py:290
  222.1 6.7 %copy-start.34 = (bf16[2048,768]{1,0:T(8,128)(2,1)S(1)}, bf16[2048,768]{1,0:T(8,128)(2,1)}, u32[]{:S(2)}) copy-start(bf16[2048,768]{1,0:T(8,128)(2,1)} %all-gather.10.cloned.1.call-done) | copy-start | bytes 9437188
  222.1 6.7 %copy-start.39 = (bf16[2048,768]{1,0:T(8,128)(2,1)S(1)}, bf16[2048,768]{1,0:T(8,128)(2,1)}, u32[]{:S(2)}) copy-start(bf16[2048,768]{1,0:T(8,128)(2,1)} %get-tuple-element.153) | copy-start | bytes 9437188
  265.3 132.5 %reduce-scatter.8.cloned.1.call-start = ((), (), s32[]{:S(2)}) async-start(), calls=%async_computation.13 | async-start | bytes 2985984 | tf_op jit(solution)/shard_map/reduce_scatter | solution.py:309
  315.2 5.0 copy-start.21
  315.2 78.9 %all-to-all-start.2 = ((bf16[4,512,768]{2,1,0:T(8,128)(2,1)}), bf16[4,512,768]{2,1,0:T(8,128)(2,1)}, u32[]{:S(2)}, u32[]{:S(2)}) async-start(bf16[4,512,768]{2,1,0:T(8,128)(2,1)} %bitcast.114), calls=%async_computation.3 | async-start | bytes 6291456 | tf_op jit(solution)/shard_map/all_to_all | solution.py:292
  406.4 33.3 %all-to-all-start.3 = ((bf16[4,3,3,512,64]{3,4,2,1,0:T(8,128)(2,1)}), bf16[4,3,3,512,64]{3,4,2,1,0:T(8,128)(2,1)}, u32[]{:S(2)}, u32[]{:S(2)}) async-start(bf16[4,3,3,512,64]{3,4,2,1,0:T(8,128)(2,1)} %copy.121), calls=%async_computation.5 | async-start | bytes 4718592 | tf_op jit(solution)/shard_map/all_to_all | solution.py:338
  411.2 86.1 %reduce-scatter.10.cloned.1.call-start = ((), (), s32[]{:S(2)}) async-start(), calls=%async_computation.15 | async-start | bytes 2211840
  426.8 12.9 %copy-start.10 = (f32[512,768]{1,0:T(8,128)S(1)}, f32[512,768]{1,0:T(8,128)}, u32[]{:S(2)}) copy-start(f32[512,768]{1,0:T(8,128)} %copy-done.8) | copy-start | bytes 4718596
  439.7 5.5 %copy-start.12 = (f32[512,768]{1,0:T(8,128)S(1)}, f32[512,768]{1,0:T(8,128)}, u32[]{:S(2)}) copy-start(f32[512,768]{1,0:T(8,128)} %copy-done.11) | copy-start | bytes 4718596
  445.2 54.0 %copy-start.1 = (f32[5,768]{1,0:T(8,128)S(1)}, f32[5,768]{1,0:T(8,128)}, u32[]{:S(2)}) copy-start(f32[5,768]{1,0:T(8,128)} %param.33) | copy-start | bytes 46084
  445.9 53.3 %copy-start.13 = (f32[512,768]{1,0:T(8,128)}, f32[512,768]{1,0:T(8,128)S(1)}, u32[]{:S(2)}) copy-start(f32[512,768]{1,0:T(8,128)S(1)} %multiply_add_fusion) | copy-start | bytes 4718596
  (28 other events, 60.9 us)
Sparse Core Ops, SparseCore 0:
  12.6 31.2 all-gather.7
  49.4 55.5 all-gather.17
  106.5 27.0 all-gather.9
  135.6 17.4 all-gather.11
  174.4 28.4 all-gather.13
  221.8 37.8 reduce-scatter.5
  265.4 28.4 all-gather.15
  315.3 71.3 reduce-scatter.7
  423.0 69.6 reduce-scatter.9

commit v14 on v12

--- a/solution.py
+++ b/solution.py
@@ -56,7 +56,7 @@
     return jnp.where(allowed[None], raw, NEG_FILL)
 
 
-ATT_QB = 256
+ATT_QB = 512
 
 
 def _mask(prefix_len, qb, rows, cols):

time: 511 us -> 495 us (0.969); the launches traced: 501 us -> 491 us
  Pallas kernels: 105 us -> 92.9 us
    pallas_call x1, Pallas kernels: 65.9 us -> 48.3 us  [attn_backward(): pl.pallas_call(functools.partial(_bwd_kernel, scale), out_shape=shape, gr...]
    reduce_scatter x1, waiting for transfers between devices: 0.01 us -> 6.56 us  [on_device(): lax.psum_scatter(dense_packed.reshape(-1, grad_fc1.shape[1]).astype(jnp.b...]
    pallas_call x1, Pallas kernels: 38.6 us -> 44.6 us  [attn_forward(): pl.pallas_call(functools.partial(_fwd_kernel, scale), out_shape=(jax.Shap...]
  transfers between devices with their start and end apart: 12 -> 12, of which waited for: 6 -> 7; matrix products, arithmetic and copies ran while one was open for 23% -> 23% of each run, Pallas kernels for 21% -> 19%
where the time goes in v14:
time: 495 us; the launch traced here: 491 us
  local copies, waits for them, and re-layouts  99.1 us (20%)
  Pallas kernels  92.9 us (19%)
  blocking collectives  91.1 us (18%)
  waiting for transfers between devices  88.5 us (18%)
  matrix products  59.3 us (12%)
  other arithmetic  28.2 us (6%)
  starting transfers between devices  16.1 us (3%)
  between operations  15.3 us (3%)
    pallas_call x1, Pallas kernels, attn_backward(): pl.pallas_call(functools.partial(_bwd_kernel, scale), out_shape=shape, gr...  48.3 us
    pallas_call x1, Pallas kernels, attn_forward(): pl.pallas_call(functools.partial(_fwd_kernel, scale), out_shape=(jax.Shap...  44.6 us
    psum x1, blocking collectives, on_device(): lax.psum((grad_ln1_gain, grad_ln1_bias, grad_qv_bias, grad_out_bias, grad...  40.7 us
    all_gather x1, blocking collectives, on_device(): qkv_cols = lax.all_gather(qkv_weight, 'fsdp', axis=1, tiled=True)  35.2 us
    all_gather x1, waiting for transfers between devices, on_device(): normed_rows = lax.all_gather(normed_two, 'tp', axis=0, tiled=True)  27.8 us
    unnamed x89, local copies, waits for them, and re-layouts  27 us
    reduce_scatter x1, waiting for transfers between devices, on_device(): lax.psum_scatter(matmul_nt(grad_before, fc1_part).astype(jnp.bfloat16), '...  23.3 us
    dot_general x3, matrix products, matmul_nt(): lax.dot_general(left, right, (((1,), (1,)), ((), ())), preferred_element_...  15.8 us
  transfers between devices with their start and end apart: 12, of which 7 were waited for; matrix products, arithmetic and copies ran while one was open for 23% of the time, Pallas kernels for 19%

profile of v14, /device:TPU:0, one launch (start us, length us, event | category | flops | bytes accessed | tf_op | source)
XLA Modules:
  0.0 490.5 jit_solution(13751616481885880738)
XLA Ops:
  13.3 35.2 %all_gather.24 = bf16[3,768,192]{2,1,0:T(8,128)(2,1)S(1)} all-gather(bf16[3,96,192]{2,1,0:T(8,128)(2,1)S(1)} %copy-done.25), channel_id=1, replica_groups=mesh['fsdp'=8,'tp'=4] {'fsdp'}, dimensions={1}, use_global_device_ids=true | all-gather | bytes 995328 | tf_op jit(solution)/shard_map/all_gather | solution.py:209
  52.8 4.7 all-to-all-start
  59.5 4.6 convolution_bitcast_fusion
  76.1 4.8 fusion.11
  80.9 44.6 %shard_map.280 = (bf16[4,3,512,64]{3,2,1,0:T(8,128)(2,1)S(1)}, f32[3,2048,1]{2,1,0:T(8,128)}) custom-call(s32[1]{0:T(128)S(6)} %copy.160.prefix_ref, bf16[3,2048,64]{2,1,0:T(8,128)(2,1)S(1)} %get-tuple-element.155.q_ref, bf16[3,2048,64]{2,1,0:T(8,128)(2,1)S(1)} %bitcast.106, bf16[3,2048,64]{2,1,0:T(8,128)(2,1)} %get-tuple-element.156.v_ref), custom_call_target="tpu_custom_call" | custom-call | flops 3221225472 | bytes 3145728 | tf_op jit(solution)/shard_map/pallas_call | solution.py:135
  157.1 15.2 %all_to_all.20 = bf16[4,3,512,64]{2,3,1,0:T(8,128)(2,1)S(1)} all-to-all(bf16[4,3,512,64]{2,3,1,0:T(8,128)(2,1)} %copy.112), channel_id=1, replica_groups=mesh['fsdp'=8,'tp'=4] {'tp'}, dimensions={0} | all-to-all | bytes 1572864 | tf_op jit(solution)/shard_map/all_to_all | solution.py:249
  177.7 27.8 %all-gather.14.cloned.1.call-done = bf16[2048,768]{1,0:T(8,128)(2,1)} async-done(((bf16[512,768]{1,0:T(8,128)(2,1)}), bf16[2048,768]{1,0:T(8,128)(2,1)}) %all-gather.14.cloned.1.call-update) | async-done | bytes 3145744 | tf_op jit(solution)/shard_map/all_gather | solution.py:264
  205.6 5.1 %fusion.29 = f32[2048,768]{1,0:T(8,128)S(1)} fusion(bf16[2048,768]{1,0:T(8,128)(2,1)} %all-gather.14.cloned.1.call-done, bf16[768,768]{1,0:T(8,128)(2,1)} %reshape_reshape.8), kind=kOutput, calls=%fused_computation.81 | convolution fusion | flops 2415919104 | bytes 10616832 | tf_op jit(solution)/shard_map/dot_general | solution.py:265
  210.7 7.8 %convert_reduce_fusion = (f32[768]{0:T(1024)S(1)}, bf16[2048,768]{1,0:T(8,128)(2,1)S(1)}, bf16[2048,768]{1,0:T(8,128)(2,1)}) fusion(f32[2048,768]{1,0:T(8,128)S(1)} %fusion.29, f32[768]{0:T(1024)S(1)} %dynamic_slice.7, bf16[2048,768]{1,0:T(8,128)(2,1)S(1)} %copy-done.33, bf16[768,768]{0,1:T(8,128)(2,1)S(1)} %bitcast.125), kind=kOutput, calls=%fused_computation.9 | convolution fusion | flops 2455239936 | bytes 16914432 | tf_op jit(solution)/shard_map/dot_general | solution.py:37
  224.7 6.6 %convolution_convert_fusion = bf16[2048,768]{1,0:T(8,128)(2,1)} fusion(bf16[2048,768]{1,0:T(8,128)(2,1)} %get-tuple-element.144, bf16[768,768]{0,1:T(8,128)(2,1)} %bitcast.124), kind=kOutput, calls=%fused_computation.14 | convolution fusion | flops 2417491968 | bytes 7471104 | tf_op jit(solution)/shard_map/dot_general | solution.py:267
  238.9 23.3 %reduce-scatter.6.cloned.1.call-done = bf16[512,768]{1,0:T(8,128)(2,1)} async-done(((bf16[2048,768]{1,0:T(8,128)(2,1)}), bf16[512,768]{1,0:T(8,128)(2,1)}) %reduce-scatter.6.cloned.1.call-update) | async-done | bytes 786448 | tf_op jit(solution)/shard_map/reduce_scatter | solution.py:278
  281.8 14.8 %all-gather.16.cloned.1.call-done = bf16[2048,768]{1,0:T(8,128)(2,1)} async-done(((bf16[512,768]{1,0:T(8,128)(2,1)}), bf16[2048,768]{1,0:T(8,128)(2,1)}) %all-gather.16.cloned.1.call-update) | async-done | bytes 3145744 | tf_op jit(solution)/shard_map/all_gather | solution.py:290
  296.6 4.6 copy.117
  305.2 8.0 %pad_maximum_fusion = bf16[8,165888]{1,0:T(8,128)(2,1)} fusion(bf16[8,73728]{1,0:T(8,128)(2,1)} %reshape.184, bf16[8,73728]{1,0:T(8,128)(2,1)S(1)} %copy-done.14, bf16[8,18432]{1,0:T(8,128)(2,1)S(1)} %reshape.182), kind=kLoop, calls=%fused_computation.22 | loop fusion | flops 7962624 | bytes 5308416 | tf_op jit(solution)/shard_map/concatenate | solution.py:308
  313.2 4.5 convert_element_type.97
  317.8 5.0 %all-to-all-start.2 = ((bf16[4,512,768]{2,1,0:T(8,128)(2,1)}), bf16[4,512,768]{2,1,0:T(8,128)(2,1)}, u32[]{:S(2)}, u32[]{:S(2)}) async-start(bf16[4,512,768]{2,1,0:T(8,128)(2,1)} %bitcast.114), calls=%async_computation.3 | async-start | bytes 6291456 | tf_op jit(solution)/shard_map/all_to_all | solution.py:292
  330.7 48.3 %shard_map.281 = bf16[4,3,3,512,64]{4,3,2,1,0:T(8,128)(2,1)} custom-call(s32[1]{0:T(128)S(6)} %copy.160.prefix_ref, bf16[3,2048,64]{2,1,0:T(8,128)(2,1)S(1)} %copy-done.3, bf16[3,2048,64]{2,1,0:T(8,128)(2,1)S(1)} %bitcast.107, bf16[3,2048,64]{2,1,0:T(8,128)(2,1)S(1)} %copy-done.4, bf16[3,2048,64]{2,1,0:T(8,128)(2,1)} %bitcast.121, ...), custom_call_target="tpu_custom_call" | custom-call | flops 8053063680 | bytes 6291456 | tf_op jit(solution)/shard_map/pallas_call | solution.py:162
  382.9 6.6 %reduce-scatter.8.cloned.1.call-done = bf16[216,768]{1,0:T(8,128)(2,1)} async-done(((bf16[1728,768]{1,0:T(8,128)(2,1)}), bf16[216,768]{1,0:T(8,128)(2,1)}) %reduce-scatter.8.cloned.1.call-update) | async-done | bytes 331792 | tf_op jit(solution)/shard_map/reduce_scatter | solution.py:309
  392.0 6.0 %copy.121 = bf16[4,3,3,512,64]{3,4,2,1,0:T(8,128)(2,1)} copy(bf16[4,3,3,512,64]{4,3,2,1,0:T(8,128)(2,1)} %shard_map.281) | data formatting | bytes 4718592 | tf_op jit(solution)/shard_map/optimization_barrier | solution.py:322
  398.0 4.8 all-to-all-start.3
  403.1 5.8 %fusion.32 = f32[3,3,64,768,1]{3,2,1,0,4:T(8,128)} fusion(bf16[4,3,3,512,64]{4,3,2,1,0:T(8,128)(2,1)} %shard_map.281, bf16[4,512,768,1,1]{2,1,4,3,0:T(8,128)(2,1)S(1)} %bitcast.118), kind=kOutput, calls=%fused_computation.84 | convolution fusion | flops 1811939328 | bytes 7274496 | tf_op jit(solution)/shard_map/trd,tkhre->kdhe/dot_general | solution.py:335
  422.2 9.1 %all-to-all-done.3 = bf16[4,3,3,512,64]{3,4,2,1,0:T(8,128)(2,1)} async-done(((bf16[4,3,3,512,64]{3,4,2,1,0:T(8,128)(2,1)}), bf16[4,3,3,512,64]{3,4,2,1,0:T(8,128)(2,1)}, u32[]{:S(2)}, u32[]{:S(2)}) %all-to-all-start.3) | async-done | bytes 2359328 | tf_op jit(solution)/shard_map/all_to_all | solution.py:338
  431.3 5.4 %fusion.14 = (f32[768]{0:T(1024)S(1)}, f32[512]{0:T(512)S(1)}, f32[512]{0:T(512)S(1)}, f32[768]{0:T(1024)S(1)}, f32[512,768,1,1,1]{1,0,4,3,2:T(8,128)S(1)}) fusion(f32[512,768]{1,0:T(8,128)S(1)} %copy-done.10, f32[512]{0:T(512)S(1)} %add_rsqrt_fusion.1, f32[512]{0:T(512)S(1)} %broadcast_multiply_fusion.5, f32[768]{0:T(1024)S(1)} %copy-done.28, ...), kind=kOutput, calls=%fused_computation.35 | convolution fusion | flops 1815475712 | bytes 9061376 | tf_op jit(solution)/shard_map/skhre,skdhe->rd/dot_general | solution.py:340
  438.2 40.7 %all-reduce = (f32[768]{0:T(1024)}, f32[768]{0:T(1024)}, f32[2,768]{1,0:T(2,128)}, f32[768]{0:T(1024)}, f32[768]{0:T(1024)}, /*index=5*/f32[768]{0:T(1024)}, f32[3072]{0:T(1024)}, f32[768]{0:T(1024)}, f32[5,768]{1,0:T(8,128)}) all-reduce(f32[768]{0:T(1024)S(1)} %get-tuple-element.121, ...), channel_id=1, replica_groups=mesh['fsdp'=8,'tp'=4] {'fsdp','tp'}, use_global_device_ids=true, to_apply=%region_13.0 | all-reduce | flops 13056 | bytes 104448 | tf_op jit(solution)/shard_map/psum | solution.py:362
  (187 shorter events, 131.7 us)
Async XLA Ops:
  7.2 42.0 %all-gather.8.cloned.1.call-start = ((), (), s32[]{:S(2)}) async-start(), calls=%async_computation.7 | async-start | bytes 3932160 | tf_op jit(solution)/shard_map/all_gather | solution.py:218
  12.4 114.2 %all-gather.18.cloned.1.call-start = ((), (), s32[]{:S(2)}) async-start(), calls=%async_computation.14 | async-start | bytes 2985984 | tf_op jit(solution)/shard_map/all_gather | solution.py:223
  49.3 103.3 %all-gather.10.cloned.1.call-start = ((), (), s32[]{:S(2)}) async-start(), calls=%async_computation.8 | async-start | bytes 3932160 | tf_op jit(solution)/shard_map/all_gather | solution.py:226
  52.8 73.8 %all-to-all-start = ((bf16[4,3,768,192]{2,3,1,0:T(8,128)(2,1)}), bf16[4,3,768,192]{2,3,1,0:T(8,128)(2,1)}, u32[]{:S(2)}, u32[]{:S(2)}) async-start(bf16[4,3,768,192]{2,3,1,0:T(8,128)(2,1)} %broadcast_in_dim.6), calls=%async_computation | async-start | bytes 7077888 | tf_op jit(solution)/shard_map/all_to_all | solution.py:225
  57.6 98.2 %all-gather.12.cloned.1.call-start = ((), (), s32[]{:S(2)}) async-start(), calls=%async_computation.9 | async-start | bytes 1474560 | tf_op jit(solution)/shard_map/all_gather | solution.py:245
  137.3 68.3 %all-gather.14.cloned.1.call-start = ((), (), s32[]{:S(2)}) async-start(), calls=%async_computation.10 | async-start | bytes 3932160 | tf_op jit(solution)/shard_map/all_gather | solution.py:264
  155.7 16.6 %copy-start.36 = (f32[768]{0:T(1024)S(1)}, f32[768]{0:T(1024)}, u32[]{:S(2)}) copy-start(f32[768]{0:T(1024)} %param.28) | copy-start | bytes 9220
  157.1 15.2 %copy-start.9 = (f32[512,768]{1,0:T(8,128)S(1)}, f32[512,768]{1,0:T(8,128)}, u32[]{:S(2)}) copy-start(f32[512,768]{1,0:T(8,128)} %copy-done.8) | copy-start | bytes 4718596
  176.9 85.4 %reduce-scatter.6.cloned.1.call-start = ((), (), s32[]{:S(2)}) async-start(), calls=%async_computation.11 | async-start | bytes 3932160 | tf_op jit(solution)/shard_map/reduce_scatter | solution.py:278
  205.6 5.1 %copy-start.22 = (bf16[768,8,96]{0,2,1:T(8,128)(2,1)S(1)}, bf16[768,8,96]{0,2,1:T(8,128)(2,1)}, u32[]{:S(2)}) copy-start(bf16[768,8,96]{0,2,1:T(8,128)(2,1)} %copy.111) | copy-start | bytes 3538948
  205.6 5.1 %copy-start.33 = (bf16[2048,768]{1,0:T(8,128)(2,1)S(1)}, bf16[2048,768]{1,0:T(8,128)(2,1)}, u32[]{:S(2)}) copy-start(bf16[2048,768]{1,0:T(8,128)(2,1)} %all-gather.10.cloned.1.call-done) | copy-start | bytes 9437188
  210.6 9.6 %copy-start.19 = (bf16[768,768]{1,0:T(8,128)(2,1)S(1)}, bf16[768,768]{1,0:T(8,128)(2,1)}, u32[]{:S(2)}) copy-start(bf16[768,768]{1,0:T(8,128)(2,1)} %reshape_reshape.8) | copy-start | bytes 3538948
  224.2 72.3 %all-gather.16.cloned.1.call-start = ((), (), s32[]{:S(2)}) async-start(), calls=%async_computation.12 | async-start | bytes 3932160 | tf_op jit(solution)/shard_map/all_gather | solution.py:290
  224.7 6.7 %copy-start.34 = (bf16[2048,768]{1,0:T(8,128)(2,1)S(1)}, bf16[2048,768]{1,0:T(8,128)(2,1)}, u32[]{:S(2)}) copy-start(bf16[2048,768]{1,0:T(8,128)(2,1)} %all-gather.10.cloned.1.call-done) | copy-start | bytes 9437188
  224.7 6.6 %copy-start.39 = (bf16[2048,768]{1,0:T(8,128)(2,1)S(1)}, bf16[2048,768]{1,0:T(8,128)(2,1)}, u32[]{:S(2)}) copy-start(bf16[2048,768]{1,0:T(8,128)(2,1)} %get-tuple-element.144) | copy-start | bytes 9437188
  267.9 121.5 %reduce-scatter.8.cloned.1.call-start = ((), (), s32[]{:S(2)}) async-start(), calls=%async_computation.13 | async-start | bytes 2985984 | tf_op jit(solution)/shard_map/reduce_scatter | solution.py:309
  317.8 61.3 %all-to-all-start.2 = ((bf16[4,512,768]{2,1,0:T(8,128)(2,1)}), bf16[4,512,768]{2,1,0:T(8,128)(2,1)}, u32[]{:S(2)}, u32[]{:S(2)}) async-start(bf16[4,512,768]{2,1,0:T(8,128)(2,1)} %bitcast.114), calls=%async_computation.3 | async-start | bytes 6291456 | tf_op jit(solution)/shard_map/all_to_all | solution.py:292
  398.0 5.1 %copy-start.17 = (bf16[2048,768]{1,0:T(8,128)(2,1)S(1)}, bf16[2048,768]{1,0:T(8,128)(2,1)}, u32[]{:S(2)}) copy-start(bf16[2048,768]{1,0:T(8,128)(2,1)} %all-gather.8.cloned.1.call-done) | copy-start | bytes 9437188
  398.0 33.3 %all-to-all-start.3 = ((bf16[4,3,3,512,64]{3,4,2,1,0:T(8,128)(2,1)}), bf16[4,3,3,512,64]{3,4,2,1,0:T(8,128)(2,1)}, u32[]{:S(2)}, u32[]{:S(2)}) async-start(bf16[4,3,3,512,64]{3,4,2,1,0:T(8,128)(2,1)} %copy.121), calls=%async_computation.5 | async-start | bytes 4718592 | tf_op jit(solution)/shard_map/all_to_all | solution.py:338
  402.8 79.0 %reduce-scatter.10.cloned.1.call-start = ((), (), s32[]{:S(2)}) async-start(), calls=%async_computation.15 | async-start | bytes 2211840
  418.7 12.6 %copy-start.10 = (f32[512,768]{1,0:T(8,128)S(1)}, f32[512,768]{1,0:T(8,128)}, u32[]{:S(2)}) copy-start(f32[512,768]{1,0:T(8,128)} %copy-done.8) | copy-start | bytes 4718596
  431.3 5.4 %copy-start.12 = (f32[512,768]{1,0:T(8,128)S(1)}, f32[512,768]{1,0:T(8,128)}, u32[]{:S(2)}) copy-start(f32[512,768]{1,0:T(8,128)} %copy-done.11) | copy-start | bytes 4718596
  436.8 46.9 %copy-start.1 = (f32[5,768]{1,0:T(8,128)S(1)}, f32[5,768]{1,0:T(8,128)}, u32[]{:S(2)}) copy-start(f32[5,768]{1,0:T(8,128)} %param.33) | copy-start | bytes 46084
  437.5 46.3 %copy-start.13 = (f32[512,768]{1,0:T(8,128)}, f32[512,768]{1,0:T(8,128)S(1)}, u32[]{:S(2)}) copy-start(f32[512,768]{1,0:T(8,128)S(1)} %multiply_add_fusion) | copy-start | bytes 4718596
  (28 other events, 61.1 us)
Sparse Core Ops, SparseCore 0:
  12.6 31.2 all-gather.7
  49.4 55.5 all-gather.17
  106.5 27.0 all-gather.9
  137.4 18.2 all-gather.11
  177.0 28.4 all-gather.13
  224.4 37.8 reduce-scatter.5
  268.0 28.4 all-gather.15
  317.9 71.4 reduce-scatter.7
  414.9 66.9 reduce-scatter.9

commit v15 on v12

--- a/solution.py
+++ b/solution.py
@@ -57,6 +57,7 @@
 
 
 ATT_QB = 256
+ATT_QB_BACK = 512
 
 
 def _mask(prefix_len, qb, rows, cols):
@@ -151,7 +152,7 @@
 
 def attn_backward(prefix, q, k, v, grad_out, lse, scale, groups):
     heads, seq, hd = q.shape
-    qb = min(ATT_QB, seq // groups)
+    qb = min(ATT_QB_BACK, seq // groups)
     per = seq // groups // qb
     grid = (heads, seq // qb)
     q_spec = pl.BlockSpec((1, qb, hd), lambda h, i, p: (h, i, 0))

time: 511 us -> 498 us (0.975)
  Pallas kernels: 105 us -> 87 us
  waiting for transfers between devices: 86.7 us -> 92.2 us
    pallas_call x1, Pallas kernels: 65.9 us -> 48.3 us  [attn_backward(): pl.pallas_call(functools.partial(_bwd_kernel, scale), out_shape=shape, gr...]
    reduce_scatter x1, waiting for transfers between devices: 0.01 us -> 6.68 us  [on_device(): lax.psum_scatter(dense_packed.reshape(-1, grad_fc1.shape[1]).astype(jnp.b...]
  transfers between devices with their start and end apart: 12 -> 12, of which waited for: 6 -> 7; matrix products, arithmetic and copies ran while one was open for 23% -> 24% of each run, Pallas kernels for 21% -> 18%
where the time goes in v15:
time: 498 us; the launch traced here: 488 us
  local copies, waits for them, and re-layouts  99 us (20%)
  waiting for transfers between devices  92.2 us (19%)
  blocking collectives  91.2 us (18%)
  Pallas kernels  87 us (17%)
  matrix products  59.3 us (12%)
  other arithmetic  28.1 us (6%)
  starting transfers between devices  15.9 us (3%)
  between operations  15.5 us (3%)
    pallas_call x1, Pallas kernels, attn_backward(): pl.pallas_call(functools.partial(_bwd_kernel, scale), out_shape=shape, gr...  48.3 us
    psum x1, blocking collectives, on_device(): lax.psum((grad_ln1_gain, grad_ln1_bias, grad_qv_bias, grad_out_bias, grad...  40.7 us
    pallas_call x1, Pallas kernels, attn_forward(): pl.pallas_call(functools.partial(_fwd_kernel, scale), out_shape=(jax.Shap...  38.6 us
    all_gather x1, blocking collectives, on_device(): qkv_cols = lax.all_gather(qkv_weight, 'fsdp', axis=1, tiled=True)  35.2 us
    all_gather x1, waiting for transfers between devices, on_device(): normed_rows = lax.all_gather(normed_two, 'tp', axis=0, tiled=True)  27.8 us
    unnamed x89, local copies, waits for them, and re-layouts  27 us
    reduce_scatter x1, waiting for transfers between devices, on_device(): lax.psum_scatter(matmul_nt(grad_before, fc1_part).astype(jnp.bfloat16), '...  23.3 us
    dot_general x3, matrix products, matmul_nt(): lax.dot_general(left, right, (((1,), (1,)), ((), ())), preferred_element_...  15.7 us
  transfers between devices with their start and end apart: 12, of which 7 were waited for; matrix products, arithmetic and copies ran while one was open for 24% of the time, Pallas kernels for 18%

profile of v15, /device:TPU:0, one launch (start us, length us, event | category | flops | bytes accessed | tf_op | source)
XLA Modules:
  0.0 488.2 jit_solution(3771520865016461216)
XLA Ops:
  13.3 35.2 %all_gather.24 = bf16[3,768,192]{2,1,0:T(8,128)(2,1)S(1)} all-gather(bf16[3,96,192]{2,1,0:T(8,128)(2,1)S(1)} %copy-done.25), channel_id=1, replica_groups=mesh['fsdp'=8,'tp'=4] {'fsdp'}, dimensions={1}, use_global_device_ids=true | all-gather | bytes 995328 | tf_op jit(solution)/shard_map/all_gather | solution.py:210
  52.8 4.7 all-to-all-start
  59.3 4.6 convolution_bitcast_fusion
  75.9 4.7 fusion.11
  80.6 38.6 %shard_map.280 = (bf16[4,3,512,64]{3,2,1,0:T(8,128)(2,1)S(1)}, f32[3,2048,1]{2,1,0:T(8,128)}) custom-call(s32[1]{0:T(128)S(6)} %copy.160.prefix_ref, bf16[3,2048,64]{2,1,0:T(8,128)(2,1)S(1)} %get-tuple-element.155.q_ref, bf16[3,2048,64]{2,1,0:T(8,128)(2,1)S(1)} %bitcast.106, bf16[3,2048,64]{2,1,0:T(8,128)(2,1)} %get-tuple-element.156.v_ref), custom_call_target="tpu_custom_call" | custom-call | flops 3221225472 | bytes 3145728 | tf_op jit(solution)/shard_map/pallas_call | solution.py:136
  146.4 6.7 %all-gather.12.cloned.1.call-done = bf16[768,768]{1,0:T(8,128)(2,1)} async-done(((bf16[192,768]{1,0:T(8,128)(2,1)}), bf16[768,768]{1,0:T(8,128)(2,1)}) %all-gather.12.cloned.1.call-update) | async-done | bytes 1179664 | tf_op jit(solution)/shard_map/all_gather | solution.py:246
  154.5 15.2 %all_to_all.20 = bf16[4,3,512,64]{2,3,1,0:T(8,128)(2,1)S(1)} all-to-all(bf16[4,3,512,64]{2,3,1,0:T(8,128)(2,1)} %copy.112), channel_id=1, replica_groups=mesh['fsdp'=8,'tp'=4] {'tp'}, dimensions={0} | all-to-all | bytes 1572864 | tf_op jit(solution)/shard_map/all_to_all | solution.py:250
  175.1 27.8 %all-gather.14.cloned.1.call-done = bf16[2048,768]{1,0:T(8,128)(2,1)} async-done(((bf16[512,768]{1,0:T(8,128)(2,1)}), bf16[2048,768]{1,0:T(8,128)(2,1)}) %all-gather.14.cloned.1.call-update) | async-done | bytes 3145744 | tf_op jit(solution)/shard_map/all_gather | solution.py:265
  203.0 5.1 %fusion.29 = f32[2048,768]{1,0:T(8,128)S(1)} fusion(bf16[2048,768]{1,0:T(8,128)(2,1)} %all-gather.14.cloned.1.call-done, bf16[768,768]{1,0:T(8,128)(2,1)} %reshape_reshape.8), kind=kOutput, calls=%fused_computation.81 | convolution fusion | flops 2415919104 | bytes 10616832 | tf_op jit(solution)/shard_map/dot_general | solution.py:266
  208.0 7.8 %convert_reduce_fusion = (f32[768]{0:T(1024)S(1)}, bf16[2048,768]{1,0:T(8,128)(2,1)S(1)}, bf16[2048,768]{1,0:T(8,128)(2,1)}) fusion(f32[2048,768]{1,0:T(8,128)S(1)} %fusion.29, f32[768]{0:T(1024)S(1)} %dynamic_slice.7, bf16[2048,768]{1,0:T(8,128)(2,1)S(1)} %copy-done.33, bf16[768,768]{0,1:T(8,128)(2,1)S(1)} %bitcast.125), kind=kOutput, calls=%fused_computation.9 | convolution fusion | flops 2455239936 | bytes 16914432 | tf_op jit(solution)/shard_map/dot_general | solution.py:37
  222.1 6.6 %convolution_convert_fusion = bf16[2048,768]{1,0:T(8,128)(2,1)} fusion(bf16[2048,768]{1,0:T(8,128)(2,1)} %get-tuple-element.144, bf16[768,768]{0,1:T(8,128)(2,1)} %bitcast.124), kind=kOutput, calls=%fused_computation.14 | convolution fusion | flops 2417491968 | bytes 7471104 | tf_op jit(solution)/shard_map/dot_general | solution.py:268
  236.3 23.3 %reduce-scatter.6.cloned.1.call-done = bf16[512,768]{1,0:T(8,128)(2,1)} async-done(((bf16[2048,768]{1,0:T(8,128)(2,1)}), bf16[512,768]{1,0:T(8,128)(2,1)}) %reduce-scatter.6.cloned.1.call-update) | async-done | bytes 786448 | tf_op jit(solution)/shard_map/reduce_scatter | solution.py:279
  279.2 14.8 %all-gather.16.cloned.1.call-done = bf16[2048,768]{1,0:T(8,128)(2,1)} async-done(((bf16[512,768]{1,0:T(8,128)(2,1)}), bf16[2048,768]{1,0:T(8,128)(2,1)}) %all-gather.16.cloned.1.call-update) | async-done | bytes 3145744 | tf_op jit(solution)/shard_map/all_gather | solution.py:291
  294.0 4.6 copy.117
  302.6 8.0 %pad_maximum_fusion = bf16[8,165888]{1,0:T(8,128)(2,1)} fusion(bf16[8,73728]{1,0:T(8,128)(2,1)} %reshape.184, bf16[8,73728]{1,0:T(8,128)(2,1)S(1)} %copy-done.14, bf16[8,18432]{1,0:T(8,128)(2,1)S(1)} %reshape.182), kind=kLoop, calls=%fused_computation.22 | loop fusion | flops 7962624 | bytes 5308416 | tf_op jit(solution)/shard_map/concatenate | solution.py:309
  315.2 5.0 %all-to-all-start.2 = ((bf16[4,512,768]{2,1,0:T(8,128)(2,1)}), bf16[4,512,768]{2,1,0:T(8,128)(2,1)}, u32[]{:S(2)}, u32[]{:S(2)}) async-start(bf16[4,512,768]{2,1,0:T(8,128)(2,1)} %bitcast.114), calls=%async_computation.3 | async-start | bytes 6291456 | tf_op jit(solution)/shard_map/all_to_all | solution.py:293
  328.1 48.3 %shard_map.281 = bf16[4,3,3,512,64]{4,3,2,1,0:T(8,128)(2,1)} custom-call(s32[1]{0:T(128)S(6)} %copy.160.prefix_ref, bf16[3,2048,64]{2,1,0:T(8,128)(2,1)S(1)} %copy-done.3, bf16[3,2048,64]{2,1,0:T(8,128)(2,1)S(1)} %bitcast.107, bf16[3,2048,64]{2,1,0:T(8,128)(2,1)S(1)} %copy-done.4, bf16[3,2048,64]{2,1,0:T(8,128)(2,1)} %bitcast.121, ...), custom_call_target="tpu_custom_call" | custom-call | flops 8053063680 | bytes 6291456 | tf_op jit(solution)/shard_map/pallas_call | solution.py:163
  380.3 6.7 %reduce-scatter.8.cloned.1.call-done = bf16[216,768]{1,0:T(8,128)(2,1)} async-done(((bf16[1728,768]{1,0:T(8,128)(2,1)}), bf16[216,768]{1,0:T(8,128)(2,1)}) %reduce-scatter.8.cloned.1.call-update) | async-done | bytes 331792 | tf_op jit(solution)/shard_map/reduce_scatter | solution.py:310
  389.5 6.0 %copy.121 = bf16[4,3,3,512,64]{3,4,2,1,0:T(8,128)(2,1)} copy(bf16[4,3,3,512,64]{4,3,2,1,0:T(8,128)(2,1)} %shard_map.281) | data formatting | bytes 4718592 | tf_op jit(solution)/shard_map/optimization_barrier | solution.py:323
  395.5 4.8 all-to-all-start.3
  400.6 5.8 %fusion.32 = f32[3,3,64,768,1]{3,2,1,0,4:T(8,128)} fusion(bf16[4,3,3,512,64]{4,3,2,1,0:T(8,128)(2,1)} %shard_map.281, bf16[4,512,768,1,1]{2,1,4,3,0:T(8,128)(2,1)S(1)} %bitcast.118), kind=kOutput, calls=%fused_computation.84 | convolution fusion | flops 1811939328 | bytes 7274496 | tf_op jit(solution)/shard_map/trd,tkhre->kdhe/dot_general | solution.py:336
  419.7 9.1 %all-to-all-done.3 = bf16[4,3,3,512,64]{3,4,2,1,0:T(8,128)(2,1)} async-done(((bf16[4,3,3,512,64]{3,4,2,1,0:T(8,128)(2,1)}), bf16[4,3,3,512,64]{3,4,2,1,0:T(8,128)(2,1)}, u32[]{:S(2)}, u32[]{:S(2)}) %all-to-all-start.3) | async-done | bytes 2359328 | tf_op jit(solution)/shard_map/all_to_all | solution.py:339
  428.8 5.4 %fusion.14 = (f32[768]{0:T(1024)S(1)}, f32[512]{0:T(512)S(1)}, f32[512]{0:T(512)S(1)}, f32[768]{0:T(1024)S(1)}, f32[512,768,1,1,1]{1,0,4,3,2:T(8,128)S(1)}) fusion(f32[512,768]{1,0:T(8,128)S(1)} %copy-done.10, f32[512]{0:T(512)S(1)} %add_rsqrt_fusion.1, f32[512]{0:T(512)S(1)} %broadcast_multiply_fusion.5, f32[768]{0:T(1024)S(1)} %copy-done.28, ...), kind=kOutput, calls=%fused_computation.35 | convolution fusion | flops 1815475712 | bytes 9061376 | tf_op jit(solution)/shard_map/skhre,skdhe->rd/dot_general | solution.py:341
  435.7 40.7 %all-reduce = (f32[768]{0:T(1024)}, f32[768]{0:T(1024)}, f32[2,768]{1,0:T(2,128)}, f32[768]{0:T(1024)}, f32[768]{0:T(1024)}, /*index=5*/f32[768]{0:T(1024)}, f32[3072]{0:T(1024)}, f32[768]{0:T(1024)}, f32[5,768]{1,0:T(8,128)}) all-reduce(f32[768]{0:T(1024)S(1)} %get-tuple-element.121, ...), channel_id=1, replica_groups=mesh['fsdp'=8,'tp'=4] {'fsdp','tp'}, use_global_device_ids=true, to_apply=%region_13.0 | all-reduce | flops 13056 | bytes 104448 | tf_op jit(solution)/shard_map/psum | solution.py:363
  (187 shorter events, 132.9 us)
Async XLA Ops:
  7.2 42.0 %all-gather.8.cloned.1.call-start = ((), (), s32[]{:S(2)}) async-start(), calls=%async_computation.7 | async-start | bytes 3932160 | tf_op jit(solution)/shard_map/all_gather | solution.py:219
  12.4 108.0 %all-gather.18.cloned.1.call-start = ((), (), s32[]{:S(2)}) async-start(), calls=%async_computation.14 | async-start | bytes 2985984 | tf_op jit(solution)/shard_map/all_gather | solution.py:224
  49.3 97.1 %all-gather.10.cloned.1.call-start = ((), (), s32[]{:S(2)}) async-start(), calls=%async_computation.8 | async-start | bytes 3932160 | tf_op jit(solution)/shard_map/all_gather | solution.py:227
  52.8 67.6 %all-to-all-start = ((bf16[4,3,768,192]{2,3,1,0:T(8,128)(2,1)}), bf16[4,3,768,192]{2,3,1,0:T(8,128)(2,1)}, u32[]{:S(2)}, u32[]{:S(2)}) async-start(bf16[4,3,768,192]{2,3,1,0:T(8,128)(2,1)} %broadcast_in_dim.6), calls=%async_computation | async-start | bytes 7077888 | tf_op jit(solution)/shard_map/all_to_all | solution.py:226
  57.5 95.6 %all-gather.12.cloned.1.call-start = ((), (), s32[]{:S(2)}) async-start(), calls=%async_computation.9 | async-start | bytes 1474560 | tf_op jit(solution)/shard_map/all_gather | solution.py:246
  131.1 71.9 %all-gather.14.cloned.1.call-start = ((), (), s32[]{:S(2)}) async-start(), calls=%async_computation.10 | async-start | bytes 3932160 | tf_op jit(solution)/shard_map/all_gather | solution.py:265
  153.1 16.6 %copy-start.36 = (f32[768]{0:T(1024)S(1)}, f32[768]{0:T(1024)}, u32[]{:S(2)}) copy-start(f32[768]{0:T(1024)} %param.28) | copy-start | bytes 9220
  154.5 15.2 %copy-start.9 = (f32[512,768]{1,0:T(8,128)S(1)}, f32[512,768]{1,0:T(8,128)}, u32[]{:S(2)}) copy-start(f32[512,768]{1,0:T(8,128)} %copy-done.8) | copy-start | bytes 4718596
  174.3 85.4 %reduce-scatter.6.cloned.1.call-start = ((), (), s32[]{:S(2)}) async-start(), calls=%async_computation.11 | async-start | bytes 3932160 | tf_op jit(solution)/shard_map/reduce_scatter | solution.py:279
  202.9 5.1 %copy-start.22 = (bf16[768,8,96]{0,2,1:T(8,128)(2,1)S(1)}, bf16[768,8,96]{0,2,1:T(8,128)(2,1)}, u32[]{:S(2)}) copy-start(bf16[768,8,96]{0,2,1:T(8,128)(2,1)} %copy.111) | copy-start | bytes 3538948
  202.9 5.1 %copy-start.33 = (bf16[2048,768]{1,0:T(8,128)(2,1)S(1)}, bf16[2048,768]{1,0:T(8,128)(2,1)}, u32[]{:S(2)}) copy-start(bf16[2048,768]{1,0:T(8,128)(2,1)} %all-gather.10.cloned.1.call-done) | copy-start | bytes 9437188
  208.0 9.6 %copy-start.19 = (bf16[768,768]{1,0:T(8,128)(2,1)S(1)}, bf16[768,768]{1,0:T(8,128)(2,1)}, u32[]{:S(2)}) copy-start(bf16[768,768]{1,0:T(8,128)(2,1)} %reshape_reshape.8) | copy-start | bytes 3538948
  221.6 72.4 %all-gather.16.cloned.1.call-start = ((), (), s32[]{:S(2)}) async-start(), calls=%async_computation.12 | async-start | bytes 3932160 | tf_op jit(solution)/shard_map/all_gather | solution.py:291
  222.1 6.7 %copy-start.34 = (bf16[2048,768]{1,0:T(8,128)(2,1)S(1)}, bf16[2048,768]{1,0:T(8,128)(2,1)}, u32[]{:S(2)}) copy-start(bf16[2048,768]{1,0:T(8,128)(2,1)} %all-gather.10.cloned.1.call-done) | copy-start | bytes 9437188
  222.1 6.6 %copy-start.39 = (bf16[2048,768]{1,0:T(8,128)(2,1)S(1)}, bf16[2048,768]{1,0:T(8,128)(2,1)}, u32[]{:S(2)}) copy-start(bf16[2048,768]{1,0:T(8,128)(2,1)} %get-tuple-element.144) | copy-start | bytes 9437188
  265.3 121.6 %reduce-scatter.8.cloned.1.call-start = ((), (), s32[]{:S(2)}) async-start(), calls=%async_computation.13 | async-start | bytes 2985984 | tf_op jit(solution)/shard_map/reduce_scatter | solution.py:310
  315.2 61.3 %all-to-all-start.2 = ((bf16[4,512,768]{2,1,0:T(8,128)(2,1)}), bf16[4,512,768]{2,1,0:T(8,128)(2,1)}, u32[]{:S(2)}, u32[]{:S(2)}) async-start(bf16[4,512,768]{2,1,0:T(8,128)(2,1)} %bitcast.114), calls=%async_computation.3 | async-start | bytes 6291456 | tf_op jit(solution)/shard_map/all_to_all | solution.py:293
  395.5 5.1 %copy-start.17 = (bf16[2048,768]{1,0:T(8,128)(2,1)S(1)}, bf16[2048,768]{1,0:T(8,128)(2,1)}, u32[]{:S(2)}) copy-start(bf16[2048,768]{1,0:T(8,128)(2,1)} %all-gather.8.cloned.1.call-done) | copy-start | bytes 9437188
  395.5 33.3 %all-to-all-start.3 = ((bf16[4,3,3,512,64]{3,4,2,1,0:T(8,128)(2,1)}), bf16[4,3,3,512,64]{3,4,2,1,0:T(8,128)(2,1)}, u32[]{:S(2)}, u32[]{:S(2)}) async-start(bf16[4,3,3,512,64]{3,4,2,1,0:T(8,128)(2,1)} %copy.121), calls=%async_computation.5 | async-start | bytes 4718592 | tf_op jit(solution)/shard_map/all_to_all | solution.py:339
  400.3 79.1 %reduce-scatter.10.cloned.1.call-start = ((), (), s32[]{:S(2)}) async-start(), calls=%async_computation.15 | async-start | bytes 2211840
  416.2 12.6 %copy-start.10 = (f32[512,768]{1,0:T(8,128)S(1)}, f32[512,768]{1,0:T(8,128)}, u32[]{:S(2)}) copy-start(f32[512,768]{1,0:T(8,128)} %copy-done.8) | copy-start | bytes 4718596
  428.8 5.4 %copy-start.12 = (f32[512,768]{1,0:T(8,128)S(1)}, f32[512,768]{1,0:T(8,128)}, u32[]{:S(2)}) copy-start(f32[512,768]{1,0:T(8,128)} %copy-done.11) | copy-start | bytes 4718596
  434.3 47.0 %copy-start.1 = (f32[5,768]{1,0:T(8,128)S(1)}, f32[5,768]{1,0:T(8,128)}, u32[]{:S(2)}) copy-start(f32[5,768]{1,0:T(8,128)} %param.33) | copy-start | bytes 46084
  435.0 46.3 %copy-start.13 = (f32[512,768]{1,0:T(8,128)}, f32[512,768]{1,0:T(8,128)S(1)}, u32[]{:S(2)}) copy-start(f32[512,768]{1,0:T(8,128)S(1)} %multiply_add_fusion) | copy-start | bytes 4718596
  (28 other events, 61.1 us)
Sparse Core Ops, SparseCore 0:
  12.6 31.2 all-gather.7
  49.4 55.5 all-gather.17
  106.5 27.0 all-gather.9
  135.6 17.4 all-gather.11
  174.4 28.4 all-gather.13
  221.7 37.8 reduce-scatter.5
  265.4 28.5 all-gather.15
  315.3 71.6 reduce-scatter.7
  412.4 66.9 reduce-scatter.9

commit v16 on v14

--- a/solution.py
+++ b/solution.py
@@ -287,8 +287,19 @@
     )
     grad_middle = grad_top + grad_from_norm
     grad_out_bias = jnp.sum(grad_middle, axis=0)
+    width = grad_fc1.shape[1]
+    fsdp_count = lax.axis_size("fsdp")
+    dense_grads = (
+        grad_fc1.reshape(fsdp_count, -1, width),
+        jnp.moveaxis(grad_fc2.reshape(grad_fc2.shape[0], fsdp_count, -1), 1, 0),
+    )
+    dense_packed = jnp.concatenate(
+        [g.reshape(fsdp_count, -1, width) for g in dense_grads], axis=1
+    ).astype(jnp.bfloat16)
     grad_attn_rows = lax.all_gather(grad_middle.astype(jnp.bfloat16), "tp", axis=0, tiled=True)
-    fc2_partial, grad_attn_rows = lax.optimization_barrier((fc2_partial, grad_attn_rows))
+    fc2_partial, grad_attn_rows, dense_packed = lax.optimization_barrier(
+        (fc2_partial, grad_attn_rows, dense_packed)
+    )
     fc2_parts = lax.all_to_all(
         fc2_partial.reshape(tp_count, local_rows, -1), "tp", 0, 0, tiled=True
     )
@@ -299,18 +310,8 @@
         grad_attn_rows.reshape(tp_count, local_rows, -1),
         preferred_element_type=jnp.float32,
     ).reshape(cols_here, -1)
-    fsdp_count = lax.axis_size("fsdp")
-    dense_grads = (
-        jnp.moveaxis(grad_out_w.reshape(grad_out_w.shape[0], fsdp_count, -1), 1, 0),
-        grad_fc1.reshape(fsdp_count, -1, grad_fc1.shape[1]),
-        jnp.moveaxis(grad_fc2.reshape(grad_fc2.shape[0], fsdp_count, -1), 1, 0),
-    )
-    dense_packed = jnp.concatenate([g.reshape(fsdp_count, -1) for g in dense_grads], axis=1)
     dense_summed = lax.psum_scatter(
-        dense_packed.reshape(-1, grad_fc1.shape[1]).astype(jnp.bfloat16),
-        "fsdp",
-        scatter_dimension=0,
-        tiled=True,
+        dense_packed.reshape(-1, width), "fsdp", scatter_dimension=0, tiled=True
     ).reshape(1, -1).astype(jnp.float32)
     grad_mixed = (
         matmul_nt(grad_attn_rows, out_full).astype(jnp.bfloat16).reshape(seq_len, heads_here, HD)
@@ -346,7 +347,7 @@
         size = g[0].size
         dense_shards.append(dense_summed[0, offset : offset + size].reshape(g.shape[1:]))
         offset += size
-    out_shard, fc1_shard, fc2_shard = dense_shards
+    fc1_shard, fc2_shard = dense_shards
     grad_in_norm, grad_ln1_gain, grad_ln1_bias = norm_backward(
         grad_normed, unit_one, inv_one, ln1_gain
     )
@@ -358,7 +359,21 @@
         precision=HIGH,
         preferred_element_type=jnp.float32,
     )
-    qkv_shard = lax.psum_scatter(grad_qkv_w, "fsdp", scatter_dimension=1, tiled=True)
+    tail_grads = (
+        jnp.moveaxis(grad_qkv_w.reshape(3, fsdp_count, -1, cols_here), 1, 0),
+        jnp.moveaxis(grad_out_w.reshape(grad_out_w.shape[0], fsdp_count, -1), 1, 0),
+    )
+    tail_packed = jnp.concatenate([g.reshape(fsdp_count, -1, width) for g in tail_grads], axis=1)
+    tail_summed = lax.psum_scatter(
+        tail_packed.reshape(-1, width), "fsdp", scatter_dimension=0, tiled=True
+    ).reshape(-1)
+    tail_shards = []
+    offset = 0
+    for g in tail_grads:
+        size = g[0].size
+        tail_shards.append(tail_summed[offset : offset + size].reshape(g.shape[1:]))
+        offset += size
+    qkv_shard, out_shard = tail_shards
     summed = lax.psum(
         (
             grad_ln1_gain,

time: 495 us -> 494 us (level)
    all_to_all x1, waiting for transfers between devices: 9.12 us -> 22.1 us  [on_device(): grad_rows_all = lax.all_to_all(grad_all, 'tp', 0, 0, tiled=True)]
    unnamed x89 -> x78, local copies, waits for them, and re-layouts: 27 us -> 15.2 us
    reshape x2 -> x5, local copies, waits for them, and re-layouts: 3.29 us -> 10.2 us  [the longest x3 8.58 us: on_device(): g.reshape(fsdp_count, -1, width)]
    reduce_scatter x1 -> x2, waiting for transfers between devices: 6.56 us -> 0.01 us  [the longest x1 0.01 us: on_device(): lax.psum_scatter(tail_packed.reshape(-1, width), 'fsdp', scatter_dimensio...]
  transfers between devices with their start and end apart: 12 -> 12, of which waited for: 7 -> 5; matrix products, arithmetic and copies ran while one was open for 23% -> 24% of each run, Pallas kernels for 19% -> 19%
where the time goes in v16:
time: 494 us; the launch traced here: 489 us
  local copies, waits for them, and re-layouts  94.3 us (19%)
  waiting for transfers between devices  93.4 us (19%)
  Pallas kernels  92.9 us (19%)
  blocking collectives  92.5 us (19%)
  matrix products  59.4 us (12%)
  other arithmetic  25.1 us (5%)
  starting transfers between devices  15.6 us (3%)
  between operations  15.5 us (3%)
    pallas_call x1, Pallas kernels, attn_backward(): pl.pallas_call(functools.partial(_bwd_kernel, scale), out_shape=shape, gr...  48.3 us
    pallas_call x1, Pallas kernels, attn_forward(): pl.pallas_call(functools.partial(_fwd_kernel, scale), out_shape=(jax.Shap...  44.5 us
    psum x1, blocking collectives, on_device(): lax.psum((grad_ln1_gain, grad_ln1_bias, grad_qv_bias, grad_out_bias, grad...  42 us
    all_gather x1, blocking collectives, on_device(): qkv_cols = lax.all_gather(qkv_weight, 'fsdp', axis=1, tiled=True)  35.2 us
    all_gather x1, waiting for transfers between devices, on_device(): normed_rows = lax.all_gather(normed_two, 'tp', axis=0, tiled=True)  27.8 us
    reduce_scatter x1, waiting for transfers between devices, on_device(): lax.psum_scatter(matmul_nt(grad_before, fc1_part).astype(jnp.bfloat16), '...  23.4 us
    all_to_all x1, waiting for transfers between devices, on_device(): grad_rows_all = lax.all_to_all(grad_all, 'tp', 0, 0, tiled=True)  22.1 us
    all_gather x1, waiting for transfers between devices, on_device(): lax.all_gather(grad_middle.astype(jnp.bfloat16), 'tp', axis=0, tiled=True)  16.5 us
  transfers between devices with their start and end apart: 12, of which 5 were waited for; matrix products, arithmetic and copies ran while one was open for 24% of the time, Pallas kernels for 19%

profile of v16, /device:TPU:0, one launch (start us, length us, event | category | flops | bytes accessed | tf_op | source)
XLA Modules:
  0.0 488.7 jit_solution(3967684664323277559)
XLA Ops:
  13.3 35.2 %all_gather.24 = bf16[3,768,192]{2,1,0:T(8,128)(2,1)S(1)} all-gather(bf16[3,96,192]{2,1,0:T(8,128)(2,1)S(1)} %copy-done.22), channel_id=1, replica_groups=mesh['fsdp'=8,'tp'=4] {'fsdp'}, dimensions={1}, use_global_device_ids=true | all-gather | bytes 995328 | tf_op jit(solution)/shard_map/all_gather | solution.py:209
  52.9 4.8 all-to-all-start
  59.7 4.7 convolution_bitcast_fusion
  76.2 4.8 fusion.13
  81.0 44.5 %shard_map.280 = (bf16[4,3,512,64]{3,2,1,0:T(8,128)(2,1)S(1)}, f32[3,2048,1]{2,1,0:T(8,128)}) custom-call(s32[1]{0:T(128)S(6)} %copy.136.prefix_ref, bf16[3,2048,64]{2,1,0:T(8,128)(2,1)S(1)} %get-tuple-element.142.q_ref, bf16[3,2048,64]{2,1,0:T(8,128)(2,1)S(1)} %bitcast.108, bf16[3,2048,64]{2,1,0:T(8,128)(2,1)} %get-tuple-element.143.v_ref), custom_call_target="tpu_custom_call" | custom-call | flops 3221225472 | bytes 3145728 | tf_op jit(solution)/shard_map/pallas_call | solution.py:135
  126.7 4.5 reshape.212
  157.2 15.2 %all_to_all.20 = bf16[4,3,512,64]{2,3,1,0:T(8,128)(2,1)S(1)} all-to-all(bf16[4,3,512,64]{2,3,1,0:T(8,128)(2,1)} %copy.88), channel_id=1, replica_groups=mesh['fsdp'=8,'tp'=4] {'tp'}, dimensions={0} | all-to-all | bytes 1572864 | tf_op jit(solution)/shard_map/all_to_all | solution.py:249
  177.8 27.8 %all-gather.14.cloned.1.call-done = bf16[2048,768]{1,0:T(8,128)(2,1)} async-done(((bf16[512,768]{1,0:T(8,128)(2,1)}), bf16[2048,768]{1,0:T(8,128)(2,1)}) %all-gather.14.cloned.1.call-update) | async-done | bytes 3145744 | tf_op jit(solution)/shard_map/all_gather | solution.py:264
  205.7 5.1 %fusion.29 = f32[2048,768]{1,0:T(8,128)S(1)} fusion(bf16[2048,768]{1,0:T(8,128)(2,1)} %all-gather.14.cloned.1.call-done, bf16[768,768]{1,0:T(8,128)(2,1)} %reshape_reshape.7), kind=kOutput, calls=%fused_computation.82 | convolution fusion | flops 2415919104 | bytes 10616832 | tf_op jit(solution)/shard_map/dot_general | solution.py:265
  210.8 7.8 %convert_reduce_fusion = (f32[768]{0:T(1024)S(1)}, bf16[2048,768]{1,0:T(8,128)(2,1)S(1)}, bf16[2048,768]{1,0:T(8,128)(2,1)}) fusion(f32[2048,768]{1,0:T(8,128)S(1)} %fusion.29, f32[768]{0:T(1024)S(1)} %dynamic_slice.7, bf16[2048,768]{1,0:T(8,128)(2,1)S(1)} %copy-done.30, bf16[768,768]{0,1:T(8,128)(2,1)S(1)} %bitcast.127), kind=kOutput, calls=%fused_computation.9 | convolution fusion | flops 2455239936 | bytes 16914432 | tf_op jit(solution)/shard_map/dot_general | solution.py:37
  220.3 4.0 convolution_convert_fusion.1
  224.6 6.8 %convolution_convert_fusion = bf16[2048,768]{1,0:T(8,128)(2,1)} fusion(bf16[2048,768]{1,0:T(8,128)(2,1)} %get-tuple-element.131, bf16[768,768]{0,1:T(8,128)(2,1)} %bitcast.126), kind=kOutput, calls=%fused_computation.16 | convolution fusion | flops 2417491968 | bytes 7471104 | tf_op jit(solution)/shard_map/dot_general | solution.py:267
  239.0 23.4 %reduce-scatter.4.cloned.1.call-done = bf16[512,768]{1,0:T(8,128)(2,1)} async-done(((bf16[2048,768]{1,0:T(8,128)(2,1)}), bf16[512,768]{1,0:T(8,128)(2,1)}) %reduce-scatter.4.cloned.1.call-update) | async-done | bytes 786448 | tf_op jit(solution)/shard_map/reduce_scatter | solution.py:278
  280.1 16.5 %all-gather.16.cloned.1.call-done = bf16[2048,768]{1,0:T(8,128)(2,1)} async-done(((bf16[512,768]{1,0:T(8,128)(2,1)}), bf16[2048,768]{1,0:T(8,128)(2,1)}) %all-gather.16.cloned.1.call-update) | async-done | bytes 3145744 | tf_op jit(solution)/shard_map/all_gather | solution.py:299
  296.7 4.7 all-to-all-start.2
  307.7 4.6 copy.100
  312.4 4.4 convolution_bitcast_fusion.1
  320.4 48.3 %shard_map.281 = bf16[4,3,3,512,64]{4,3,2,1,0:T(8,128)(2,1)} custom-call(s32[1]{0:T(128)S(6)} %copy.136.prefix_ref, bf16[3,2048,64]{2,1,0:T(8,128)(2,1)S(1)} %copy-done.3, bf16[3,2048,64]{2,1,0:T(8,128)(2,1)S(1)} %bitcast.109, bf16[3,2048,64]{2,1,0:T(8,128)(2,1)S(1)} %copy-done.4, bf16[3,2048,64]{2,1,0:T(8,128)(2,1)} %bitcast.124, ...), custom_call_target="tpu_custom_call" | custom-call | flops 8053063680 | bytes 6291456 | tf_op jit(solution)/shard_map/pallas_call | solution.py:162
  374.2 5.6 %fusion.7 = f32[3,3,64,768,1]{3,2,0,1,4:T(8,128)S(1)} fusion(bf16[4,512,768,1,1]{2,1,3,4,0:T(8,128)(2,1)} %bitcast.122, bf16[4,3,3,512,64]{4,3,2,1,0:T(8,128)(2,1)} %shard_map.281), kind=kOutput, calls=%fused_computation.12 | convolution fusion | flops 1811939328 | bytes 7274496 | tf_op jit(solution)/shard_map/trd,tkhre->kdhe/dot_general | solution.py:336
  390.1 6.1 %copy.94 = bf16[4,3,3,512,64]{3,4,2,1,0:T(8,128)(2,1)} copy(bf16[4,3,3,512,64]{4,3,2,1,0:T(8,128)(2,1)} %shard_map.281) | data formatting | bytes 4718592 | tf_op jit(solution)/shard_map/optimization_barrier | solution.py:323
  396.2 4.6 all-to-all-start.3
  407.3 22.1 %all-to-all-done.3 = bf16[4,3,3,512,64]{3,4,2,1,0:T(8,128)(2,1)} async-done(((bf16[4,3,3,512,64]{3,4,2,1,0:T(8,128)(2,1)}), bf16[4,3,3,512,64]{3,4,2,1,0:T(8,128)(2,1)}, u32[]{:S(2)}, u32[]{:S(2)}) %all-to-all-start.3) | async-done | bytes 2359328 | tf_op jit(solution)/shard_map/all_to_all | solution.py:339
  429.4 5.4 %fusion.16 = (f32[768]{0:T(1024)S(1)}, f32[512]{0:T(512)S(1)}, f32[512]{0:T(512)S(1)}, f32[768]{0:T(1024)S(1)}, f32[512,768,1,1,1]{1,0,4,3,2:T(8,128)S(1)}) fusion(f32[512,768]{1,0:T(8,128)S(1)} %copy-done.10, f32[512]{0:T(512)S(1)} %add_rsqrt_fusion.1, f32[512]{0:T(512)S(1)} %broadcast_multiply_fusion.5, f32[768]{0:T(1024)S(1)} %copy-done.25, ...), kind=kOutput, calls=%fused_computation.39 | convolution fusion | flops 1815475712 | bytes 9061376 | tf_op jit(solution)/shard_map/skhre,skdhe->rd/dot_general | solution.py:341
  436.2 42.0 %all-reduce = (f32[768]{0:T(1024)}, f32[768]{0:T(1024)}, f32[2,768]{1,0:T(2,128)}, f32[768]{0:T(1024)}, f32[768]{0:T(1024)}, /*index=5*/f32[768]{0:T(1024)}, f32[3072]{0:T(1024)}, f32[768]{0:T(1024)}, f32[5,768]{1,0:T(8,128)}) all-reduce(f32[768]{0:T(1024)S(1)} %get-tuple-element.108, ...), channel_id=1, replica_groups=mesh['fsdp'=8,'tp'=4] {'fsdp','tp'}, use_global_device_ids=true, to_apply=%region_13.0 | all-reduce | flops 13056 | bytes 104448 | tf_op jit(solution)/shard_map/psum | solution.py:377
  (181 shorter events, 120.2 us)
Async XLA Ops:
  7.2 42.0 %all-gather.8.cloned.1.call-start = ((), (), s32[]{:S(2)}) async-start(), calls=%async_computation.7 | async-start | bytes 3932160 | tf_op jit(solution)/shard_map/all_gather | solution.py:218
  12.4 114.2 %all-gather.18.cloned.1.call-start = ((), (), s32[]{:S(2)}) async-start(), calls=%async_computation.15 | async-start | bytes 2985984 | tf_op jit(solution)/shard_map/all_gather | solution.py:223
  49.3 103.8 %all-gather.10.cloned.1.call-start = ((), (), s32[]{:S(2)}) async-start(), calls=%async_computation.8 | async-start | bytes 3932160 | tf_op jit(solution)/shard_map/all_gather | solution.py:226
  52.9 73.8 %all-to-all-start = ((bf16[4,3,768,192]{2,3,1,0:T(8,128)(2,1)}), bf16[4,3,768,192]{2,3,1,0:T(8,128)(2,1)}, u32[]{:S(2)}, u32[]{:S(2)}) async-start(bf16[4,3,768,192]{2,3,1,0:T(8,128)(2,1)} %broadcast_in_dim.6), calls=%async_computation | async-start | bytes 7077888 | tf_op jit(solution)/shard_map/all_to_all | solution.py:225
  57.6 98.2 %all-gather.12.cloned.1.call-start = ((), (), s32[]{:S(2)}) async-start(), calls=%async_computation.9 | async-start | bytes 1474560 | tf_op jit(solution)/shard_map/all_gather | solution.py:245
  137.3 68.3 %all-gather.14.cloned.1.call-start = ((), (), s32[]{:S(2)}) async-start(), calls=%async_computation.10 | async-start | bytes 3932160 | tf_op jit(solution)/shard_map/all_gather | solution.py:264
  155.8 16.6 %copy-start.33 = (f32[768]{0:T(1024)S(1)}, f32[768]{0:T(1024)}, u32[]{:S(2)}) copy-start(f32[768]{0:T(1024)} %param.28) | copy-start | bytes 9220
  157.2 15.2 %copy-start.9 = (f32[512,768]{1,0:T(8,128)S(1)}, f32[512,768]{1,0:T(8,128)}, u32[]{:S(2)}) copy-start(f32[512,768]{1,0:T(8,128)} %copy-done.8) | copy-start | bytes 4718596
  177.0 85.4 %reduce-scatter.4.cloned.1.call-start = ((), (), s32[]{:S(2)}) async-start(), calls=%async_computation.11 | async-start | bytes 3932160 | tf_op jit(solution)/shard_map/reduce_scatter | solution.py:278
  205.7 5.1 %copy-start.19 = (bf16[768,8,96]{0,2,1:T(8,128)(2,1)S(1)}, bf16[768,8,96]{0,2,1:T(8,128)(2,1)}, u32[]{:S(2)}) copy-start(bf16[768,8,96]{0,2,1:T(8,128)(2,1)} %copy.87) | copy-start | bytes 3538948
  205.7 5.1 %copy-start.30 = (bf16[2048,768]{1,0:T(8,128)(2,1)S(1)}, bf16[2048,768]{1,0:T(8,128)(2,1)}, u32[]{:S(2)}) copy-start(bf16[2048,768]{1,0:T(8,128)(2,1)} %all-gather.10.cloned.1.call-done) | copy-start | bytes 9437188
  210.7 9.6 %copy-start.17 = (bf16[768,768]{1,0:T(8,128)(2,1)S(1)}, bf16[768,768]{1,0:T(8,128)(2,1)}, u32[]{:S(2)}) copy-start(bf16[768,768]{1,0:T(8,128)(2,1)} %reshape_reshape.7) | copy-start | bytes 3538948
  224.4 72.3 %all-gather.16.cloned.1.call-start = ((), (), s32[]{:S(2)}) async-start(), calls=%async_computation.12 | async-start | bytes 3932160 | tf_op jit(solution)/shard_map/all_gather | solution.py:299
  224.6 6.8 %copy-start.31 = (bf16[2048,768]{1,0:T(8,128)(2,1)S(1)}, bf16[2048,768]{1,0:T(8,128)(2,1)}, u32[]{:S(2)}) copy-start(bf16[2048,768]{1,0:T(8,128)(2,1)} %all-gather.10.cloned.1.call-done) | copy-start | bytes 9437188
  224.6 6.8 %copy-start.36 = (bf16[2048,768]{1,0:T(8,128)(2,1)S(1)}, bf16[2048,768]{1,0:T(8,128)(2,1)}, u32[]{:S(2)}) copy-start(bf16[2048,768]{1,0:T(8,128)(2,1)} %get-tuple-element.131) | copy-start | bytes 9437188
  268.0 104.5 %reduce-scatter.6.cloned.1.call-start = ((), (), s32[]{:S(2)}) async-start(), calls=%async_computation.13 | async-start | bytes 2654208 | tf_op jit(solution)/shard_map/reduce_scatter | solution.py:313
  296.7 72.1 %all-to-all-start.2 = ((bf16[4,512,768]{2,1,0:T(8,128)(2,1)}), bf16[4,512,768]{2,1,0:T(8,128)(2,1)}, u32[]{:S(2)}, u32[]{:S(2)}) async-start(bf16[4,512,768]{2,1,0:T(8,128)(2,1)} %bitcast.118), calls=%async_computation.3 | async-start | bytes 6291456 | tf_op jit(solution)/shard_map/all_to_all | solution.py:303
  301.4 176.8 %reduce-scatter.8.cloned.1.call-start = ((), (), s32[]{:S(2)}) async-start(), calls=%async_computation.14 | async-start | bytes 2654208 | tf_op jit(solution)/shard_map/reduce_scatter | solution.py:367
  312.4 6.6 %copy-start.3 = (bf16[3,2048,64]{2,1,0:T(8,128)(2,1)S(1)}, bf16[3,2048,64]{2,1,0:T(8,128)(2,1)}, u32[]{:S(2)}) copy-start(bf16[3,2048,64]{2,1,0:T(8,128)(2,1)} %copy-done.2) | copy-start | bytes 2359300
  396.2 33.1 %all-to-all-start.3 = ((bf16[4,3,3,512,64]{3,4,2,1,0:T(8,128)(2,1)}), bf16[4,3,3,512,64]{3,4,2,1,0:T(8,128)(2,1)}, u32[]{:S(2)}, u32[]{:S(2)}) async-start(bf16[4,3,3,512,64]{3,4,2,1,0:T(8,128)(2,1)} %copy.94), calls=%async_computation.5 | async-start | bytes 4718592 | tf_op jit(solution)/shard_map/all_to_all | solution.py:339
  403.8 25.6 %copy-start.10 = (f32[512,768]{1,0:T(8,128)S(1)}, f32[512,768]{1,0:T(8,128)}, u32[]{:S(2)}) copy-start(f32[512,768]{1,0:T(8,128)} %copy-done.8) | copy-start | bytes 4718596
  429.4 5.5 %copy-start.12 = (f32[512,768]{1,0:T(8,128)S(1)}, f32[512,768]{1,0:T(8,128)}, u32[]{:S(2)}) copy-start(f32[512,768]{1,0:T(8,128)} %copy-done.11) | copy-start | bytes 4718596
  434.8 46.9 %copy-start.1 = (f32[5,768]{1,0:T(8,128)S(1)}, f32[5,768]{1,0:T(8,128)}, u32[]{:S(2)}) copy-start(f32[5,768]{1,0:T(8,128)} %param.33) | copy-start | bytes 46084
  435.5 46.2 %copy-start.13 = (f32[512,768]{1,0:T(8,128)}, f32[512,768]{1,0:T(8,128)S(1)}, u32[]{:S(2)}) copy-start(f32[512,768]{1,0:T(8,128)S(1)} %multiply_add_fusion) | copy-start | bytes 4718596
  (25 other events, 47.9 us)
Sparse Core Ops, SparseCore 0:
  12.6 31.2 all-gather.7
  49.4 55.5 all-gather.17
  106.5 27.0 all-gather.9
  137.5 18.3 all-gather.11
  177.1 28.4 all-gather.13
  224.5 37.8 reduce-scatter.3
  268.1 28.4 all-gather.15
  300.2 69.5 reduce-scatter.5
  390.3 71.3 reduce-scatter.7

commit v17 on v16

--- a/solution.py
+++ b/solution.py
@@ -304,12 +304,6 @@
         fc2_partial.reshape(tp_count, local_rows, -1), "tp", 0, 0, tiled=True
     )
     result = middle + jnp.sum(fc2_parts.astype(jnp.float32), axis=0) + fc2_bias
-    grad_out_w = jnp.einsum(
-        "thre,trm->hem",
-        mixed,
-        grad_attn_rows.reshape(tp_count, local_rows, -1),
-        preferred_element_type=jnp.float32,
-    ).reshape(cols_here, -1)
     dense_summed = lax.psum_scatter(
         dense_packed.reshape(-1, width), "fsdp", scatter_dimension=0, tiled=True
     ).reshape(1, -1).astype(jnp.float32)
@@ -320,7 +314,15 @@
         prefix, q_heads, k_heads, v_heads, jnp.transpose(grad_mixed, (1, 0, 2)), log_mass, scale,
         tp_count,
     )
-    grad_all, result, dense_summed = lax.optimization_barrier((grad_all, result, dense_summed))
+    grad_all, result, dense_summed, grad_attn_late = lax.optimization_barrier(
+        (grad_all, result, dense_summed, grad_attn_rows)
+    )
+    grad_out_w = jnp.einsum(
+        "thre,trm->hem",
+        mixed,
+        grad_attn_late.reshape(tp_count, local_rows, -1),
+        preferred_element_type=jnp.float32,
+    ).reshape(cols_here, -1)
     grad_q_heads, grad_v_heads = grad_all[:, 0], grad_all[:, 2]
     grad_qv_here = jnp.stack(
         [

time: 494 us -> 498 us (level)
  waiting for transfers between devices: 93.4 us -> 100 us
    reduce_scatter x1, waiting for transfers between devices: 0.01 us -> 6.67 us  [on_device(): lax.psum_scatter(dense_packed.reshape(-1, width), 'fsdp', scatter_dimensi...]
    unnamed x78 -> x80, local copies, waits for them, and re-layouts: 15.2 us -> 17.2 us
  transfers between devices with their start and end apart: 12 -> 12, of which waited for: 5 -> 6; matrix products, arithmetic and copies ran while one was open for 24% -> 22% of each run, Pallas kernels for 19% -> 19%
where the time goes in v17:
time: 498 us; the launch traced here: 493 us
  waiting for transfers between devices  100 us (20%)
  local copies, waits for them, and re-layouts  93.6 us (19%)
  Pallas kernels  92.8 us (19%)
  blocking collectives  91.5 us (18%)
  matrix products  59.3 us (12%)
  other arithmetic  25.1 us (5%)
  starting transfers between devices  15.5 us (3%)
  between operations  15.5 us (3%)
    pallas_call x1, Pallas kernels, attn_backward(): pl.pallas_call(functools.partial(_bwd_kernel, scale), out_shape=shape, gr...  48.3 us
    pallas_call x1, Pallas kernels, attn_forward(): pl.pallas_call(functools.partial(_fwd_kernel, scale), out_shape=(jax.Shap...  44.5 us
    psum x1, blocking collectives, on_device(): lax.psum((grad_ln1_gain, grad_ln1_bias, grad_qv_bias, grad_out_bias, grad...  41.1 us
    all_gather x1, blocking collectives, on_device(): qkv_cols = lax.all_gather(qkv_weight, 'fsdp', axis=1, tiled=True)  35.2 us
    all_gather x1, waiting for transfers between devices, on_device(): normed_rows = lax.all_gather(normed_two, 'tp', axis=0, tiled=True)  27.8 us
    reduce_scatter x1, waiting for transfers between devices, on_device(): lax.psum_scatter(matmul_nt(grad_before, fc1_part).astype(jnp.bfloat16), '...  23.4 us
    all_to_all x1, waiting for transfers between devices, on_device(): grad_rows_all = lax.all_to_all(grad_all, 'tp', 0, 0, tiled=True)  22 us
    unnamed x80, local copies, waits for them, and re-layouts  17.2 us
  transfers between devices with their start and end apart: 12, of which 6 were waited for; matrix products, arithmetic and copies ran while one was open for 22% of the time, Pallas kernels for 19%

profile of v17, /device:TPU:0, one launch (start us, length us, event | category | flops | bytes accessed | tf_op | source)
XLA Modules:
  0.0 493.3 jit_solution(13409063985548119797)
XLA Ops:
  13.3 35.2 %all_gather.24 = bf16[3,768,192]{2,1,0:T(8,128)(2,1)S(1)} all-gather(bf16[3,96,192]{2,1,0:T(8,128)(2,1)S(1)} %copy-done.23), channel_id=1, replica_groups=mesh['fsdp'=8,'tp'=4] {'fsdp'}, dimensions={1}, use_global_device_ids=true | all-gather | bytes 995328 | tf_op jit(solution)/shard_map/all_gather | solution.py:209
  52.9 4.8 all-to-all-start
  59.6 4.6 convolution_bitcast_fusion
  76.2 4.8 fusion.13
  81.0 44.5 %shard_map.280 = (bf16[4,3,512,64]{3,2,1,0:T(8,128)(2,1)S(1)}, f32[3,2048,1]{2,1,0:T(8,128)}) custom-call(s32[1]{0:T(128)S(6)} %copy.136.prefix_ref, bf16[3,2048,64]{2,1,0:T(8,128)(2,1)S(1)} %get-tuple-element.144.q_ref, bf16[3,2048,64]{2,1,0:T(8,128)(2,1)S(1)} %bitcast.108, bf16[3,2048,64]{2,1,0:T(8,128)(2,1)} %get-tuple-element.145.v_ref), custom_call_target="tpu_custom_call" | custom-call | flops 3221225472 | bytes 3145728 | tf_op jit(solution)/shard_map/pallas_call | solution.py:135
  126.7 4.4 reshape.212
  157.2 15.2 %all_to_all.20 = bf16[4,3,512,64]{2,3,1,0:T(8,128)(2,1)S(1)} all-to-all(bf16[4,3,512,64]{2,3,1,0:T(8,128)(2,1)} %copy.88), channel_id=1, replica_groups=mesh['fsdp'=8,'tp'=4] {'tp'}, dimensions={0} | all-to-all | bytes 1572864 | tf_op jit(solution)/shard_map/all_to_all | solution.py:249
  177.8 27.8 %all-gather.14.cloned.1.call-done = bf16[2048,768]{1,0:T(8,128)(2,1)} async-done(((bf16[512,768]{1,0:T(8,128)(2,1)}), bf16[2048,768]{1,0:T(8,128)(2,1)}) %all-gather.14.cloned.1.call-update) | async-done | bytes 3145744 | tf_op jit(solution)/shard_map/all_gather | solution.py:264
  205.6 5.1 %fusion.29 = f32[2048,768]{1,0:T(8,128)S(1)} fusion(bf16[2048,768]{1,0:T(8,128)(2,1)} %all-gather.14.cloned.1.call-done, bf16[768,768]{1,0:T(8,128)(2,1)} %reshape_reshape.7), kind=kOutput, calls=%fused_computation.82 | convolution fusion | flops 2415919104 | bytes 10616832 | tf_op jit(solution)/shard_map/dot_general | solution.py:265
  210.7 7.9 %convert_reduce_fusion = (f32[768]{0:T(1024)S(1)}, bf16[2048,768]{1,0:T(8,128)(2,1)S(1)}, bf16[2048,768]{1,0:T(8,128)(2,1)}) fusion(f32[2048,768]{1,0:T(8,128)S(1)} %fusion.29, f32[768]{0:T(1024)S(1)} %dynamic_slice.7, bf16[2048,768]{1,0:T(8,128)(2,1)S(1)} %copy-done.31, bf16[768,768]{0,1:T(8,128)(2,1)S(1)} %bitcast.127), kind=kOutput, calls=%fused_computation.9 | convolution fusion | flops 2455239936 | bytes 16914432 | tf_op jit(solution)/shard_map/dot_general | solution.py:37
  220.4 4.0 convolution_convert_fusion.1
  224.7 6.8 %convolution_convert_fusion = bf16[2048,768]{1,0:T(8,128)(2,1)} fusion(bf16[2048,768]{1,0:T(8,128)(2,1)} %get-tuple-element.133, bf16[768,768]{0,1:T(8,128)(2,1)} %bitcast.126), kind=kOutput, calls=%fused_computation.16 | convolution fusion | flops 2417491968 | bytes 7471104 | tf_op jit(solution)/shard_map/dot_general | solution.py:267
  239.0 23.4 %reduce-scatter.4.cloned.1.call-done = bf16[512,768]{1,0:T(8,128)(2,1)} async-done(((bf16[2048,768]{1,0:T(8,128)(2,1)}), bf16[512,768]{1,0:T(8,128)(2,1)}) %reduce-scatter.4.cloned.1.call-update) | async-done | bytes 786448 | tf_op jit(solution)/shard_map/reduce_scatter | solution.py:278
  280.2 16.5 %all-gather.16.cloned.1.call-done = bf16[2048,768]{1,0:T(8,128)(2,1)} async-done(((bf16[512,768]{1,0:T(8,128)(2,1)}), bf16[2048,768]{1,0:T(8,128)(2,1)}) %all-gather.16.cloned.1.call-update) | async-done | bytes 3145744 | tf_op jit(solution)/shard_map/all_gather | solution.py:299
  296.8 4.6 all-to-all-start.2
  303.1 3.9 convolution_convert_fusion.2
  311.1 48.3 %shard_map.281 = bf16[4,3,3,512,64]{4,3,2,1,0:T(8,128)(2,1)} custom-call(s32[1]{0:T(128)S(6)} %copy.136.prefix_ref, bf16[3,2048,64]{2,1,0:T(8,128)(2,1)S(1)} %copy-done.3, bf16[3,2048,64]{2,1,0:T(8,128)(2,1)S(1)} %bitcast.109, bf16[3,2048,64]{2,1,0:T(8,128)(2,1)S(1)} %copy-done.4, bf16[3,2048,64]{2,1,0:T(8,128)(2,1)} %bitcast.124, ...), custom_call_target="tpu_custom_call" | custom-call | flops 8053063680 | bytes 6291456 | tf_op jit(solution)/shard_map/pallas_call | solution.py:162
  363.2 6.7 %reduce-scatter.6.cloned.1.call-done = bf16[192,768]{1,0:T(8,128)(2,1)} async-done(((bf16[1536,768]{1,0:T(8,128)(2,1)}), bf16[192,768]{1,0:T(8,128)(2,1)}) %reduce-scatter.6.cloned.1.call-update) | async-done | bytes 294928 | tf_op jit(solution)/shard_map/reduce_scatter | solution.py:307
  372.3 5.6 %fusion.7 = f32[3,3,64,768,1]{3,2,0,1,4:T(8,128)S(1)} fusion(bf16[4,512,768,1,1]{2,1,3,4,0:T(8,128)(2,1)} %bitcast.122, bf16[4,3,3,512,64]{4,3,2,1,0:T(8,128)(2,1)} %shard_map.281), kind=kOutput, calls=%fused_computation.12 | convolution fusion | flops 1811939328 | bytes 7274496 | tf_op jit(solution)/shard_map/trd,tkhre->kdhe/dot_general | solution.py:338
  395.8 6.1 %copy.94 = bf16[4,3,3,512,64]{3,4,2,1,0:T(8,128)(2,1)} copy(bf16[4,3,3,512,64]{4,3,2,1,0:T(8,128)(2,1)} %shard_map.281) | data formatting | bytes 4718592 | tf_op jit(solution)/shard_map/optimization_barrier | solution.py:317
  401.9 4.5 all-to-all-start.3
  413.0 22.0 %all-to-all-done.3 = bf16[4,3,3,512,64]{3,4,2,1,0:T(8,128)(2,1)} async-done(((bf16[4,3,3,512,64]{3,4,2,1,0:T(8,128)(2,1)}), bf16[4,3,3,512,64]{3,4,2,1,0:T(8,128)(2,1)}, u32[]{:S(2)}, u32[]{:S(2)}) %all-to-all-start.3) | async-done | bytes 2359328 | tf_op jit(solution)/shard_map/all_to_all | solution.py:341
  434.9 5.4 %fusion.16 = (f32[768]{0:T(1024)S(1)}, f32[512]{0:T(512)S(1)}, f32[512]{0:T(512)S(1)}, f32[768]{0:T(1024)S(1)}, f32[512,768,1,1,1]{1,0,4,3,2:T(8,128)S(1)}) fusion(f32[512,768]{1,0:T(8,128)S(1)} %copy-done.10, f32[512]{0:T(512)S(1)} %add_rsqrt_fusion.1, f32[512]{0:T(512)S(1)} %broadcast_multiply_fusion.5, f32[768]{0:T(1024)S(1)} %copy-done.26, ...), kind=kOutput, calls=%fused_computation.39 | convolution fusion | flops 1815475712 | bytes 9061376 | tf_op jit(solution)/shard_map/skhre,skdhe->rd/dot_general | solution.py:343
  441.8 41.1 %all-reduce = (f32[768]{0:T(1024)}, f32[768]{0:T(1024)}, f32[2,768]{1,0:T(2,128)}, f32[768]{0:T(1024)}, f32[768]{0:T(1024)}, /*index=5*/f32[768]{0:T(1024)}, f32[3072]{0:T(1024)}, f32[768]{0:T(1024)}, f32[5,768]{1,0:T(8,128)}) all-reduce(f32[768]{0:T(1024)S(1)} %get-tuple-element.110, ...), channel_id=1, replica_groups=mesh['fsdp'=8,'tp'=4] {'fsdp','tp'}, use_global_device_ids=true, to_apply=%region_13.0 | all-reduce | flops 13056 | bytes 104448 | tf_op jit(solution)/shard_map/psum | solution.py:379
  (183 shorter events, 124.5 us)
Async XLA Ops:
  7.2 4.0 copy-start.26
  7.2 42.0 %all-gather.8.cloned.1.call-start = ((), (), s32[]{:S(2)}) async-start(), calls=%async_computation.7 | async-start | bytes 3932160 | tf_op jit(solution)/shard_map/all_gather | solution.py:218
  12.4 114.2 %all-gather.18.cloned.1.call-start = ((), (), s32[]{:S(2)}) async-start(), calls=%async_computation.15 | async-start | bytes 2985984 | tf_op jit(solution)/shard_map/all_gather | solution.py:223
  49.3 103.8 %all-gather.10.cloned.1.call-start = ((), (), s32[]{:S(2)}) async-start(), calls=%async_computation.8 | async-start | bytes 3932160 | tf_op jit(solution)/shard_map/all_gather | solution.py:226
  52.9 73.8 %all-to-all-start = ((bf16[4,3,768,192]{2,3,1,0:T(8,128)(2,1)}), bf16[4,3,768,192]{2,3,1,0:T(8,128)(2,1)}, u32[]{:S(2)}, u32[]{:S(2)}) async-start(bf16[4,3,768,192]{2,3,1,0:T(8,128)(2,1)} %broadcast_in_dim.6), calls=%async_computation | async-start | bytes 7077888 | tf_op jit(solution)/shard_map/all_to_all | solution.py:225
  57.6 98.2 %all-gather.12.cloned.1.call-start = ((), (), s32[]{:S(2)}) async-start(), calls=%async_computation.9 | async-start | bytes 1474560 | tf_op jit(solution)/shard_map/all_gather | solution.py:245
  137.3 68.3 %all-gather.14.cloned.1.call-start = ((), (), s32[]{:S(2)}) async-start(), calls=%async_computation.10 | async-start | bytes 3932160 | tf_op jit(solution)/shard_map/all_gather | solution.py:264
  155.8 16.6 %copy-start.34 = (f32[768]{0:T(1024)S(1)}, f32[768]{0:T(1024)}, u32[]{:S(2)}) copy-start(f32[768]{0:T(1024)} %param.28) | copy-start | bytes 9220
  157.2 15.2 %copy-start.9 = (f32[512,768]{1,0:T(8,128)S(1)}, f32[512,768]{1,0:T(8,128)}, u32[]{:S(2)}) copy-start(f32[512,768]{1,0:T(8,128)} %copy-done.8) | copy-start | bytes 4718596
  177.0 85.5 %reduce-scatter.4.cloned.1.call-start = ((), (), s32[]{:S(2)}) async-start(), calls=%async_computation.11 | async-start | bytes 3932160 | tf_op jit(solution)/shard_map/reduce_scatter | solution.py:278
  205.6 5.1 %copy-start.20 = (bf16[768,8,96]{0,2,1:T(8,128)(2,1)S(1)}, bf16[768,8,96]{0,2,1:T(8,128)(2,1)}, u32[]{:S(2)}) copy-start(bf16[768,8,96]{0,2,1:T(8,128)(2,1)} %copy.87) | copy-start | bytes 3538948
  205.6 5.1 %copy-start.31 = (bf16[2048,768]{1,0:T(8,128)(2,1)S(1)}, bf16[2048,768]{1,0:T(8,128)(2,1)}, u32[]{:S(2)}) copy-start(bf16[2048,768]{1,0:T(8,128)(2,1)} %all-gather.10.cloned.1.call-done) | copy-start | bytes 9437188
  210.7 9.7 %copy-start.18 = (bf16[768,768]{1,0:T(8,128)(2,1)S(1)}, bf16[768,768]{1,0:T(8,128)(2,1)}, u32[]{:S(2)}) copy-start(bf16[768,768]{1,0:T(8,128)(2,1)} %reshape_reshape.7) | copy-start | bytes 3538948
  224.4 72.3 %all-gather.16.cloned.1.call-start = ((), (), s32[]{:S(2)}) async-start(), calls=%async_computation.12 | async-start | bytes 3932160 | tf_op jit(solution)/shard_map/all_gather | solution.py:299
  224.6 6.8 %copy-start.32 = (bf16[2048,768]{1,0:T(8,128)(2,1)S(1)}, bf16[2048,768]{1,0:T(8,128)(2,1)}, u32[]{:S(2)}) copy-start(bf16[2048,768]{1,0:T(8,128)(2,1)} %all-gather.10.cloned.1.call-done) | copy-start | bytes 9437188
  224.7 6.8 %copy-start.37 = (bf16[2048,768]{1,0:T(8,128)(2,1)S(1)}, bf16[2048,768]{1,0:T(8,128)(2,1)}, u32[]{:S(2)}) copy-start(bf16[2048,768]{1,0:T(8,128)(2,1)} %get-tuple-element.133) | copy-start | bytes 9437188
  268.1 101.8 %reduce-scatter.6.cloned.1.call-start = ((), (), s32[]{:S(2)}) async-start(), calls=%async_computation.13 | async-start | bytes 2654208 | tf_op jit(solution)/shard_map/reduce_scatter | solution.py:307
  296.8 62.6 %all-to-all-start.2 = ((bf16[4,512,768]{2,1,0:T(8,128)(2,1)}), bf16[4,512,768]{2,1,0:T(8,128)(2,1)}, u32[]{:S(2)}, u32[]{:S(2)}) async-start(bf16[4,512,768]{2,1,0:T(8,128)(2,1)} %bitcast.118), calls=%async_computation.3 | async-start | bytes 6291456 | tf_op jit(solution)/shard_map/all_to_all | solution.py:303
  301.4 181.5 %reduce-scatter.8.cloned.1.call-start = ((), (), s32[]{:S(2)}) async-start(), calls=%async_computation.14 | async-start | bytes 2654208 | tf_op jit(solution)/shard_map/reduce_scatter | solution.py:369
  401.9 33.0 %all-to-all-start.3 = ((bf16[4,3,3,512,64]{3,4,2,1,0:T(8,128)(2,1)}), bf16[4,3,3,512,64]{3,4,2,1,0:T(8,128)(2,1)}, u32[]{:S(2)}, u32[]{:S(2)}) async-start(bf16[4,3,3,512,64]{3,4,2,1,0:T(8,128)(2,1)} %copy.94), calls=%async_computation.5 | async-start | bytes 4718592 | tf_op jit(solution)/shard_map/all_to_all | solution.py:341
  409.5 25.5 %copy-start.10 = (f32[512,768]{1,0:T(8,128)S(1)}, f32[512,768]{1,0:T(8,128)}, u32[]{:S(2)}) copy-start(f32[512,768]{1,0:T(8,128)} %copy-done.8) | copy-start | bytes 4718596
  434.9 5.5 %copy-start.12 = (f32[512,768]{1,0:T(8,128)S(1)}, f32[512,768]{1,0:T(8,128)}, u32[]{:S(2)}) copy-start(f32[512,768]{1,0:T(8,128)} %copy-done.11) | copy-start | bytes 4718596
  440.4 45.9 %copy-start.1 = (f32[5,768]{1,0:T(8,128)S(1)}, f32[5,768]{1,0:T(8,128)}, u32[]{:S(2)}) copy-start(f32[5,768]{1,0:T(8,128)} %param.33) | copy-start | bytes 46084
  441.1 45.3 %copy-start.13 = (f32[512,768]{1,0:T(8,128)}, f32[512,768]{1,0:T(8,128)S(1)}, u32[]{:S(2)}) copy-start(f32[512,768]{1,0:T(8,128)S(1)} %multiply_add_fusion) | copy-start | bytes 4718596
  (26 other events, 49.4 us)
Sparse Core Ops, SparseCore 0:
  12.6 31.2 all-gather.7
  49.4 55.5 all-gather.17
  106.5 27.0 all-gather.9
  137.4 18.3 all-gather.11
  177.1 28.4 all-gather.13
  224.5 37.8 reduce-scatter.3
  268.2 28.4 all-gather.15
  300.2 69.5 reduce-scatter.5
  396.0 68.8 reduce-scatter.7

commit v18 on v16

--- a/solution.py
+++ b/solution.py
@@ -365,8 +365,8 @@
     )
     tail_packed = jnp.concatenate([g.reshape(fsdp_count, -1, width) for g in tail_grads], axis=1)
     tail_summed = lax.psum_scatter(
-        tail_packed.reshape(-1, width), "fsdp", scatter_dimension=0, tiled=True
-    ).reshape(-1)
+        tail_packed.reshape(-1, width).astype(jnp.bfloat16), "fsdp", scatter_dimension=0, tiled=True
+    ).reshape(-1).astype(jnp.float32)
     tail_shards = []
     offset = 0
     for g in tail_grads:

time: 494 us -> 484 us (0.980)
  local copies, waits for them, and re-layouts: 94.3 us -> 88.8 us
    all_to_all x1, waiting for transfers between devices: 22.1 us -> 3.66 us  [on_device(): grad_rows_all = lax.all_to_all(grad_all, 'tp', 0, 0, tiled=True)]
    reduce_scatter x1, waiting for transfers between devices: 0.01 us -> 9.53 us  [on_device(): lax.psum_scatter(tail_packed.reshape(-1, width).astype(jnp.bfloat16), 'fs...]
    reduce_scatter x1, waiting for transfers between devices: 0.01 us -> 6.64 us  [on_device(): lax.psum_scatter(dense_packed.reshape(-1, width), 'fsdp', scatter_dimensi...]
    unnamed x78 -> x82, local copies, waits for them, and re-layouts: 15.2 us -> 17.6 us
  transfers between devices with their start and end apart: 12 -> 12, of which waited for: 5 -> 7; matrix products, arithmetic and copies ran while one was open for 24% -> 25% of each run, Pallas kernels for 19% -> 19%
where the time goes in v18:
time: 484 us; the launch traced here: 479 us
  Pallas kernels  92.9 us (19%)
  waiting for transfers between devices  91.6 us (19%)
  blocking collectives  91.3 us (19%)
  local copies, waits for them, and re-layouts  88.8 us (18%)
  matrix products  59.1 us (12%)
  other arithmetic  24.3 us (5%)
  starting transfers between devices  15.9 us (3%)
  between operations  15.3 us (3%)
    pallas_call x1, Pallas kernels, attn_backward(): pl.pallas_call(functools.partial(_bwd_kernel, scale), out_shape=shape, gr...  48.3 us
    pallas_call x1, Pallas kernels, attn_forward(): pl.pallas_call(functools.partial(_fwd_kernel, scale), out_shape=(jax.Shap...  44.5 us
    psum x1, blocking collectives, on_device(): lax.psum((grad_ln1_gain, grad_ln1_bias, grad_qv_bias, grad_out_bias, grad...  40.9 us
    all_gather x1, blocking collectives, on_device(): qkv_cols = lax.all_gather(qkv_weight, 'fsdp', axis=1, tiled=True)  35.2 us
    all_gather x1, waiting for transfers between devices, on_device(): normed_rows = lax.all_gather(normed_two, 'tp', axis=0, tiled=True)  27.8 us
    reduce_scatter x1, waiting for transfers between devices, on_device(): lax.psum_scatter(matmul_nt(grad_before, fc1_part).astype(jnp.bfloat16), '...  23.4 us
    unnamed x82, local copies, waits for them, and re-layouts  17.6 us
    all_gather x1, waiting for transfers between devices, on_device(): lax.all_gather(grad_middle.astype(jnp.bfloat16), 'tp', axis=0, tiled=True)  16.6 us
  transfers between devices with their start and end apart: 12, of which 7 were waited for; matrix products, arithmetic and copies ran while one was open for 25% of the time, Pallas kernels for 19%

profile of v18, /device:TPU:0, one launch (start us, length us, event | category | flops | bytes accessed | tf_op | source)
XLA Modules:
  0.0 479.3 jit_solution(4978852711337257646)
XLA Ops:
  13.3 35.2 %all_gather.24 = bf16[3,768,192]{2,1,0:T(8,128)(2,1)S(1)} all-gather(bf16[3,96,192]{2,1,0:T(8,128)(2,1)S(1)} %copy-done.22), channel_id=1, replica_groups=mesh['fsdp'=8,'tp'=4] {'fsdp'}, dimensions={1}, use_global_device_ids=true | all-gather | bytes 995328 | tf_op jit(solution)/shard_map/all_gather | solution.py:209
  52.9 4.8 all-to-all-start
  59.9 4.6 convolution_bitcast_fusion
  76.4 4.8 %fusion.13 = (bf16[3,2048,64]{2,1,0:T(8,128)(2,1)S(1)}, bf16[3,2048,64]{2,1,0:T(8,128)(2,1)}) fusion(f32[2048,3,64]{2,0,1:T(8,128)} %copy.82, f32[3,64]{1,0:T(4,128)S(1)} %add.139, f32[2048,3,64]{2,0,1:T(8,128)} %copy.84, f32[3,64]{1,0:T(4,128)S(1)} %add.142), kind=kLoop, calls=%fused_computation.30 | loop fusion | flops 1572864 | bytes 4720128 | tf_op jit(solution)/shard_map/transpose | solution.py:231
  81.3 44.5 %shard_map.280 = (bf16[4,3,512,64]{3,2,1,0:T(8,128)(2,1)S(1)}, f32[3,2048,1]{2,1,0:T(8,128)}) custom-call(s32[1]{0:T(128)S(6)} %copy.138.prefix_ref, bf16[3,2048,64]{2,1,0:T(8,128)(2,1)S(1)} %get-tuple-element.142.q_ref, bf16[3,2048,64]{2,1,0:T(8,128)(2,1)S(1)} %bitcast.115, bf16[3,2048,64]{2,1,0:T(8,128)(2,1)} %get-tuple-element.143.v_ref), custom_call_target="tpu_custom_call" | custom-call | flops 3221225472 | bytes 3145728 | tf_op jit(solution)/shard_map/pallas_call | solution.py:135
  127.0 4.5 reshape.214
  157.6 15.2 %all_to_all.20 = bf16[4,3,512,64]{2,3,1,0:T(8,128)(2,1)S(1)} all-to-all(bf16[4,3,512,64]{2,3,1,0:T(8,128)(2,1)} %copy.88), channel_id=1, replica_groups=mesh['fsdp'=8,'tp'=4] {'tp'}, dimensions={0} | all-to-all | bytes 1572864 | tf_op jit(solution)/shard_map/all_to_all | solution.py:249
  178.3 27.8 %all-gather.14.cloned.1.call-done = bf16[2048,768]{1,0:T(8,128)(2,1)} async-done(((bf16[512,768]{1,0:T(8,128)(2,1)}), bf16[2048,768]{1,0:T(8,128)(2,1)}) %all-gather.14.cloned.1.call-update) | async-done | bytes 3145744 | tf_op jit(solution)/shard_map/all_gather | solution.py:264
  206.1 5.1 %fusion.32 = f32[2048,768]{1,0:T(8,128)S(1)} fusion(bf16[2048,768]{1,0:T(8,128)(2,1)} %all-gather.14.cloned.1.call-done, bf16[768,768]{1,0:T(8,128)(2,1)} %reshape_reshape.8), kind=kOutput, calls=%fused_computation.87 | convolution fusion | flops 2415919104 | bytes 10616832 | tf_op jit(solution)/shard_map/dot_general | solution.py:265
  211.2 7.9 %convert_reduce_fusion = (f32[768]{0:T(1024)S(1)}, bf16[2048,768]{1,0:T(8,128)(2,1)S(1)}, bf16[2048,768]{1,0:T(8,128)(2,1)}) fusion(f32[2048,768]{1,0:T(8,128)S(1)} %fusion.32, f32[768]{0:T(1024)S(1)} %dynamic_slice.7, bf16[2048,768]{1,0:T(8,128)(2,1)S(1)} %copy-done.30, bf16[768,768]{0,1:T(8,128)(2,1)S(1)} %bitcast.136), kind=kOutput, calls=%fused_computation.9 | convolution fusion | flops 2455239936 | bytes 16914432 | tf_op jit(solution)/shard_map/dot_general | solution.py:37
  220.9 4.0 convolution_convert_fusion.1
  225.2 6.8 %convolution_convert_fusion = bf16[2048,768]{1,0:T(8,128)(2,1)} fusion(bf16[2048,768]{1,0:T(8,128)(2,1)} %get-tuple-element.131, bf16[768,768]{0,1:T(8,128)(2,1)} %bitcast.135), kind=kOutput, calls=%fused_computation.16 | convolution fusion | flops 2417491968 | bytes 7471104 | tf_op jit(solution)/shard_map/dot_general | solution.py:267
  239.5 23.4 %reduce-scatter.4.cloned.1.call-done = bf16[512,768]{1,0:T(8,128)(2,1)} async-done(((bf16[2048,768]{1,0:T(8,128)(2,1)}), bf16[512,768]{1,0:T(8,128)(2,1)}) %reduce-scatter.4.cloned.1.call-update) | async-done | bytes 786448 | tf_op jit(solution)/shard_map/reduce_scatter | solution.py:278
  280.6 16.6 %all-gather.16.cloned.1.call-done = bf16[2048,768]{1,0:T(8,128)(2,1)} async-done(((bf16[512,768]{1,0:T(8,128)(2,1)}), bf16[2048,768]{1,0:T(8,128)(2,1)}) %all-gather.16.cloned.1.call-update) | async-done | bytes 3145744 | tf_op jit(solution)/shard_map/all_gather | solution.py:299
  297.2 5.2 %all-to-all-start.2 = ((bf16[4,512,768]{2,1,0:T(8,128)(2,1)}), bf16[4,512,768]{2,1,0:T(8,128)(2,1)}, u32[]{:S(2)}, u32[]{:S(2)}) async-start(bf16[4,512,768]{2,1,0:T(8,128)(2,1)} %bitcast.128), calls=%async_computation.3 | async-start | bytes 6291456 | tf_op jit(solution)/shard_map/all_to_all | solution.py:303
  302.4 3.9 convolution_convert_fusion.2
  311.7 48.3 %shard_map.281 = bf16[4,3,3,512,64]{4,3,2,1,0:T(8,128)(2,1)} custom-call(s32[1]{0:T(128)S(6)} %copy.138.prefix_ref, bf16[3,2048,64]{2,1,0:T(8,128)(2,1)S(1)} %copy-done.3, bf16[3,2048,64]{2,1,0:T(8,128)(2,1)S(1)} %bitcast.116, bf16[3,2048,64]{2,1,0:T(8,128)(2,1)S(1)} %copy-done.4, bf16[3,2048,64]{2,1,0:T(8,128)(2,1)} %bitcast.133, ...), custom_call_target="tpu_custom_call" | custom-call | flops 8053063680 | bytes 6291456 | tf_op jit(solution)/shard_map/pallas_call | solution.py:162
  363.8 6.6 %reduce-scatter.6.cloned.1.call-done = bf16[192,768]{1,0:T(8,128)(2,1)} async-done(((bf16[1536,768]{1,0:T(8,128)(2,1)}), bf16[192,768]{1,0:T(8,128)(2,1)}) %reduce-scatter.6.cloned.1.call-update) | async-done | bytes 294928 | tf_op jit(solution)/shard_map/reduce_scatter | solution.py:313
  372.9 6.1 %copy.94 = bf16[4,3,3,512,64]{3,4,2,1,0:T(8,128)(2,1)} copy(bf16[4,3,3,512,64]{4,3,2,1,0:T(8,128)(2,1)} %shard_map.281) | data formatting | bytes 4718592 | tf_op jit(solution)/shard_map/optimization_barrier | solution.py:323
  378.9 4.5 all-to-all-start.3
  393.0 5.7 %fusion.7 = bf16[3,3,64,768,1]{3,2,0,1,4:T(8,128)(2,1)S(1)} fusion(bf16[4,512,768,1,1]{2,1,3,4,0:T(8,128)(2,1)} %bitcast.127, bf16[4,3,3,512,64]{4,3,2,1,0:T(8,128)(2,1)} %shard_map.281), kind=kOutput, calls=%fused_computation.12 | convolution fusion | flops 1811939328 | bytes 6389760 | tf_op jit(solution)/shard_map/trd,tkhre->kdhe/dot_general | solution.py:336
  412.0 5.4 %fusion.16 = (f32[768]{0:T(1024)S(1)}, f32[512]{0:T(512)S(1)}, f32[512]{0:T(512)S(1)}, f32[768]{0:T(1024)S(1)}, f32[512,768,1,1,1]{1,0,4,3,2:T(8,128)S(1)}) fusion(f32[512,768]{1,0:T(8,128)S(1)} %copy-done.10, f32[512]{0:T(512)S(1)} %add_rsqrt_fusion.1, f32[512]{0:T(512)S(1)} %broadcast_multiply_fusion.5, f32[768]{0:T(1024)S(1)} %copy-done.25, ...), kind=kOutput, calls=%fused_computation.38 | convolution fusion | flops 1815475712 | bytes 9061376 | tf_op jit(solution)/shard_map/skhre,skdhe->rd/dot_general | solution.py:341
  418.8 40.9 %all-reduce = (f32[768]{0:T(1024)}, f32[768]{0:T(1024)}, f32[2,768]{1,0:T(2,128)}, f32[768]{0:T(1024)}, f32[768]{0:T(1024)}, /*index=5*/f32[768]{0:T(1024)}, f32[3072]{0:T(1024)}, f32[768]{0:T(1024)}, f32[5,768]{1,0:T(8,128)}) all-reduce(f32[768]{0:T(1024)S(1)} %get-tuple-element.108, ...), channel_id=1, replica_groups=mesh['fsdp'=8,'tp'=4] {'fsdp','tp'}, use_global_device_ids=true, to_apply=%region_13.0 | all-reduce | flops 13056 | bytes 104448 | tf_op jit(solution)/shard_map/psum | solution.py:377
  459.7 9.5 %reduce-scatter.8.cloned.1.call-done = bf16[96,768]{1,0:T(8,128)(2,1)} async-done(((bf16[768,768]{1,0:T(8,128)(2,1)}), bf16[96,768]{1,0:T(8,128)(2,1)}) %reduce-scatter.8.cloned.1.call-update) | async-done | bytes 147472 | tf_op jit(solution)/shard_map/reduce_scatter | solution.py:367
  (186 shorter events, 122.6 us)
Async XLA Ops:
  7.2 42.1 %all-gather.8.cloned.1.call-start = ((), (), s32[]{:S(2)}) async-start(), calls=%async_computation.7 | async-start | bytes 3932160 | tf_op jit(solution)/shard_map/all_gather | solution.py:218
  12.4 114.5 %all-gather.18.cloned.1.call-start = ((), (), s32[]{:S(2)}) async-start(), calls=%async_computation.15 | async-start | bytes 2985984 | tf_op jit(solution)/shard_map/all_gather | solution.py:223
  49.3 103.7 %all-gather.10.cloned.1.call-start = ((), (), s32[]{:S(2)}) async-start(), calls=%async_computation.8 | async-start | bytes 3932160 | tf_op jit(solution)/shard_map/all_gather | solution.py:226
  52.9 74.1 %all-to-all-start = ((bf16[4,3,768,192]{2,3,1,0:T(8,128)(2,1)}), bf16[4,3,768,192]{2,3,1,0:T(8,128)(2,1)}, u32[]{:S(2)}, u32[]{:S(2)}) async-start(bf16[4,3,768,192]{2,3,1,0:T(8,128)(2,1)} %broadcast_in_dim.6), calls=%async_computation | async-start | bytes 7077888 | tf_op jit(solution)/shard_map/all_to_all | solution.py:225
  57.6 98.6 %all-gather.12.cloned.1.call-start = ((), (), s32[]{:S(2)}) async-start(), calls=%async_computation.9 | async-start | bytes 1474560 | tf_op jit(solution)/shard_map/all_gather | solution.py:245
  137.6 68.5 %all-gather.14.cloned.1.call-start = ((), (), s32[]{:S(2)}) async-start(), calls=%async_computation.10 | async-start | bytes 3932160 | tf_op jit(solution)/shard_map/all_gather | solution.py:264
  156.2 16.6 %copy-start.33 = (f32[768]{0:T(1024)S(1)}, f32[768]{0:T(1024)}, u32[]{:S(2)}) copy-start(f32[768]{0:T(1024)} %param.28) | copy-start | bytes 9220
  157.6 15.2 %copy-start.9 = (f32[512,768]{1,0:T(8,128)S(1)}, f32[512,768]{1,0:T(8,128)}, u32[]{:S(2)}) copy-start(f32[512,768]{1,0:T(8,128)} %copy-done.8) | copy-start | bytes 4718596
  177.4 85.5 %reduce-scatter.4.cloned.1.call-start = ((), (), s32[]{:S(2)}) async-start(), calls=%async_computation.11 | async-start | bytes 3932160 | tf_op jit(solution)/shard_map/reduce_scatter | solution.py:278
  211.2 9.7 %copy-start.17 = (bf16[768,768]{1,0:T(8,128)(2,1)S(1)}, bf16[768,768]{1,0:T(8,128)(2,1)}, u32[]{:S(2)}) copy-start(bf16[768,768]{1,0:T(8,128)(2,1)} %reshape_reshape.8) | copy-start | bytes 3538948
  224.9 72.3 %all-gather.16.cloned.1.call-start = ((), (), s32[]{:S(2)}) async-start(), calls=%async_computation.12 | async-start | bytes 3932160 | tf_op jit(solution)/shard_map/all_gather | solution.py:299
  225.2 6.8 %copy-start.31 = (bf16[2048,768]{1,0:T(8,128)(2,1)S(1)}, bf16[2048,768]{1,0:T(8,128)(2,1)}, u32[]{:S(2)}) copy-start(bf16[2048,768]{1,0:T(8,128)(2,1)} %all-gather.10.cloned.1.call-done) | copy-start | bytes 9437188
  225.2 6.8 %copy-start.36 = (bf16[2048,768]{1,0:T(8,128)(2,1)S(1)}, bf16[2048,768]{1,0:T(8,128)(2,1)}, u32[]{:S(2)}) copy-start(bf16[2048,768]{1,0:T(8,128)(2,1)} %get-tuple-element.131) | copy-start | bytes 9437188
  268.5 101.9 %reduce-scatter.6.cloned.1.call-start = ((), (), s32[]{:S(2)}) async-start(), calls=%async_computation.13 | async-start | bytes 2654208 | tf_op jit(solution)/shard_map/reduce_scatter | solution.py:313
  297.2 5.2 %copy-start.18 = (bf16[192,768]{1,0:T(8,128)(2,1)S(1)}, bf16[192,768]{1,0:T(8,128)(2,1)}, u32[]{:S(2)}) copy-start(bf16[192,768]{1,0:T(8,128)(2,1)} %reshape.196) | copy-start | bytes 884740
  297.2 62.8 %all-to-all-start.2 = ((bf16[4,512,768]{2,1,0:T(8,128)(2,1)}), bf16[4,512,768]{2,1,0:T(8,128)(2,1)}, u32[]{:S(2)}, u32[]{:S(2)}) async-start(bf16[4,512,768]{2,1,0:T(8,128)(2,1)} %bitcast.128), calls=%async_computation.3 | async-start | bytes 6291456 | tf_op jit(solution)/shard_map/all_to_all | solution.py:303
  378.9 33.1 %all-to-all-start.3 = ((bf16[4,3,3,512,64]{3,4,2,1,0:T(8,128)(2,1)}), bf16[4,3,3,512,64]{3,4,2,1,0:T(8,128)(2,1)}, u32[]{:S(2)}, u32[]{:S(2)}) async-start(bf16[4,3,3,512,64]{3,4,2,1,0:T(8,128)(2,1)} %copy.94), calls=%async_computation.5 | async-start | bytes 4718592 | tf_op jit(solution)/shard_map/all_to_all | solution.py:339
  383.4 85.8 %reduce-scatter.8.cloned.1.call-start = ((), (), s32[]{:S(2)}) async-start(), calls=%async_computation.14 | async-start | bytes 1327104 | tf_op jit(solution)/shard_map/reduce_scatter | solution.py:367
  391.6 7.2 %slice-start = ((s8[4718592]{0:T(1024)(128)(4,1)}), s8[524288]{0:T(1024)(128)(4,1)S(1)}, s32[]{:S(2)}) async-start(s8[4718592]{0:T(1024)(128)(4,1)} %bitcast.117), calls=%async_computation.16 | async-start | bytes 1048576
  393.0 5.8 %slice-start.1 = ((s8[4718592]{0:T(1024)(128)(4,1)}), s8[4194304]{0:T(1024)(128)(4,1)S(1)}, s32[]{:S(2)}) async-start(s8[4718592]{0:T(1024)(128)(4,1)} %bitcast.117), calls=%async_computation.17 | async-start | bytes 8388608
  404.6 7.4 %copy-start.10 = (f32[512,768]{1,0:T(8,128)S(1)}, f32[512,768]{1,0:T(8,128)}, u32[]{:S(2)}) copy-start(f32[512,768]{1,0:T(8,128)} %copy-done.8) | copy-start | bytes 4718596
  412.0 5.4 %copy-start.12 = (f32[512,768]{1,0:T(8,128)S(1)}, f32[512,768]{1,0:T(8,128)}, u32[]{:S(2)}) copy-start(f32[512,768]{1,0:T(8,128)} %copy-done.11) | copy-start | bytes 4718596
  417.4 55.1 %copy-start.1 = (f32[5,768]{1,0:T(8,128)S(1)}, f32[5,768]{1,0:T(8,128)}, u32[]{:S(2)}) copy-start(f32[5,768]{1,0:T(8,128)} %param.33) | copy-start | bytes 46084
  418.1 54.4 %copy-start.13 = (f32[512,768]{1,0:T(8,128)}, f32[512,768]{1,0:T(8,128)S(1)}, u32[]{:S(2)}) copy-start(f32[512,768]{1,0:T(8,128)S(1)} %multiply_add_fusion) | copy-start | bytes 4718596
  (27 other events, 56.6 us)
Sparse Core Ops, SparseCore 0:
  12.6 31.2 all-gather.7
  49.4 55.5 all-gather.17
  106.5 27.1 all-gather.9
  137.7 18.4 all-gather.11
  177.6 28.4 all-gather.13
  225.0 37.8 reduce-scatter.3
  268.6 28.4 all-gather.15
  300.7 69.6 reduce-scatter.5
  404.6 64.5 reduce-scatter.7
